TPU v7x, 32 devices: a whole 2x2x4 slice. The times are simulated.
32 devices in a mesh: groups: 2 (over x), tm: 16 (over z, y, core).
Axes of the slice: x: 2, y: 2, z: 4, core: 2. Of those that a mesh axis runs over, the one named last changes fastest.
Arguments:
- queries: bfloat16 [6144, 2560], P(('groups', 'tm')), parts along dimension 0, may hold values from -6 to 6
- keys: bfloat16 [6144, 2560], P(('groups', 'tm')), parts along dimension 0, may hold values from -6 to 6
- values: bfloat16 [6144, 2560], P(('groups', 'tm')), parts along dimension 0, may hold values from -6 to 6
- q_gain: float32 [2560], replicated, may hold values from 0.5 to 1.5
- k_gain: float32 [2560], replicated, may hold values from 0.5 to 1.5
- out_weight: bfloat16 [2560, 5120], P('tm'), may hold values from -0.125 to 0.125
- out_gate: float32 [5120], replicated, may hold values from 0.5 to 2
- reach: int32 [32, 2], P(('groups', 'tm')), parts along dimension 0, may hold values from 0 to 1
Outputs:
- mixed: bfloat16 [6144, 5120], P(('groups', 'tm')), parts along dimension 0
There are 2 independent parts, one for each index of `groups`. A program takes and returns all parts, laid end to end along the dimension named above; an argument that names none is the same for every part. Nothing has to cross between parts.
Inputs may be any that keep to these rules, and one draw needn't show every extreme that they name: `reach`: requests past the first or last tile are ignored.
All inputs are finite; a program needn't handle non-finite values.
Results may differ from a plain program's by a relative error of at most 0.0076.
Values may be sent and summed in bfloat16 or wider, within the bound.
No kernel may reach another device: no remote copies, remote signals or barrier semaphores. Data moves between devices by JAX's collectives and lax.ppermute only.
A program may use at most 128 MiB of HBM per device.

v0:
```python
import functools

import jax
import jax.numpy as jnp
from jax import lax
from jax.experimental import pallas as pl
from jax.experimental.pallas import tpu as pltpu
from jax.sharding import PartitionSpec as P


HD = 128


def whole(count):
    return [pl.BlockSpec(memory_space=pltpu.VMEM)] * count


def prepare_kernel(q_ref, k_ref, v_ref, qg_ref, kg_ref, qn_ref, *kv_refs):
    def scaled(ref, gain_ref):
        block = ref[...].astype(jnp.float32)
        inverse = lax.rsqrt(jnp.mean(block * block, axis=-1, keepdims=True) + 1e-06)
        return (block * inverse * gain_ref[...]).astype(jnp.bfloat16)

    wide = kv_refs[0].shape[1] // 2
    kn = scaled(k_ref, kg_ref)
    for i, kv_ref in enumerate(kv_refs):
        kv_ref[:, :wide] = kn[:, i * wide : (i + 1) * wide]
        kv_ref[:, wide:] = v_ref[:, i * wide : (i + 1) * wide]
    qn_ref[...] = scaled(q_ref, qg_ref)


def prepare(queries, keys, values, q_gain, k_gain, chunks):
    rows, chans = queries.shape
    kv = jax.ShapeDtypeStruct((rows, 2 * chans // chunks), jnp.bfloat16)
    return pl.pallas_call(
        prepare_kernel,
        out_shape=[jax.ShapeDtypeStruct((rows, chans), jnp.bfloat16)] + [kv] * chunks,
        in_specs=whole(5),
        out_specs=whole(1 + chunks),
        name="prepare",
    )(queries, keys, values, q_gain.reshape(1, chans), k_gain.reshape(1, chans))


def attend_kernel(seen_ref, q_ref, kb_ref, k_ref, ka_ref, vb_ref, v_ref, va_ref, o_ref):
    scale = HD ** (-0.5)
    bias = [(1.0 - seen_ref[i].astype(jnp.float32)) * -1e30 for i in range(2)]
    for h in range(q_ref.shape[1] // HD):
        at = slice(h * HD, (h + 1) * HD)
        query = q_ref[:, at]
        parts = []
        for ref, extra in ((kb_ref, bias[0]), (k_ref, None), (ka_ref, bias[1])):
            part = lax.dot_general(query, ref[:, at], (((1,), (1,)), ((), ())), preferred_element_type=jnp.float32)
            part = part * scale
            parts.append(part if extra is None else part + extra)
        top = functools.reduce(jnp.maximum, [jnp.max(part, axis=-1, keepdims=True) for part in parts])
        expo = [jnp.exp(part - top) for part in parts]
        total = functools.reduce(jnp.add, [jnp.sum(part, axis=-1, keepdims=True) for part in expo])
        share = 1.0 / total
        out = None
        for part, ref in zip(expo, (vb_ref, v_ref, va_ref)):
            weights = (part * share).astype(jnp.bfloat16)
            term = jnp.dot(weights, ref[:, at], preferred_element_type=jnp.float32)
            out = term if out is None else out + term
        o_ref[:, at] = out.astype(jnp.bfloat16)


def attend(seen, qn, before, kv, after, chunk, chunks):
    rows, chans = qn.shape
    wide = chans // chunks
    heads = wide // HD
    step = next(n for n in (5, 4, 3, 2, 1) if heads % n == 0)
    cols = step * HD
    steps = wide // cols
    q_spec = pl.BlockSpec((rows, cols), lambda i: (0, chunk * steps + i))
    k_spec = pl.BlockSpec((rows, cols), lambda i: (0, i))
    v_spec = pl.BlockSpec((rows, cols), lambda i: (0, steps + i))
    return pl.pallas_call(
        attend_kernel,
        grid=(steps,),
        out_shape=jax.ShapeDtypeStruct((rows, wide), jnp.bfloat16),
        in_specs=[pl.BlockSpec(memory_space=pltpu.SMEM), q_spec] + [k_spec] * 3 + [v_spec] * 3,
        out_specs=pl.BlockSpec((rows, cols), lambda i: (0, i)),
    )(seen, qn, before, kv, after, before, kv, after)


def project_kernel(count, starts_ref, gate_ref, *refs):
    slots = starts_ref.shape[0]
    att_refs, w_refs = refs[:count], refs[count : count + slots]
    outs = refs[count + slots : count + slots + 4]
    a_ref, w_ref, sems = refs[count + slots + 4 :]
    rows, wide = att_refs[0].shape
    depth = w_refs[0].shape[0]
    chunks = count // 4
    copies = []
    for i, ref in enumerate(w_refs):
        start = pl.multiple_of(starts_ref[i], depth)
        copies.append(pltpu.make_async_copy(ref, w_ref.at[pl.ds(start, depth)], sems.at[i]))
    for i, ref in enumerate(att_refs):
        p, j = i // chunks, i % chunks
        dst = a_ref.at[pl.ds(p * rows, rows), pl.ds(j * wide, wide)]
        copies.append(pltpu.make_async_copy(ref, dst, sems.at[slots + i]))
    for copy in copies:
        copy.start()
    for copy in copies:
        copy.wait()
    for p in range(4):
        acc = jnp.dot(a_ref[p * rows : (p + 1) * rows, :], w_ref[...], preferred_element_type=jnp.float32)
        outs[p][...] = (gate_ref[...] * acc).astype(jnp.bfloat16)


def project(starts, gate, att, weights):
    rows, wide = att[0].shape
    chans = wide * len(att) // 4
    cols = weights[0].shape[1]
    slots = len(weights)
    anywhere = pl.BlockSpec(memory_space=pl.ANY)
    return pl.pallas_call(
        functools.partial(project_kernel, len(att)),
        out_shape=[jax.ShapeDtypeStruct((rows, cols), jnp.bfloat16)] * 4,
        in_specs=[pl.BlockSpec(memory_space=pltpu.SMEM)] + whole(1) + [anywhere] * (len(att) + slots),
        out_specs=whole(4),
        scratch_shapes=[
            pltpu.VMEM((4 * rows, chans), jnp.bfloat16),
            pltpu.VMEM((chans, cols), jnp.bfloat16),
            pltpu.SemaphoreType.DMA((slots + len(att),)),
        ],
    )(starts, gate.reshape(1, cols), *att, *weights)


def place_kernel(starts_ref, *refs):
    pieces, out_ref, sems = refs[:-2], refs[-2], refs[-1]
    cols = pieces[0].shape[1]
    copies = []
    for i, ref in enumerate(pieces):
        start = pl.multiple_of(starts_ref[i], 128)
        copies.append(pltpu.make_async_copy(ref, out_ref.at[:, pl.ds(start, cols)], sems.at[i]))
    for copy in copies:
        copy.start()
    for copy in copies:
        copy.wait()


def place_pieces(starts, pieces):
    rows, cols = pieces[0].shape
    anywhere = pl.BlockSpec(memory_space=pl.ANY)
    return pl.pallas_call(
        place_kernel,
        out_shape=jax.ShapeDtypeStruct((rows, cols * len(pieces)), jnp.bfloat16),
        in_specs=[pl.BlockSpec(memory_space=pltpu.SMEM)] + [anywhere] * len(pieces),
        out_specs=anywhere,
        scratch_shapes=[pltpu.SemaphoreType.DMA((len(pieces),))],
        name="place",
    )(starts, *pieces)


def local(queries, keys, values, q_gain, k_gain, out_weight, out_gate, reach):
    peers = lax.axis_size("tm")
    place = lax.axis_index("tm")
    group = lax.axis_index("groups")
    low = place % 4
    line = place // 4
    lines = peers // 4
    depth, width = out_weight.shape
    _, chans = queries.shape
    cols = width // 8
    chunks = 2 if chans // HD % 2 == 0 else 1

    def swap(x, bits):
        return lax.ppermute(x, "tm", [(i, i ^ bits) for i in range(peers)])

    def group_swap(x):
        return lax.ppermute(x, "groups", [(0, 1), (1, 0)])

    def along(x, moves):
        return lax.ppermute(x, "tm", [(4 * a + i, 4 * b + i) for a, b in moves for i in range(4)])

    def shifted(x, by):
        return lax.ppermute(x, "tm", [(i, i + by) for i in range(peers) if 0 <= i + by < peers])

    def choose(flag, a, b):
        return jnp.where(flag, a, b)

    def column(quarter, share):
        return (quarter * 2 + share) * cols

    def weight_part(quarter):
        return lax.dynamic_slice_in_dim(out_weight, column(quarter, group), cols, 1)

    parts = [weight_part(low)] + [swap(weight_part(low ^ i), i) for i in (1, 2, 3)]
    odd, upper = (low % 2) == 1, low >= 2
    pairs = [
        jnp.concatenate([choose(odd, b, a), choose(odd, a, b)], axis=0)
        for a, b in ((parts[0], parts[1]), (parts[2], parts[3]))
    ]
    block = jnp.concatenate([choose(upper, pairs[1], pairs[0]), choose(upper, pairs[0], pairs[1])], axis=0)

    qn, *kvs = prepare(queries, keys, values, q_gain, k_gain, chunks)
    before = [shifted(kv, 1) for kv in kvs]
    after = [shifted(kv, -1) for kv in kvs]

    if lines == 4:
        middle = (line == 1) | (line == 2)
        near = along(block, ((0, 1), (1, 0), (2, 3), (3, 2)))
        across = along(block, ((1, 2), (2, 1)))
        across_far = along(near, ((1, 2), (2, 1)))
        edge = along(across, ((1, 0), (2, 3)))
        edge_far = along(across_far, ((1, 0), (2, 3)))
        second = choose(middle, across_far, edge)
        third = choose(middle, across, edge_far)
        slots = [block, near, second, third]
        starts = jnp.stack([(line ^ i) * (4 * depth) for i in range(4)]).astype(jnp.int32)
    else:
        members = [[z * 4 + i for z in range(lines)] for i in range(4)]
        slots = [lax.all_gather(block, "tm", axis_index_groups=members, axis=0, tiled=True)]
        starts = jnp.zeros((1,), jnp.int32)
    shares = [slots, [group_swap(slot) for slot in slots]]

    seen = jnp.stack([(reach[0, 0] == 1) & (place > 0), (reach[0, 1] == 1) & (place < peers - 1)]).astype(jnp.int32)
    att = [[None] * chunks for _ in range(4)]
    for i in range(chunks):
        own = attend(seen, qn, before[i], kvs[i], after[i], i, chunks)
        att[0][i] = own
        att[2][i] = swap(own, 2)
        att[1][i] = swap(own, 1)
        att[3][i] = swap(att[2][i], 1)
    att = [piece for pieces in att for piece in pieces]

    outs, columns = [], []
    for j in range(2):
        share = group ^ j
        gate = lax.dynamic_slice_in_dim(out_gate, column(low, share), cols, 0)
        made = project(starts, gate, att, shares[j])
        outs += [made[0]] + [swap(made[i], i) for i in (1, 2, 3)]
        columns += [column(low ^ i, share) for i in range(4)]
    return place_pieces(jnp.stack(columns).astype(jnp.int32), outs)


def solution(mesh):
    return jax.shard_map(
        local,
        mesh=mesh,
        in_specs=(
            P(("groups", "tm"), None),
            P(("groups", "tm"), None),
            P(("groups", "tm"), None),
            P(),
            P(),
            P("tm", None),
            P(),
            P(("groups", "tm"), None),
        ),
        out_specs=P(("groups", "tm"), None),
        check_vma=False,
    )
```

profile of v0, /device:TPU:11, one launch (start us, length us, event | category | flops | bytes accessed | tf_op | source)
XLA Modules:
  0.0 257.7 jit_solution(13952810300093912563)
XLA Ops:
  0.0 0.9 constant_dynamic-slice_fusion
  1.0 0.7 collective-permute-start.12
  1.7 1.1 collective-permute-done.12
  2.8 1.2 constant_dynamic-slice_fusion.2
  4.0 1.6 collective-permute-start.10
  5.8 5.6 %collective-permute-done.10 = bf16[160,640]{1,0:T(8,128)(2,1)S(1)} collective-permute-done((bf16[160,640]{1,0:T(8,128)(2,1)S(1)}, bf16[160,640]{1,0:T(8,128)(2,1)S(1)}, u32[]{:S(2)}, u32[]{:S(2)}) %collective-permute-start.10) | collective-permute-done | bytes 204832 | tf_op jit(solution)/shard_map/ppermute | solution.py:169
  11.4 4.1 %collective-permute-done.11 = bf16[160,640]{1,0:T(8,128)(2,1)S(1)} collective-permute-done((bf16[160,640]{1,0:T(8,128)(2,1)S(1)}, bf16[160,640]{1,0:T(8,128)(2,1)S(1)}, u32[]{:S(2)}, u32[]{:S(2)}) %collective-permute-start.11) | collective-permute-done | bytes 204832 | tf_op jit(solution)/shard_map/ppermute | solution.py:169
  15.7 1.0 pad_maximum_fusion.refs_8_
  18.1 4.0 %prepare.1 = (bf16[192,2560]{1,0:T(8,128)(2,1)}, bf16[192,2560]{1,0:T(8,128)(2,1)}, bf16[192,2560]{1,0:T(8,128)(2,1)}) custom-call(bf16[192,2560]{1,0:T(8,128)(2,1)} %q_ref.1, bf16[192,2560]{1,0:T(8,128)(2,1)} %k_ref.1, bf16[192,2560]{1,0:T(8,128)(2,1)} %v_ref.1, f32[1,2560]{1,0:T(1,128)} %reshape.17.qg_ref, f32[1,2560]{1,0:T(1,128)} %reshape.18.kg_ref), custom_call_target="tpu_custom_call" | custom-call | tf_op jit(solution)/shard_map/prepare/pallas_call | solution.py:35
  22.1 4.0 %collective-permute-start = (bf16[192,2560]{1,0:T(8,128)(2,1)}, bf16[192,2560]{1,0:T(8,128)(2,1)S(1)}, u32[]{:S(2)}, u32[]{:S(2)}) collective-permute-start(bf16[192,2560]{1,0:T(8,128)(2,1)} %get-tuple-element.17.k_ref.v_ref), channel_id=1, source_target_pairs={{0,1},{1,2},{2,3},{3,4},{4,5},{5,6},{6,7},{7,8},{8,9},{9,10},{10,1... | collective-permute-start | bytes 2949128 | tf_op jit(solution)/shard_map/ppermute | solution.py:178
  26.1 4.3 %collective-permute-start.15 = (bf16[640,640]{1,0:T(8,128)(2,1)}, bf16[640,640]{1,0:T(8,128)(2,1)}, u32[]{:S(2)}, u32[]{:S(2)}) collective-permute-start(bf16[640,640]{1,0:T(8,128)(2,1)} %pad_maximum_fusion.refs_8_), channel_id=1, source_target_pairs={{4,8},{5,9},{6,10},{7,11},{8,4},{9,5},{10,6},{11,7},{20,24},{21,25... | collective-permute-start | bytes 2457608 | tf_op jit(solution)/shard_map/ppermute | solution.py:175
  30.4 1.9 collective-permute-start.1
  32.4 3.8 %collective-permute-done.13.refs_9_ = bf16[640,640]{1,0:T(8,128)(2,1)} collective-permute-done((bf16[640,640]{1,0:T(8,128)(2,1)}, bf16[640,640]{1,0:T(8,128)(2,1)}, u32[]{:S(2)}, u32[]{:S(2)}) %collective-permute-start.13) | collective-permute-done | bytes 819232 | tf_op jit(solution)/shard_map/ppermute | solution.py:175
  36.1 3.2 %collective-permute-start.14 = (bf16[640,640]{1,0:T(8,128)(2,1)}, bf16[640,640]{1,0:T(8,128)(2,1)}, u32[]{:S(2)}, u32[]{:S(2)}) collective-permute-start(bf16[640,640]{1,0:T(8,128)(2,1)} %collective-permute-done.13.refs_9_), channel_id=1, source_target_pairs={{4,8},{5,9},{6,10},{7,11},{8,4},{9,5},{10,6},{11,7},{20,24},{21,25... | collective-permute-start | bytes 2457608 | tf_op jit(solution)/shard_map/ppermute | solution.py:175
  39.3 5.1 %collective-permute-start.2 = (bf16[192,2560]{1,0:T(8,128)(2,1)}, bf16[192,2560]{1,0:T(8,128)(2,1)S(1)}, u32[]{:S(2)}, u32[]{:S(2)}) collective-permute-start(bf16[192,2560]{1,0:T(8,128)(2,1)} %get-tuple-element.18.k_ref.v_ref), channel_id=1, source_target_pairs={{0,1},{1,2},{2,3},{3,4},{4,5},{5,6},{6,7},{7,8},{8,9},{9,10},{10,1... | collective-permute-start | bytes 2949128 | tf_op jit(solution)/shard_map/ppermute | solution.py:178
  44.5 6.6 %collective-permute-start.3 = (bf16[192,2560]{1,0:T(8,128)(2,1)}, bf16[192,2560]{1,0:T(8,128)(2,1)S(1)}, u32[]{:S(2)}, u32[]{:S(2)}) collective-permute-start(bf16[192,2560]{1,0:T(8,128)(2,1)} %get-tuple-element.18.k_ref.v_ref), channel_id=1, source_target_pairs={{1,0},{2,1},{3,2},{4,3},{5,4},{6,5},{7,6},{8,7},{9,8},{10,9},{11,1... | collective-permute-start | bytes 2949128 | tf_op jit(solution)/shard_map/ppermute | solution.py:178
  51.1 2.9 %collective-permute-start.16 = (bf16[640,640]{1,0:T(8,128)(2,1)}, bf16[640,640]{1,0:T(8,128)(2,1)}, u32[]{:S(2)}, u32[]{:S(2)}) collective-permute-start(bf16[640,640]{1,0:T(8,128)(2,1)} %collective-permute-done.15), channel_id=1, source_target_pairs={{4,0},{5,1},{6,2},{7,3},{8,12},{9,13},{10,14},{11,15},{20,16},{21,... | collective-permute-start | bytes 2457608 | tf_op jit(solution)/shard_map/ppermute | solution.py:175
  55.9 10.9 %collective-permute-done.14 = bf16[640,640]{1,0:T(8,128)(2,1)} collective-permute-done((bf16[640,640]{1,0:T(8,128)(2,1)}, bf16[640,640]{1,0:T(8,128)(2,1)}, u32[]{:S(2)}, u32[]{:S(2)}) %collective-permute-start.14) | collective-permute-done | bytes 819232 | tf_op jit(solution)/shard_map/ppermute | solution.py:175
  66.8 2.3 collective-permute-start.17
  69.7 5.9 %shard_map.82.refs_0_ = bf16[192,1280]{1,0:T(8,128)(2,1)} custom-call(s32[2]{0:T(128)} %add_convert_fusion.seen_ref, bf16[192,2560]{1,0:T(8,128)(2,1)} %get-tuple-element.16.q_ref, bf16[192,2560]{1,0:T(8,128)(2,1)} %copy-done.2, bf16[192,2560]{1,0:T(8,128)(2,1)} %get-tuple-element.17.k_ref.v_ref, bf16[192,2560]{1,0:T(8,128)(2,1)} %collective-permute-done.1.ka_ref.va_ref, ...), custom_call_target="tpu_custom_call" | custom-call | tf_op jit(solution)/shard_map/pallas_call | solution.py:77
  75.6 8.1 %collective-permute-start.6 = (bf16[192,1280]{1,0:T(8,128)(2,1)}, bf16[192,1280]{1,0:T(8,128)(2,1)S(1)}, u32[]{:S(2)}, u32[]{:S(2)}) collective-permute-start(bf16[192,1280]{1,0:T(8,128)(2,1)} %shard_map.82.refs_0_), channel_id=1, source_target_pairs={{0,2},{1,3},{2,0},{3,1},{4,6},{5,7},{6,4},{7,5},{8,10},{9,11},{10,... | collective-permute-start | bytes 1474568 | tf_op jit(solution)/shard_map/ppermute | solution.py:169
  83.7 2.3 collective-permute-start.4
  86.0 0.9 copy-done.1
  86.9 5.8 %shard_map.83.refs_1_ = bf16[192,1280]{1,0:T(8,128)(2,1)} custom-call(s32[2]{0:T(128)} %add_convert_fusion.seen_ref, bf16[192,2560]{1,0:T(8,128)(2,1)} %get-tuple-element.16.q_ref, bf16[192,2560]{1,0:T(8,128)(2,1)} %copy-done, bf16[192,2560]{1,0:T(8,128)(2,1)} %get-tuple-element.18.k_ref.v_ref, bf16[192,2560]{1,0:T(8,128)(2,1)} %copy-done.1, ...), custom_call_target="tpu_custom_call" | custom-call | tf_op jit(solution)/shard_map/pallas_call | solution.py:77
  92.7 0.9 collective-permute-start.5
  93.7 2.4 collective-permute-done.6.refs_4_
  96.0 2.1 collective-permute-start.7
  98.1 1.4 collective-permute-start.8
  99.5 1.2 broadcast_select_fusion.1.refs_10_
  101.1 1.2 broadcast_select_fusion.refs_11_
  102.4 1.3 collective-permute-start.22
  103.9 5.1 %collective-permute-done.7.refs_5_ = bf16[192,1280]{1,0:T(8,128)(2,1)} collective-permute-done((bf16[192,1280]{1,0:T(8,128)(2,1)}, bf16[192,1280]{1,0:T(8,128)(2,1)}, u32[]{:S(2)}, u32[]{:S(2)}) %collective-permute-start.7) | collective-permute-done | bytes 491552 | tf_op jit(solution)/shard_map/ppermute | solution.py:169
  109.2 0.8 copy-done.8
  110.0 1.9 collective-permute-start.9
  112.0 0.8 fusion
  114.1 0.8 copy-done.9
  114.9 7.8 %shard_map.84 = (bf16[192,640]{1,0:T(8,128)(2,1)}, bf16[192,640]{1,0:T(8,128)(2,1)}, bf16[192,640]{1,0:T(8,128)(2,1)}, bf16[192,640]{1,0:T(8,128)(2,1)}) custom-call(s32[4]{0:T(128)} %pad_add_fusion.starts_ref, f32[1,640]{1,0:T(1,128)} %reshape.16.gate_ref, bf16[192,1280]{1,0:T(8,128)(2,1)} %shard_map.82.refs_0_, bf16[192,1280]{1,0:T(8,128)(2,1)} %shard_map.83.refs_1_, ...), custom_call_target="tpu_custom_call" | custom-call | tf_op jit(solution)/shard_map/pallas_call | solution.py:117
  123.3 1.5 collective-permute-start.19
  124.7 13.8 %collective-permute-done.22.refs_9_ = bf16[640,640]{1,0:T(8,128)(2,1)} collective-permute-done((bf16[640,640]{1,0:T(8,128)(2,1)}, bf16[640,640]{1,0:T(8,128)(2,1)}, u32[]{:S(2)}, u32[]{:S(2)}) %collective-permute-start.22) | collective-permute-done | bytes 819232 | tf_op jit(solution)/shard_map/ppermute | solution.py:172
  138.5 1.1 collective-permute-start.20
  139.6 16.4 %collective-permute-done.23.refs_10_ = bf16[640,640]{1,0:T(8,128)(2,1)} collective-permute-done((bf16[640,640]{1,0:T(8,128)(2,1)S(1)}, bf16[640,640]{1,0:T(8,128)(2,1)}, u32[]{:S(2)}, u32[]{:S(2)}) %collective-permute-start.23) | collective-permute-done | bytes 819232 | tf_op jit(solution)/shard_map/ppermute | solution.py:172
  156.1 17.6 %collective-permute-done.24.refs_11_ = bf16[640,640]{1,0:T(8,128)(2,1)} collective-permute-done((bf16[640,640]{1,0:T(8,128)(2,1)S(1)}, bf16[640,640]{1,0:T(8,128)(2,1)}, u32[]{:S(2)}, u32[]{:S(2)}) %collective-permute-start.24) | collective-permute-done | bytes 819232 | tf_op jit(solution)/shard_map/ppermute | solution.py:172
  173.6 7.7 %shard_map.85 = (bf16[192,640]{1,0:T(8,128)(2,1)}, bf16[192,640]{1,0:T(8,128)(2,1)}, bf16[192,640]{1,0:T(8,128)(2,1)}, bf16[192,640]{1,0:T(8,128)(2,1)}) custom-call(s32[4]{0:T(128)} %pad_add_fusion.starts_ref, f32[1,640]{1,0:T(1,128)} %reshape.19.gate_ref, bf16[192,1280]{1,0:T(8,128)(2,1)} %shard_map.82.refs_0_, bf16[192,1280]{1,0:T(8,128)(2,1)} %shard_map.83.refs_1_, ...), custom_call_target="tpu_custom_call" | custom-call | tf_op jit(solution)/shard_map/pallas_call | solution.py:117
  181.4 0.9 collective-permute-start.25
  182.3 1.7 collective-permute-start.27
  184.7 5.2 %collective-permute-done.26.refs_6_ = bf16[192,640]{1,0:T(8,128)(2,1)S(1)} collective-permute-done((bf16[192,640]{1,0:T(8,128)(2,1)}, bf16[192,640]{1,0:T(8,128)(2,1)S(1)}, u32[]{:S(2)}, u32[]{:S(2)}) %collective-permute-start.26) | collective-permute-done | bytes 245792 | tf_op jit(solution)/shard_map/ppermute | solution.py:169
  189.9 5.5 %collective-permute-done.27.refs_7_ = bf16[192,640]{1,0:T(8,128)(2,1)S(1)} collective-permute-done((bf16[192,640]{1,0:T(8,128)(2,1)}, bf16[192,640]{1,0:T(8,128)(2,1)S(1)}, u32[]{:S(2)}, u32[]{:S(2)}) %collective-permute-start.27) | collective-permute-done | bytes 245792 | tf_op jit(solution)/shard_map/ppermute | solution.py:169
  196.2 61.4 %place.1 = bf16[192,5120]{1,0:T(8,128)(2,1)} custom-call(s32[8]{0:T(128)} %stack.59.starts_ref, bf16[192,640]{1,0:T(8,128)(2,1)} %get-tuple-element.19.refs_0_, bf16[192,640]{1,0:T(8,128)(2,1)} %copy-done.10, bf16[192,640]{1,0:T(8,128)(2,1)} %copy-done.11, bf16[192,640]{1,0:T(8,128)(2,1)} %copy-done.12, bf16[192,640]{1,0:T(8,128)(2,1)} %get-tuple-element.23.refs_4_, ...), custom_call_target="tpu_custom_call" | custom-call | tf_op jit(solution)/shard_map/place/pallas_call | solution.py:146
  (68 shorter events, 7.2 us)
Async XLA Ops:
  1.0 1.8 collective-permute-start.12
  4.0 7.4 %collective-permute-start.10 = (bf16[160,640]{1,0:T(8,128)(2,1)S(1)}, bf16[160,640]{1,0:T(8,128)(2,1)S(1)}, u32[]{:S(2)}, u32[]{:S(2)}) collective-permute-start(bf16[160,640]{1,0:T(8,128)(2,1)S(1)} %get-tuple-element.29), channel_id=1, source_target_pairs={{0,3},{1,2},{2,1},{3,0},{4,7},{5,6},{6,5},{7,4},{8,11},{9,10},{10,... | collective-permute-start | bytes 614408 | tf_op jit(solution)/shard_map/ppermute | solution.py:169
  5.5 9.9 %collective-permute-start.11 = (bf16[160,640]{1,0:T(8,128)(2,1)S(1)}, bf16[160,640]{1,0:T(8,128)(2,1)S(1)}, u32[]{:S(2)}, u32[]{:S(2)}) collective-permute-start(bf16[160,640]{1,0:T(8,128)(2,1)S(1)} %get-tuple-element.30), channel_id=1, source_target_pairs={{0,2},{1,3},{2,0},{3,1},{4,6},{5,7},{6,4},{7,5},{8,10},{9,11},{10,... | collective-permute-start | bytes 614408 | tf_op jit(solution)/shard_map/ppermute | solution.py:169
  15.5 1.3 copy-start.16
  15.5 1.9 copy-start.17
  16.7 37.3 %copy-start.18 = (s32[1,2]{1,0:T(1,128)S(1)}, s32[1,2]{1,0:T(1,128)}, u32[]{:S(2)}) copy-start(s32[1,2]{1,0:T(1,128)} %param.15) | copy-start | bytes 28
  16.7 19.4 %collective-permute-start.13 = (bf16[640,640]{1,0:T(8,128)(2,1)}, bf16[640,640]{1,0:T(8,128)(2,1)}, u32[]{:S(2)}, u32[]{:S(2)}) collective-permute-start(bf16[640,640]{1,0:T(8,128)(2,1)} %pad_maximum_fusion.refs_8_), channel_id=1, source_target_pairs={{0,4},{1,5},{2,6},{3,7},{4,0},{5,1},{6,2},{7,3},{8,12},{9,13},{10,... | collective-permute-start | bytes 2457608 | tf_op jit(solution)/shard_map/ppermute | solution.py:175
  22.1 22.4 %collective-permute-start = (bf16[192,2560]{1,0:T(8,128)(2,1)}, bf16[192,2560]{1,0:T(8,128)(2,1)S(1)}, u32[]{:S(2)}, u32[]{:S(2)}) collective-permute-start(bf16[192,2560]{1,0:T(8,128)(2,1)} %get-tuple-element.17.k_ref.v_ref), channel_id=1, source_target_pairs={{0,1},{1,2},{2,3},{3,4},{4,5},{5,6},{6,7},{7,8},{8,9},{9,10},{10,1... | collective-permute-start | bytes 2949128 | tf_op jit(solution)/shard_map/ppermute | solution.py:178
  26.1 25.0 %collective-permute-start.15 = (bf16[640,640]{1,0:T(8,128)(2,1)}, bf16[640,640]{1,0:T(8,128)(2,1)}, u32[]{:S(2)}, u32[]{:S(2)}) collective-permute-start(bf16[640,640]{1,0:T(8,128)(2,1)} %pad_maximum_fusion.refs_8_), channel_id=1, source_target_pairs={{4,8},{5,9},{6,10},{7,11},{8,4},{9,5},{10,6},{11,7},{20,24},{21,25... | collective-permute-start | bytes 2457608 | tf_op jit(solution)/shard_map/ppermute | solution.py:175
  30.4 39.3 %collective-permute-start.1 = (bf16[192,2560]{1,0:T(8,128)(2,1)}, bf16[192,2560]{1,0:T(8,128)(2,1)}, u32[]{:S(2)}, u32[]{:S(2)}) collective-permute-start(bf16[192,2560]{1,0:T(8,128)(2,1)} %get-tuple-element.17.k_ref.v_ref), channel_id=1, source_target_pairs={{1,0},{2,1},{3,2},{4,3},{5,4},{6,5},{7,6},{8,7},{9,8},{10,9},{11,1... | collective-permute-start | bytes 2949128 | tf_op jit(solution)/shard_map/ppermute | solution.py:178
  36.1 30.7 %collective-permute-start.14 = (bf16[640,640]{1,0:T(8,128)(2,1)}, bf16[640,640]{1,0:T(8,128)(2,1)}, u32[]{:S(2)}, u32[]{:S(2)}) collective-permute-start(bf16[640,640]{1,0:T(8,128)(2,1)} %collective-permute-done.13.refs_9_), channel_id=1, source_target_pairs={{4,8},{5,9},{6,10},{7,11},{8,4},{9,5},{10,6},{11,7},{20,24},{21,25... | collective-permute-start | bytes 2457608 | tf_op jit(solution)/shard_map/ppermute | solution.py:175
  39.3 44.4 %collective-permute-start.2 = (bf16[192,2560]{1,0:T(8,128)(2,1)}, bf16[192,2560]{1,0:T(8,128)(2,1)S(1)}, u32[]{:S(2)}, u32[]{:S(2)}) collective-permute-start(bf16[192,2560]{1,0:T(8,128)(2,1)} %get-tuple-element.18.k_ref.v_ref), channel_id=1, source_target_pairs={{0,1},{1,2},{2,3},{3,4},{4,5},{5,6},{6,7},{7,8},{8,9},{9,10},{10,1... | collective-permute-start | bytes 2949128 | tf_op jit(solution)/shard_map/ppermute | solution.py:178
  44.5 25.2 %copy-start.2 = (bf16[192,2560]{1,0:T(8,128)(2,1)}, bf16[192,2560]{1,0:T(8,128)(2,1)S(1)}, u32[]{:S(2)}) copy-start(bf16[192,2560]{1,0:T(8,128)(2,1)S(1)} %collective-permute-done.kb_ref.vb_ref) | copy-start | bytes 2949124
  44.5 41.5 %collective-permute-start.3 = (bf16[192,2560]{1,0:T(8,128)(2,1)}, bf16[192,2560]{1,0:T(8,128)(2,1)S(1)}, u32[]{:S(2)}, u32[]{:S(2)}) collective-permute-start(bf16[192,2560]{1,0:T(8,128)(2,1)} %get-tuple-element.18.k_ref.v_ref), channel_id=1, source_target_pairs={{1,0},{2,1},{3,2},{4,3},{5,4},{6,5},{7,6},{8,7},{9,8},{10,9},{11,1... | collective-permute-start | bytes 2949128 | tf_op jit(solution)/shard_map/ppermute | solution.py:178
  51.1 47.1 %collective-permute-start.16 = (bf16[640,640]{1,0:T(8,128)(2,1)}, bf16[640,640]{1,0:T(8,128)(2,1)}, u32[]{:S(2)}, u32[]{:S(2)}) collective-permute-start(bf16[640,640]{1,0:T(8,128)(2,1)} %collective-permute-done.15), channel_id=1, source_target_pairs={{4,0},{5,1},{6,2},{7,3},{8,12},{9,13},{10,14},{11,15},{20,16},{21,... | collective-permute-start | bytes 2457608 | tf_op jit(solution)/shard_map/ppermute | solution.py:175
  66.8 34.0 %collective-permute-start.17 = (bf16[640,640]{1,0:T(8,128)(2,1)}, bf16[640,640]{1,0:T(8,128)(2,1)}, u32[]{:S(2)}, u32[]{:S(2)}) collective-permute-start(bf16[640,640]{1,0:T(8,128)(2,1)} %collective-permute-done.14), channel_id=1, source_target_pairs={{4,0},{5,1},{6,2},{7,3},{8,12},{9,13},{10,14},{11,15},{20,16},{21,... | collective-permute-start | bytes 2457608 | tf_op jit(solution)/shard_map/ppermute | solution.py:175
  75.6 20.5 %collective-permute-start.6 = (bf16[192,1280]{1,0:T(8,128)(2,1)}, bf16[192,1280]{1,0:T(8,128)(2,1)S(1)}, u32[]{:S(2)}, u32[]{:S(2)}) collective-permute-start(bf16[192,1280]{1,0:T(8,128)(2,1)} %shard_map.82.refs_0_), channel_id=1, source_target_pairs={{0,2},{1,3},{2,0},{3,1},{4,6},{5,7},{6,4},{7,5},{8,10},{9,11},{10,... | collective-permute-start | bytes 1474568 | tf_op jit(solution)/shard_map/ppermute | solution.py:169
  83.7 2.3 copy-start
  83.7 18.7 %collective-permute-start.4 = (bf16[192,1280]{1,0:T(8,128)(2,1)}, bf16[192,1280]{1,0:T(8,128)(2,1)S(1)}, u32[]{:S(2)}, u32[]{:S(2)}) collective-permute-start(bf16[192,1280]{1,0:T(8,128)(2,1)} %shard_map.82.refs_0_), channel_id=1, source_target_pairs={{0,1},{1,0},{2,3},{3,2},{4,5},{5,4},{6,7},{7,6},{8,9},{9,8},{10,11... | collective-permute-start | bytes 1474568 | tf_op jit(solution)/shard_map/ppermute | solution.py:169
  86.0 0.9 copy-start.1
  92.7 10.9 %collective-permute-start.5 = (bf16[192,1280]{1,0:T(8,128)(2,1)}, bf16[192,1280]{1,0:T(8,128)(2,1)S(1)}, u32[]{:S(2)}, u32[]{:S(2)}) collective-permute-start(bf16[192,1280]{1,0:T(8,128)(2,1)} %shard_map.83.refs_1_), channel_id=1, source_target_pairs={{0,1},{1,0},{2,3},{3,2},{4,5},{5,4},{6,7},{7,6},{8,9},{9,8},{10,11... | collective-permute-start | bytes 1474568 | tf_op jit(solution)/shard_map/ppermute | solution.py:169
  96.0 6.3 %copy-start.5 = (bf16[192,1280]{1,0:T(8,128)(2,1)}, bf16[192,1280]{1,0:T(8,128)(2,1)S(1)}, u32[]{:S(2)}) copy-start(bf16[192,1280]{1,0:T(8,128)(2,1)S(1)} %collective-permute-done.6.refs_4_) | copy-start | bytes 1474564
  96.0 12.9 %collective-permute-start.7 = (bf16[192,1280]{1,0:T(8,128)(2,1)}, bf16[192,1280]{1,0:T(8,128)(2,1)}, u32[]{:S(2)}, u32[]{:S(2)}) collective-permute-start(bf16[192,1280]{1,0:T(8,128)(2,1)} %shard_map.83.refs_1_), channel_id=1, source_target_pairs={{0,2},{1,3},{2,0},{3,1},{4,6},{5,7},{6,4},{7,5},{8,10},{9,11},{10,... | collective-permute-start | bytes 1474568 | tf_op jit(solution)/shard_map/ppermute | solution.py:169
  98.1 11.1 %collective-permute-start.8 = (bf16[192,1280]{1,0:T(8,128)(2,1)S(1)}, bf16[192,1280]{1,0:T(8,128)(2,1)S(1)}, u32[]{:S(2)}, u32[]{:S(2)}) collective-permute-start(bf16[192,1280]{1,0:T(8,128)(2,1)S(1)} %collective-permute-done.6.refs_4_), channel_id=1, source_target_pairs={{0,1},{1,0},{2,3},{3,2},{4,5},{5,4},{6,7},{7,6},{8,9},{9,8},{10,11... | collective-permute-start | bytes 1474568 | tf_op jit(solution)/shard_map/ppermute | solution.py:169
  100.7 13.3 %copy-start.3 = (bf16[640,640]{1,0:T(8,128)(2,1)}, bf16[640,640]{1,0:T(8,128)(2,1)S(1)}, u32[]{:S(2)}) copy-start(bf16[640,640]{1,0:T(8,128)(2,1)S(1)} %broadcast_select_fusion.1.refs_10_) | copy-start | bytes 2457604
  100.8 22.5 %collective-permute-start.21 = (bf16[640,640]{1,0:T(8,128)(2,1)}, bf16[640,640]{1,0:T(8,128)(2,1)}, u32[]{:S(2)}, u32[]{:S(2)}) collective-permute-start(bf16[640,640]{1,0:T(8,128)(2,1)} %pad_maximum_fusion.refs_8_), channel_id=1, source_target_pairs={{0,16},{16,0},{1,17},{17,1},{2,18},{18,2},{3,19},{19,3},{4,20},{20... | collective-permute-start | bytes 2457608 | tf_op jit(solution)/shard_map/ppermute | solution.py:172
  102.3 11.7 %copy-start.4 = (bf16[640,640]{1,0:T(8,128)(2,1)}, bf16[640,640]{1,0:T(8,128)(2,1)S(1)}, u32[]{:S(2)}) copy-start(bf16[640,640]{1,0:T(8,128)(2,1)S(1)} %broadcast_select_fusion.refs_11_) | copy-start | bytes 2457604
  102.4 11.7 %copy-start.6 = (bf16[192,1280]{1,0:T(8,128)(2,1)}, bf16[192,1280]{1,0:T(8,128)(2,1)S(1)}, u32[]{:S(2)}) copy-start(bf16[192,1280]{1,0:T(8,128)(2,1)S(1)} %collective-permute-done.4.refs_2_) | copy-start | bytes 1474564
  102.4 36.1 %collective-permute-start.22 = (bf16[640,640]{1,0:T(8,128)(2,1)}, bf16[640,640]{1,0:T(8,128)(2,1)}, u32[]{:S(2)}, u32[]{:S(2)}) collective-permute-start(bf16[640,640]{1,0:T(8,128)(2,1)} %collective-permute-done.13.refs_9_), channel_id=1, source_target_pairs={{0,16},{16,0},{1,17},{17,1},{2,18},{18,2},{3,19},{19,3},{4,20},{20... | collective-permute-start | bytes 2457608 | tf_op jit(solution)/shard_map/ppermute | solution.py:172
  103.7 10.4 %copy-start.7 = (bf16[192,1280]{1,0:T(8,128)(2,1)}, bf16[192,1280]{1,0:T(8,128)(2,1)S(1)}, u32[]{:S(2)}) copy-start(bf16[192,1280]{1,0:T(8,128)(2,1)S(1)} %collective-permute-done.5.refs_3_) | copy-start | bytes 1474564
  103.7 52.4 %collective-permute-start.23 = (bf16[640,640]{1,0:T(8,128)(2,1)S(1)}, bf16[640,640]{1,0:T(8,128)(2,1)}, u32[]{:S(2)}, u32[]{:S(2)}) collective-permute-start(bf16[640,640]{1,0:T(8,128)(2,1)S(1)} %broadcast_select_fusion.1.refs_10_), channel_id=1, source_target_pairs={{0,16},{16,0},{1,17},{17,1},{2,18},{18,2},{3,19},{19,3},{4,20},{20... | collective-permute-start | bytes 2457608 | tf_op jit(solution)/shard_map/ppermute | solution.py:172
  109.0 64.6 %collective-permute-start.24 = (bf16[640,640]{1,0:T(8,128)(2,1)S(1)}, bf16[640,640]{1,0:T(8,128)(2,1)}, u32[]{:S(2)}, u32[]{:S(2)}) collective-permute-start(bf16[640,640]{1,0:T(8,128)(2,1)S(1)} %broadcast_select_fusion.refs_11_), channel_id=1, source_target_pairs={{0,16},{16,0},{1,17},{17,1},{2,18},{18,2},{3,19},{19,3},{4,20},{20... | collective-permute-start | bytes 2457608 | tf_op jit(solution)/shard_map/ppermute | solution.py:172
  109.2 0.8 copy-start.8
  110.0 4.0 %collective-permute-start.9 = (bf16[192,1280]{1,0:T(8,128)(2,1)}, bf16[192,1280]{1,0:T(8,128)(2,1)S(1)}, u32[]{:S(2)}, u32[]{:S(2)}) collective-permute-start(bf16[192,1280]{1,0:T(8,128)(2,1)} %collective-permute-done.7.refs_5_), channel_id=1, source_target_pairs={{0,1},{1,0},{2,3},{3,2},{4,5},{5,4},{6,7},{7,6},{8,9},{9,8},{10,11... | collective-permute-start | bytes 1474568 | tf_op jit(solution)/shard_map/ppermute | solution.py:169
  114.0 0.8 copy-start.9
  122.6 59.7 %collective-permute-start.18 = (bf16[192,640]{1,0:T(8,128)(2,1)}, bf16[192,640]{1,0:T(8,128)(2,1)S(1)}, u32[]{:S(2)}, u32[]{:S(2)}) collective-permute-start(bf16[192,640]{1,0:T(8,128)(2,1)} %get-tuple-element.20), channel_id=1, source_target_pairs={{0,1},{1,0},{2,3},{3,2},{4,5},{5,4},{6,7},{7,6},{8,9},{9,8},{10,11... | collective-permute-start | bytes 737288 | tf_op jit(solution)/shard_map/ppermute | solution.py:169
  123.3 61.4 %collective-permute-start.19 = (bf16[192,640]{1,0:T(8,128)(2,1)}, bf16[192,640]{1,0:T(8,128)(2,1)S(1)}, u32[]{:S(2)}, u32[]{:S(2)}) collective-permute-start(bf16[192,640]{1,0:T(8,128)(2,1)} %get-tuple-element.21), channel_id=1, source_target_pairs={{0,2},{1,3},{2,0},{3,1},{4,6},{5,7},{6,4},{7,5},{8,10},{9,11},{10,... | collective-permute-start | bytes 737288 | tf_op jit(solution)/shard_map/ppermute | solution.py:169
  138.5 46.2 %collective-permute-start.20 = (bf16[192,640]{1,0:T(8,128)(2,1)}, bf16[192,640]{1,0:T(8,128)(2,1)S(1)}, u32[]{:S(2)}, u32[]{:S(2)}) collective-permute-start(bf16[192,640]{1,0:T(8,128)(2,1)} %get-tuple-element.22), channel_id=1, source_target_pairs={{0,3},{1,2},{2,1},{3,0},{4,7},{5,6},{6,5},{7,4},{8,11},{9,10},{10,... | collective-permute-start | bytes 737288 | tf_op jit(solution)/shard_map/ppermute | solution.py:169
  181.4 3.3 %collective-permute-start.25 = (bf16[192,640]{1,0:T(8,128)(2,1)}, bf16[192,640]{1,0:T(8,128)(2,1)S(1)}, u32[]{:S(2)}, u32[]{:S(2)}) collective-permute-start(bf16[192,640]{1,0:T(8,128)(2,1)} %get-tuple-element.24), channel_id=1, source_target_pairs={{0,1},{1,0},{2,3},{3,2},{4,5},{5,4},{6,7},{7,6},{8,9},{9,8},{10,11... | collective-permute-start | bytes 737288 | tf_op jit(solution)/shard_map/ppermute | solution.py:169
  182.3 7.6 %collective-permute-start.26 = (bf16[192,640]{1,0:T(8,128)(2,1)}, bf16[192,640]{1,0:T(8,128)(2,1)S(1)}, u32[]{:S(2)}, u32[]{:S(2)}) collective-permute-start(bf16[192,640]{1,0:T(8,128)(2,1)} %get-tuple-element.25), channel_id=1, source_target_pairs={{0,2},{1,3},{2,0},{3,1},{4,6},{5,7},{6,4},{7,5},{8,10},{9,11},{10,... | collective-permute-start | bytes 737288 | tf_op jit(solution)/shard_map/ppermute | solution.py:169
  182.3 13.2 %copy-start.10 = (bf16[192,640]{1,0:T(8,128)(2,1)}, bf16[192,640]{1,0:T(8,128)(2,1)S(1)}, u32[]{:S(2)}) copy-start(bf16[192,640]{1,0:T(8,128)(2,1)S(1)} %collective-permute-done.18.refs_1_) | copy-start | bytes 737284
  182.3 13.1 %collective-permute-start.27 = (bf16[192,640]{1,0:T(8,128)(2,1)}, bf16[192,640]{1,0:T(8,128)(2,1)S(1)}, u32[]{:S(2)}, u32[]{:S(2)}) collective-permute-start(bf16[192,640]{1,0:T(8,128)(2,1)} %get-tuple-element.26), channel_id=1, source_target_pairs={{0,3},{1,2},{2,1},{3,0},{4,7},{5,6},{6,5},{7,4},{8,11},{9,10},{10,... | collective-permute-start | bytes 737288 | tf_op jit(solution)/shard_map/ppermute | solution.py:169
  184.7 10.8 %copy-start.11 = (bf16[192,640]{1,0:T(8,128)(2,1)}, bf16[192,640]{1,0:T(8,128)(2,1)S(1)}, u32[]{:S(2)}) copy-start(bf16[192,640]{1,0:T(8,128)(2,1)S(1)} %collective-permute-done.19.refs_2_) | copy-start | bytes 737284
  184.7 10.8 %copy-start.12 = (bf16[192,640]{1,0:T(8,128)(2,1)}, bf16[192,640]{1,0:T(8,128)(2,1)S(1)}, u32[]{:S(2)}) copy-start(bf16[192,640]{1,0:T(8,128)(2,1)S(1)} %collective-permute-done.20.refs_3_) | copy-start | bytes 737284
  184.7 10.8 %copy-start.13 = (bf16[192,640]{1,0:T(8,128)(2,1)}, bf16[192,640]{1,0:T(8,128)(2,1)S(1)}, u32[]{:S(2)}) copy-start(bf16[192,640]{1,0:T(8,128)(2,1)S(1)} %collective-permute-done.25.refs_5_) | copy-start | bytes 737284
  189.9 5.5 %copy-start.14 = (bf16[192,640]{1,0:T(8,128)(2,1)}, bf16[192,640]{1,0:T(8,128)(2,1)S(1)}, u32[]{:S(2)}) copy-start(bf16[192,640]{1,0:T(8,128)(2,1)S(1)} %collective-permute-done.26.refs_6_) | copy-start | bytes 737284
  195.5 0.7 copy-start.15
where the time goes:
time: 258 us
  Pallas kernels  92.6 us (36%)
  waiting for transfers between devices  91.4 us (35%)
  starting transfers between devices  57.2 us (22%)
  local copies, waits for them, and re-layouts  8.73 us (3%)
  other arithmetic  6.14 us (2%)
    pallas_call x1, Pallas kernels, place_pieces(): pl.pallas_call(place_kernel, out_shape=jax.ShapeDtypeStruct((rows, cols *...  61.4 us
    ppermute x4, waiting for transfers between devices, group_swap(): return lax.ppermute(x, 'groups', [(0, 1), (1, 0)])  47.8 us
    ppermute x15, waiting for transfers between devices, swap(): return lax.ppermute(x, 'tm', [(i, i ^ bits) for i in range(peers)])  29 us
    ppermute x15, starting transfers between devices, swap(): return lax.ppermute(x, 'tm', [(i, i ^ bits) for i in range(peers)])  24.5 us
    ppermute x4, starting transfers between devices, shifted(): lax.ppermute(x, 'tm', [(i, i + by) for i in range(peers) if 0 <= i + by <...  17.7 us
    pallas_call x2, Pallas kernels, project(): pl.pallas_call(functools.partial(project_kernel, len(att)), out_shape=[ja...  15.5 us
    ppermute x5, waiting for transfers between devices, along(): lax.ppermute(x, 'tm', [(4 * a + i, 4 * b + i) for a, b in moves for i in...  14.6 us
    ppermute x5, starting transfers between devices, along(): lax.ppermute(x, 'tm', [(4 * a + i, 4 * b + i) for a, b in moves for i in...  12.9 us
  transfers between devices with their start and end apart: 28, of which 12 were waited for; matrix products, arithmetic and copies ran while one was open for 3% of the time, Pallas kernels for 12%

commit v1 on v0

--- a/solution.py
+++ b/solution.py
@@ -15,30 +15,23 @@
     return [pl.BlockSpec(memory_space=pltpu.VMEM)] * count
 
 
-def prepare_kernel(q_ref, k_ref, v_ref, qg_ref, kg_ref, qn_ref, *kv_refs):
-    def scaled(ref, gain_ref):
-        block = ref[...].astype(jnp.float32)
-        inverse = lax.rsqrt(jnp.mean(block * block, axis=-1, keepdims=True) + 1e-06)
-        return (block * inverse * gain_ref[...]).astype(jnp.bfloat16)
-
-    wide = kv_refs[0].shape[1] // 2
-    kn = scaled(k_ref, kg_ref)
-    for i, kv_ref in enumerate(kv_refs):
-        kv_ref[:, :wide] = kn[:, i * wide : (i + 1) * wide]
-        kv_ref[:, wide:] = v_ref[:, i * wide : (i + 1) * wide]
-    qn_ref[...] = scaled(q_ref, qg_ref)
-
-
-def prepare(queries, keys, values, q_gain, k_gain, chunks):
-    rows, chans = queries.shape
-    kv = jax.ShapeDtypeStruct((rows, 2 * chans // chunks), jnp.bfloat16)
-    return pl.pallas_call(
-        prepare_kernel,
-        out_shape=[jax.ShapeDtypeStruct((rows, chans), jnp.bfloat16)] + [kv] * chunks,
-        in_specs=whole(5),
-        out_specs=whole(1 + chunks),
-        name="prepare",
-    )(queries, keys, values, q_gain.reshape(1, chans), k_gain.reshape(1, chans))
+def norm_kernel(x_ref, gain_ref, *out_refs):
+    wide = out_refs[0].shape[1]
+    block = x_ref[...].astype(jnp.float32)
+    inverse = lax.rsqrt(jnp.mean(block * block, axis=-1, keepdims=True) + 1e-06)
+    for i in range(x_ref.shape[1] // HD):
+        piece = x_ref[:, i * HD : (i + 1) * HD].astype(jnp.float32)
+        at = i * HD % wide
+        scaled = piece * inverse * gain_ref[i : i + 1, :]
+        out_refs[i * HD // wide][:, at : at + HD] = scaled.astype(jnp.bfloat16)
+
+
+def norm(x, gain, chunks):
+    rows, chans = x.shape
+    out = jax.ShapeDtypeStruct((rows, chans // chunks), jnp.bfloat16)
+    return pl.pallas_call(
+        norm_kernel, out_shape=[out] * chunks, in_specs=whole(2), out_specs=whole(chunks)
+    )(x, gain.reshape(chans // HD, HD))
 
 
 def attend_kernel(seen_ref, q_ref, kb_ref, k_ref, ka_ref, vb_ref, v_ref, va_ref, o_ref):
@@ -64,47 +57,49 @@
         o_ref[:, at] = out.astype(jnp.bfloat16)
 
 
-def attend(seen, qn, before, kv, after, chunk, chunks):
-    rows, chans = qn.shape
-    wide = chans // chunks
+def attend(seen, qn, keys, values, chunk):
+    rows, _ = values[0].shape
+    wide = qn.shape[1]
     heads = wide // HD
     step = next(n for n in (5, 4, 3, 2, 1) if heads % n == 0)
     cols = step * HD
     steps = wide // cols
-    q_spec = pl.BlockSpec((rows, cols), lambda i: (0, chunk * steps + i))
     k_spec = pl.BlockSpec((rows, cols), lambda i: (0, i))
-    v_spec = pl.BlockSpec((rows, cols), lambda i: (0, steps + i))
+    v_spec = pl.BlockSpec((rows, cols), lambda i: (0, chunk * steps + i))
     return pl.pallas_call(
         attend_kernel,
         grid=(steps,),
         out_shape=jax.ShapeDtypeStruct((rows, wide), jnp.bfloat16),
-        in_specs=[pl.BlockSpec(memory_space=pltpu.SMEM), q_spec] + [k_spec] * 3 + [v_spec] * 3,
-        out_specs=pl.BlockSpec((rows, cols), lambda i: (0, i)),
-    )(seen, qn, before, kv, after, before, kv, after)
+        in_specs=[pl.BlockSpec(memory_space=pltpu.SMEM)] + [k_spec] * 4 + [v_spec] * 3,
+        out_specs=k_spec,
+    )(seen, qn, *keys, *values)
 
 
 def project_kernel(count, starts_ref, gate_ref, *refs):
     slots = starts_ref.shape[0]
     att_refs, w_refs = refs[:count], refs[count : count + slots]
     outs = refs[count + slots : count + slots + 4]
-    a_ref, w_ref, sems = refs[count + slots + 4 :]
-    rows, wide = att_refs[0].shape
+    w_ref, sems = refs[count + slots + 4 :]
+    wide = att_refs[0].shape[1]
     depth = w_refs[0].shape[0]
     chunks = count // 4
     copies = []
     for i, ref in enumerate(w_refs):
         start = pl.multiple_of(starts_ref[i], depth)
         copies.append(pltpu.make_async_copy(ref, w_ref.at[pl.ds(start, depth)], sems.at[i]))
-    for i, ref in enumerate(att_refs):
-        p, j = i // chunks, i % chunks
-        dst = a_ref.at[pl.ds(p * rows, rows), pl.ds(j * wide, wide)]
-        copies.append(pltpu.make_async_copy(ref, dst, sems.at[slots + i]))
     for copy in copies:
         copy.start()
     for copy in copies:
         copy.wait()
     for p in range(4):
-        acc = jnp.dot(a_ref[p * rows : (p + 1) * rows, :], w_ref[...], preferred_element_type=jnp.float32)
+        acc = None
+        for j in range(chunks):
+            term = jnp.dot(
+                att_refs[p * chunks + j][...],
+                w_ref[j * wide : (j + 1) * wide, :],
+                preferred_element_type=jnp.float32,
+            )
+            acc = term if acc is None else acc + term
         outs[p][...] = (gate_ref[...] * acc).astype(jnp.bfloat16)
 
 
@@ -113,42 +108,32 @@
     chans = wide * len(att) // 4
     cols = weights[0].shape[1]
     slots = len(weights)
-    anywhere = pl.BlockSpec(memory_space=pl.ANY)
     return pl.pallas_call(
         functools.partial(project_kernel, len(att)),
         out_shape=[jax.ShapeDtypeStruct((rows, cols), jnp.bfloat16)] * 4,
-        in_specs=[pl.BlockSpec(memory_space=pltpu.SMEM)] + whole(1) + [anywhere] * (len(att) + slots),
+        in_specs=[pl.BlockSpec(memory_space=pltpu.SMEM)]
+        + whole(1 + len(att))
+        + [pl.BlockSpec(memory_space=pl.ANY)] * slots,
         out_specs=whole(4),
-        scratch_shapes=[
-            pltpu.VMEM((4 * rows, chans), jnp.bfloat16),
-            pltpu.VMEM((chans, cols), jnp.bfloat16),
-            pltpu.SemaphoreType.DMA((slots + len(att),)),
-        ],
+        scratch_shapes=[pltpu.VMEM((chans, cols), jnp.bfloat16), pltpu.SemaphoreType.DMA((slots,))],
     )(starts, gate.reshape(1, cols), *att, *weights)
 
 
 def place_kernel(starts_ref, *refs):
-    pieces, out_ref, sems = refs[:-2], refs[-2], refs[-1]
+    pieces, out_ref = refs[:-1], refs[-1]
     cols = pieces[0].shape[1]
-    copies = []
     for i, ref in enumerate(pieces):
         start = pl.multiple_of(starts_ref[i], 128)
-        copies.append(pltpu.make_async_copy(ref, out_ref.at[:, pl.ds(start, cols)], sems.at[i]))
-    for copy in copies:
-        copy.start()
-    for copy in copies:
-        copy.wait()
+        out_ref[:, pl.ds(start, cols)] = ref[...]
 
 
 def place_pieces(starts, pieces):
     rows, cols = pieces[0].shape
-    anywhere = pl.BlockSpec(memory_space=pl.ANY)
     return pl.pallas_call(
         place_kernel,
         out_shape=jax.ShapeDtypeStruct((rows, cols * len(pieces)), jnp.bfloat16),
-        in_specs=[pl.BlockSpec(memory_space=pltpu.SMEM)] + [anywhere] * len(pieces),
-        out_specs=anywhere,
-        scratch_shapes=[pltpu.SemaphoreType.DMA((len(pieces),))],
+        in_specs=[pl.BlockSpec(memory_space=pltpu.SMEM)] + whole(len(pieces)),
+        out_specs=pl.BlockSpec(memory_space=pltpu.VMEM),
         name="place",
     )(starts, *pieces)
 
@@ -186,7 +171,8 @@
     def weight_part(quarter):
         return lax.dynamic_slice_in_dim(out_weight, column(quarter, group), cols, 1)
 
-    parts = [weight_part(low)] + [swap(weight_part(low ^ i), i) for i in (1, 2, 3)]
+    cuts = lax.optimization_barrier([weight_part(low ^ i) for i in range(4)])
+    parts = [cuts[0]] + [swap(cuts[i], i) for i in (1, 2, 3)]
     odd, upper = (low % 2) == 1, low >= 2
     pairs = [
         jnp.concatenate([choose(odd, b, a), choose(odd, a, b)], axis=0)
@@ -194,9 +180,10 @@
     ]
     block = jnp.concatenate([choose(upper, pairs[1], pairs[0]), choose(upper, pairs[0], pairs[1])], axis=0)
 
-    qn, *kvs = prepare(queries, keys, values, q_gain, k_gain, chunks)
-    before = [shifted(kv, 1) for kv in kvs]
-    after = [shifted(kv, -1) for kv in kvs]
+    vals = [shifted(values, 1), values, shifted(values, -1)]
+    kns = norm(keys, k_gain, chunks)
+    keyed = [[shifted(kn, 1), kn, shifted(kn, -1)] for kn in kns]
+    qns = norm(queries, q_gain, chunks)
 
     if lines == 4:
         middle = (line == 1) | (line == 2)
@@ -218,7 +205,7 @@
     seen = jnp.stack([(reach[0, 0] == 1) & (place > 0), (reach[0, 1] == 1) & (place < peers - 1)]).astype(jnp.int32)
     att = [[None] * chunks for _ in range(4)]
     for i in range(chunks):
-        own = attend(seen, qn, before[i], kvs[i], after[i], i, chunks)
+        own = attend(seen, qns[i], keyed[i], vals, i)
         att[0][i] = own
         att[2][i] = swap(own, 2)
         att[1][i] = swap(own, 1)

time: 258 us -> 204 us (0.79)
  the two profiles are of different devices: /device:TPU:11 before, /device:TPU:17 now
where the time goes in v1:
time: 204 us; the launch traced here: 203 us
  waiting for transfers between devices  81.5 us (40%)
  starting transfers between devices  71.7 us (35%)
  Pallas kernels  35.6 us (17%)
  local copies, waits for them, and re-layouts  7.8 us (4%)
  other arithmetic  4.97 us (2%)
    ppermute x4, waiting for transfers between devices, group_swap(): return lax.ppermute(x, 'groups', [(0, 1), (1, 0)])  46.1 us
    ppermute x6, starting transfers between devices, shifted(): lax.ppermute(x, 'tm', [(i, i + by) for i in range(peers) if 0 <= i + by <...  36.3 us
    ppermute x15, waiting for transfers between devices, swap(): return lax.ppermute(x, 'tm', [(i, i ^ bits) for i in range(peers)])  28.4 us
    ppermute x15, starting transfers between devices, swap(): return lax.ppermute(x, 'tm', [(i, i ^ bits) for i in range(peers)])  21.6 us
    pallas_call x2, Pallas kernels, project(): pl.pallas_call(functools.partial(project_kernel, len(att)), out_shape=[ja...  15.9 us
    pallas_call x2, Pallas kernels, attend(): pl.pallas_call(attend_kernel, grid=(steps,), out_shape=jax.ShapeDtypeStru...  11.6 us
    ppermute x5, starting transfers between devices, along(): lax.ppermute(x, 'tm', [(4 * a + i, 4 * b + i) for a, b in moves for i in...  9.7 us
    ppermute x5, waiting for transfers between devices, along(): lax.ppermute(x, 'tm', [(4 * a + i, 4 * b + i) for a, b in moves for i in...  5.74 us
  transfers between devices with their start and end apart: 30, of which 12 were waited for; matrix products, arithmetic and copies ran while one was open for 3% of the time, Pallas kernels for 16%

profile of v1, /device:TPU:17, one launch (start us, length us, event | category | flops | bytes accessed | tf_op | source)
XLA Modules:
  0.0 203.2 jit_solution(6283897304071954563)
XLA Ops:
  0.0 1.3 constant_dynamic-slice_fusion
  2.1 1.2 collective-permute-start.12
  3.5 5.9 %collective-permute-done.12 = bf16[160,640]{1,0:T(8,128)(2,1)S(1)} collective-permute-done((bf16[160,640]{1,0:T(8,128)(2,1)S(1)}, bf16[160,640]{1,0:T(8,128)(2,1)S(1)}, u32[]{:S(2)}, u32[]{:S(2)}) %collective-permute-start.12) | collective-permute-done | bytes 204832 | tf_op jit(solution)/shard_map/ppermute | solution.py:154
  9.4 3.5 %collective-permute-done.13 = bf16[160,640]{1,0:T(8,128)(2,1)S(1)} collective-permute-done((bf16[160,640]{1,0:T(8,128)(2,1)S(1)}, bf16[160,640]{1,0:T(8,128)(2,1)S(1)}, u32[]{:S(2)}, u32[]{:S(2)}) %collective-permute-start.13) | collective-permute-done | bytes 204832 | tf_op jit(solution)/shard_map/ppermute | solution.py:154
  13.1 1.0 pad_maximum_fusion.refs_8_
  14.1 1.3 collective-permute-start.15
  15.4 1.9 collective-permute-start.17
  17.3 2.5 %shard_map.83 = (bf16[192,1280]{1,0:T(8,128)(2,1)}, bf16[192,1280]{1,0:T(8,128)(2,1)}) custom-call(bf16[192,2560]{1,0:T(8,128)(2,1)} %x_ref.3, f32[20,128]{1,0:T(8,128)} %bitcast.18), custom_call_target="tpu_custom_call" | custom-call | tf_op jit(solution)/shard_map/pallas_call | solution.py:32
  19.8 4.3 %collective-permute-start = (bf16[192,1280]{1,0:T(8,128)(2,1)}, bf16[192,1280]{1,0:T(8,128)(2,1)S(1)}, u32[]{:S(2)}, u32[]{:S(2)}) collective-permute-start(bf16[192,1280]{1,0:T(8,128)(2,1)} %get-tuple-element.22.k_ref), channel_id=1, source_target_pairs={{0,1},{1,2},{2,3},{3,4},{4,5},{5,6},{6,7},{7,8},{8,9},{9,10},{10,1... | collective-permute-start | bytes 1474568 | tf_op jit(solution)/shard_map/ppermute | solution.py:163
  24.1 1.9 collective-permute-start.2
  26.1 2.4 %collective-permute-start.3 = (bf16[192,2560]{1,0:T(8,128)(2,1)S(1)}, bf16[192,2560]{1,0:T(8,128)(2,1)S(1)}, u32[]{:S(2)}, u32[]{:S(2)}) collective-permute-start(bf16[192,2560]{1,0:T(8,128)(2,1)S(1)} %copy-done), channel_id=1, source_target_pairs={{1,0},{2,1},{3,2},{4,3},{5,4},{6,5},{7,6},{8,7},{9,8},{10,9},{11,1... | collective-permute-start | bytes 2949128 | tf_op jit(solution)/shard_map/ppermute | solution.py:163
  28.5 4.7 %collective-permute-done.15.refs_9_ = bf16[640,640]{1,0:T(8,128)(2,1)} collective-permute-done((bf16[640,640]{1,0:T(8,128)(2,1)}, bf16[640,640]{1,0:T(8,128)(2,1)}, u32[]{:S(2)}, u32[]{:S(2)}) %collective-permute-start.15) | collective-permute-done | bytes 819232 | tf_op jit(solution)/shard_map/ppermute | solution.py:160
  33.2 2.1 %collective-permute-start.16 = (bf16[640,640]{1,0:T(8,128)(2,1)}, bf16[640,640]{1,0:T(8,128)(2,1)}, u32[]{:S(2)}, u32[]{:S(2)}) collective-permute-start(bf16[640,640]{1,0:T(8,128)(2,1)} %collective-permute-done.15.refs_9_), channel_id=1, source_target_pairs={{4,8},{5,9},{6,10},{7,11},{8,4},{9,5},{10,6},{11,7},{20,24},{21,25... | collective-permute-start | bytes 2457608 | tf_op jit(solution)/shard_map/ppermute | solution.py:160
  35.3 13.2 %collective-permute-start.1 = (bf16[192,1280]{1,0:T(8,128)(2,1)}, bf16[192,1280]{1,0:T(8,128)(2,1)}, u32[]{:S(2)}, u32[]{:S(2)}) collective-permute-start(bf16[192,1280]{1,0:T(8,128)(2,1)} %get-tuple-element.22.k_ref), channel_id=1, source_target_pairs={{1,0},{2,1},{3,2},{4,3},{5,4},{6,5},{7,6},{8,7},{9,8},{10,9},{11,1... | collective-permute-start | bytes 1474568 | tf_op jit(solution)/shard_map/ppermute | solution.py:163
  48.5 2.2 %collective-permute-start.18 = (bf16[640,640]{1,0:T(8,128)(2,1)}, bf16[640,640]{1,0:T(8,128)(2,1)}, u32[]{:S(2)}, u32[]{:S(2)}) collective-permute-start(bf16[640,640]{1,0:T(8,128)(2,1)} %collective-permute-done.17), channel_id=1, source_target_pairs={{4,0},{5,1},{6,2},{7,3},{8,12},{9,13},{10,14},{11,15},{20,16},{21,... | collective-permute-start | bytes 2457608 | tf_op jit(solution)/shard_map/ppermute | solution.py:160
  52.6 1.0 collective-permute-done.16
  53.6 2.2 %collective-permute-start.19 = (bf16[640,640]{1,0:T(8,128)(2,1)}, bf16[640,640]{1,0:T(8,128)(2,1)}, u32[]{:S(2)}, u32[]{:S(2)}) collective-permute-start(bf16[640,640]{1,0:T(8,128)(2,1)} %collective-permute-done.16), channel_id=1, source_target_pairs={{4,0},{5,1},{6,2},{7,3},{8,12},{9,13},{10,14},{11,15},{20,16},{21,... | collective-permute-start | bytes 2457608 | tf_op jit(solution)/shard_map/ppermute | solution.py:160
  56.4 2.5 %shard_map.82 = (bf16[192,1280]{1,0:T(8,128)(2,1)}, bf16[192,1280]{1,0:T(8,128)(2,1)}) custom-call(bf16[192,2560]{1,0:T(8,128)(2,1)} %x_ref.2, f32[20,128]{1,0:T(8,128)} %bitcast.19), custom_call_target="tpu_custom_call" | custom-call | tf_op jit(solution)/shard_map/pallas_call | solution.py:32
  59.0 8.3 %collective-permute-start.4 = (bf16[192,1280]{1,0:T(8,128)(2,1)}, bf16[192,1280]{1,0:T(8,128)(2,1)}, u32[]{:S(2)}, u32[]{:S(2)}) collective-permute-start(bf16[192,1280]{1,0:T(8,128)(2,1)} %get-tuple-element.24.k_ref), channel_id=1, source_target_pairs={{0,1},{1,2},{2,3},{3,4},{4,5},{5,6},{6,7},{7,8},{8,9},{9,10},{10,1... | collective-permute-start | bytes 1474568 | tf_op jit(solution)/shard_map/ppermute | solution.py:163
  67.3 6.2 %collective-permute-start.5 = (bf16[192,1280]{1,0:T(8,128)(2,1)}, bf16[192,1280]{1,0:T(8,128)(2,1)}, u32[]{:S(2)}, u32[]{:S(2)}) collective-permute-start(bf16[192,1280]{1,0:T(8,128)(2,1)} %get-tuple-element.24.k_ref), channel_id=1, source_target_pairs={{1,0},{2,1},{3,2},{4,3},{5,4},{6,5},{7,6},{8,7},{9,8},{10,9},{11,1... | collective-permute-start | bytes 1474568 | tf_op jit(solution)/shard_map/ppermute | solution.py:163
  73.6 0.9 copy-done.2
  74.5 5.8 %shard_map.84.refs_0_ = bf16[192,1280]{1,0:T(8,128)(2,1)} custom-call(s32[2]{0:T(128)} %add_convert_fusion.seen_ref, bf16[192,1280]{1,0:T(8,128)(2,1)} %get-tuple-element.21.q_ref, bf16[192,1280]{1,0:T(8,128)(2,1)} %copy-done.10, bf16[192,1280]{1,0:T(8,128)(2,1)} %get-tuple-element.22.k_ref, bf16[192,1280]{1,0:T(8,128)(2,1)} %collective-permute-done.1.ka_ref, ...), custom_call_target="tpu_custom_call" | custom-call | tf_op jit(solution)/shard_map/pallas_call | solution.py:69
  80.3 8.8 %collective-permute-start.8 = (bf16[192,1280]{1,0:T(8,128)(2,1)}, bf16[192,1280]{1,0:T(8,128)(2,1)S(1)}, u32[]{:S(2)}, u32[]{:S(2)}) collective-permute-start(bf16[192,1280]{1,0:T(8,128)(2,1)} %shard_map.84.refs_0_), channel_id=1, source_target_pairs={{0,2},{1,3},{2,0},{3,1},{4,6},{5,7},{6,4},{7,5},{8,10},{9,11},{10,... | collective-permute-start | bytes 1474568 | tf_op jit(solution)/shard_map/ppermute | solution.py:154
  89.5 1.2 collective-permute-done.5.ka_ref
  90.6 5.8 %shard_map.85.refs_1_ = bf16[192,1280]{1,0:T(8,128)(2,1)} custom-call(s32[2]{0:T(128)} %add_convert_fusion.seen_ref, bf16[192,1280]{1,0:T(8,128)(2,1)} %get-tuple-element.23.q_ref, bf16[192,1280]{1,0:T(8,128)(2,1)} %collective-permute-done.4.kb_ref, bf16[192,1280]{1,0:T(8,128)(2,1)} %get-tuple-element.24.k_ref, ...), custom_call_target="tpu_custom_call" | custom-call | tf_op jit(solution)/shard_map/pallas_call | solution.py:69
  96.5 4.1 %collective-permute-done.8.refs_4_ = bf16[192,1280]{1,0:T(8,128)(2,1)S(1)} collective-permute-done((bf16[192,1280]{1,0:T(8,128)(2,1)}, bf16[192,1280]{1,0:T(8,128)(2,1)S(1)}, u32[]{:S(2)}, u32[]{:S(2)}) %collective-permute-start.8) | collective-permute-done | bytes 491552 | tf_op jit(solution)/shard_map/ppermute | solution.py:154
  100.5 1.6 collective-permute-start.9
  102.1 1.2 collective-permute-start.10
  103.3 1.2 broadcast_select_fusion.1.refs_10_
  104.6 1.3 collective-permute-start.23
  105.8 1.2 broadcast_select_fusion.refs_11_
  107.4 1.2 collective-permute-start.25
  108.6 4.1 %collective-permute-done.9.refs_5_ = bf16[192,1280]{1,0:T(8,128)(2,1)} collective-permute-done((bf16[192,1280]{1,0:T(8,128)(2,1)}, bf16[192,1280]{1,0:T(8,128)(2,1)}, u32[]{:S(2)}, u32[]{:S(2)}) %collective-permute-start.9) | collective-permute-done | bytes 491552 | tf_op jit(solution)/shard_map/ppermute | solution.py:154
  112.8 1.2 collective-permute-start.26
  114.8 2.1 %collective-permute-start.11 = (bf16[192,1280]{1,0:T(8,128)(2,1)}, bf16[192,1280]{1,0:T(8,128)(2,1)S(1)}, u32[]{:S(2)}, u32[]{:S(2)}) collective-permute-start(bf16[192,1280]{1,0:T(8,128)(2,1)} %collective-permute-done.9.refs_5_), channel_id=1, source_target_pairs={{0,1},{1,0},{2,3},{3,2},{4,5},{5,4},{6,7},{7,6},{8,9},{9,8},{10,11... | collective-permute-start | bytes 1474568 | tf_op jit(solution)/shard_map/ppermute | solution.py:154
  116.9 0.8 fusion
  119.9 7.9 %shard_map.86 = (bf16[192,640]{1,0:T(8,128)(2,1)}, bf16[192,640]{1,0:T(8,128)(2,1)}, bf16[192,640]{1,0:T(8,128)(2,1)}, bf16[192,640]{1,0:T(8,128)(2,1)}) custom-call(s32[4]{0:T(128)} %pad_add_fusion.starts_ref, f32[1,640]{1,0:T(1,128)} %reshape.16.gate_ref, bf16[192,1280]{1,0:T(8,128)(2,1)} %shard_map.84.refs_0_, bf16[192,1280]{1,0:T(8,128)(2,1)} %shard_map.85.refs_1_, ...), custom_call_target="tpu_custom_call" | custom-call | tf_op jit(solution)/shard_map/pallas_call | solution.py:111
  128.5 1.5 collective-permute-start.21
  129.9 12.3 %collective-permute-done.24.refs_9_ = bf16[640,640]{1,0:T(8,128)(2,1)} collective-permute-done((bf16[640,640]{1,0:T(8,128)(2,1)}, bf16[640,640]{1,0:T(8,128)(2,1)}, u32[]{:S(2)}, u32[]{:S(2)}) %collective-permute-start.24) | collective-permute-done | bytes 819232 | tf_op jit(solution)/shard_map/ppermute | solution.py:157
  142.3 1.3 collective-permute-start.22
  143.6 16.2 %collective-permute-done.25.refs_10_ = bf16[640,640]{1,0:T(8,128)(2,1)} collective-permute-done((bf16[640,640]{1,0:T(8,128)(2,1)S(1)}, bf16[640,640]{1,0:T(8,128)(2,1)}, u32[]{:S(2)}, u32[]{:S(2)}) %collective-permute-start.25) | collective-permute-done | bytes 819232 | tf_op jit(solution)/shard_map/ppermute | solution.py:157
  159.8 17.6 %collective-permute-done.26.refs_11_ = bf16[640,640]{1,0:T(8,128)(2,1)} collective-permute-done((bf16[640,640]{1,0:T(8,128)(2,1)S(1)}, bf16[640,640]{1,0:T(8,128)(2,1)}, u32[]{:S(2)}, u32[]{:S(2)}) %collective-permute-start.26) | collective-permute-done | bytes 819232 | tf_op jit(solution)/shard_map/ppermute | solution.py:157
  177.4 7.9 %shard_map.87 = (bf16[192,640]{1,0:T(8,128)(2,1)}, bf16[192,640]{1,0:T(8,128)(2,1)}, bf16[192,640]{1,0:T(8,128)(2,1)}, bf16[192,640]{1,0:T(8,128)(2,1)}) custom-call(s32[4]{0:T(128)} %pad_add_fusion.starts_ref, f32[1,640]{1,0:T(1,128)} %reshape.19.gate_ref, bf16[192,1280]{1,0:T(8,128)(2,1)} %shard_map.84.refs_0_, bf16[192,1280]{1,0:T(8,128)(2,1)} %shard_map.85.refs_1_, ...), custom_call_target="tpu_custom_call" | custom-call | tf_op jit(solution)/shard_map/pallas_call | solution.py:111
  185.3 0.9 collective-permute-start.27
  186.4 1.6 collective-permute-start.29
  188.6 5.3 %collective-permute-done.28.refs_6_ = bf16[192,640]{1,0:T(8,128)(2,1)S(1)} collective-permute-done((bf16[192,640]{1,0:T(8,128)(2,1)}, bf16[192,640]{1,0:T(8,128)(2,1)S(1)}, u32[]{:S(2)}, u32[]{:S(2)}) %collective-permute-start.28) | collective-permute-done | bytes 245792 | tf_op jit(solution)/shard_map/ppermute | solution.py:154
  193.9 5.5 %collective-permute-done.29.refs_7_ = bf16[192,640]{1,0:T(8,128)(2,1)S(1)} collective-permute-done((bf16[192,640]{1,0:T(8,128)(2,1)}, bf16[192,640]{1,0:T(8,128)(2,1)S(1)}, u32[]{:S(2)}, u32[]{:S(2)}) %collective-permute-start.29) | collective-permute-done | bytes 245792 | tf_op jit(solution)/shard_map/ppermute | solution.py:154
  200.1 3.0 %place.1 = bf16[192,5120]{1,0:T(8,128)(2,1)} custom-call(s32[8]{0:T(128)} %stack.59.starts_ref, bf16[192,640]{1,0:T(8,128)(2,1)} %get-tuple-element.29.refs_0_, bf16[192,640]{1,0:T(8,128)(2,1)} %copy-done.11, bf16[192,640]{1,0:T(8,128)(2,1)} %copy-done.12, bf16[192,640]{1,0:T(8,128)(2,1)} %copy-done.13, bf16[192,640]{1,0:T(8,128)(2,1)} %get-tuple-element.33.refs_4_, ...), custom_call_target="tpu_custom_call" | custom-call | tf_op jit(solution)/shard_map/place/pallas_call | solution.py:132
  (69 shorter events, 8.0 us)
Async XLA Ops:
  1.3 2.2 %collective-permute-start.14 = (bf16[160,640]{1,0:T(8,128)(2,1)S(1)}, bf16[160,640]{1,0:T(8,128)(2,1)S(1)}, u32[]{:S(2)}, u32[]{:S(2)}) collective-permute-start(bf16[160,640]{1,0:T(8,128)(2,1)S(1)} %get-tuple-element.27), channel_id=1, source_target_pairs={{0,1},{1,0},{2,3},{3,2},{4,5},{5,4},{6,7},{7,6},{8,9},{9,8},{10,11... | collective-permute-start | bytes 614408 | tf_op jit(solution)/shard_map/ppermute | solution.py:154
  2.1 7.4 %collective-permute-start.12 = (bf16[160,640]{1,0:T(8,128)(2,1)S(1)}, bf16[160,640]{1,0:T(8,128)(2,1)S(1)}, u32[]{:S(2)}, u32[]{:S(2)}) collective-permute-start(bf16[160,640]{1,0:T(8,128)(2,1)S(1)} %get-tuple-element.25), channel_id=1, source_target_pairs={{0,3},{1,2},{2,1},{3,0},{4,7},{5,6},{6,5},{7,4},{8,11},{9,10},{10,... | collective-permute-start | bytes 614408 | tf_op jit(solution)/shard_map/ppermute | solution.py:154
  3.3 9.6 %collective-permute-start.13 = (bf16[160,640]{1,0:T(8,128)(2,1)S(1)}, bf16[160,640]{1,0:T(8,128)(2,1)S(1)}, u32[]{:S(2)}, u32[]{:S(2)}) collective-permute-start(bf16[160,640]{1,0:T(8,128)(2,1)S(1)} %get-tuple-element.26), channel_id=1, source_target_pairs={{0,2},{1,3},{2,0},{3,1},{4,6},{5,7},{6,4},{7,5},{8,10},{9,11},{10,... | collective-permute-start | bytes 614408 | tf_op jit(solution)/shard_map/ppermute | solution.py:154
  13.1 11.0 %copy-start = (bf16[192,2560]{1,0:T(8,128)(2,1)S(1)}, bf16[192,2560]{1,0:T(8,128)(2,1)}, u32[]{:S(2)}) copy-start(bf16[192,2560]{1,0:T(8,128)(2,1)} %v_ref.3) | copy-start | bytes 2949124
  13.1 37.6 %copy-start.17 = (s32[1,2]{1,0:T(1,128)S(1)}, s32[1,2]{1,0:T(1,128)}, u32[]{:S(2)}) copy-start(s32[1,2]{1,0:T(1,128)} %param.15) | copy-start | bytes 28
  14.1 19.1 %collective-permute-start.15 = (bf16[640,640]{1,0:T(8,128)(2,1)}, bf16[640,640]{1,0:T(8,128)(2,1)}, u32[]{:S(2)}, u32[]{:S(2)}) collective-permute-start(bf16[640,640]{1,0:T(8,128)(2,1)} %pad_maximum_fusion.refs_8_), channel_id=1, source_target_pairs={{0,4},{1,5},{2,6},{3,7},{4,0},{5,1},{6,2},{7,3},{8,12},{9,13},{10,... | collective-permute-start | bytes 2457608 | tf_op jit(solution)/shard_map/ppermute | solution.py:160
  15.4 33.1 %collective-permute-start.17 = (bf16[640,640]{1,0:T(8,128)(2,1)}, bf16[640,640]{1,0:T(8,128)(2,1)}, u32[]{:S(2)}, u32[]{:S(2)}) collective-permute-start(bf16[640,640]{1,0:T(8,128)(2,1)} %pad_maximum_fusion.refs_8_), channel_id=1, source_target_pairs={{4,8},{5,9},{6,10},{7,11},{8,4},{9,5},{10,6},{11,7},{20,24},{21,25... | collective-permute-start | bytes 2457608 | tf_op jit(solution)/shard_map/ppermute | solution.py:160
  19.8 15.5 %collective-permute-start = (bf16[192,1280]{1,0:T(8,128)(2,1)}, bf16[192,1280]{1,0:T(8,128)(2,1)S(1)}, u32[]{:S(2)}, u32[]{:S(2)}) collective-permute-start(bf16[192,1280]{1,0:T(8,128)(2,1)} %get-tuple-element.22.k_ref), channel_id=1, source_target_pairs={{0,1},{1,2},{2,3},{3,4},{4,5},{5,6},{6,7},{7,8},{8,9},{9,10},{10,1... | collective-permute-start | bytes 1474568 | tf_op jit(solution)/shard_map/ppermute | solution.py:163
  24.1 43.2 %collective-permute-start.2 = (bf16[192,2560]{1,0:T(8,128)(2,1)S(1)}, bf16[192,2560]{1,0:T(8,128)(2,1)S(1)}, u32[]{:S(2)}, u32[]{:S(2)}) collective-permute-start(bf16[192,2560]{1,0:T(8,128)(2,1)S(1)} %copy-done), channel_id=1, source_target_pairs={{0,1},{1,2},{2,3},{3,4},{4,5},{5,6},{6,7},{7,8},{8,9},{9,10},{10,1... | collective-permute-start | bytes 2949128 | tf_op jit(solution)/shard_map/ppermute | solution.py:163
  26.1 47.5 %collective-permute-start.3 = (bf16[192,2560]{1,0:T(8,128)(2,1)S(1)}, bf16[192,2560]{1,0:T(8,128)(2,1)S(1)}, u32[]{:S(2)}, u32[]{:S(2)}) collective-permute-start(bf16[192,2560]{1,0:T(8,128)(2,1)S(1)} %copy-done), channel_id=1, source_target_pairs={{1,0},{2,1},{3,2},{4,3},{5,4},{6,5},{7,6},{8,7},{9,8},{10,9},{11,1... | collective-permute-start | bytes 2949128 | tf_op jit(solution)/shard_map/ppermute | solution.py:163
  33.2 20.4 %collective-permute-start.16 = (bf16[640,640]{1,0:T(8,128)(2,1)}, bf16[640,640]{1,0:T(8,128)(2,1)}, u32[]{:S(2)}, u32[]{:S(2)}) collective-permute-start(bf16[640,640]{1,0:T(8,128)(2,1)} %collective-permute-done.15.refs_9_), channel_id=1, source_target_pairs={{4,8},{5,9},{6,10},{7,11},{8,4},{9,5},{10,6},{11,7},{20,24},{21,25... | collective-permute-start | bytes 2457608 | tf_op jit(solution)/shard_map/ppermute | solution.py:160
  35.3 38.3 %copy-start.10 = (bf16[192,1280]{1,0:T(8,128)(2,1)}, bf16[192,1280]{1,0:T(8,128)(2,1)S(1)}, u32[]{:S(2)}) copy-start(bf16[192,1280]{1,0:T(8,128)(2,1)S(1)} %collective-permute-done.kb_ref) | copy-start | bytes 1474564
  35.3 23.7 %collective-permute-start.1 = (bf16[192,1280]{1,0:T(8,128)(2,1)}, bf16[192,1280]{1,0:T(8,128)(2,1)}, u32[]{:S(2)}, u32[]{:S(2)}) collective-permute-start(bf16[192,1280]{1,0:T(8,128)(2,1)} %get-tuple-element.22.k_ref), channel_id=1, source_target_pairs={{1,0},{2,1},{3,2},{4,3},{5,4},{6,5},{7,6},{8,7},{9,8},{10,9},{11,1... | collective-permute-start | bytes 1474568 | tf_op jit(solution)/shard_map/ppermute | solution.py:163
  48.5 53.6 %collective-permute-start.18 = (bf16[640,640]{1,0:T(8,128)(2,1)}, bf16[640,640]{1,0:T(8,128)(2,1)}, u32[]{:S(2)}, u32[]{:S(2)}) collective-permute-start(bf16[640,640]{1,0:T(8,128)(2,1)} %collective-permute-done.17), channel_id=1, source_target_pairs={{4,0},{5,1},{6,2},{7,3},{8,12},{9,13},{10,14},{11,15},{20,16},{21,... | collective-permute-start | bytes 2457608 | tf_op jit(solution)/shard_map/ppermute | solution.py:160
  53.6 50.9 %collective-permute-start.19 = (bf16[640,640]{1,0:T(8,128)(2,1)}, bf16[640,640]{1,0:T(8,128)(2,1)}, u32[]{:S(2)}, u32[]{:S(2)}) collective-permute-start(bf16[640,640]{1,0:T(8,128)(2,1)} %collective-permute-done.16), channel_id=1, source_target_pairs={{4,0},{5,1},{6,2},{7,3},{8,12},{9,13},{10,14},{11,15},{20,16},{21,... | collective-permute-start | bytes 2457608 | tf_op jit(solution)/shard_map/ppermute | solution.py:160
  59.0 30.2 %collective-permute-start.4 = (bf16[192,1280]{1,0:T(8,128)(2,1)}, bf16[192,1280]{1,0:T(8,128)(2,1)}, u32[]{:S(2)}, u32[]{:S(2)}) collective-permute-start(bf16[192,1280]{1,0:T(8,128)(2,1)} %get-tuple-element.24.k_ref), channel_id=1, source_target_pairs={{0,1},{1,2},{2,3},{3,4},{4,5},{5,6},{6,7},{7,8},{8,9},{9,10},{10,1... | collective-permute-start | bytes 1474568 | tf_op jit(solution)/shard_map/ppermute | solution.py:163
  67.3 6.2 %copy-start.1 = (bf16[192,2560]{1,0:T(8,128)(2,1)}, bf16[192,2560]{1,0:T(8,128)(2,1)S(1)}, u32[]{:S(2)}) copy-start(bf16[192,2560]{1,0:T(8,128)(2,1)S(1)} %collective-permute-done.2.vb_ref) | copy-start | bytes 2949124
  67.3 23.3 %collective-permute-start.5 = (bf16[192,1280]{1,0:T(8,128)(2,1)}, bf16[192,1280]{1,0:T(8,128)(2,1)}, u32[]{:S(2)}, u32[]{:S(2)}) collective-permute-start(bf16[192,1280]{1,0:T(8,128)(2,1)} %get-tuple-element.24.k_ref), channel_id=1, source_target_pairs={{1,0},{2,1},{3,2},{4,3},{5,4},{6,5},{7,6},{8,7},{9,8},{10,9},{11,1... | collective-permute-start | bytes 1474568 | tf_op jit(solution)/shard_map/ppermute | solution.py:163
  73.5 1.0 copy-start.2
  80.3 20.2 %collective-permute-start.8 = (bf16[192,1280]{1,0:T(8,128)(2,1)}, bf16[192,1280]{1,0:T(8,128)(2,1)S(1)}, u32[]{:S(2)}, u32[]{:S(2)}) collective-permute-start(bf16[192,1280]{1,0:T(8,128)(2,1)} %shard_map.84.refs_0_), channel_id=1, source_target_pairs={{0,2},{1,3},{2,0},{3,1},{4,6},{5,7},{6,4},{7,5},{8,10},{9,11},{10,... | collective-permute-start | bytes 1474568 | tf_op jit(solution)/shard_map/ppermute | solution.py:154
  89.2 17.9 %collective-permute-start.6 = (bf16[192,1280]{1,0:T(8,128)(2,1)}, bf16[192,1280]{1,0:T(8,128)(2,1)S(1)}, u32[]{:S(2)}, u32[]{:S(2)}) collective-permute-start(bf16[192,1280]{1,0:T(8,128)(2,1)} %shard_map.84.refs_0_), channel_id=1, source_target_pairs={{0,1},{1,0},{2,3},{3,2},{4,5},{5,4},{6,7},{7,6},{8,9},{9,8},{10,11... | collective-permute-start | bytes 1474568 | tf_op jit(solution)/shard_map/ppermute | solution.py:154
  96.4 11.0 %collective-permute-start.7 = (bf16[192,1280]{1,0:T(8,128)(2,1)}, bf16[192,1280]{1,0:T(8,128)(2,1)S(1)}, u32[]{:S(2)}, u32[]{:S(2)}) collective-permute-start(bf16[192,1280]{1,0:T(8,128)(2,1)} %shard_map.85.refs_1_), channel_id=1, source_target_pairs={{0,1},{1,0},{2,3},{3,2},{4,5},{5,4},{6,7},{7,6},{8,9},{9,8},{10,11... | collective-permute-start | bytes 1474568 | tf_op jit(solution)/shard_map/ppermute | solution.py:154
  100.5 6.5 %copy-start.5 = (bf16[192,1280]{1,0:T(8,128)(2,1)}, bf16[192,1280]{1,0:T(8,128)(2,1)S(1)}, u32[]{:S(2)}) copy-start(bf16[192,1280]{1,0:T(8,128)(2,1)S(1)} %collective-permute-done.8.refs_4_) | copy-start | bytes 1474564
  100.5 12.3 %collective-permute-start.9 = (bf16[192,1280]{1,0:T(8,128)(2,1)}, bf16[192,1280]{1,0:T(8,128)(2,1)}, u32[]{:S(2)}, u32[]{:S(2)}) collective-permute-start(bf16[192,1280]{1,0:T(8,128)(2,1)} %shard_map.85.refs_1_), channel_id=1, source_target_pairs={{0,2},{1,3},{2,0},{3,1},{4,6},{5,7},{6,4},{7,5},{8,10},{9,11},{10,... | collective-permute-start | bytes 1474568 | tf_op jit(solution)/shard_map/ppermute | solution.py:154
  102.1 11.9 %collective-permute-start.10 = (bf16[192,1280]{1,0:T(8,128)(2,1)S(1)}, bf16[192,1280]{1,0:T(8,128)(2,1)S(1)}, u32[]{:S(2)}, u32[]{:S(2)}) collective-permute-start(bf16[192,1280]{1,0:T(8,128)(2,1)S(1)} %collective-permute-done.8.refs_4_), channel_id=1, source_target_pairs={{0,1},{1,0},{2,3},{3,2},{4,5},{5,4},{6,7},{7,6},{8,9},{9,8},{10,11... | collective-permute-start | bytes 1474568 | tf_op jit(solution)/shard_map/ppermute | solution.py:154
  104.5 14.5 %copy-start.3 = (bf16[640,640]{1,0:T(8,128)(2,1)}, bf16[640,640]{1,0:T(8,128)(2,1)S(1)}, u32[]{:S(2)}) copy-start(bf16[640,640]{1,0:T(8,128)(2,1)S(1)} %broadcast_select_fusion.1.refs_10_) | copy-start | bytes 2457604
  104.6 23.9 %collective-permute-start.23 = (bf16[640,640]{1,0:T(8,128)(2,1)}, bf16[640,640]{1,0:T(8,128)(2,1)}, u32[]{:S(2)}, u32[]{:S(2)}) collective-permute-start(bf16[640,640]{1,0:T(8,128)(2,1)} %pad_maximum_fusion.refs_8_), channel_id=1, source_target_pairs={{0,16},{16,0},{1,17},{17,1},{2,18},{18,2},{3,19},{19,3},{4,20},{20... | collective-permute-start | bytes 2457608 | tf_op jit(solution)/shard_map/ppermute | solution.py:157
  107.1 12.0 %copy-start.4 = (bf16[640,640]{1,0:T(8,128)(2,1)}, bf16[640,640]{1,0:T(8,128)(2,1)S(1)}, u32[]{:S(2)}) copy-start(bf16[640,640]{1,0:T(8,128)(2,1)S(1)} %broadcast_select_fusion.refs_11_) | copy-start | bytes 2457604
  107.1 11.9 %copy-start.6 = (bf16[192,1280]{1,0:T(8,128)(2,1)}, bf16[192,1280]{1,0:T(8,128)(2,1)S(1)}, u32[]{:S(2)}) copy-start(bf16[192,1280]{1,0:T(8,128)(2,1)S(1)} %collective-permute-done.6.refs_2_) | copy-start | bytes 1474564
  107.1 35.2 %collective-permute-start.24 = (bf16[640,640]{1,0:T(8,128)(2,1)}, bf16[640,640]{1,0:T(8,128)(2,1)}, u32[]{:S(2)}, u32[]{:S(2)}) collective-permute-start(bf16[640,640]{1,0:T(8,128)(2,1)} %collective-permute-done.15.refs_9_), channel_id=1, source_target_pairs={{0,16},{16,0},{1,17},{17,1},{2,18},{18,2},{3,19},{19,3},{4,20},{20... | collective-permute-start | bytes 2457608 | tf_op jit(solution)/shard_map/ppermute | solution.py:157
  107.4 11.6 %copy-start.7 = (bf16[192,1280]{1,0:T(8,128)(2,1)}, bf16[192,1280]{1,0:T(8,128)(2,1)S(1)}, u32[]{:S(2)}) copy-start(bf16[192,1280]{1,0:T(8,128)(2,1)S(1)} %collective-permute-done.7.refs_3_) | copy-start | bytes 1474564
  107.4 52.4 %collective-permute-start.25 = (bf16[640,640]{1,0:T(8,128)(2,1)S(1)}, bf16[640,640]{1,0:T(8,128)(2,1)}, u32[]{:S(2)}, u32[]{:S(2)}) collective-permute-start(bf16[640,640]{1,0:T(8,128)(2,1)S(1)} %broadcast_select_fusion.1.refs_10_), channel_id=1, source_target_pairs={{0,16},{16,0},{1,17},{17,1},{2,18},{18,2},{3,19},{19,3},{4,20},{20... | collective-permute-start | bytes 2457608 | tf_op jit(solution)/shard_map/ppermute | solution.py:157
  112.8 64.6 %collective-permute-start.26 = (bf16[640,640]{1,0:T(8,128)(2,1)S(1)}, bf16[640,640]{1,0:T(8,128)(2,1)}, u32[]{:S(2)}, u32[]{:S(2)}) collective-permute-start(bf16[640,640]{1,0:T(8,128)(2,1)S(1)} %broadcast_select_fusion.refs_11_), channel_id=1, source_target_pairs={{0,16},{16,0},{1,17},{17,1},{2,18},{18,2},{3,19},{19,3},{4,20},{20... | collective-permute-start | bytes 2457608 | tf_op jit(solution)/shard_map/ppermute | solution.py:157
  114.0 0.8 copy-start.8
  114.8 4.2 %collective-permute-start.11 = (bf16[192,1280]{1,0:T(8,128)(2,1)}, bf16[192,1280]{1,0:T(8,128)(2,1)S(1)}, u32[]{:S(2)}, u32[]{:S(2)}) collective-permute-start(bf16[192,1280]{1,0:T(8,128)(2,1)} %collective-permute-done.9.refs_5_), channel_id=1, source_target_pairs={{0,1},{1,0},{2,3},{3,2},{4,5},{5,4},{6,7},{7,6},{8,9},{9,8},{10,11... | collective-permute-start | bytes 1474568 | tf_op jit(solution)/shard_map/ppermute | solution.py:154
  119.1 0.8 copy-start.9
  127.8 58.6 %collective-permute-start.20 = (bf16[192,640]{1,0:T(8,128)(2,1)}, bf16[192,640]{1,0:T(8,128)(2,1)S(1)}, u32[]{:S(2)}, u32[]{:S(2)}) collective-permute-start(bf16[192,640]{1,0:T(8,128)(2,1)} %get-tuple-element.30), channel_id=1, source_target_pairs={{0,1},{1,0},{2,3},{3,2},{4,5},{5,4},{6,7},{7,6},{8,9},{9,8},{10,11... | collective-permute-start | bytes 737288 | tf_op jit(solution)/shard_map/ppermute | solution.py:154
  128.5 60.1 %collective-permute-start.21 = (bf16[192,640]{1,0:T(8,128)(2,1)}, bf16[192,640]{1,0:T(8,128)(2,1)S(1)}, u32[]{:S(2)}, u32[]{:S(2)}) collective-permute-start(bf16[192,640]{1,0:T(8,128)(2,1)} %get-tuple-element.31), channel_id=1, source_target_pairs={{0,2},{1,3},{2,0},{3,1},{4,6},{5,7},{6,4},{7,5},{8,10},{9,11},{10,... | collective-permute-start | bytes 737288 | tf_op jit(solution)/shard_map/ppermute | solution.py:154
  142.3 46.3 %collective-permute-start.22 = (bf16[192,640]{1,0:T(8,128)(2,1)}, bf16[192,640]{1,0:T(8,128)(2,1)S(1)}, u32[]{:S(2)}, u32[]{:S(2)}) collective-permute-start(bf16[192,640]{1,0:T(8,128)(2,1)} %get-tuple-element.32), channel_id=1, source_target_pairs={{0,3},{1,2},{2,1},{3,0},{4,7},{5,6},{6,5},{7,4},{8,11},{9,10},{10,... | collective-permute-start | bytes 737288 | tf_op jit(solution)/shard_map/ppermute | solution.py:154
  185.3 3.3 %collective-permute-start.27 = (bf16[192,640]{1,0:T(8,128)(2,1)}, bf16[192,640]{1,0:T(8,128)(2,1)S(1)}, u32[]{:S(2)}, u32[]{:S(2)}) collective-permute-start(bf16[192,640]{1,0:T(8,128)(2,1)} %get-tuple-element.34), channel_id=1, source_target_pairs={{0,1},{1,0},{2,3},{3,2},{4,5},{5,4},{6,7},{7,6},{8,9},{9,8},{10,11... | collective-permute-start | bytes 737288 | tf_op jit(solution)/shard_map/ppermute | solution.py:154
  186.3 7.6 %collective-permute-start.28 = (bf16[192,640]{1,0:T(8,128)(2,1)}, bf16[192,640]{1,0:T(8,128)(2,1)S(1)}, u32[]{:S(2)}, u32[]{:S(2)}) collective-permute-start(bf16[192,640]{1,0:T(8,128)(2,1)} %get-tuple-element.35), channel_id=1, source_target_pairs={{0,2},{1,3},{2,0},{3,1},{4,6},{5,7},{6,4},{7,5},{8,10},{9,11},{10,... | collective-permute-start | bytes 737288 | tf_op jit(solution)/shard_map/ppermute | solution.py:154
  186.4 13.1 %copy-start.11 = (bf16[192,640]{1,0:T(8,128)(2,1)}, bf16[192,640]{1,0:T(8,128)(2,1)S(1)}, u32[]{:S(2)}) copy-start(bf16[192,640]{1,0:T(8,128)(2,1)S(1)} %collective-permute-done.20.refs_1_) | copy-start | bytes 737284
  186.4 13.1 %collective-permute-start.29 = (bf16[192,640]{1,0:T(8,128)(2,1)}, bf16[192,640]{1,0:T(8,128)(2,1)S(1)}, u32[]{:S(2)}, u32[]{:S(2)}) collective-permute-start(bf16[192,640]{1,0:T(8,128)(2,1)} %get-tuple-element.36), channel_id=1, source_target_pairs={{0,3},{1,2},{2,1},{3,0},{4,7},{5,6},{6,5},{7,4},{8,11},{9,10},{10,... | collective-permute-start | bytes 737288 | tf_op jit(solution)/shard_map/ppermute | solution.py:154
  188.6 10.9 %copy-start.12 = (bf16[192,640]{1,0:T(8,128)(2,1)}, bf16[192,640]{1,0:T(8,128)(2,1)S(1)}, u32[]{:S(2)}) copy-start(bf16[192,640]{1,0:T(8,128)(2,1)S(1)} %collective-permute-done.21.refs_2_) | copy-start | bytes 737284
  188.6 10.8 %copy-start.13 = (bf16[192,640]{1,0:T(8,128)(2,1)}, bf16[192,640]{1,0:T(8,128)(2,1)S(1)}, u32[]{:S(2)}) copy-start(bf16[192,640]{1,0:T(8,128)(2,1)S(1)} %collective-permute-done.22.refs_3_) | copy-start | bytes 737284
  188.6 10.8 %copy-start.14 = (bf16[192,640]{1,0:T(8,128)(2,1)}, bf16[192,640]{1,0:T(8,128)(2,1)S(1)}, u32[]{:S(2)}) copy-start(bf16[192,640]{1,0:T(8,128)(2,1)S(1)} %collective-permute-done.27.refs_5_) | copy-start | bytes 737284
  193.9 5.5 %copy-start.15 = (bf16[192,640]{1,0:T(8,128)(2,1)}, bf16[192,640]{1,0:T(8,128)(2,1)S(1)}, u32[]{:S(2)}) copy-start(bf16[192,640]{1,0:T(8,128)(2,1)S(1)} %collective-permute-done.28.refs_6_) | copy-start | bytes 737284
  199.4 0.7 copy-start.16

commit v2 on v1

v2 whole, which is shorter than its diff:
```python
import functools

import jax
import jax.numpy as jnp
from jax import lax
from jax.experimental import pallas as pl
from jax.experimental.pallas import tpu as pltpu
from jax.sharding import PartitionSpec as P


HD = 128


def whole(count):
    return [pl.BlockSpec(memory_space=pltpu.VMEM)] * count


def scaled_heads(x_ref, gain_ref):
    block = x_ref[...].astype(jnp.float32)
    inverse = lax.rsqrt(jnp.mean(block * block, axis=-1, keepdims=True) + 1e-06)
    for i in range(x_ref.shape[1] // HD):
        piece = x_ref[:, i * HD : (i + 1) * HD].astype(jnp.float32)
        yield i, (piece * inverse * gain_ref[i : i + 1, :]).astype(jnp.bfloat16)


def norm_kernel(x_ref, gain_ref, out_ref):
    for i, piece in scaled_heads(x_ref, gain_ref):
        out_ref[:, i * HD : (i + 1) * HD] = piece


def pair_kernel(k_ref, v_ref, gain_ref, *out_refs):
    wide = out_refs[0].shape[1] // 2
    for i, piece in scaled_heads(k_ref, gain_ref):
        at = i * HD % wide
        out_refs[i * HD // wide][:, at : at + HD] = piece
    for i, ref in enumerate(out_refs):
        ref[:, wide:] = v_ref[:, i * wide : (i + 1) * wide]


def norm(x, gain):
    return pl.pallas_call(
        norm_kernel,
        out_shape=jax.ShapeDtypeStruct(x.shape, jnp.bfloat16),
        in_specs=whole(2),
        out_specs=pl.BlockSpec(memory_space=pltpu.VMEM),
    )(x, gain.reshape(-1, HD))


def pair(keys, values, gain, chunks):
    rows, chans = keys.shape
    out = jax.ShapeDtypeStruct((rows, 2 * chans // chunks), jnp.bfloat16)
    return pl.pallas_call(
        pair_kernel, out_shape=[out] * chunks, in_specs=whole(3), out_specs=whole(chunks)
    )(keys, values, gain.reshape(-1, HD))


def attend_kernel(relayed, reach_ref, q_ref, *refs):
    sources = len(refs) // 2
    o_ref = refs[-1]
    k_refs, v_refs = refs[:sources], refs[sources : 2 * sources]
    scale = HD ** (-0.5)
    place = lax.axis_index("tm")
    peers = lax.axis_size("tm")
    low = place % 4
    seen = ((reach_ref[0, 0] == 1) & (place > 0), (reach_ref[0, 1] == 1) & (place < peers - 1))
    bias = [jnp.where(flag, 0.0, -1e30).astype(jnp.float32) for flag in seen]

    def three(group, at):
        before, own, after = [ref[:, at] for ref in group[:3]]
        if relayed:
            other = group[3][:, at]
            before = jnp.where(low == 0, other, before)
            after = jnp.where(low == 3, other, after)
        return before, own, after

    for h in range(q_ref.shape[1] // HD):
        at = slice(h * HD, (h + 1) * HD)
        query = q_ref[:, at]
        parts = []
        for key, extra in zip(three(k_refs, at), (bias[0], None, bias[1])):
            part = lax.dot_general(query, key, (((1,), (1,)), ((), ())), preferred_element_type=jnp.float32)
            part = part * scale
            parts.append(part if extra is None else part + extra)
        top = functools.reduce(jnp.maximum, [jnp.max(part, axis=-1, keepdims=True) for part in parts])
        expo = [jnp.exp(part - top) for part in parts]
        total = functools.reduce(jnp.add, [jnp.sum(part, axis=-1, keepdims=True) for part in expo])
        share = 1.0 / total
        out = None
        for part, value in zip(expo, three(v_refs, at)):
            weights = (part * share).astype(jnp.bfloat16)
            term = jnp.dot(weights, value, preferred_element_type=jnp.float32)
            out = term if out is None else out + term
        o_ref[:, at] = out.astype(jnp.bfloat16)


def attend(reach, qn, pairs, chunk):
    rows, double = pairs[0].shape
    wide = double // 2
    heads = wide // HD
    step = next(n for n in (5, 4, 3, 2, 1) if heads % n == 0)
    cols = step * HD
    steps = wide // cols
    q_spec = pl.BlockSpec((rows, cols), lambda i: (0, chunk * steps + i))
    k_spec = pl.BlockSpec((rows, cols), lambda i: (0, i))
    v_spec = pl.BlockSpec((rows, cols), lambda i: (0, steps + i))
    return pl.pallas_call(
        functools.partial(attend_kernel, len(pairs) == 4),
        grid=(steps,),
        out_shape=jax.ShapeDtypeStruct((rows, wide), jnp.bfloat16),
        in_specs=[pl.BlockSpec(memory_space=pltpu.SMEM), q_spec] + [k_spec] * len(pairs) + [v_spec] * len(pairs),
        out_specs=k_spec,
    )(reach, qn, *pairs, *pairs)


def project_kernel(count, share, gate_ref, *refs):
    slots = len(refs) - count - 6
    att_refs, w_refs = refs[:count], refs[count : count + slots]
    outs = refs[count + slots : count + slots + 4]
    w_ref, sems = refs[count + slots + 4 :]
    wide = att_refs[0].shape[1]
    depth, cols = w_refs[0].shape
    chunks = count // 4
    place = lax.axis_index("tm")
    line = place // 4
    copies = []
    for i, ref in enumerate(w_refs):
        start = pl.multiple_of((line ^ i) * depth, depth) if slots > 1 else 0
        copies.append(pltpu.make_async_copy(ref, w_ref.at[pl.ds(start, depth)], sems.at[i]))
    for copy in copies:
        copy.start()
    for copy in copies:
        copy.wait()
    first = ((place % 4) * 2 + (lax.axis_index("groups") ^ share)) * (cols // HD)
    for p in range(4):
        acc = None
        for j in range(chunks):
            term = jnp.dot(
                att_refs[p * chunks + j][...],
                w_ref[j * wide : (j + 1) * wide, :],
                preferred_element_type=jnp.float32,
            )
            acc = term if acc is None else acc + term
        for b in range(cols // HD):
            at = slice(b * HD, (b + 1) * HD)
            outs[p][:, at] = (gate_ref[pl.ds(first + b, 1), :] * acc[:, at]).astype(jnp.bfloat16)


def project(gate, att, weights, share):
    rows, wide = att[0].shape
    chans = wide * len(att) // 4
    cols = weights[0].shape[1]
    slots = len(weights)
    return pl.pallas_call(
        functools.partial(project_kernel, len(att), share),
        out_shape=[jax.ShapeDtypeStruct((rows, cols), jnp.bfloat16)] * 4,
        in_specs=whole(1 + len(att)) + [pl.BlockSpec(memory_space=pl.ANY)] * slots,
        out_specs=whole(4),
        scratch_shapes=[pltpu.VMEM((chans, cols), jnp.bfloat16), pltpu.SemaphoreType.DMA((slots,))],
    )(gate.reshape(-1, HD), *att, *weights)


def place_kernel(*refs):
    pieces, out_ref = refs[:-1], refs[-1]
    cols = pieces[0].shape[1]
    low = lax.axis_index("tm") % 4
    group = lax.axis_index("groups")
    for i, ref in enumerate(pieces):
        start = pl.multiple_of(((low ^ (i % 4)) * 2 + (group ^ (i // 4))) * cols, HD)
        out_ref[:, pl.ds(start, cols)] = ref[...]


def place_pieces(pieces):
    rows, cols = pieces[0].shape
    return pl.pallas_call(
        place_kernel,
        out_shape=jax.ShapeDtypeStruct((rows, cols * len(pieces)), jnp.bfloat16),
        in_specs=whole(len(pieces)),
        out_specs=pl.BlockSpec(memory_space=pltpu.VMEM),
        name="place",
    )(*pieces)


def local(queries, keys, values, q_gain, k_gain, out_weight, out_gate, reach):
    peers = lax.axis_size("tm")
    place = lax.axis_index("tm")
    group = lax.axis_index("groups")
    low = place % 4
    line = place // 4
    lines = peers // 4
    _, width = out_weight.shape
    _, chans = queries.shape
    cols = width // 8
    chunks = 2 if chans // HD % 2 == 0 else 1

    def swap(x, bits):
        return lax.ppermute(x, "tm", [(i, i ^ bits) for i in range(peers)])

    def group_swap(x):
        return lax.ppermute(x, "groups", [(0, 1), (1, 0)])

    def along(x, moves):
        return lax.ppermute(x, "tm", [(4 * a + i, 4 * b + i) for a, b in moves for i in range(4)])

    def send(x, pairs):
        return lax.ppermute(x, "tm", pairs)

    up = [(i, i + 1) for i in range(peers - 1)]
    down = [(j, i) for i, j in up]

    def inside(pairs):
        return [(i, j) for i, j in pairs if i // 4 == j // 4]

    def choose(flag, a, b):
        return jnp.where(flag, a, b)

    def column(quarter, share):
        return (quarter * 2 + share) * cols

    def weight_part(quarter):
        return lax.dynamic_slice_in_dim(out_weight, column(quarter, group), cols, 1)

    cuts = lax.optimization_barrier([weight_part(low ^ i) for i in range(4)])
    parts = [cuts[0]] + [swap(cuts[i], i) for i in (1, 2, 3)]
    odd, upper = (low % 2) == 1, low >= 2
    halves = [
        jnp.concatenate([choose(odd, b, a), choose(odd, a, b)], axis=0)
        for a, b in ((parts[0], parts[1]), (parts[2], parts[3]))
    ]
    block = jnp.concatenate([choose(upper, halves[1], halves[0]), choose(upper, halves[0], halves[1])], axis=0)

    pairs = pair(keys, values, k_gain, chunks)
    seen = [[send(kv, up), kv, send(kv, down)] for kv in pairs[:1]]
    for i, kv in enumerate(pairs[1:], 1):
        over = send(kv, [(4 * z + 3, 4 * z + 1) for z in range(lines)] + [(4 * z, 4 * z + 2) for z in range(lines)])
        hops = [(4 * z + 1, 4 * z + 4) for z in range(lines - 1)] + [(4 * z + 2, 4 * z - 1) for z in range(1, lines)]
        over = send(over, hops)
        seen.append([send(kv, inside(up)), kv, send(kv, inside(down)), over])
    qn = norm(queries, q_gain)

    if lines == 4:
        middle = (line == 1) | (line == 2)
        near = along(block, ((0, 1), (1, 0), (2, 3), (3, 2)))
        across = along(block, ((1, 2), (2, 1)))
        across_far = along(near, ((1, 2), (2, 1)))
        edge = along(across, ((1, 0), (2, 3)))
        edge_far = along(across_far, ((1, 0), (2, 3)))
        second = choose(middle, across_far, edge)
        third = choose(middle, across, edge_far)
        slots = [block, near, second, third]
    else:
        members = [[z * 4 + i for z in range(lines)] for i in range(4)]
        slots = [lax.all_gather(block, "tm", axis_index_groups=members, axis=0, tiled=True)]
    shares = [slots, [group_swap(slot) for slot in slots]]

    att = [[None] * chunks for _ in range(4)]
    for i in range(chunks):
        own = attend(reach, qn, seen[i], i)
        att[0][i] = own
        att[2][i] = swap(own, 2)
        att[1][i] = swap(own, 1)
        att[3][i] = swap(att[2][i], 1)
    att = [piece for pieces in att for piece in pieces]

    outs = []
    for j in range(2):
        made = project(out_gate, att, shares[j], j)
        outs += [made[0]] + [swap(made[i], i) for i in (1, 2, 3)]
    return place_pieces(outs)


def solution(mesh):
    return jax.shard_map(
        local,
        mesh=mesh,
        in_specs=(
            P(("groups", "tm"), None),
            P(("groups", "tm"), None),
            P(("groups", "tm"), None),
            P(),
            P(),
            P("tm", None),
            P(),
            P(("groups", "tm"), None),
        ),
        out_specs=P(("groups", "tm"), None),
        check_vma=False,
    )
```

time: 204 us -> 209 us (1.025)
  the two profiles are of different devices: /device:TPU:17 before, /device:TPU:27 now
where the time goes in v2:
time: 209 us; the launch traced here: 208 us
  waiting for transfers between devices  124 us (59%)
  starting transfers between devices  39.9 us (19%)
  Pallas kernels  36.8 us (18%)
  local copies, waits for them, and re-layouts  3.71 us (2%)
  other arithmetic  2.79 us (1%)
    ppermute x4, waiting for transfers between devices, group_swap(): return lax.ppermute(x, 'groups', [(0, 1), (1, 0)])  55.3 us
    ppermute x15, waiting for transfers between devices, swap(): return lax.ppermute(x, 'tm', [(i, i ^ bits) for i in range(peers)])  39.7 us
    ppermute x5, waiting for transfers between devices, along(): lax.ppermute(x, 'tm', [(4 * a + i, 4 * b + i) for a, b in moves for i in...  24.3 us
    ppermute x6, starting transfers between devices, send(): return lax.ppermute(x, 'tm', pairs)  18.6 us
    pallas_call x2, Pallas kernels, project(): pl.pallas_call(functools.partial(project_kernel, len(att), share), out_sh...  15.9 us
    pallas_call x2, Pallas kernels, attend(): pl.pallas_call(functools.partial(attend_kernel, len(pairs) == 4), grid=(s...  12 us
    ppermute x15, starting transfers between devices, swap(): return lax.ppermute(x, 'tm', [(i, i ^ bits) for i in range(peers)])  11.1 us
    ppermute x5, starting transfers between devices, along(): lax.ppermute(x, 'tm', [(4 * a + i, 4 * b + i) for a, b in moves for i in...  7.19 us
  transfers between devices with their start and end apart: 30, of which 14 were waited for; matrix products, arithmetic and copies ran while one was open for 1% of the time, Pallas kernels for 16%

profile of v2, /device:TPU:27, one launch (start us, length us, event | category | flops | bytes accessed | tf_op | source)
XLA Modules:
  0.0 207.5 jit_solution(4736474757929771215)
XLA Ops:
  0.0 1.3 constant_dynamic-slice_fusion
  1.3 0.7 collective-permute-start.14
  2.1 3.3 %shard_map.83 = (bf16[192,2560]{1,0:T(8,128)(2,1)}, bf16[192,2560]{1,0:T(8,128)(2,1)}) custom-call(bf16[192,2560]{1,0:T(8,128)(2,1)} %k_ref.1, bf16[192,2560]{1,0:T(8,128)(2,1)} %v_ref.1, f32[20,128]{1,0:T(8,128)} %bitcast.5), custom_call_target="tpu_custom_call" | custom-call | tf_op jit(solution)/shard_map/pallas_call | solution.py:52
  5.3 3.0 %collective-permute-start = (bf16[192,2560]{1,0:T(8,128)(2,1)}, bf16[192,2560]{1,0:T(8,128)(2,1)}, u32[]{:S(2)}, u32[]{:S(2)}) collective-permute-start(bf16[192,2560]{1,0:T(8,128)(2,1)} %get-tuple-element.19.refs_1_.refs_4_), channel_id=1, source_target_pairs={{0,1},{1,2},{2,3},{3,4},{4,5},{5,6},{6,7},{7,8},{8,9},{9,10},{10,1... | collective-permute-start | bytes 2949128 | tf_op jit(solution)/shard_map/ppermute | solution.py:205
  8.4 0.6 collective-permute-start.12
  8.9 0.2 collective-permute-start.13
  9.2 16.9 %collective-permute-done.12 = bf16[160,640]{1,0:T(8,128)(2,1)S(1)} collective-permute-done((bf16[160,640]{1,0:T(8,128)(2,1)S(1)}, bf16[160,640]{1,0:T(8,128)(2,1)S(1)}, u32[]{:S(2)}, u32[]{:S(2)}) %collective-permute-start.12) | collective-permute-done | bytes 204832 | tf_op jit(solution)/shard_map/ppermute | solution.py:196
  26.1 3.0 %collective-permute-done.13 = bf16[160,640]{1,0:T(8,128)(2,1)S(1)} collective-permute-done((bf16[160,640]{1,0:T(8,128)(2,1)S(1)}, bf16[160,640]{1,0:T(8,128)(2,1)S(1)}, u32[]{:S(2)}, u32[]{:S(2)}) %collective-permute-start.13) | collective-permute-done | bytes 204832 | tf_op jit(solution)/shard_map/ppermute | solution.py:196
  29.4 1.3 collective-permute-start.15
  30.7 2.7 %collective-permute-start.1 = (bf16[192,2560]{1,0:T(8,128)(2,1)S(1)}, bf16[192,2560]{1,0:T(8,128)(2,1)S(1)}, u32[]{:S(2)}, u32[]{:S(2)}) collective-permute-start(bf16[192,2560]{1,0:T(8,128)(2,1)S(1)} %copy-done.3), channel_id=1, source_target_pairs={{1,0},{2,1},{3,2},{4,3},{5,4},{6,5},{7,6},{8,7},{9,8},{10,9},{11,1... | collective-permute-start | bytes 2949128 | tf_op jit(solution)/shard_map/ppermute | solution.py:205
  33.4 1.3 collective-permute-start.4
  34.7 1.6 collective-permute-start.17
  36.3 2.9 %collective-permute-start.2 = (bf16[192,2560]{1,0:T(8,128)(2,1)S(1)}, bf16[192,2560]{1,0:T(8,128)(2,1)S(1)}, u32[]{:S(2)}, u32[]{:S(2)}) collective-permute-start(bf16[192,2560]{1,0:T(8,128)(2,1)S(1)} %copy-done), channel_id=1, source_target_pairs={{0,1},{1,2},{2,3},{4,5},{5,6},{6,7},{8,9},{9,10},{10,11},{12,13},{... | collective-permute-start | bytes 2949128 | tf_op jit(solution)/shard_map/ppermute | solution.py:205
  39.2 9.2 %collective-permute-done.15.refs_9_ = bf16[640,640]{1,0:T(8,128)(2,1)} collective-permute-done((bf16[640,640]{1,0:T(8,128)(2,1)S(1)}, bf16[640,640]{1,0:T(8,128)(2,1)}, u32[]{:S(2)}, u32[]{:S(2)}) %collective-permute-start.15) | collective-permute-done | bytes 819232 | tf_op jit(solution)/shard_map/ppermute | solution.py:202
  48.4 1.5 collective-permute-start.16
  49.9 4.6 %collective-permute-done.1.refs_2_.refs_5_ = bf16[192,2560]{1,0:T(8,128)(2,1)S(1)} collective-permute-done((bf16[192,2560]{1,0:T(8,128)(2,1)S(1)}, bf16[192,2560]{1,0:T(8,128)(2,1)S(1)}, u32[]{:S(2)}, u32[]{:S(2)}) %collective-permute-start.1) | collective-permute-done | bytes 983072 | tf_op jit(solution)/shard_map/ppermute | solution.py:205
  54.5 7.1 %collective-permute-start.3 = (bf16[192,2560]{1,0:T(8,128)(2,1)S(1)}, bf16[192,2560]{1,0:T(8,128)(2,1)S(1)}, u32[]{:S(2)}, u32[]{:S(2)}) collective-permute-start(bf16[192,2560]{1,0:T(8,128)(2,1)S(1)} %copy-done), channel_id=1, source_target_pairs={{1,0},{2,1},{3,2},{5,4},{6,5},{7,6},{9,8},{10,9},{11,10},{13,12},{... | collective-permute-start | bytes 2949128 | tf_op jit(solution)/shard_map/ppermute | solution.py:205
  61.7 1.6 collective-permute-start.5
  63.3 1.3 collective-permute-start.18
  64.6 1.5 collective-permute-start.19
  66.1 2.6 %shard_map.82.q_ref = bf16[192,2560]{1,0:T(8,128)(2,1)} custom-call(bf16[192,2560]{1,0:T(8,128)(2,1)} %x_ref.1, f32[20,128]{1,0:T(8,128)} %bitcast.6), custom_call_target="tpu_custom_call" | custom-call | tf_op jit(solution)/shard_map/pallas_call | solution.py:41
  68.7 5.8 %shard_map.84.refs_0_ = bf16[192,1280]{1,0:T(8,128)(2,1)} custom-call(s32[1,2]{1,0:T(1,128)} %reach_ref.3, bf16[192,2560]{1,0:T(8,128)(2,1)} %shard_map.82.q_ref, bf16[192,2560]{1,0:T(8,128)(2,1)} %collective-permute-done.refs_0_.refs_3_, bf16[192,2560]{1,0:T(8,128)(2,1)} %get-tuple-element.19.refs_1_.refs_4_, bf16[192,2560]{1,0:T(8,128)(2,1)} %copy-done.4, ...), custom_call_target="tpu_custom_call" | custom-call | tf_op jit(solution)/shard_map/pallas_call | solution.py:106
  74.7 4.1 %collective-permute-start.6 = (bf16[192,1280]{1,0:T(8,128)(2,1)}, bf16[192,1280]{1,0:T(8,128)(2,1)}, u32[]{:S(2)}, u32[]{:S(2)}) collective-permute-start(bf16[192,1280]{1,0:T(8,128)(2,1)} %shard_map.84.refs_0_), channel_id=1, source_target_pairs={{0,1},{1,0},{2,3},{3,2},{4,5},{5,4},{6,7},{7,6},{8,9},{9,8},{10,11... | collective-permute-start | bytes 1474568 | tf_op jit(solution)/shard_map/ppermute | solution.py:196
  78.7 6.9 %collective-permute-done.8.refs_4_ = bf16[192,1280]{1,0:T(8,128)(2,1)S(1)} collective-permute-done((bf16[192,1280]{1,0:T(8,128)(2,1)}, bf16[192,1280]{1,0:T(8,128)(2,1)S(1)}, u32[]{:S(2)}, u32[]{:S(2)}) %collective-permute-start.8) | collective-permute-done | bytes 491552 | tf_op jit(solution)/shard_map/ppermute | solution.py:196
  85.6 2.8 %collective-permute-start.10 = (bf16[192,1280]{1,0:T(8,128)(2,1)S(1)}, bf16[192,1280]{1,0:T(8,128)(2,1)}, u32[]{:S(2)}, u32[]{:S(2)}) collective-permute-start(bf16[192,1280]{1,0:T(8,128)(2,1)S(1)} %collective-permute-done.8.refs_4_), channel_id=1, source_target_pairs={{0,1},{1,0},{2,3},{3,2},{4,5},{5,4},{6,7},{7,6},{8,9},{9,8},{10,11... | collective-permute-start | bytes 1474568 | tf_op jit(solution)/shard_map/ppermute | solution.py:196
  88.5 6.1 %shard_map.85.refs_1_ = bf16[192,1280]{1,0:T(8,128)(2,1)} custom-call(s32[1,2]{1,0:T(1,128)} %reach_ref.3, bf16[192,2560]{1,0:T(8,128)(2,1)} %shard_map.82.q_ref, bf16[192,2560]{1,0:T(8,128)(2,1)} %copy-done.1, bf16[192,2560]{1,0:T(8,128)(2,1)} %get-tuple-element.20.refs_1_.refs_5_, bf16[192,2560]{1,0:T(8,128)(2,1)} %copy-done.2, ...), custom_call_target="tpu_custom_call" | custom-call | tf_op jit(solution)/shard_map/pallas_call | solution.py:106
  94.8 1.7 collective-permute-done.18
  96.5 1.2 broadcast_select_fusion.1.refs_10_
  97.8 13.4 %collective-permute-done.19 = bf16[640,640]{1,0:T(8,128)(2,1)} collective-permute-done((bf16[640,640]{1,0:T(8,128)(2,1)}, bf16[640,640]{1,0:T(8,128)(2,1)}, u32[]{:S(2)}, u32[]{:S(2)}) %collective-permute-start.19) | collective-permute-done | bytes 819232 | tf_op jit(solution)/shard_map/ppermute | solution.py:202
  111.2 0.3 collective-permute-start.23
  111.5 1.2 broadcast_select_fusion.refs_11_
  112.7 1.3 collective-permute-start.24
  114.0 0.3 collective-permute-start.25
  114.3 1.2 collective-permute-start.26
  115.5 0.8 copy-done.11
  116.3 1.9 collective-permute-done.11.refs_7_
  118.2 0.8 copy-done.12
  119.0 8.0 %shard_map.86 = (bf16[192,640]{1,0:T(8,128)(2,1)}, bf16[192,640]{1,0:T(8,128)(2,1)}, bf16[192,640]{1,0:T(8,128)(2,1)}, bf16[192,640]{1,0:T(8,128)(2,1)}) custom-call(f32[40,128]{1,0:T(8,128)} %bitcast.3, bf16[192,1280]{1,0:T(8,128)(2,1)} %shard_map.84.refs_0_, bf16[192,1280]{1,0:T(8,128)(2,1)} %shard_map.85.refs_1_, ...), custom_call_target="tpu_custom_call" | custom-call | tf_op jit(solution)/shard_map/pallas_call | solution.py:153
  127.2 4.4 %collective-permute-done.23.refs_8_ = bf16[640,640]{1,0:T(8,128)(2,1)} collective-permute-done((bf16[640,640]{1,0:T(8,128)(2,1)S(1)}, bf16[640,640]{1,0:T(8,128)(2,1)}, u32[]{:S(2)}, u32[]{:S(2)}) %collective-permute-start.23) | collective-permute-done | bytes 819232 | tf_op jit(solution)/shard_map/ppermute | solution.py:199
  131.6 17.6 %collective-permute-done.24.refs_9_ = bf16[640,640]{1,0:T(8,128)(2,1)} collective-permute-done((bf16[640,640]{1,0:T(8,128)(2,1)}, bf16[640,640]{1,0:T(8,128)(2,1)}, u32[]{:S(2)}, u32[]{:S(2)}) %collective-permute-start.24) | collective-permute-done | bytes 819232 | tf_op jit(solution)/shard_map/ppermute | solution.py:199
  149.1 17.6 %collective-permute-done.25.refs_10_ = bf16[640,640]{1,0:T(8,128)(2,1)} collective-permute-done((bf16[640,640]{1,0:T(8,128)(2,1)S(1)}, bf16[640,640]{1,0:T(8,128)(2,1)}, u32[]{:S(2)}, u32[]{:S(2)}) %collective-permute-start.25) | collective-permute-done | bytes 819232 | tf_op jit(solution)/shard_map/ppermute | solution.py:199
  166.7 15.8 %collective-permute-done.26.refs_11_ = bf16[640,640]{1,0:T(8,128)(2,1)} collective-permute-done((bf16[640,640]{1,0:T(8,128)(2,1)S(1)}, bf16[640,640]{1,0:T(8,128)(2,1)}, u32[]{:S(2)}, u32[]{:S(2)}) %collective-permute-start.26) | collective-permute-done | bytes 819232 | tf_op jit(solution)/shard_map/ppermute | solution.py:199
  182.5 7.9 %shard_map.87 = (bf16[192,640]{1,0:T(8,128)(2,1)}, bf16[192,640]{1,0:T(8,128)(2,1)}, bf16[192,640]{1,0:T(8,128)(2,1)}, bf16[192,640]{1,0:T(8,128)(2,1)}) custom-call(f32[40,128]{1,0:T(8,128)} %bitcast.4, bf16[192,1280]{1,0:T(8,128)(2,1)} %shard_map.84.refs_0_, bf16[192,1280]{1,0:T(8,128)(2,1)} %shard_map.85.refs_1_, ...), custom_call_target="tpu_custom_call" | custom-call | tf_op jit(solution)/shard_map/pallas_call | solution.py:153
  190.6 2.0 collective-permute-start.29
  192.7 5.2 %collective-permute-done.28.refs_6_ = bf16[192,640]{1,0:T(8,128)(2,1)S(1)} collective-permute-done((bf16[192,640]{1,0:T(8,128)(2,1)}, bf16[192,640]{1,0:T(8,128)(2,1)S(1)}, u32[]{:S(2)}, u32[]{:S(2)}) %collective-permute-start.28) | collective-permute-done | bytes 245792 | tf_op jit(solution)/shard_map/ppermute | solution.py:196
  197.9 5.9 %collective-permute-done.29.refs_7_ = bf16[192,640]{1,0:T(8,128)(2,1)S(1)} collective-permute-done((bf16[192,640]{1,0:T(8,128)(2,1)}, bf16[192,640]{1,0:T(8,128)(2,1)S(1)}, u32[]{:S(2)}, u32[]{:S(2)}) %collective-permute-start.29) | collective-permute-done | bytes 245792 | tf_op jit(solution)/shard_map/ppermute | solution.py:196
  203.8 0.7 copy-done.18
  204.5 3.0 %place.1 = bf16[192,5120]{1,0:T(8,128)(2,1)} custom-call(bf16[192,640]{1,0:T(8,128)(2,1)} %get-tuple-element.25.refs_0_, bf16[192,640]{1,0:T(8,128)(2,1)} %copy-done.13, bf16[192,640]{1,0:T(8,128)(2,1)} %copy-done.14, bf16[192,640]{1,0:T(8,128)(2,1)} %copy-done.15, bf16[192,640]{1,0:T(8,128)(2,1)} %get-tuple-element.29.refs_4_, bf16[192,640]{1,0:T(8,128)(2,1)} %copy-done.16, ...), custom_call_target="tpu_custom_call" | custom-call | tf_op jit(solution)/shard_map/place/pallas_call | solution.py:174
  (64 shorter events, 1.1 us)
Async XLA Ops:
  1.3 7.9 %collective-permute-start.14 = (bf16[160,640]{1,0:T(8,128)(2,1)S(1)}, bf16[160,640]{1,0:T(8,128)(2,1)S(1)}, u32[]{:S(2)}, u32[]{:S(2)}) collective-permute-start(bf16[160,640]{1,0:T(8,128)(2,1)S(1)} %get-tuple-element.23), channel_id=1, source_target_pairs={{0,1},{1,0},{2,3},{3,2},{4,5},{5,4},{6,7},{7,6},{8,9},{9,8},{10,11... | collective-permute-start | bytes 614408 | tf_op jit(solution)/shard_map/ppermute | solution.py:196
  5.3 31.0 %collective-permute-start = (bf16[192,2560]{1,0:T(8,128)(2,1)}, bf16[192,2560]{1,0:T(8,128)(2,1)}, u32[]{:S(2)}, u32[]{:S(2)}) collective-permute-start(bf16[192,2560]{1,0:T(8,128)(2,1)} %get-tuple-element.19.refs_1_.refs_4_), channel_id=1, source_target_pairs={{0,1},{1,2},{2,3},{3,4},{4,5},{5,6},{6,7},{7,8},{8,9},{9,10},{10,1... | collective-permute-start | bytes 2949128 | tf_op jit(solution)/shard_map/ppermute | solution.py:205
  8.4 17.7 %collective-permute-start.12 = (bf16[160,640]{1,0:T(8,128)(2,1)S(1)}, bf16[160,640]{1,0:T(8,128)(2,1)S(1)}, u32[]{:S(2)}, u32[]{:S(2)}) collective-permute-start(bf16[160,640]{1,0:T(8,128)(2,1)S(1)} %get-tuple-element.21), channel_id=1, source_target_pairs={{0,3},{1,2},{2,1},{3,0},{4,7},{5,6},{6,5},{7,4},{8,11},{9,10},{10,... | collective-permute-start | bytes 614408 | tf_op jit(solution)/shard_map/ppermute | solution.py:196
  8.9 20.1 %collective-permute-start.13 = (bf16[160,640]{1,0:T(8,128)(2,1)S(1)}, bf16[160,640]{1,0:T(8,128)(2,1)S(1)}, u32[]{:S(2)}, u32[]{:S(2)}) collective-permute-start(bf16[160,640]{1,0:T(8,128)(2,1)S(1)} %get-tuple-element.22), channel_id=1, source_target_pairs={{0,2},{1,3},{2,0},{3,1},{4,6},{5,7},{6,4},{7,5},{8,10},{9,11},{10,... | collective-permute-start | bytes 614408 | tf_op jit(solution)/shard_map/ppermute | solution.py:196
  29.1 1.6 copy-start.3
  29.2 4.2 %copy-start = (bf16[192,2560]{1,0:T(8,128)(2,1)S(1)}, bf16[192,2560]{1,0:T(8,128)(2,1)}, u32[]{:S(2)}) copy-start(bf16[192,2560]{1,0:T(8,128)(2,1)} %get-tuple-element.20.refs_1_.refs_5_) | copy-start | bytes 2949124
  29.4 33.9 %copy-start.5 = (bf16[640,640]{1,0:T(8,128)(2,1)}, bf16[640,640]{1,0:T(8,128)(2,1)S(1)}, u32[]{:S(2)}) copy-start(bf16[640,640]{1,0:T(8,128)(2,1)S(1)} %pad_maximum_fusion.refs_8_) | copy-start | bytes 2457604
  29.4 18.9 %collective-permute-start.15 = (bf16[640,640]{1,0:T(8,128)(2,1)S(1)}, bf16[640,640]{1,0:T(8,128)(2,1)}, u32[]{:S(2)}, u32[]{:S(2)}) collective-permute-start(bf16[640,640]{1,0:T(8,128)(2,1)S(1)} %pad_maximum_fusion.refs_8_), channel_id=1, source_target_pairs={{0,4},{1,5},{2,6},{3,7},{4,0},{5,1},{6,2},{7,3},{8,12},{9,13},{10,... | collective-permute-start | bytes 2457608 | tf_op jit(solution)/shard_map/ppermute | solution.py:202
  30.7 23.8 %collective-permute-start.1 = (bf16[192,2560]{1,0:T(8,128)(2,1)S(1)}, bf16[192,2560]{1,0:T(8,128)(2,1)S(1)}, u32[]{:S(2)}, u32[]{:S(2)}) collective-permute-start(bf16[192,2560]{1,0:T(8,128)(2,1)S(1)} %copy-done.3), channel_id=1, source_target_pairs={{1,0},{2,1},{3,2},{4,3},{5,4},{6,5},{7,6},{8,7},{9,8},{10,9},{11,1... | collective-permute-start | bytes 2949128 | tf_op jit(solution)/shard_map/ppermute | solution.py:205
  33.4 28.3 %collective-permute-start.4 = (bf16[192,2560]{1,0:T(8,128)(2,1)S(1)}, bf16[192,2560]{1,0:T(8,128)(2,1)}, u32[]{:S(2)}, u32[]{:S(2)}) collective-permute-start(bf16[192,2560]{1,0:T(8,128)(2,1)S(1)} %copy-done), channel_id=1, source_target_pairs={{3,1},{7,5},{11,9},{15,13},{0,2},{4,6},{8,10},{12,14},{19,17},{23,... | collective-permute-start | bytes 2949128 | tf_op jit(solution)/shard_map/ppermute | solution.py:205
  34.7 28.6 %collective-permute-start.17 = (bf16[640,640]{1,0:T(8,128)(2,1)S(1)}, bf16[640,640]{1,0:T(8,128)(2,1)}, u32[]{:S(2)}, u32[]{:S(2)}) collective-permute-start(bf16[640,640]{1,0:T(8,128)(2,1)S(1)} %pad_maximum_fusion.refs_8_), channel_id=1, source_target_pairs={{4,8},{5,9},{6,10},{7,11},{8,4},{9,5},{10,6},{11,7},{20,24},{21,25... | collective-permute-start | bytes 2457608 | tf_op jit(solution)/shard_map/ppermute | solution.py:202
  36.3 38.2 %collective-permute-start.2 = (bf16[192,2560]{1,0:T(8,128)(2,1)S(1)}, bf16[192,2560]{1,0:T(8,128)(2,1)S(1)}, u32[]{:S(2)}, u32[]{:S(2)}) collective-permute-start(bf16[192,2560]{1,0:T(8,128)(2,1)S(1)} %copy-done), channel_id=1, source_target_pairs={{0,1},{1,2},{2,3},{4,5},{5,6},{6,7},{8,9},{9,10},{10,11},{12,13},{... | collective-permute-start | bytes 2949128 | tf_op jit(solution)/shard_map/ppermute | solution.py:205
  48.4 16.2 %collective-permute-start.16 = (bf16[640,640]{1,0:T(8,128)(2,1)}, bf16[640,640]{1,0:T(8,128)(2,1)}, u32[]{:S(2)}, u32[]{:S(2)}) collective-permute-start(bf16[640,640]{1,0:T(8,128)(2,1)} %collective-permute-done.15.refs_9_), channel_id=1, source_target_pairs={{4,8},{5,9},{6,10},{7,11},{8,4},{9,5},{10,6},{11,7},{20,24},{21,25... | collective-permute-start | bytes 2457608 | tf_op jit(solution)/shard_map/ppermute | solution.py:202
  54.5 7.2 %copy-start.4 = (bf16[192,2560]{1,0:T(8,128)(2,1)}, bf16[192,2560]{1,0:T(8,128)(2,1)S(1)}, u32[]{:S(2)}) copy-start(bf16[192,2560]{1,0:T(8,128)(2,1)S(1)} %collective-permute-done.1.refs_2_.refs_5_) | copy-start | bytes 2949124
  54.5 20.2 %collective-permute-start.3 = (bf16[192,2560]{1,0:T(8,128)(2,1)S(1)}, bf16[192,2560]{1,0:T(8,128)(2,1)S(1)}, u32[]{:S(2)}, u32[]{:S(2)}) collective-permute-start(bf16[192,2560]{1,0:T(8,128)(2,1)S(1)} %copy-done), channel_id=1, source_target_pairs={{1,0},{2,1},{3,2},{5,4},{6,5},{7,6},{9,8},{10,9},{11,10},{13,12},{... | collective-permute-start | bytes 2949128 | tf_op jit(solution)/shard_map/ppermute | solution.py:205
  61.7 26.8 %collective-permute-start.5 = (bf16[192,2560]{1,0:T(8,128)(2,1)}, bf16[192,2560]{1,0:T(8,128)(2,1)}, u32[]{:S(2)}, u32[]{:S(2)}) collective-permute-start(bf16[192,2560]{1,0:T(8,128)(2,1)} %collective-permute-done.4), channel_id=1, source_target_pairs={{1,4},{5,8},{9,12},{6,3},{10,7},{14,11},{17,20},{21,24},{25,28},{2... | collective-permute-start | bytes 2949128 | tf_op jit(solution)/shard_map/ppermute | solution.py:205
  63.3 33.2 %collective-permute-start.18 = (bf16[640,640]{1,0:T(8,128)(2,1)}, bf16[640,640]{1,0:T(8,128)(2,1)}, u32[]{:S(2)}, u32[]{:S(2)}) collective-permute-start(bf16[640,640]{1,0:T(8,128)(2,1)} %collective-permute-done.17), channel_id=1, source_target_pairs={{4,0},{5,1},{6,2},{7,3},{8,12},{9,13},{10,14},{11,15},{20,16},{21,... | collective-permute-start | bytes 2457608 | tf_op jit(solution)/shard_map/ppermute | solution.py:202
  64.6 46.6 %collective-permute-start.19 = (bf16[640,640]{1,0:T(8,128)(2,1)}, bf16[640,640]{1,0:T(8,128)(2,1)}, u32[]{:S(2)}, u32[]{:S(2)}) collective-permute-start(bf16[640,640]{1,0:T(8,128)(2,1)} %collective-permute-done.16), channel_id=1, source_target_pairs={{4,0},{5,1},{6,2},{7,3},{8,12},{9,13},{10,14},{11,15},{20,16},{21,... | collective-permute-start | bytes 2457608 | tf_op jit(solution)/shard_map/ppermute | solution.py:202
  74.5 13.9 %copy-start.1 = (bf16[192,2560]{1,0:T(8,128)(2,1)}, bf16[192,2560]{1,0:T(8,128)(2,1)S(1)}, u32[]{:S(2)}) copy-start(bf16[192,2560]{1,0:T(8,128)(2,1)S(1)} %collective-permute-done.2.refs_0_.refs_4_) | copy-start | bytes 2949124
  74.6 11.1 %collective-permute-start.8 = (bf16[192,1280]{1,0:T(8,128)(2,1)}, bf16[192,1280]{1,0:T(8,128)(2,1)S(1)}, u32[]{:S(2)}, u32[]{:S(2)}) collective-permute-start(bf16[192,1280]{1,0:T(8,128)(2,1)} %shard_map.84.refs_0_), channel_id=1, source_target_pairs={{0,2},{1,3},{2,0},{3,1},{4,6},{5,7},{6,4},{7,5},{8,10},{9,11},{10,... | collective-permute-start | bytes 1474568 | tf_op jit(solution)/shard_map/ppermute | solution.py:196
  74.7 13.8 %copy-start.2 = (bf16[192,2560]{1,0:T(8,128)(2,1)}, bf16[192,2560]{1,0:T(8,128)(2,1)S(1)}, u32[]{:S(2)}) copy-start(bf16[192,2560]{1,0:T(8,128)(2,1)S(1)} %collective-permute-done.3.refs_2_.refs_6_) | copy-start | bytes 2949124
  74.7 38.0 %collective-permute-start.6 = (bf16[192,1280]{1,0:T(8,128)(2,1)}, bf16[192,1280]{1,0:T(8,128)(2,1)}, u32[]{:S(2)}, u32[]{:S(2)}) collective-permute-start(bf16[192,1280]{1,0:T(8,128)(2,1)} %shard_map.84.refs_0_), channel_id=1, source_target_pairs={{0,1},{1,0},{2,3},{3,2},{4,5},{5,4},{6,7},{7,6},{8,9},{9,8},{10,11... | collective-permute-start | bytes 1474568 | tf_op jit(solution)/shard_map/ppermute | solution.py:196
  85.6 9.0 %copy-start.9 = (bf16[192,1280]{1,0:T(8,128)(2,1)}, bf16[192,1280]{1,0:T(8,128)(2,1)S(1)}, u32[]{:S(2)}) copy-start(bf16[192,1280]{1,0:T(8,128)(2,1)S(1)} %collective-permute-done.8.refs_4_) | copy-start | bytes 1474564
  85.6 28.4 %collective-permute-start.10 = (bf16[192,1280]{1,0:T(8,128)(2,1)S(1)}, bf16[192,1280]{1,0:T(8,128)(2,1)}, u32[]{:S(2)}, u32[]{:S(2)}) collective-permute-start(bf16[192,1280]{1,0:T(8,128)(2,1)S(1)} %collective-permute-done.8.refs_4_), channel_id=1, source_target_pairs={{0,1},{1,0},{2,3},{3,2},{4,5},{5,4},{6,7},{7,6},{8,9},{9,8},{10,11... | collective-permute-start | bytes 1474568 | tf_op jit(solution)/shard_map/ppermute | solution.py:196
  94.6 16.6 %copy-start.6 = (bf16[640,640]{1,0:T(8,128)(2,1)S(1)}, bf16[640,640]{1,0:T(8,128)(2,1)}, u32[]{:S(2)}) copy-start(bf16[640,640]{1,0:T(8,128)(2,1)} %copy-done.5) | copy-start | bytes 2457604
  94.6 19.6 %collective-permute-start.7 = (bf16[192,1280]{1,0:T(8,128)(2,1)}, bf16[192,1280]{1,0:T(8,128)(2,1)S(1)}, u32[]{:S(2)}, u32[]{:S(2)}) collective-permute-start(bf16[192,1280]{1,0:T(8,128)(2,1)} %shard_map.85.refs_1_), channel_id=1, source_target_pairs={{0,1},{1,0},{2,3},{3,2},{4,5},{5,4},{6,7},{7,6},{8,9},{9,8},{10,11... | collective-permute-start | bytes 1474568 | tf_op jit(solution)/shard_map/ppermute | solution.py:196
  96.5 18.9 %collective-permute-start.9 = (bf16[192,1280]{1,0:T(8,128)(2,1)}, bf16[192,1280]{1,0:T(8,128)(2,1)S(1)}, u32[]{:S(2)}, u32[]{:S(2)}) collective-permute-start(bf16[192,1280]{1,0:T(8,128)(2,1)} %shard_map.85.refs_1_), channel_id=1, source_target_pairs={{0,2},{1,3},{2,0},{3,1},{4,6},{5,7},{6,4},{7,5},{8,10},{9,11},{10,... | collective-permute-start | bytes 1474568 | tf_op jit(solution)/shard_map/ppermute | solution.py:196
  97.8 20.4 %copy-start.7 = (bf16[640,640]{1,0:T(8,128)(2,1)}, bf16[640,640]{1,0:T(8,128)(2,1)S(1)}, u32[]{:S(2)}) copy-start(bf16[640,640]{1,0:T(8,128)(2,1)S(1)} %broadcast_select_fusion.1.refs_10_) | copy-start | bytes 2457604
  111.2 20.4 %collective-permute-start.23 = (bf16[640,640]{1,0:T(8,128)(2,1)S(1)}, bf16[640,640]{1,0:T(8,128)(2,1)}, u32[]{:S(2)}, u32[]{:S(2)}) collective-permute-start(bf16[640,640]{1,0:T(8,128)(2,1)S(1)} %copy-done.6), channel_id=1, source_target_pairs={{0,16},{16,0},{1,17},{17,1},{2,18},{18,2},{3,19},{19,3},{4,20},{20... | collective-permute-start | bytes 2457608 | tf_op jit(solution)/shard_map/ppermute | solution.py:199
  112.7 5.5 %copy-start.8 = (bf16[640,640]{1,0:T(8,128)(2,1)}, bf16[640,640]{1,0:T(8,128)(2,1)S(1)}, u32[]{:S(2)}) copy-start(bf16[640,640]{1,0:T(8,128)(2,1)S(1)} %broadcast_select_fusion.refs_11_) | copy-start | bytes 2457604
  112.7 36.4 %collective-permute-start.24 = (bf16[640,640]{1,0:T(8,128)(2,1)}, bf16[640,640]{1,0:T(8,128)(2,1)}, u32[]{:S(2)}, u32[]{:S(2)}) collective-permute-start(bf16[640,640]{1,0:T(8,128)(2,1)} %collective-permute-done.15.refs_9_), channel_id=1, source_target_pairs={{0,16},{16,0},{1,17},{17,1},{2,18},{18,2},{3,19},{19,3},{4,20},{20... | collective-permute-start | bytes 2457608 | tf_op jit(solution)/shard_map/ppermute | solution.py:199
  114.0 52.7 %collective-permute-start.25 = (bf16[640,640]{1,0:T(8,128)(2,1)S(1)}, bf16[640,640]{1,0:T(8,128)(2,1)}, u32[]{:S(2)}, u32[]{:S(2)}) collective-permute-start(bf16[640,640]{1,0:T(8,128)(2,1)S(1)} %broadcast_select_fusion.1.refs_10_), channel_id=1, source_target_pairs={{0,16},{16,0},{1,17},{17,1},{2,18},{18,2},{3,19},{19,3},{4,20},{20... | collective-permute-start | bytes 2457608 | tf_op jit(solution)/shard_map/ppermute | solution.py:199
  114.3 3.9 %copy-start.10 = (bf16[192,1280]{1,0:T(8,128)(2,1)}, bf16[192,1280]{1,0:T(8,128)(2,1)S(1)}, u32[]{:S(2)}) copy-start(bf16[192,1280]{1,0:T(8,128)(2,1)S(1)} %collective-permute-done.7.refs_3_) | copy-start | bytes 1474564
  114.3 68.2 %collective-permute-start.26 = (bf16[640,640]{1,0:T(8,128)(2,1)S(1)}, bf16[640,640]{1,0:T(8,128)(2,1)}, u32[]{:S(2)}, u32[]{:S(2)}) collective-permute-start(bf16[640,640]{1,0:T(8,128)(2,1)S(1)} %broadcast_select_fusion.refs_11_), channel_id=1, source_target_pairs={{0,16},{16,0},{1,17},{17,1},{2,18},{18,2},{3,19},{19,3},{4,20},{20... | collective-permute-start | bytes 2457608 | tf_op jit(solution)/shard_map/ppermute | solution.py:199
  115.5 0.8 copy-start.11
  116.3 1.9 collective-permute-start.11
  118.2 0.8 copy-start.12
  127.0 63.6 %collective-permute-start.20 = (bf16[192,640]{1,0:T(8,128)(2,1)}, bf16[192,640]{1,0:T(8,128)(2,1)S(1)}, u32[]{:S(2)}, u32[]{:S(2)}) collective-permute-start(bf16[192,640]{1,0:T(8,128)(2,1)} %get-tuple-element.26), channel_id=1, source_target_pairs={{0,1},{1,0},{2,3},{3,2},{4,5},{5,4},{6,7},{7,6},{8,9},{9,8},{10,11... | collective-permute-start | bytes 737288 | tf_op jit(solution)/shard_map/ppermute | solution.py:196
  131.6 61.1 %collective-permute-start.21 = (bf16[192,640]{1,0:T(8,128)(2,1)}, bf16[192,640]{1,0:T(8,128)(2,1)S(1)}, u32[]{:S(2)}, u32[]{:S(2)}) collective-permute-start(bf16[192,640]{1,0:T(8,128)(2,1)} %get-tuple-element.27), channel_id=1, source_target_pairs={{0,2},{1,3},{2,0},{3,1},{4,6},{5,7},{6,4},{7,5},{8,10},{9,11},{10,... | collective-permute-start | bytes 737288 | tf_op jit(solution)/shard_map/ppermute | solution.py:196
  149.1 43.5 %collective-permute-start.22 = (bf16[192,640]{1,0:T(8,128)(2,1)}, bf16[192,640]{1,0:T(8,128)(2,1)S(1)}, u32[]{:S(2)}, u32[]{:S(2)}) collective-permute-start(bf16[192,640]{1,0:T(8,128)(2,1)} %get-tuple-element.28), channel_id=1, source_target_pairs={{0,3},{1,2},{2,1},{3,0},{4,7},{5,6},{6,5},{7,4},{8,11},{9,10},{10,... | collective-permute-start | bytes 737288 | tf_op jit(solution)/shard_map/ppermute | solution.py:196
  190.5 2.2 %collective-permute-start.27 = (bf16[192,640]{1,0:T(8,128)(2,1)}, bf16[192,640]{1,0:T(8,128)(2,1)S(1)}, u32[]{:S(2)}, u32[]{:S(2)}) collective-permute-start(bf16[192,640]{1,0:T(8,128)(2,1)} %get-tuple-element.30), channel_id=1, source_target_pairs={{0,1},{1,0},{2,3},{3,2},{4,5},{5,4},{6,7},{7,6},{8,9},{9,8},{10,11... | collective-permute-start | bytes 737288 | tf_op jit(solution)/shard_map/ppermute | solution.py:196
  190.5 7.4 %collective-permute-start.28 = (bf16[192,640]{1,0:T(8,128)(2,1)}, bf16[192,640]{1,0:T(8,128)(2,1)S(1)}, u32[]{:S(2)}, u32[]{:S(2)}) collective-permute-start(bf16[192,640]{1,0:T(8,128)(2,1)} %get-tuple-element.31), channel_id=1, source_target_pairs={{0,2},{1,3},{2,0},{3,1},{4,6},{5,7},{6,4},{7,5},{8,10},{9,11},{10,... | collective-permute-start | bytes 737288 | tf_op jit(solution)/shard_map/ppermute | solution.py:196
  190.6 13.1 %copy-start.13 = (bf16[192,640]{1,0:T(8,128)(2,1)}, bf16[192,640]{1,0:T(8,128)(2,1)S(1)}, u32[]{:S(2)}) copy-start(bf16[192,640]{1,0:T(8,128)(2,1)S(1)} %collective-permute-done.20.refs_1_) | copy-start | bytes 737284
  190.6 13.1 %collective-permute-start.29 = (bf16[192,640]{1,0:T(8,128)(2,1)}, bf16[192,640]{1,0:T(8,128)(2,1)S(1)}, u32[]{:S(2)}, u32[]{:S(2)}) collective-permute-start(bf16[192,640]{1,0:T(8,128)(2,1)} %get-tuple-element.32), channel_id=1, source_target_pairs={{0,3},{1,2},{2,1},{3,0},{4,7},{5,6},{6,5},{7,4},{8,11},{9,10},{10,... | collective-permute-start | bytes 737288 | tf_op jit(solution)/shard_map/ppermute | solution.py:196
  192.7 11.1 %copy-start.14 = (bf16[192,640]{1,0:T(8,128)(2,1)}, bf16[192,640]{1,0:T(8,128)(2,1)S(1)}, u32[]{:S(2)}) copy-start(bf16[192,640]{1,0:T(8,128)(2,1)S(1)} %collective-permute-done.21.refs_2_) | copy-start | bytes 737284
  192.7 11.1 %copy-start.15 = (bf16[192,640]{1,0:T(8,128)(2,1)}, bf16[192,640]{1,0:T(8,128)(2,1)S(1)}, u32[]{:S(2)}) copy-start(bf16[192,640]{1,0:T(8,128)(2,1)S(1)} %collective-permute-done.22.refs_3_) | copy-start | bytes 737284
  192.7 11.1 %copy-start.16 = (bf16[192,640]{1,0:T(8,128)(2,1)}, bf16[192,640]{1,0:T(8,128)(2,1)S(1)}, u32[]{:S(2)}) copy-start(bf16[192,640]{1,0:T(8,128)(2,1)S(1)} %collective-permute-done.27.refs_5_) | copy-start | bytes 737284
  197.9 5.9 %copy-start.17 = (bf16[192,640]{1,0:T(8,128)(2,1)}, bf16[192,640]{1,0:T(8,128)(2,1)S(1)}, u32[]{:S(2)}) copy-start(bf16[192,640]{1,0:T(8,128)(2,1)S(1)} %collective-permute-done.28.refs_6_) | copy-start | bytes 737284
  (1 other events, 0.7 us)

commit v3 on v2

v3 whole, which is shorter than its diff:
```python
import functools

import jax
import jax.numpy as jnp
from jax import lax
from jax.experimental import pallas as pl
from jax.experimental.pallas import tpu as pltpu
from jax.sharding import PartitionSpec as P


HD = 128


def whole(count):
    return [pl.BlockSpec(memory_space=pltpu.VMEM)] * count


def scaled_heads(x_ref, gain_ref):
    block = x_ref[...].astype(jnp.float32)
    inverse = lax.rsqrt(jnp.mean(block * block, axis=-1, keepdims=True) + 1e-06)
    for i in range(x_ref.shape[1] // HD):
        piece = x_ref[:, i * HD : (i + 1) * HD].astype(jnp.float32)
        yield i, (piece * inverse * gain_ref[i : i + 1, :]).astype(jnp.bfloat16)


def norm_kernel(x_ref, gain_ref, out_ref):
    for i, piece in scaled_heads(x_ref, gain_ref):
        out_ref[:, i * HD : (i + 1) * HD] = piece


def pair_kernel(k_ref, v_ref, gain_ref, out_ref):
    chans = k_ref.shape[1]
    for i, piece in scaled_heads(k_ref, gain_ref):
        out_ref[:, i * HD : (i + 1) * HD] = piece
    out_ref[:, chans:] = v_ref[...]


def norm(x, gain):
    return pl.pallas_call(
        norm_kernel,
        out_shape=jax.ShapeDtypeStruct(x.shape, jnp.bfloat16),
        in_specs=whole(2),
        out_specs=pl.BlockSpec(memory_space=pltpu.VMEM),
    )(x, gain.reshape(-1, HD))


def pair(keys, values, gain):
    rows, chans = keys.shape
    return pl.pallas_call(
        pair_kernel,
        out_shape=jax.ShapeDtypeStruct((rows, 2 * chans), jnp.bfloat16),
        in_specs=whole(3),
        out_specs=pl.BlockSpec(memory_space=pltpu.VMEM),
    )(keys, values, gain.reshape(-1, HD))


def attend_kernel(reach_ref, q_ref, kb_ref, k_ref, ka_ref, vb_ref, v_ref, va_ref, o_ref):
    scale = HD ** (-0.5)
    place = lax.axis_index("tm")
    peers = lax.axis_size("tm")
    seen = ((reach_ref[0, 0] == 1) & (place > 0), (reach_ref[0, 1] == 1) & (place < peers - 1))
    bias = [jnp.where(flag, 0.0, -1e30).astype(jnp.float32) for flag in seen]
    for h in range(q_ref.shape[1] // HD):
        at = slice(h * HD, (h + 1) * HD)
        query = q_ref[:, at]
        parts = []
        for ref, extra in ((kb_ref, bias[0]), (k_ref, None), (ka_ref, bias[1])):
            part = lax.dot_general(query, ref[:, at], (((1,), (1,)), ((), ())), preferred_element_type=jnp.float32)
            part = part * scale
            parts.append(part if extra is None else part + extra)
        top = functools.reduce(jnp.maximum, [jnp.max(part, axis=-1, keepdims=True) for part in parts])
        expo = [jnp.exp(part - top) for part in parts]
        total = functools.reduce(jnp.add, [jnp.sum(part, axis=-1, keepdims=True) for part in expo])
        share = 1.0 / total
        out = None
        for part, ref in zip(expo, (vb_ref, v_ref, va_ref)):
            weights = (part * share).astype(jnp.bfloat16)
            term = jnp.dot(weights, ref[:, at], preferred_element_type=jnp.float32)
            out = term if out is None else out + term
        o_ref[:, at] = out.astype(jnp.bfloat16)


def attend(reach, qn, pairs):
    rows, chans = qn.shape
    heads = chans // HD
    step = next(n for n in (5, 4, 3, 2, 1) if heads % n == 0)
    cols = step * HD
    steps = chans // cols
    k_spec = pl.BlockSpec((rows, cols), lambda i: (0, i))
    v_spec = pl.BlockSpec((rows, cols), lambda i: (0, steps + i))
    return pl.pallas_call(
        attend_kernel,
        grid=(steps,),
        out_shape=jax.ShapeDtypeStruct((rows, chans), jnp.bfloat16),
        in_specs=[pl.BlockSpec(memory_space=pltpu.SMEM)] + [k_spec] * 4 + [v_spec] * 3,
        out_specs=k_spec,
        name="attend",
    )(reach, qn, *pairs, *pairs)


def project_kernel(share, gate_ref, *refs):
    slots = len(refs) - 6
    att_refs, w_refs, outs = refs[:2], refs[2 : 2 + slots], refs[2 + slots : 4 + slots]
    w_ref, sems = refs[4 + slots :]
    depth, cols = w_refs[0].shape
    place = lax.axis_index("tm")
    line = place // 4
    copies = []
    for i, ref in enumerate(w_refs):
        start = pl.multiple_of((line ^ i) * depth, depth) if slots > 1 else 0
        copies.append(pltpu.make_async_copy(ref, w_ref.at[pl.ds(start, depth)], sems.at[i]))
    for copy in copies:
        copy.start()
    accs = [None, None]
    group = 2 if slots > 1 else 1
    for i in range(0, slots, group):
        for copy in copies[i : i + group]:
            copy.wait()
        start = pl.multiple_of((line // 2 ^ i // 2) * 2 * depth, HD) if slots > 1 else 0
        weight = w_ref[pl.ds(start, group * depth), :]
        for p in range(2):
            term = jnp.dot(att_refs[p][:, pl.ds(start, group * depth)], weight, preferred_element_type=jnp.float32)
            accs[p] = term if accs[p] is None else accs[p] + term
    first = ((place % 4) * 2 + (lax.axis_index("groups") ^ share)) * (cols // HD)
    for p in range(2):
        for b in range(cols // HD):
            at = slice(b * HD, (b + 1) * HD)
            outs[p][:, at] = (gate_ref[pl.ds(first + b, 1), :] * accs[p][:, at]).astype(jnp.bfloat16)


def project(gate, att, weights, share):
    rows, chans = att[0].shape
    cols = weights[0].shape[1]
    slots = len(weights)
    return pl.pallas_call(
        functools.partial(project_kernel, share),
        out_shape=[jax.ShapeDtypeStruct((rows, cols), jnp.bfloat16)] * 2,
        in_specs=whole(3) + [pl.BlockSpec(memory_space=pl.ANY)] * slots,
        out_specs=whole(2),
        scratch_shapes=[pltpu.VMEM((chans, cols), jnp.bfloat16), pltpu.SemaphoreType.DMA((slots,))],
    )(gate.reshape(-1, HD), *att, *weights)


def place_kernel(spots, aliased, *refs):
    pieces, out_ref, sems = refs[aliased:-2], refs[-2], refs[-1]
    cols = pieces[0].shape[1]
    low = lax.axis_index("tm") % 4
    group = lax.axis_index("groups")
    copies = []
    for i, (ref, (near, share)) in enumerate(zip(pieces, spots)):
        start = pl.multiple_of(((low ^ near) * 2 + (group ^ share)) * cols, HD)
        copies.append(pltpu.make_async_copy(ref, out_ref.at[:, pl.ds(start, cols)], sems.at[i]))
    for copy in copies:
        copy.start()
    for copy in copies:
        copy.wait()


def place_pieces(base, pieces, spots):
    rows, cols = pieces[0].shape
    anywhere = pl.BlockSpec(memory_space=pl.ANY)
    aliased = 0 if base is None else 1
    return pl.pallas_call(
        functools.partial(place_kernel, spots, aliased),
        out_shape=jax.ShapeDtypeStruct((rows, cols * 8), jnp.bfloat16),
        in_specs=[anywhere] * aliased + whole(len(pieces)),
        out_specs=anywhere,
        scratch_shapes=[pltpu.SemaphoreType.DMA((len(pieces),))],
        input_output_aliases={0: 0} if aliased else {},
    )(*([] if base is None else [base]), *pieces)


def local(queries, keys, values, q_gain, k_gain, out_weight, out_gate, reach):
    peers = lax.axis_size("tm")
    place = lax.axis_index("tm")
    group = lax.axis_index("groups")
    low = place % 4
    line = place // 4
    lines = peers // 4
    _, width = out_weight.shape
    cols = width // 8

    def swap(x, bits):
        return lax.ppermute(x, "tm", [(i, i ^ bits) for i in range(peers)])

    def group_swap(x):
        return lax.ppermute(x, "groups", [(0, 1), (1, 0)])

    def along(x, moves):
        return lax.ppermute(x, "tm", [(4 * a + i, 4 * b + i) for a, b in moves for i in range(4)])

    def send(x, pairs):
        return lax.ppermute(x, "tm", pairs)

    up = [(i, i + 1) for i in range(peers - 1)]
    down = [(j, i) for i, j in up]

    def choose(flag, a, b):
        return jnp.where(flag, a, b)

    def column(quarter, share):
        return (quarter * 2 + share) * cols

    def weight_part(quarter):
        return lax.dynamic_slice_in_dim(out_weight, column(quarter, group), cols, 1)

    cuts = lax.optimization_barrier([weight_part(low ^ i) for i in range(4)])
    parts = [cuts[0]] + [swap(cuts[i], i) for i in (1, 2, 3)]
    odd, upper = (low % 2) == 1, low >= 2
    halves = [
        jnp.concatenate([choose(odd, b, a), choose(odd, a, b)], axis=0)
        for a, b in ((parts[0], parts[1]), (parts[2], parts[3]))
    ]
    block = jnp.concatenate([choose(upper, halves[1], halves[0]), choose(upper, halves[0], halves[1])], axis=0)

    kv = pair(keys, values, k_gain)
    seen = [send(kv, up), kv, send(kv, down)]
    qn = norm(queries, q_gain)

    if lines == 4:
        middle = (line == 1) | (line == 2)
        near = along(block, ((0, 1), (1, 0), (2, 3), (3, 2)))
        across = along(block, ((1, 2), (2, 1)))
        across_far = along(near, ((1, 2), (2, 1)))
        edge = along(across, ((1, 0), (2, 3)))
        edge_far = along(across_far, ((1, 0), (2, 3)))
        second = choose(middle, across_far, edge)
        third = choose(middle, across, edge_far)
        slots = [block, near, second, third]
    else:
        members = [[z * 4 + i for z in range(lines)] for i in range(4)]
        slots = [lax.all_gather(block, "tm", axis_index_groups=members, axis=0, tiled=True)]
    shares = [slots, [group_swap(slot) for slot in slots]]

    own = attend(reach, qn, seen)
    over = swap(own, 2)
    here, there = [own, swap(own, 1)], [over, swap(over, 1)]
    pieces = {}
    for j in range(2):
        made = project(out_gate, here, shares[j], j)
        pieces[0, j], pieces[1, j] = made[0], swap(made[1], 1)
        made = project(out_gate, there, shares[j], j)
        pieces[2, j], pieces[3, j] = swap(made[0], 2), swap(made[1], 3)
    last = [(2, 1), (3, 1)]
    most = [spot for spot in pieces if spot not in last]
    out = place_pieces(None, [pieces[spot] for spot in most], most)
    return place_pieces(out, [pieces[spot] for spot in last], last)


def solution(mesh):
    return jax.shard_map(
        local,
        mesh=mesh,
        in_specs=(
            P(("groups", "tm"), None),
            P(("groups", "tm"), None),
            P(("groups", "tm"), None),
            P(),
            P(),
            P("tm", None),
            P(),
            P(("groups", "tm"), None),
        ),
        out_specs=P(("groups", "tm"), None),
        check_vma=False,
    )
```

time: 209 us -> 218 us (1.043)
  the two profiles are of different devices: /device:TPU:27 before, /device:TPU:21 now
where the time goes in v3:
time: 218 us
  waiting for transfers between devices  139 us (64%)
  Pallas kernels  43.4 us (20%)
  starting transfers between devices  27.4 us (13%)
  local copies, waits for them, and re-layouts  4.18 us (2%)
  other arithmetic  2.79 us (1%)
    ppermute x12, waiting for transfers between devices, swap(): return lax.ppermute(x, 'tm', [(i, i ^ bits) for i in range(peers)])  59.2 us
    ppermute x4, waiting for transfers between devices, group_swap(): return lax.ppermute(x, 'groups', [(0, 1), (1, 0)])  45.7 us
    ppermute x5, waiting for transfers between devices, along(): lax.ppermute(x, 'tm', [(4 * a + i, 4 * b + i) for a, b in moves for i in...  34.5 us
    pallas_call x4, Pallas kernels, project(): pl.pallas_call(functools.partial(project_kernel, share), out_shape=[jax.S...  23.5 us
    ppermute x12, starting transfers between devices, swap(): return lax.ppermute(x, 'tm', [(i, i ^ bits) for i in range(peers)])  11.1 us
    pallas_call x1, Pallas kernels, attend(): pl.pallas_call(attend_kernel, grid=(steps,), out_shape=jax.ShapeDtypeStru...  9.43 us
    ppermute x5, starting transfers between devices, along(): lax.ppermute(x, 'tm', [(4 * a + i, 4 * b + i) for a, b in moves for i in...  8.05 us
    ppermute x2, starting transfers between devices, send(): return lax.ppermute(x, 'tm', pairs)  4.96 us
  transfers between devices with their start and end apart: 23, of which 11 were waited for; matrix products, arithmetic and copies ran while one was open for 1% of the time, Pallas kernels for 19%

profile of v3, /device:TPU:21, one launch (start us, length us, event | category | flops | bytes accessed | tf_op | source)
XLA Modules:
  0.0 217.6 jit_solution(16360608691259874404)
XLA Ops:
  0.0 1.3 constant_dynamic-slice_fusion
  1.3 0.7 collective-permute-start.5
  2.1 3.4 %shard_map.83.k_ref.v_ref = bf16[192,5120]{1,0:T(8,128)(2,1)} custom-call(bf16[192,2560]{1,0:T(8,128)(2,1)} %k_ref.1, bf16[192,2560]{1,0:T(8,128)(2,1)} %v_ref.1, f32[20,128]{1,0:T(8,128)} %bitcast.7), custom_call_target="tpu_custom_call" | custom-call | tf_op jit(solution)/shard_map/pallas_call | solution.py:49
  5.4 3.0 %collective-permute-start = (bf16[192,5120]{1,0:T(8,128)(2,1)}, bf16[192,5120]{1,0:T(8,128)(2,1)S(1)}, u32[]{:S(2)}, u32[]{:S(2)}) collective-permute-start(bf16[192,5120]{1,0:T(8,128)(2,1)} %shard_map.83.k_ref.v_ref), channel_id=1, source_target_pairs={{0,1},{1,2},{2,3},{3,4},{4,5},{5,6},{6,7},{7,8},{8,9},{9,10},{10,1... | collective-permute-start | bytes 5898248 | tf_op jit(solution)/shard_map/ppermute | solution.py:193
  8.5 1.9 collective-permute-start.1
  10.4 1.7 collective-permute-start.3
  12.1 0.3 collective-permute-start.4
  12.5 26.7 %collective-permute-done.3 = bf16[160,640]{1,0:T(8,128)(2,1)S(1)} collective-permute-done((bf16[160,640]{1,0:T(8,128)(2,1)S(1)}, bf16[160,640]{1,0:T(8,128)(2,1)S(1)}, u32[]{:S(2)}, u32[]{:S(2)}) %collective-permute-start.3) | collective-permute-done | bytes 204832 | tf_op jit(solution)/shard_map/ppermute | solution.py:184
  39.2 21.5 %collective-permute-done.4 = bf16[160,640]{1,0:T(8,128)(2,1)S(1)} collective-permute-done((bf16[160,640]{1,0:T(8,128)(2,1)S(1)}, bf16[160,640]{1,0:T(8,128)(2,1)S(1)}, u32[]{:S(2)}, u32[]{:S(2)}) %collective-permute-start.4) | collective-permute-done | bytes 204832 | tf_op jit(solution)/shard_map/ppermute | solution.py:184
  60.8 0.2 broadcast_select_fusion.3
  61.0 0.1 pad_maximum_fusion.refs_2_
  61.1 2.2 %collective-permute-start.8 = (bf16[640,640]{1,0:T(8,128)(2,1)S(1)}, bf16[640,640]{1,0:T(8,128)(2,1)}, u32[]{:S(2)}, u32[]{:S(2)}) collective-permute-start(bf16[640,640]{1,0:T(8,128)(2,1)S(1)} %pad_maximum_fusion.refs_2_), channel_id=1, source_target_pairs={{4,8},{5,9},{6,10},{7,11},{8,4},{9,5},{10,6},{11,7},{20,24},{21,25... | collective-permute-start | bytes 2457608 | tf_op jit(solution)/shard_map/ppermute | solution.py:190
  63.4 18.0 %collective-permute-done.6.refs_3_ = bf16[640,640]{1,0:T(8,128)(2,1)} collective-permute-done((bf16[640,640]{1,0:T(8,128)(2,1)S(1)}, bf16[640,640]{1,0:T(8,128)(2,1)}, u32[]{:S(2)}, u32[]{:S(2)}) %collective-permute-start.6) | collective-permute-done | bytes 819232 | tf_op jit(solution)/shard_map/ppermute | solution.py:190
  81.4 2.1 collective-permute-start.7
  83.5 2.2 %collective-permute-start.9 = (bf16[640,640]{1,0:T(8,128)(2,1)}, bf16[640,640]{1,0:T(8,128)(2,1)}, u32[]{:S(2)}, u32[]{:S(2)}) collective-permute-start(bf16[640,640]{1,0:T(8,128)(2,1)} %collective-permute-done.8), channel_id=1, source_target_pairs={{4,0},{5,1},{6,2},{7,3},{8,12},{9,13},{10,14},{11,15},{20,16},{21,... | collective-permute-start | bytes 2457608 | tf_op jit(solution)/shard_map/ppermute | solution.py:190
  85.7 2.7 %shard_map.82.q_ref = bf16[192,2560]{1,0:T(8,128)(2,1)} custom-call(bf16[192,2560]{1,0:T(8,128)(2,1)} %x_ref.1, f32[20,128]{1,0:T(8,128)} %bitcast.8), custom_call_target="tpu_custom_call" | custom-call | tf_op jit(solution)/shard_map/pallas_call | solution.py:39
  88.3 1.3 copy-done
  89.6 9.4 %attend.1.refs_0_ = bf16[192,2560]{1,0:T(8,128)(2,1)} custom-call(s32[1,2]{1,0:T(1,128)} %reach_ref.1, bf16[192,2560]{1,0:T(8,128)(2,1)} %shard_map.82.q_ref, bf16[192,5120]{1,0:T(8,128)(2,1)} %copy-done, bf16[192,5120]{1,0:T(8,128)(2,1)} %shard_map.83.k_ref.v_ref, bf16[192,5120]{1,0:T(8,128)(2,1)} %collective-permute-done.1.ka_ref.va_ref, ...), custom_call_target="tpu_custom_call" | custom-call | tf_op jit(solution)/shard_map/attend/pallas_call | solution.py:91
  99.0 3.9 %collective-permute-done.7 = bf16[640,640]{1,0:T(8,128)(2,1)} collective-permute-done((bf16[640,640]{1,0:T(8,128)(2,1)}, bf16[640,640]{1,0:T(8,128)(2,1)}, u32[]{:S(2)}, u32[]{:S(2)}) %collective-permute-start.7) | collective-permute-done | bytes 819232 | tf_op jit(solution)/shard_map/ppermute | solution.py:190
  102.9 1.5 collective-permute-start.10
  104.5 1.4 collective-permute-start.2
  105.8 1.2 collective-permute-start.16
  107.1 0.3 collective-permute-start.17
  107.3 1.2 broadcast_select_fusion.1.refs_4_
  108.6 12.5 %collective-permute-done.10 = bf16[640,640]{1,0:T(8,128)(2,1)S(1)} collective-permute-done((bf16[640,640]{1,0:T(8,128)(2,1)}, bf16[640,640]{1,0:T(8,128)(2,1)S(1)}, u32[]{:S(2)}, u32[]{:S(2)}) %collective-permute-start.10) | collective-permute-done | bytes 819232 | tf_op jit(solution)/shard_map/ppermute | solution.py:190
  121.1 1.2 collective-permute-start.18
  122.3 2.2 %collective-permute-start.13 = (bf16[192,2560]{1,0:T(8,128)(2,1)}, bf16[192,2560]{1,0:T(8,128)(2,1)}, u32[]{:S(2)}, u32[]{:S(2)}) collective-permute-start(bf16[192,2560]{1,0:T(8,128)(2,1)} %collective-permute-done.12.refs_0_), channel_id=1, source_target_pairs={{0,1},{1,0},{2,3},{3,2},{4,5},{5,4},{6,7},{7,6},{8,9},{9,8},{10,11... | collective-permute-start | bytes 2949128 | tf_op jit(solution)/shard_map/ppermute | solution.py:184
  124.5 1.2 broadcast_select_fusion.refs_5_
  125.7 0.7 collective-permute-start.19
  126.4 0.2 copy-done.3
  126.6 5.9 %shard_map.84 = (bf16[192,640]{1,0:T(8,128)(2,1)}, bf16[192,640]{1,0:T(8,128)(2,1)}) custom-call(f32[40,128]{1,0:T(8,128)} %bitcast.3, bf16[192,2560]{1,0:T(8,128)(2,1)} %attend.1.refs_0_, bf16[192,2560]{1,0:T(8,128)(2,1)} %collective-permute-done.2.refs_1_, bf16[640,640]{1,0:T(8,128)(2,1)} %copy-done.1, bf16[640,640]{1,0:T(8,128)(2,1)} %collective-permute-done.6.refs_3_, ...), custom_call_target="tpu_custom_call" | custom-call | tf_op jit(solution)/shard_map/pallas_call | solution.py:135
  132.5 0.1 collective-permute-start.11
  132.6 10.6 %collective-permute-done.17.refs_3_ = bf16[640,640]{1,0:T(8,128)(2,1)} collective-permute-done((bf16[640,640]{1,0:T(8,128)(2,1)}, bf16[640,640]{1,0:T(8,128)(2,1)}, u32[]{:S(2)}, u32[]{:S(2)}) %collective-permute-start.17) | collective-permute-done | bytes 819232 | tf_op jit(solution)/shard_map/ppermute | solution.py:187
  143.2 17.6 %collective-permute-done.18.refs_4_ = bf16[640,640]{1,0:T(8,128)(2,1)} collective-permute-done((bf16[640,640]{1,0:T(8,128)(2,1)S(1)}, bf16[640,640]{1,0:T(8,128)(2,1)}, u32[]{:S(2)}, u32[]{:S(2)}) %collective-permute-start.18) | collective-permute-done | bytes 819232 | tf_op jit(solution)/shard_map/ppermute | solution.py:187
  160.8 17.6 %collective-permute-done.19.refs_5_ = bf16[640,640]{1,0:T(8,128)(2,1)} collective-permute-done((bf16[640,640]{1,0:T(8,128)(2,1)S(1)}, bf16[640,640]{1,0:T(8,128)(2,1)}, u32[]{:S(2)}, u32[]{:S(2)}) %collective-permute-start.19) | collective-permute-done | bytes 819232 | tf_op jit(solution)/shard_map/ppermute | solution.py:187
  178.3 5.9 %shard_map.86 = (bf16[192,640]{1,0:T(8,128)(2,1)}, bf16[192,640]{1,0:T(8,128)(2,1)}) custom-call(f32[40,128]{1,0:T(8,128)} %bitcast.4, bf16[192,2560]{1,0:T(8,128)(2,1)} %attend.1.refs_0_, bf16[192,2560]{1,0:T(8,128)(2,1)} %collective-permute-done.2.refs_1_, bf16[640,640]{1,0:T(8,128)(2,1)} %collective-permute-done.16.refs_2_, ...), custom_call_target="tpu_custom_call" | custom-call | tf_op jit(solution)/shard_map/pallas_call | solution.py:135
  184.2 1.0 collective-permute-start.20
  185.2 5.9 %shard_map.85 = (bf16[192,640]{1,0:T(8,128)(2,1)}, bf16[192,640]{1,0:T(8,128)(2,1)}) custom-call(f32[40,128]{1,0:T(8,128)} %bitcast.5, bf16[192,2560]{1,0:T(8,128)(2,1)} %collective-permute-done.12.refs_0_, bf16[192,2560]{1,0:T(8,128)(2,1)} %collective-permute-done.13.refs_1_, bf16[640,640]{1,0:T(8,128)(2,1)} %copy-done.1, ...), custom_call_target="tpu_custom_call" | custom-call | tf_op jit(solution)/shard_map/pallas_call | solution.py:135
  191.2 1.7 collective-permute-start.15
  192.9 5.9 %shard_map.88 = (bf16[192,640]{1,0:T(8,128)(2,1)}, bf16[192,640]{1,0:T(8,128)(2,1)}) custom-call(f32[40,128]{1,0:T(8,128)} %bitcast.6, bf16[192,2560]{1,0:T(8,128)(2,1)} %collective-permute-done.12.refs_0_, bf16[192,2560]{1,0:T(8,128)(2,1)} %collective-permute-done.13.refs_1_, bf16[640,640]{1,0:T(8,128)(2,1)} %collective-permute-done.16.refs_2_, ...), custom_call_target="tpu_custom_call" | custom-call | tf_op jit(solution)/shard_map/pallas_call | solution.py:135
  198.9 1.8 collective-permute-start.22
  200.7 4.2 %collective-permute-done.15.refs_3_ = bf16[192,640]{1,0:T(8,128)(2,1)S(1)} collective-permute-done((bf16[192,640]{1,0:T(8,128)(2,1)}, bf16[192,640]{1,0:T(8,128)(2,1)S(1)}, u32[]{:S(2)}, u32[]{:S(2)}) %collective-permute-start.15) | collective-permute-done | bytes 245792 | tf_op jit(solution)/shard_map/ppermute | solution.py:184
  204.9 0.7 copy-done.10
  205.5 2.6 %shard_map.87.refs_0_ = bf16[192,5120]{1,0:T(8,128)(2,1)} custom-call(bf16[192,640]{1,0:T(8,128)(2,1)} %get-tuple-element.21.refs_0_, bf16[192,640]{1,0:T(8,128)(2,1)} %copy-done.7, bf16[192,640]{1,0:T(8,128)(2,1)} %copy-done.9, bf16[192,640]{1,0:T(8,128)(2,1)} %copy-done.10, bf16[192,640]{1,0:T(8,128)(2,1)} %get-tuple-element.25.refs_4_, ...), custom_call_target="tpu_custom_call" | custom-call | tf_op jit(solution)/shard_map/pallas_call | solution.py:163
  208.2 1.3 collective-permute-done.21.refs_1_
  209.4 5.5 %collective-permute-done.22.refs_2_ = bf16[192,640]{1,0:T(8,128)(2,1)S(1)} collective-permute-done((bf16[192,640]{1,0:T(8,128)(2,1)}, bf16[192,640]{1,0:T(8,128)(2,1)S(1)}, u32[]{:S(2)}, u32[]{:S(2)}) %collective-permute-start.22) | collective-permute-done | bytes 245792 | tf_op jit(solution)/shard_map/ppermute | solution.py:184
  214.9 0.7 copy-done.6
  215.6 1.9 shard_map.89
  (36 shorter events, 0.4 us)
Async XLA Ops:
  1.3 11.1 %collective-permute-start.5 = (bf16[160,640]{1,0:T(8,128)(2,1)S(1)}, bf16[160,640]{1,0:T(8,128)(2,1)S(1)}, u32[]{:S(2)}, u32[]{:S(2)}) collective-permute-start(bf16[160,640]{1,0:T(8,128)(2,1)S(1)} %get-tuple-element.19), channel_id=1, source_target_pairs={{0,1},{1,0},{2,3},{3,2},{4,5},{5,4},{6,7},{7,6},{8,9},{9,8},{10,11... | collective-permute-start | bytes 614408 | tf_op jit(solution)/shard_map/ppermute | solution.py:184
  5.4 82.9 %collective-permute-start = (bf16[192,5120]{1,0:T(8,128)(2,1)}, bf16[192,5120]{1,0:T(8,128)(2,1)S(1)}, u32[]{:S(2)}, u32[]{:S(2)}) collective-permute-start(bf16[192,5120]{1,0:T(8,128)(2,1)} %shard_map.83.k_ref.v_ref), channel_id=1, source_target_pairs={{0,1},{1,2},{2,3},{3,4},{4,5},{5,6},{6,7},{7,8},{8,9},{9,10},{10,1... | collective-permute-start | bytes 5898248 | tf_op jit(solution)/shard_map/ppermute | solution.py:193
  8.5 79.9 %collective-permute-start.1 = (bf16[192,5120]{1,0:T(8,128)(2,1)}, bf16[192,5120]{1,0:T(8,128)(2,1)}, u32[]{:S(2)}, u32[]{:S(2)}) collective-permute-start(bf16[192,5120]{1,0:T(8,128)(2,1)} %shard_map.83.k_ref.v_ref), channel_id=1, source_target_pairs={{1,0},{2,1},{3,2},{4,3},{5,4},{6,5},{7,6},{8,7},{9,8},{10,9},{11,1... | collective-permute-start | bytes 5898248 | tf_op jit(solution)/shard_map/ppermute | solution.py:193
  10.4 28.8 %collective-permute-start.3 = (bf16[160,640]{1,0:T(8,128)(2,1)S(1)}, bf16[160,640]{1,0:T(8,128)(2,1)S(1)}, u32[]{:S(2)}, u32[]{:S(2)}) collective-permute-start(bf16[160,640]{1,0:T(8,128)(2,1)S(1)} %get-tuple-element.17), channel_id=1, source_target_pairs={{0,3},{1,2},{2,1},{3,0},{4,7},{5,6},{6,5},{7,4},{8,11},{9,10},{10,... | collective-permute-start | bytes 614408 | tf_op jit(solution)/shard_map/ppermute | solution.py:184
  12.1 48.7 %collective-permute-start.4 = (bf16[160,640]{1,0:T(8,128)(2,1)S(1)}, bf16[160,640]{1,0:T(8,128)(2,1)S(1)}, u32[]{:S(2)}, u32[]{:S(2)}) collective-permute-start(bf16[160,640]{1,0:T(8,128)(2,1)S(1)} %get-tuple-element.18), channel_id=1, source_target_pairs={{0,2},{1,3},{2,0},{3,1},{4,6},{5,7},{6,4},{7,5},{8,10},{9,11},{10,... | collective-permute-start | bytes 614408 | tf_op jit(solution)/shard_map/ppermute | solution.py:184
  61.0 44.8 %copy-start.1 = (bf16[640,640]{1,0:T(8,128)(2,1)}, bf16[640,640]{1,0:T(8,128)(2,1)S(1)}, u32[]{:S(2)}) copy-start(bf16[640,640]{1,0:T(8,128)(2,1)S(1)} %pad_maximum_fusion.refs_2_) | copy-start | bytes 2457604
  61.0 20.4 %collective-permute-start.6 = (bf16[640,640]{1,0:T(8,128)(2,1)S(1)}, bf16[640,640]{1,0:T(8,128)(2,1)}, u32[]{:S(2)}, u32[]{:S(2)}) collective-permute-start(bf16[640,640]{1,0:T(8,128)(2,1)S(1)} %pad_maximum_fusion.refs_2_), channel_id=1, source_target_pairs={{0,4},{1,5},{2,6},{3,7},{4,0},{5,1},{6,2},{7,3},{8,12},{9,13},{10,... | collective-permute-start | bytes 2457608 | tf_op jit(solution)/shard_map/ppermute | solution.py:190
  61.1 22.4 %collective-permute-start.8 = (bf16[640,640]{1,0:T(8,128)(2,1)S(1)}, bf16[640,640]{1,0:T(8,128)(2,1)}, u32[]{:S(2)}, u32[]{:S(2)}) collective-permute-start(bf16[640,640]{1,0:T(8,128)(2,1)S(1)} %pad_maximum_fusion.refs_2_), channel_id=1, source_target_pairs={{4,8},{5,9},{6,10},{7,11},{8,4},{9,5},{10,6},{11,7},{20,24},{21,25... | collective-permute-start | bytes 2457608 | tf_op jit(solution)/shard_map/ppermute | solution.py:190
  81.4 21.5 %collective-permute-start.7 = (bf16[640,640]{1,0:T(8,128)(2,1)}, bf16[640,640]{1,0:T(8,128)(2,1)}, u32[]{:S(2)}, u32[]{:S(2)}) collective-permute-start(bf16[640,640]{1,0:T(8,128)(2,1)} %collective-permute-done.6.refs_3_), channel_id=1, source_target_pairs={{4,8},{5,9},{6,10},{7,11},{8,4},{9,5},{10,6},{11,7},{20,24},{21,25... | collective-permute-start | bytes 2457608 | tf_op jit(solution)/shard_map/ppermute | solution.py:190
  83.5 23.6 %collective-permute-start.9 = (bf16[640,640]{1,0:T(8,128)(2,1)}, bf16[640,640]{1,0:T(8,128)(2,1)}, u32[]{:S(2)}, u32[]{:S(2)}) collective-permute-start(bf16[640,640]{1,0:T(8,128)(2,1)} %collective-permute-done.8), channel_id=1, source_target_pairs={{4,0},{5,1},{6,2},{7,3},{8,12},{9,13},{10,14},{11,15},{20,16},{21,... | collective-permute-start | bytes 2457608 | tf_op jit(solution)/shard_map/ppermute | solution.py:190
  88.3 1.3 copy-start
  99.0 23.3 %collective-permute-start.12 = (bf16[192,2560]{1,0:T(8,128)(2,1)}, bf16[192,2560]{1,0:T(8,128)(2,1)}, u32[]{:S(2)}, u32[]{:S(2)}) collective-permute-start(bf16[192,2560]{1,0:T(8,128)(2,1)} %attend.1.refs_0_), channel_id=1, source_target_pairs={{0,2},{1,3},{2,0},{3,1},{4,6},{5,7},{6,4},{7,5},{8,10},{9,11},{10,... | collective-permute-start | bytes 2949128 | tf_op jit(solution)/shard_map/ppermute | solution.py:184
  102.9 18.1 %collective-permute-start.10 = (bf16[640,640]{1,0:T(8,128)(2,1)}, bf16[640,640]{1,0:T(8,128)(2,1)S(1)}, u32[]{:S(2)}, u32[]{:S(2)}) collective-permute-start(bf16[640,640]{1,0:T(8,128)(2,1)} %collective-permute-done.7), channel_id=1, source_target_pairs={{4,0},{5,1},{6,2},{7,3},{8,12},{9,13},{10,14},{11,15},{20,16},{21,... | collective-permute-start | bytes 2457608 | tf_op jit(solution)/shard_map/ppermute | solution.py:190
  104.5 21.3 %collective-permute-start.2 = (bf16[192,2560]{1,0:T(8,128)(2,1)}, bf16[192,2560]{1,0:T(8,128)(2,1)}, u32[]{:S(2)}, u32[]{:S(2)}) collective-permute-start(bf16[192,2560]{1,0:T(8,128)(2,1)} %attend.1.refs_0_), channel_id=1, source_target_pairs={{0,1},{1,0},{2,3},{3,2},{4,5},{5,4},{6,7},{7,6},{8,9},{9,8},{10,11... | collective-permute-start | bytes 2949128 | tf_op jit(solution)/shard_map/ppermute | solution.py:184
  105.8 26.6 %collective-permute-start.16 = (bf16[640,640]{1,0:T(8,128)(2,1)S(1)}, bf16[640,640]{1,0:T(8,128)(2,1)}, u32[]{:S(2)}, u32[]{:S(2)}) collective-permute-start(bf16[640,640]{1,0:T(8,128)(2,1)S(1)} %pad_maximum_fusion.refs_2_), channel_id=1, source_target_pairs={{0,16},{16,0},{1,17},{17,1},{2,18},{18,2},{3,19},{19,3},{4,20},{20... | collective-permute-start | bytes 2457608 | tf_op jit(solution)/shard_map/ppermute | solution.py:187
  107.1 36.1 %collective-permute-start.17 = (bf16[640,640]{1,0:T(8,128)(2,1)}, bf16[640,640]{1,0:T(8,128)(2,1)}, u32[]{:S(2)}, u32[]{:S(2)}) collective-permute-start(bf16[640,640]{1,0:T(8,128)(2,1)} %collective-permute-done.6.refs_3_), channel_id=1, source_target_pairs={{0,16},{16,0},{1,17},{17,1},{2,18},{18,2},{3,19},{19,3},{4,20},{20... | collective-permute-start | bytes 2457608 | tf_op jit(solution)/shard_map/ppermute | solution.py:187
  108.6 17.8 %copy-start.2 = (bf16[640,640]{1,0:T(8,128)(2,1)}, bf16[640,640]{1,0:T(8,128)(2,1)S(1)}, u32[]{:S(2)}) copy-start(bf16[640,640]{1,0:T(8,128)(2,1)S(1)} %broadcast_select_fusion.1.refs_4_) | copy-start | bytes 2457604
  121.1 1.2 copy-start.4
  121.1 39.7 %collective-permute-start.18 = (bf16[640,640]{1,0:T(8,128)(2,1)S(1)}, bf16[640,640]{1,0:T(8,128)(2,1)}, u32[]{:S(2)}, u32[]{:S(2)}) collective-permute-start(bf16[640,640]{1,0:T(8,128)(2,1)S(1)} %broadcast_select_fusion.1.refs_4_), channel_id=1, source_target_pairs={{0,16},{16,0},{1,17},{17,1},{2,18},{18,2},{3,19},{19,3},{4,20},{20... | collective-permute-start | bytes 2457608 | tf_op jit(solution)/shard_map/ppermute | solution.py:187
  122.3 62.9 %collective-permute-start.13 = (bf16[192,2560]{1,0:T(8,128)(2,1)}, bf16[192,2560]{1,0:T(8,128)(2,1)}, u32[]{:S(2)}, u32[]{:S(2)}) collective-permute-start(bf16[192,2560]{1,0:T(8,128)(2,1)} %collective-permute-done.12.refs_0_), channel_id=1, source_target_pairs={{0,1},{1,0},{2,3},{3,2},{4,5},{5,4},{6,7},{7,6},{8,9},{9,8},{10,11... | collective-permute-start | bytes 2949128 | tf_op jit(solution)/shard_map/ppermute | solution.py:184
  125.7 0.9 copy-start.3
  125.7 52.6 %collective-permute-start.19 = (bf16[640,640]{1,0:T(8,128)(2,1)S(1)}, bf16[640,640]{1,0:T(8,128)(2,1)}, u32[]{:S(2)}, u32[]{:S(2)}) collective-permute-start(bf16[640,640]{1,0:T(8,128)(2,1)S(1)} %broadcast_select_fusion.refs_5_), channel_id=1, source_target_pairs={{0,16},{16,0},{1,17},{17,1},{2,18},{18,2},{3,19},{19,3},{4,20},{20... | collective-permute-start | bytes 2457608 | tf_op jit(solution)/shard_map/ppermute | solution.py:187
  132.5 66.3 %collective-permute-start.11 = (bf16[192,640]{1,0:T(8,128)(2,1)}, bf16[192,640]{1,0:T(8,128)(2,1)S(1)}, u32[]{:S(2)}, u32[]{:S(2)}) collective-permute-start(bf16[192,640]{1,0:T(8,128)(2,1)} %get-tuple-element.22), channel_id=1, source_target_pairs={{0,1},{1,0},{2,3},{3,2},{4,5},{5,4},{6,7},{7,6},{8,9},{9,8},{10,11... | collective-permute-start | bytes 737288 | tf_op jit(solution)/shard_map/ppermute | solution.py:184
  184.2 16.4 %collective-permute-start.20 = (bf16[192,640]{1,0:T(8,128)(2,1)}, bf16[192,640]{1,0:T(8,128)(2,1)S(1)}, u32[]{:S(2)}, u32[]{:S(2)}) collective-permute-start(bf16[192,640]{1,0:T(8,128)(2,1)} %get-tuple-element.26), channel_id=1, source_target_pairs={{0,1},{1,0},{2,3},{3,2},{4,5},{5,4},{6,7},{7,6},{8,9},{9,8},{10,11... | collective-permute-start | bytes 737288 | tf_op jit(solution)/shard_map/ppermute | solution.py:184
  191.1 9.5 %collective-permute-start.14 = (bf16[192,640]{1,0:T(8,128)(2,1)}, bf16[192,640]{1,0:T(8,128)(2,1)S(1)}, u32[]{:S(2)}, u32[]{:S(2)}) collective-permute-start(bf16[192,640]{1,0:T(8,128)(2,1)} %get-tuple-element.23), channel_id=1, source_target_pairs={{0,2},{1,3},{2,0},{3,1},{4,6},{5,7},{6,4},{7,5},{8,10},{9,11},{10,... | collective-permute-start | bytes 737288 | tf_op jit(solution)/shard_map/ppermute | solution.py:184
  191.2 13.6 %collective-permute-start.15 = (bf16[192,640]{1,0:T(8,128)(2,1)}, bf16[192,640]{1,0:T(8,128)(2,1)S(1)}, u32[]{:S(2)}, u32[]{:S(2)}) collective-permute-start(bf16[192,640]{1,0:T(8,128)(2,1)} %get-tuple-element.24), channel_id=1, source_target_pairs={{0,3},{1,2},{2,1},{3,0},{4,7},{5,6},{6,5},{7,4},{8,11},{9,10},{10,... | collective-permute-start | bytes 737288 | tf_op jit(solution)/shard_map/ppermute | solution.py:184
  198.8 10.7 %collective-permute-start.21 = (bf16[192,640]{1,0:T(8,128)(2,1)}, bf16[192,640]{1,0:T(8,128)(2,1)S(1)}, u32[]{:S(2)}, u32[]{:S(2)}) collective-permute-start(bf16[192,640]{1,0:T(8,128)(2,1)} %get-tuple-element.27), channel_id=1, source_target_pairs={{0,2},{1,3},{2,0},{3,1},{4,6},{5,7},{6,4},{7,5},{8,10},{9,11},{10,... | collective-permute-start | bytes 737288 | tf_op jit(solution)/shard_map/ppermute | solution.py:184
  198.8 6.0 %copy-start.7 = (bf16[192,640]{1,0:T(8,128)(2,1)}, bf16[192,640]{1,0:T(8,128)(2,1)S(1)}, u32[]{:S(2)}) copy-start(bf16[192,640]{1,0:T(8,128)(2,1)S(1)} %collective-permute-done.11.refs_1_) | copy-start | bytes 737284
  198.9 16.0 %collective-permute-start.22 = (bf16[192,640]{1,0:T(8,128)(2,1)}, bf16[192,640]{1,0:T(8,128)(2,1)S(1)}, u32[]{:S(2)}, u32[]{:S(2)}) collective-permute-start(bf16[192,640]{1,0:T(8,128)(2,1)} %get-tuple-element.28), channel_id=1, source_target_pairs={{0,3},{1,2},{2,1},{3,0},{4,7},{5,6},{6,5},{7,4},{8,11},{9,10},{10,... | collective-permute-start | bytes 737288 | tf_op jit(solution)/shard_map/ppermute | solution.py:184
  200.7 4.2 %copy-start.8 = (bf16[192,640]{1,0:T(8,128)(2,1)}, bf16[192,640]{1,0:T(8,128)(2,1)S(1)}, u32[]{:S(2)}) copy-start(bf16[192,640]{1,0:T(8,128)(2,1)S(1)} %collective-permute-done.20.refs_5_) | copy-start | bytes 737284
  200.7 4.2 %copy-start.9 = (bf16[192,640]{1,0:T(8,128)(2,1)}, bf16[192,640]{1,0:T(8,128)(2,1)S(1)}, u32[]{:S(2)}) copy-start(bf16[192,640]{1,0:T(8,128)(2,1)S(1)} %collective-permute-done.14.refs_2_) | copy-start | bytes 737284
  204.9 0.7 copy-start.10
  209.4 5.5 %copy-start.5 = (bf16[192,640]{1,0:T(8,128)(2,1)}, bf16[192,640]{1,0:T(8,128)(2,1)S(1)}, u32[]{:S(2)}) copy-start(bf16[192,640]{1,0:T(8,128)(2,1)S(1)} %collective-permute-done.21.refs_1_) | copy-start | bytes 737284
  214.9 0.7 copy-start.6

commit v4 on v3

--- a/solution.py
+++ b/solution.py
@@ -28,10 +28,11 @@
         out_ref[:, i * HD : (i + 1) * HD] = piece
 
 
-def pair_kernel(k_ref, v_ref, gain_ref, out_ref):
+def pair_kernel(k_ref, v_ref, gain_ref, out_ref, kn_ref):
     chans = k_ref.shape[1]
     for i, piece in scaled_heads(k_ref, gain_ref):
         out_ref[:, i * HD : (i + 1) * HD] = piece
+        kn_ref[:, i * HD : (i + 1) * HD] = piece
     out_ref[:, chans:] = v_ref[...]
 
 
@@ -48,24 +49,31 @@
     rows, chans = keys.shape
     return pl.pallas_call(
         pair_kernel,
-        out_shape=jax.ShapeDtypeStruct((rows, 2 * chans), jnp.bfloat16),
+        out_shape=[jax.ShapeDtypeStruct((rows, n * chans), jnp.bfloat16) for n in (2, 1)],
         in_specs=whole(3),
-        out_specs=pl.BlockSpec(memory_space=pltpu.VMEM),
+        out_specs=whole(2),
     )(keys, values, gain.reshape(-1, HD))
 
 
-def attend_kernel(reach_ref, q_ref, kb_ref, k_ref, ka_ref, vb_ref, v_ref, va_ref, o_ref):
+def attend_kernel(reach_ref, q_ref, kb_ref, k_ref, ka_ref, vb_ref, v_ref, va_ref, kd_ref, vd_ref, o_ref):
     scale = HD ** (-0.5)
     place = lax.axis_index("tm")
     peers = lax.axis_size("tm")
     seen = ((reach_ref[0, 0] == 1) & (place > 0), (reach_ref[0, 1] == 1) & (place < peers - 1))
     bias = [jnp.where(flag, 0.0, -1e30).astype(jnp.float32) for flag in seen]
+    low = place % 4
+
+    def three(before_ref, own_ref, after_ref, other_ref, at):
+        other = other_ref[:, at]
+        before = jnp.where(low == 0, other, before_ref[:, at])
+        return before, own_ref[:, at], jnp.where(low == 3, other, after_ref[:, at])
+
     for h in range(q_ref.shape[1] // HD):
         at = slice(h * HD, (h + 1) * HD)
         query = q_ref[:, at]
         parts = []
-        for ref, extra in ((kb_ref, bias[0]), (k_ref, None), (ka_ref, bias[1])):
-            part = lax.dot_general(query, ref[:, at], (((1,), (1,)), ((), ())), preferred_element_type=jnp.float32)
+        for key, extra in zip(three(kb_ref, k_ref, ka_ref, kd_ref, at), (bias[0], None, bias[1])):
+            part = lax.dot_general(query, key, (((1,), (1,)), ((), ())), preferred_element_type=jnp.float32)
             part = part * scale
             parts.append(part if extra is None else part + extra)
         top = functools.reduce(jnp.maximum, [jnp.max(part, axis=-1, keepdims=True) for part in parts])
@@ -73,14 +81,14 @@
         total = functools.reduce(jnp.add, [jnp.sum(part, axis=-1, keepdims=True) for part in expo])
         share = 1.0 / total
         out = None
-        for part, ref in zip(expo, (vb_ref, v_ref, va_ref)):
+        for part, value in zip(expo, three(vb_ref, v_ref, va_ref, vd_ref, at)):
             weights = (part * share).astype(jnp.bfloat16)
-            term = jnp.dot(weights, ref[:, at], preferred_element_type=jnp.float32)
+            term = jnp.dot(weights, value, preferred_element_type=jnp.float32)
             out = term if out is None else out + term
         o_ref[:, at] = out.astype(jnp.bfloat16)
 
 
-def attend(reach, qn, pairs):
+def attend(reach, qn, pairs, k_diag, v_diag):
     rows, chans = qn.shape
     heads = chans // HD
     step = next(n for n in (5, 4, 3, 2, 1) if heads % n == 0)
@@ -92,10 +100,10 @@
         attend_kernel,
         grid=(steps,),
         out_shape=jax.ShapeDtypeStruct((rows, chans), jnp.bfloat16),
-        in_specs=[pl.BlockSpec(memory_space=pltpu.SMEM)] + [k_spec] * 4 + [v_spec] * 3,
+        in_specs=[pl.BlockSpec(memory_space=pltpu.SMEM)] + [k_spec] * 4 + [v_spec] * 3 + [k_spec] * 2,
         out_specs=k_spec,
         name="attend",
-    )(reach, qn, *pairs, *pairs)
+    )(reach, qn, *pairs, *pairs, k_diag, v_diag)
 
 
 def project_kernel(share, gate_ref, *refs):
@@ -111,21 +119,22 @@
         copies.append(pltpu.make_async_copy(ref, w_ref.at[pl.ds(start, depth)], sems.at[i]))
     for copy in copies:
         copy.start()
-    accs = [None, None]
+    rows = att_refs[0].shape[0]
+    acc = None
     group = 2 if slots > 1 else 1
     for i in range(0, slots, group):
         for copy in copies[i : i + group]:
             copy.wait()
         start = pl.multiple_of((line // 2 ^ i // 2) * 2 * depth, HD) if slots > 1 else 0
         weight = w_ref[pl.ds(start, group * depth), :]
-        for p in range(2):
-            term = jnp.dot(att_refs[p][:, pl.ds(start, group * depth)], weight, preferred_element_type=jnp.float32)
-            accs[p] = term if accs[p] is None else accs[p] + term
+        both = jnp.concatenate([ref[:, pl.ds(start, group * depth)] for ref in att_refs], axis=0)
+        term = jnp.dot(both, weight, preferred_element_type=jnp.float32)
+        acc = term if acc is None else acc + term
     first = ((place % 4) * 2 + (lax.axis_index("groups") ^ share)) * (cols // HD)
     for p in range(2):
         for b in range(cols // HD):
             at = slice(b * HD, (b + 1) * HD)
-            outs[p][:, at] = (gate_ref[pl.ds(first + b, 1), :] * accs[p][:, at]).astype(jnp.bfloat16)
+            outs[p][:, at] = (gate_ref[pl.ds(first + b, 1), :] * acc[p * rows : (p + 1) * rows, at]).astype(jnp.bfloat16)
 
 
 def project(gate, att, weights, share):
@@ -195,6 +204,12 @@
     up = [(i, i + 1) for i in range(peers - 1)]
     down = [(j, i) for i, j in up]
 
+    def inside(pairs):
+        return [(i, j) for i, j in pairs if i // 4 == j // 4]
+
+    def outside(pairs):
+        return [(i, j) for i, j in pairs if i // 4 != j // 4]
+
     def choose(flag, a, b):
         return jnp.where(flag, a, b)
 
@@ -213,26 +228,30 @@
     ]
     block = jnp.concatenate([choose(upper, halves[1], halves[0]), choose(upper, halves[0], halves[1])], axis=0)
 
-    kv = pair(keys, values, k_gain)
-    seen = [send(kv, up), kv, send(kv, down)]
+    kv, kn = pair(keys, values, k_gain)
+    near = [send(kv, inside(up)), kv, send(kv, inside(down))]
+    k_diag = send(kn, outside(up) + outside(down))
+    turn = [(4 * z + i, 4 * z + (i ^ 2)) for z in range(lines) for i in (0, 3)]
+    leap = [(i ^ 2, j) for i, j in outside(up) + outside(down)]
+    v_diag = send(send(values, turn), leap)
     qn = norm(queries, q_gain)
 
     if lines == 4:
         middle = (line == 1) | (line == 2)
-        near = along(block, ((0, 1), (1, 0), (2, 3), (3, 2)))
+        beside = along(block, ((0, 1), (1, 0), (2, 3), (3, 2)))
         across = along(block, ((1, 2), (2, 1)))
-        across_far = along(near, ((1, 2), (2, 1)))
+        across_far = along(beside, ((1, 2), (2, 1)))
         edge = along(across, ((1, 0), (2, 3)))
         edge_far = along(across_far, ((1, 0), (2, 3)))
         second = choose(middle, across_far, edge)
         third = choose(middle, across, edge_far)
-        slots = [block, near, second, third]
+        slots = [block, beside, second, third]
     else:
         members = [[z * 4 + i for z in range(lines)] for i in range(4)]
         slots = [lax.all_gather(block, "tm", axis_index_groups=members, axis=0, tiled=True)]
     shares = [slots, [group_swap(slot) for slot in slots]]
 
-    own = attend(reach, qn, seen)
+    own = attend(reach, qn, near, k_diag, v_diag)
     over = swap(own, 2)
     here, there = [own, swap(own, 1)], [over, swap(over, 1)]
     pieces = {}

time: 218 us -> 239 us (1.096)
  the two profiles are of different devices: /device:TPU:21 before, /device:TPU:23 now
where the time goes in v4:
time: 239 us
  waiting for transfers between devices  135 us (56%)
  starting transfers between devices  53.3 us (22%)
  Pallas kernels  44.3 us (19%)
  local copies, waits for them, and re-layouts  3.31 us (1%)
  other arithmetic  2.79 us (1%)
    ppermute x12, waiting for transfers between devices, swap(): return lax.ppermute(x, 'tm', [(i, i ^ bits) for i in range(peers)])  58 us
    ppermute x4, waiting for transfers between devices, group_swap(): return lax.ppermute(x, 'groups', [(0, 1), (1, 0)])  47 us
    ppermute x12, starting transfers between devices, swap(): return lax.ppermute(x, 'tm', [(i, i ^ bits) for i in range(peers)])  31.4 us
    pallas_call x4, Pallas kernels, project(): pl.pallas_call(functools.partial(project_kernel, share), out_shape=[jax.S...  23.5 us
    ppermute x5, waiting for transfers between devices, along(): lax.ppermute(x, 'tm', [(4 * a + i, 4 * b + i) for a, b in moves for i in...  23 us
    ppermute x5, starting transfers between devices, send(): return lax.ppermute(x, 'tm', pairs)  11.8 us
    pallas_call x1, Pallas kernels, attend(): pl.pallas_call(attend_kernel, grid=(steps,), out_shape=jax.ShapeDtypeStru...  9.85 us
    ppermute x5, starting transfers between devices, along(): lax.ppermute(x, 'tm', [(4 * a + i, 4 * b + i) for a, b in moves for i in...  7.91 us
  transfers between devices with their start and end apart: 26, of which 12 were waited for; matrix products, arithmetic and copies ran while one was open for 1% of the time, Pallas kernels for 18%

profile of v4, /device:TPU:23, one launch (start us, length us, event | category | flops | bytes accessed | tf_op | source)
XLA Modules:
  0.0 238.5 jit_solution(7411372462436431025)
XLA Ops:
  0.0 1.3 constant_dynamic-slice_fusion
  1.3 0.7 collective-permute-start.8
  2.1 3.8 %shard_map.83 = (bf16[192,5120]{1,0:T(8,128)(2,1)}, bf16[192,2560]{1,0:T(8,128)(2,1)}) custom-call(bf16[192,2560]{1,0:T(8,128)(2,1)} %k_ref.1, bf16[192,2560]{1,0:T(8,128)(2,1)} %v_ref.1, f32[20,128]{1,0:T(8,128)} %bitcast.7), custom_call_target="tpu_custom_call" | custom-call | tf_op jit(solution)/shard_map/pallas_call | solution.py:50
  5.9 1.3 collective-permute-start
  7.2 4.4 %collective-permute-start.1 = (bf16[192,5120]{1,0:T(8,128)(2,1)}, bf16[192,5120]{1,0:T(8,128)(2,1)}, u32[]{:S(2)}, u32[]{:S(2)}) collective-permute-start(bf16[192,5120]{1,0:T(8,128)(2,1)} %get-tuple-element.19.k_ref.v_ref), channel_id=1, source_target_pairs={{1,0},{2,1},{3,2},{5,4},{6,5},{7,6},{9,8},{10,9},{11,10},{13,12},{... | collective-permute-start | bytes 5898248 | tf_op jit(solution)/shard_map/ppermute | solution.py:202
  11.5 2.4 %collective-permute-start.3 = (bf16[192,2560]{1,0:T(8,128)(2,1)}, bf16[192,2560]{1,0:T(8,128)(2,1)}, u32[]{:S(2)}, u32[]{:S(2)}) collective-permute-start(bf16[192,2560]{1,0:T(8,128)(2,1)} %v_ref.1), channel_id=1, source_target_pairs={{0,2},{3,1},{4,6},{7,5},{8,10},{11,9},{12,14},{15,13},{16,18},{19,... | collective-permute-start | bytes 2949128 | tf_op jit(solution)/shard_map/ppermute | solution.py:202
  14.0 2.0 collective-permute-start.6
  16.1 26.1 %collective-permute-done.6 = bf16[160,640]{1,0:T(8,128)(2,1)S(1)} collective-permute-done((bf16[160,640]{1,0:T(8,128)(2,1)S(1)}, bf16[160,640]{1,0:T(8,128)(2,1)S(1)}, u32[]{:S(2)}, u32[]{:S(2)}) %collective-permute-start.6) | collective-permute-done | bytes 204832 | tf_op jit(solution)/shard_map/ppermute | solution.py:193
  42.2 2.5 %collective-permute-start.2 = (bf16[192,2560]{1,0:T(8,128)(2,1)}, bf16[192,2560]{1,0:T(8,128)(2,1)S(1)}, u32[]{:S(2)}, u32[]{:S(2)}) collective-permute-start(bf16[192,2560]{1,0:T(8,128)(2,1)} %get-tuple-element.20), channel_id=1, source_target_pairs={{3,4},{7,8},{11,12},{4,3},{8,7},{12,11},{19,20},{23,24},{27,28},{2... | collective-permute-start | bytes 2949128 | tf_op jit(solution)/shard_map/ppermute | solution.py:202
  44.7 16.5 %collective-permute-done.7 = bf16[160,640]{1,0:T(8,128)(2,1)S(1)} collective-permute-done((bf16[160,640]{1,0:T(8,128)(2,1)S(1)}, bf16[160,640]{1,0:T(8,128)(2,1)S(1)}, u32[]{:S(2)}, u32[]{:S(2)}) %collective-permute-start.7) | collective-permute-done | bytes 204832 | tf_op jit(solution)/shard_map/ppermute | solution.py:193
  61.3 0.2 broadcast_select_fusion.3
  61.6 1.3 collective-permute-start.4
  62.9 2.2 collective-permute-start.11
  65.1 13.9 %collective-permute-done.9.refs_3_ = bf16[640,640]{1,0:T(8,128)(2,1)} collective-permute-done((bf16[640,640]{1,0:T(8,128)(2,1)S(1)}, bf16[640,640]{1,0:T(8,128)(2,1)}, u32[]{:S(2)}, u32[]{:S(2)}) %collective-permute-start.9) | collective-permute-done | bytes 819232 | tf_op jit(solution)/shard_map/ppermute | solution.py:199
  79.0 2.1 collective-permute-start.10
  81.1 2.2 collective-permute-start.12
  83.3 2.7 %shard_map.82.q_ref = bf16[192,2560]{1,0:T(8,128)(2,1)} custom-call(bf16[192,2560]{1,0:T(8,128)(2,1)} %x_ref.1, f32[20,128]{1,0:T(8,128)} %bitcast.8), custom_call_target="tpu_custom_call" | custom-call | tf_op jit(solution)/shard_map/pallas_call | solution.py:40
  86.0 6.4 %collective-permute-done.4.vd_ref = bf16[192,2560]{1,0:T(8,128)(2,1)} collective-permute-done((bf16[192,2560]{1,0:T(8,128)(2,1)}, bf16[192,2560]{1,0:T(8,128)(2,1)}, u32[]{:S(2)}, u32[]{:S(2)}) %collective-permute-start.4) | collective-permute-done | bytes 983072 | tf_op jit(solution)/shard_map/ppermute | solution.py:202
  92.5 9.9 %attend.1.refs_0_ = bf16[192,2560]{1,0:T(8,128)(2,1)} custom-call(s32[1,2]{1,0:T(1,128)} %reach_ref.1, bf16[192,2560]{1,0:T(8,128)(2,1)} %shard_map.82.q_ref, bf16[192,5120]{1,0:T(8,128)(2,1)} %copy-done, bf16[192,5120]{1,0:T(8,128)(2,1)} %get-tuple-element.19.k_ref.v_ref, bf16[192,5120]{1,0:T(8,128)(2,1)} %collective-permute-done.1.ka_ref.va_ref, ...), custom_call_target="tpu_custom_call" | custom-call | tf_op jit(solution)/shard_map/attend/pallas_call | solution.py:99
  102.3 23.1 %collective-permute-start.15 = (bf16[192,2560]{1,0:T(8,128)(2,1)}, bf16[192,2560]{1,0:T(8,128)(2,1)}, u32[]{:S(2)}, u32[]{:S(2)}) collective-permute-start(bf16[192,2560]{1,0:T(8,128)(2,1)} %attend.1.refs_0_), channel_id=1, source_target_pairs={{0,2},{1,3},{2,0},{3,1},{4,6},{5,7},{6,4},{7,5},{8,10},{9,11},{10,... | collective-permute-start | bytes 2949128 | tf_op jit(solution)/shard_map/ppermute | solution.py:193
  125.4 1.3 collective-permute-start.13
  126.8 0.3 collective-permute-start.19
  127.2 1.2 collective-permute-start.20
  128.4 1.2 broadcast_select_fusion.1.refs_4_
  129.6 9.1 %collective-permute-done.13 = bf16[640,640]{1,0:T(8,128)(2,1)S(1)} collective-permute-done((bf16[640,640]{1,0:T(8,128)(2,1)}, bf16[640,640]{1,0:T(8,128)(2,1)S(1)}, u32[]{:S(2)}, u32[]{:S(2)}) %collective-permute-start.13) | collective-permute-done | bytes 819232 | tf_op jit(solution)/shard_map/ppermute | solution.py:199
  138.8 0.2 collective-permute-start.21
  139.0 4.4 %collective-permute-done.15.refs_0_ = bf16[192,2560]{1,0:T(8,128)(2,1)} collective-permute-done((bf16[192,2560]{1,0:T(8,128)(2,1)}, bf16[192,2560]{1,0:T(8,128)(2,1)}, u32[]{:S(2)}, u32[]{:S(2)}) %collective-permute-start.15) | collective-permute-done | bytes 983072 | tf_op jit(solution)/shard_map/ppermute | solution.py:193
  143.4 1.2 broadcast_select_fusion.refs_5_
  144.7 0.3 collective-permute-start.22
  145.0 0.6 copy-done.3
  145.6 5.9 %shard_map.84 = (bf16[192,640]{1,0:T(8,128)(2,1)}, bf16[192,640]{1,0:T(8,128)(2,1)}) custom-call(f32[40,128]{1,0:T(8,128)} %bitcast.3, bf16[192,2560]{1,0:T(8,128)(2,1)} %attend.1.refs_0_, bf16[192,2560]{1,0:T(8,128)(2,1)} %collective-permute-done.5.refs_1_, bf16[640,640]{1,0:T(8,128)(2,1)} %copy-done.1, bf16[640,640]{1,0:T(8,128)(2,1)} %collective-permute-done.9.refs_3_, ...), custom_call_target="tpu_custom_call" | custom-call | tf_op jit(solution)/shard_map/pallas_call | solution.py:144
  151.5 0.6 collective-permute-start.14
  152.1 11.9 %collective-permute-done.20.refs_3_ = bf16[640,640]{1,0:T(8,128)(2,1)} collective-permute-done((bf16[640,640]{1,0:T(8,128)(2,1)}, bf16[640,640]{1,0:T(8,128)(2,1)}, u32[]{:S(2)}, u32[]{:S(2)}) %collective-permute-start.20) | collective-permute-done | bytes 819232 | tf_op jit(solution)/shard_map/ppermute | solution.py:196
  164.0 17.6 %collective-permute-done.21.refs_4_ = bf16[640,640]{1,0:T(8,128)(2,1)} collective-permute-done((bf16[640,640]{1,0:T(8,128)(2,1)S(1)}, bf16[640,640]{1,0:T(8,128)(2,1)}, u32[]{:S(2)}, u32[]{:S(2)}) %collective-permute-start.21) | collective-permute-done | bytes 819232 | tf_op jit(solution)/shard_map/ppermute | solution.py:196
  181.5 17.6 %collective-permute-done.22.refs_5_ = bf16[640,640]{1,0:T(8,128)(2,1)} collective-permute-done((bf16[640,640]{1,0:T(8,128)(2,1)S(1)}, bf16[640,640]{1,0:T(8,128)(2,1)}, u32[]{:S(2)}, u32[]{:S(2)}) %collective-permute-start.22) | collective-permute-done | bytes 819232 | tf_op jit(solution)/shard_map/ppermute | solution.py:196
  199.1 5.9 %shard_map.86 = (bf16[192,640]{1,0:T(8,128)(2,1)}, bf16[192,640]{1,0:T(8,128)(2,1)}) custom-call(f32[40,128]{1,0:T(8,128)} %bitcast.4, bf16[192,2560]{1,0:T(8,128)(2,1)} %attend.1.refs_0_, bf16[192,2560]{1,0:T(8,128)(2,1)} %collective-permute-done.5.refs_1_, bf16[640,640]{1,0:T(8,128)(2,1)} %collective-permute-done.19.refs_2_, ...), custom_call_target="tpu_custom_call" | custom-call | tf_op jit(solution)/shard_map/pallas_call | solution.py:144
  205.0 1.3 collective-permute-start.23
  206.3 5.9 %shard_map.85 = (bf16[192,640]{1,0:T(8,128)(2,1)}, bf16[192,640]{1,0:T(8,128)(2,1)}) custom-call(f32[40,128]{1,0:T(8,128)} %bitcast.5, bf16[192,2560]{1,0:T(8,128)(2,1)} %collective-permute-done.15.refs_0_, bf16[192,2560]{1,0:T(8,128)(2,1)} %collective-permute-done.16.refs_1_, bf16[640,640]{1,0:T(8,128)(2,1)} %copy-done.1, ...), custom_call_target="tpu_custom_call" | custom-call | tf_op jit(solution)/shard_map/pallas_call | solution.py:144
  212.3 1.6 collective-permute-start.18
  213.9 5.9 %shard_map.88 = (bf16[192,640]{1,0:T(8,128)(2,1)}, bf16[192,640]{1,0:T(8,128)(2,1)}) custom-call(f32[40,128]{1,0:T(8,128)} %bitcast.6, bf16[192,2560]{1,0:T(8,128)(2,1)} %collective-permute-done.15.refs_0_, bf16[192,2560]{1,0:T(8,128)(2,1)} %collective-permute-done.16.refs_1_, bf16[640,640]{1,0:T(8,128)(2,1)} %collective-permute-done.19.refs_2_, ...), custom_call_target="tpu_custom_call" | custom-call | tf_op jit(solution)/shard_map/pallas_call | solution.py:144
  219.9 1.8 collective-permute-start.25
  221.7 4.2 %collective-permute-done.18.refs_3_ = bf16[192,640]{1,0:T(8,128)(2,1)S(1)} collective-permute-done((bf16[192,640]{1,0:T(8,128)(2,1)}, bf16[192,640]{1,0:T(8,128)(2,1)S(1)}, u32[]{:S(2)}, u32[]{:S(2)}) %collective-permute-start.18) | collective-permute-done | bytes 245792 | tf_op jit(solution)/shard_map/ppermute | solution.py:193
  225.9 0.7 copy-done.11
  226.6 2.6 %shard_map.87.refs_0_ = bf16[192,5120]{1,0:T(8,128)(2,1)} custom-call(bf16[192,640]{1,0:T(8,128)(2,1)} %get-tuple-element.25.refs_0_, bf16[192,640]{1,0:T(8,128)(2,1)} %copy-done.8, bf16[192,640]{1,0:T(8,128)(2,1)} %copy-done.10, bf16[192,640]{1,0:T(8,128)(2,1)} %copy-done.11, bf16[192,640]{1,0:T(8,128)(2,1)} %get-tuple-element.29.refs_4_, ...), custom_call_target="tpu_custom_call" | custom-call | tf_op jit(solution)/shard_map/pallas_call | solution.py:172
  229.2 1.3 collective-permute-done.24.refs_1_
  230.5 5.5 %collective-permute-done.25.refs_2_ = bf16[192,640]{1,0:T(8,128)(2,1)S(1)} collective-permute-done((bf16[192,640]{1,0:T(8,128)(2,1)}, bf16[192,640]{1,0:T(8,128)(2,1)S(1)}, u32[]{:S(2)}, u32[]{:S(2)}) %collective-permute-start.25) | collective-permute-done | bytes 245792 | tf_op jit(solution)/shard_map/ppermute | solution.py:193
  235.9 0.7 copy-done.7
  236.7 1.9 shard_map.89
  (44 shorter events, 0.6 us)
Async XLA Ops:
  1.3 14.7 %collective-permute-start.8 = (bf16[160,640]{1,0:T(8,128)(2,1)S(1)}, bf16[160,640]{1,0:T(8,128)(2,1)S(1)}, u32[]{:S(2)}, u32[]{:S(2)}) collective-permute-start(bf16[160,640]{1,0:T(8,128)(2,1)S(1)} %get-tuple-element.23), channel_id=1, source_target_pairs={{0,1},{1,0},{2,3},{3,2},{4,5},{5,4},{6,7},{7,6},{8,9},{9,8},{10,11... | collective-permute-start | bytes 614408 | tf_op jit(solution)/shard_map/ppermute | solution.py:193
  5.9 80.1 %collective-permute-start = (bf16[192,5120]{1,0:T(8,128)(2,1)}, bf16[192,5120]{1,0:T(8,128)(2,1)S(1)}, u32[]{:S(2)}, u32[]{:S(2)}) collective-permute-start(bf16[192,5120]{1,0:T(8,128)(2,1)} %get-tuple-element.19.k_ref.v_ref), channel_id=1, source_target_pairs={{0,1},{1,2},{2,3},{4,5},{5,6},{6,7},{8,9},{9,10},{10,11},{12,13},{... | collective-permute-start | bytes 5898248 | tf_op jit(solution)/shard_map/ppermute | solution.py:202
  7.2 78.9 %collective-permute-start.1 = (bf16[192,5120]{1,0:T(8,128)(2,1)}, bf16[192,5120]{1,0:T(8,128)(2,1)}, u32[]{:S(2)}, u32[]{:S(2)}) collective-permute-start(bf16[192,5120]{1,0:T(8,128)(2,1)} %get-tuple-element.19.k_ref.v_ref), channel_id=1, source_target_pairs={{1,0},{2,1},{3,2},{5,4},{6,5},{7,6},{9,8},{10,9},{11,10},{13,12},{... | collective-permute-start | bytes 5898248 | tf_op jit(solution)/shard_map/ppermute | solution.py:202
  11.5 50.0 %collective-permute-start.3 = (bf16[192,2560]{1,0:T(8,128)(2,1)}, bf16[192,2560]{1,0:T(8,128)(2,1)}, u32[]{:S(2)}, u32[]{:S(2)}) collective-permute-start(bf16[192,2560]{1,0:T(8,128)(2,1)} %v_ref.1), channel_id=1, source_target_pairs={{0,2},{3,1},{4,6},{7,5},{8,10},{11,9},{12,14},{15,13},{16,18},{19,... | collective-permute-start | bytes 2949128 | tf_op jit(solution)/shard_map/ppermute | solution.py:202
  14.0 28.2 %collective-permute-start.6 = (bf16[160,640]{1,0:T(8,128)(2,1)S(1)}, bf16[160,640]{1,0:T(8,128)(2,1)S(1)}, u32[]{:S(2)}, u32[]{:S(2)}) collective-permute-start(bf16[160,640]{1,0:T(8,128)(2,1)S(1)} %get-tuple-element.21), channel_id=1, source_target_pairs={{0,3},{1,2},{2,1},{3,0},{4,7},{5,6},{6,5},{7,4},{8,11},{9,10},{10,... | collective-permute-start | bytes 614408 | tf_op jit(solution)/shard_map/ppermute | solution.py:193
  16.0 45.2 %collective-permute-start.7 = (bf16[160,640]{1,0:T(8,128)(2,1)S(1)}, bf16[160,640]{1,0:T(8,128)(2,1)S(1)}, u32[]{:S(2)}, u32[]{:S(2)}) collective-permute-start(bf16[160,640]{1,0:T(8,128)(2,1)S(1)} %get-tuple-element.22), channel_id=1, source_target_pairs={{0,2},{1,3},{2,0},{3,1},{4,6},{5,7},{6,4},{7,5},{8,10},{9,11},{10,... | collective-permute-start | bytes 614408 | tf_op jit(solution)/shard_map/ppermute | solution.py:193
  42.2 20.7 %collective-permute-start.2 = (bf16[192,2560]{1,0:T(8,128)(2,1)}, bf16[192,2560]{1,0:T(8,128)(2,1)S(1)}, u32[]{:S(2)}, u32[]{:S(2)}) collective-permute-start(bf16[192,2560]{1,0:T(8,128)(2,1)} %get-tuple-element.20), channel_id=1, source_target_pairs={{3,4},{7,8},{11,12},{4,3},{8,7},{12,11},{19,20},{23,24},{27,28},{2... | collective-permute-start | bytes 2949128 | tf_op jit(solution)/shard_map/ppermute | solution.py:202
  61.5 65.3 %copy-start.1 = (bf16[640,640]{1,0:T(8,128)(2,1)}, bf16[640,640]{1,0:T(8,128)(2,1)S(1)}, u32[]{:S(2)}) copy-start(bf16[640,640]{1,0:T(8,128)(2,1)S(1)} %pad_maximum_fusion.refs_2_) | copy-start | bytes 2457604
  61.5 17.5 %collective-permute-start.9 = (bf16[640,640]{1,0:T(8,128)(2,1)S(1)}, bf16[640,640]{1,0:T(8,128)(2,1)}, u32[]{:S(2)}, u32[]{:S(2)}) collective-permute-start(bf16[640,640]{1,0:T(8,128)(2,1)S(1)} %pad_maximum_fusion.refs_2_), channel_id=1, source_target_pairs={{0,4},{1,5},{2,6},{3,7},{4,0},{5,1},{6,2},{7,3},{8,12},{9,13},{10,... | collective-permute-start | bytes 2457608 | tf_op jit(solution)/shard_map/ppermute | solution.py:199
  61.6 30.9 %collective-permute-start.4 = (bf16[192,2560]{1,0:T(8,128)(2,1)}, bf16[192,2560]{1,0:T(8,128)(2,1)}, u32[]{:S(2)}, u32[]{:S(2)}) collective-permute-start(bf16[192,2560]{1,0:T(8,128)(2,1)} %collective-permute-done.3), channel_id=1, source_target_pairs={{1,4},{5,8},{9,12},{6,3},{10,7},{14,11},{17,20},{21,24},{25,28},{2... | collective-permute-start | bytes 2949128 | tf_op jit(solution)/shard_map/ppermute | solution.py:202
  62.9 18.2 %copy-start.4 = (bf16[192,2560]{1,0:T(8,128)(2,1)}, bf16[192,2560]{1,0:T(8,128)(2,1)S(1)}, u32[]{:S(2)}) copy-start(bf16[192,2560]{1,0:T(8,128)(2,1)S(1)} %collective-permute-done.2.kd_ref) | copy-start | bytes 2949124
  62.9 18.2 %collective-permute-start.11 = (bf16[640,640]{1,0:T(8,128)(2,1)S(1)}, bf16[640,640]{1,0:T(8,128)(2,1)}, u32[]{:S(2)}, u32[]{:S(2)}) collective-permute-start(bf16[640,640]{1,0:T(8,128)(2,1)S(1)} %pad_maximum_fusion.refs_2_), channel_id=1, source_target_pairs={{4,8},{5,9},{6,10},{7,11},{8,4},{9,5},{10,6},{11,7},{20,24},{21,25... | collective-permute-start | bytes 2457608 | tf_op jit(solution)/shard_map/ppermute | solution.py:199
  79.0 46.4 %collective-permute-start.10 = (bf16[640,640]{1,0:T(8,128)(2,1)}, bf16[640,640]{1,0:T(8,128)(2,1)}, u32[]{:S(2)}, u32[]{:S(2)}) collective-permute-start(bf16[640,640]{1,0:T(8,128)(2,1)} %collective-permute-done.9.refs_3_), channel_id=1, source_target_pairs={{4,8},{5,9},{6,10},{7,11},{8,4},{9,5},{10,6},{11,7},{20,24},{21,25... | collective-permute-start | bytes 2457608 | tf_op jit(solution)/shard_map/ppermute | solution.py:199
  81.1 46.0 %collective-permute-start.12 = (bf16[640,640]{1,0:T(8,128)(2,1)}, bf16[640,640]{1,0:T(8,128)(2,1)}, u32[]{:S(2)}, u32[]{:S(2)}) collective-permute-start(bf16[640,640]{1,0:T(8,128)(2,1)} %collective-permute-done.11), channel_id=1, source_target_pairs={{4,0},{5,1},{6,2},{7,3},{8,12},{9,13},{10,14},{11,15},{20,16},{21,... | collective-permute-start | bytes 2457608 | tf_op jit(solution)/shard_map/ppermute | solution.py:199
  86.0 6.4 %copy-start = (bf16[192,5120]{1,0:T(8,128)(2,1)}, bf16[192,5120]{1,0:T(8,128)(2,1)S(1)}, u32[]{:S(2)}) copy-start(bf16[192,5120]{1,0:T(8,128)(2,1)S(1)} %collective-permute-done.kb_ref.vb_ref) | copy-start | bytes 5898244
  102.3 41.1 %collective-permute-start.15 = (bf16[192,2560]{1,0:T(8,128)(2,1)}, bf16[192,2560]{1,0:T(8,128)(2,1)}, u32[]{:S(2)}, u32[]{:S(2)}) collective-permute-start(bf16[192,2560]{1,0:T(8,128)(2,1)} %attend.1.refs_0_), channel_id=1, source_target_pairs={{0,2},{1,3},{2,0},{3,1},{4,6},{5,7},{6,4},{7,5},{8,10},{9,11},{10,... | collective-permute-start | bytes 2949128 | tf_op jit(solution)/shard_map/ppermute | solution.py:193
  125.4 13.4 %collective-permute-start.13 = (bf16[640,640]{1,0:T(8,128)(2,1)}, bf16[640,640]{1,0:T(8,128)(2,1)S(1)}, u32[]{:S(2)}, u32[]{:S(2)}) collective-permute-start(bf16[640,640]{1,0:T(8,128)(2,1)} %collective-permute-done.10), channel_id=1, source_target_pairs={{4,0},{5,1},{6,2},{7,3},{8,12},{9,13},{10,14},{11,15},{20,16},{21,... | collective-permute-start | bytes 2457608 | tf_op jit(solution)/shard_map/ppermute | solution.py:199
  126.7 18.0 %collective-permute-start.5 = (bf16[192,2560]{1,0:T(8,128)(2,1)}, bf16[192,2560]{1,0:T(8,128)(2,1)}, u32[]{:S(2)}, u32[]{:S(2)}) collective-permute-start(bf16[192,2560]{1,0:T(8,128)(2,1)} %attend.1.refs_0_), channel_id=1, source_target_pairs={{0,1},{1,0},{2,3},{3,2},{4,5},{5,4},{6,7},{7,6},{8,9},{9,8},{10,11... | collective-permute-start | bytes 2949128 | tf_op jit(solution)/shard_map/ppermute | solution.py:193
  126.8 24.6 %collective-permute-start.19 = (bf16[640,640]{1,0:T(8,128)(2,1)S(1)}, bf16[640,640]{1,0:T(8,128)(2,1)}, u32[]{:S(2)}, u32[]{:S(2)}) collective-permute-start(bf16[640,640]{1,0:T(8,128)(2,1)S(1)} %pad_maximum_fusion.refs_2_), channel_id=1, source_target_pairs={{0,16},{16,0},{1,17},{17,1},{2,18},{18,2},{3,19},{19,3},{4,20},{20... | collective-permute-start | bytes 2457608 | tf_op jit(solution)/shard_map/ppermute | solution.py:196
  127.2 36.8 %collective-permute-start.20 = (bf16[640,640]{1,0:T(8,128)(2,1)}, bf16[640,640]{1,0:T(8,128)(2,1)}, u32[]{:S(2)}, u32[]{:S(2)}) collective-permute-start(bf16[640,640]{1,0:T(8,128)(2,1)} %collective-permute-done.9.refs_3_), channel_id=1, source_target_pairs={{0,16},{16,0},{1,17},{17,1},{2,18},{18,2},{3,19},{19,3},{4,20},{20... | collective-permute-start | bytes 2457608 | tf_op jit(solution)/shard_map/ppermute | solution.py:196
  129.6 15.4 %copy-start.2 = (bf16[640,640]{1,0:T(8,128)(2,1)}, bf16[640,640]{1,0:T(8,128)(2,1)S(1)}, u32[]{:S(2)}) copy-start(bf16[640,640]{1,0:T(8,128)(2,1)S(1)} %broadcast_select_fusion.1.refs_4_) | copy-start | bytes 2457604
  138.8 4.7 %copy-start.5 = (bf16[640,640]{1,0:T(8,128)(2,1)}, bf16[640,640]{1,0:T(8,128)(2,1)S(1)}, u32[]{:S(2)}) copy-start(bf16[640,640]{1,0:T(8,128)(2,1)S(1)} %collective-permute-done.13) | copy-start | bytes 2457604
  138.8 42.8 %collective-permute-start.21 = (bf16[640,640]{1,0:T(8,128)(2,1)S(1)}, bf16[640,640]{1,0:T(8,128)(2,1)}, u32[]{:S(2)}, u32[]{:S(2)}) collective-permute-start(bf16[640,640]{1,0:T(8,128)(2,1)S(1)} %broadcast_select_fusion.1.refs_4_), channel_id=1, source_target_pairs={{0,16},{16,0},{1,17},{17,1},{2,18},{18,2},{3,19},{19,3},{4,20},{20... | collective-permute-start | bytes 2457608 | tf_op jit(solution)/shard_map/ppermute | solution.py:196
  143.4 62.9 %collective-permute-start.16 = (bf16[192,2560]{1,0:T(8,128)(2,1)}, bf16[192,2560]{1,0:T(8,128)(2,1)}, u32[]{:S(2)}, u32[]{:S(2)}) collective-permute-start(bf16[192,2560]{1,0:T(8,128)(2,1)} %collective-permute-done.15.refs_0_), channel_id=1, source_target_pairs={{0,1},{1,0},{2,3},{3,2},{4,5},{5,4},{6,7},{7,6},{8,9},{9,8},{10,11... | collective-permute-start | bytes 2949128 | tf_op jit(solution)/shard_map/ppermute | solution.py:193
  144.7 0.9 copy-start.3
  144.7 54.4 %collective-permute-start.22 = (bf16[640,640]{1,0:T(8,128)(2,1)S(1)}, bf16[640,640]{1,0:T(8,128)(2,1)}, u32[]{:S(2)}, u32[]{:S(2)}) collective-permute-start(bf16[640,640]{1,0:T(8,128)(2,1)S(1)} %broadcast_select_fusion.refs_5_), channel_id=1, source_target_pairs={{0,16},{16,0},{1,17},{17,1},{2,18},{18,2},{3,19},{19,3},{4,20},{20... | collective-permute-start | bytes 2457608 | tf_op jit(solution)/shard_map/ppermute | solution.py:196
  151.5 68.4 %collective-permute-start.14 = (bf16[192,640]{1,0:T(8,128)(2,1)}, bf16[192,640]{1,0:T(8,128)(2,1)S(1)}, u32[]{:S(2)}, u32[]{:S(2)}) collective-permute-start(bf16[192,640]{1,0:T(8,128)(2,1)} %get-tuple-element.26), channel_id=1, source_target_pairs={{0,1},{1,0},{2,3},{3,2},{4,5},{5,4},{6,7},{7,6},{8,9},{9,8},{10,11... | collective-permute-start | bytes 737288 | tf_op jit(solution)/shard_map/ppermute | solution.py:193
  205.0 16.7 %collective-permute-start.23 = (bf16[192,640]{1,0:T(8,128)(2,1)}, bf16[192,640]{1,0:T(8,128)(2,1)S(1)}, u32[]{:S(2)}, u32[]{:S(2)}) collective-permute-start(bf16[192,640]{1,0:T(8,128)(2,1)} %get-tuple-element.30), channel_id=1, source_target_pairs={{0,1},{1,0},{2,3},{3,2},{4,5},{5,4},{6,7},{7,6},{8,9},{9,8},{10,11... | collective-permute-start | bytes 737288 | tf_op jit(solution)/shard_map/ppermute | solution.py:193
  212.2 9.5 %collective-permute-start.17 = (bf16[192,640]{1,0:T(8,128)(2,1)}, bf16[192,640]{1,0:T(8,128)(2,1)S(1)}, u32[]{:S(2)}, u32[]{:S(2)}) collective-permute-start(bf16[192,640]{1,0:T(8,128)(2,1)} %get-tuple-element.27), channel_id=1, source_target_pairs={{0,2},{1,3},{2,0},{3,1},{4,6},{5,7},{6,4},{7,5},{8,10},{9,11},{10,... | collective-permute-start | bytes 737288 | tf_op jit(solution)/shard_map/ppermute | solution.py:193
  212.3 13.6 %collective-permute-start.18 = (bf16[192,640]{1,0:T(8,128)(2,1)}, bf16[192,640]{1,0:T(8,128)(2,1)S(1)}, u32[]{:S(2)}, u32[]{:S(2)}) collective-permute-start(bf16[192,640]{1,0:T(8,128)(2,1)} %get-tuple-element.28), channel_id=1, source_target_pairs={{0,3},{1,2},{2,1},{3,0},{4,7},{5,6},{6,5},{7,4},{8,11},{9,10},{10,... | collective-permute-start | bytes 737288 | tf_op jit(solution)/shard_map/ppermute | solution.py:193
  219.8 10.7 %collective-permute-start.24 = (bf16[192,640]{1,0:T(8,128)(2,1)}, bf16[192,640]{1,0:T(8,128)(2,1)S(1)}, u32[]{:S(2)}, u32[]{:S(2)}) collective-permute-start(bf16[192,640]{1,0:T(8,128)(2,1)} %get-tuple-element.31), channel_id=1, source_target_pairs={{0,2},{1,3},{2,0},{3,1},{4,6},{5,7},{6,4},{7,5},{8,10},{9,11},{10,... | collective-permute-start | bytes 737288 | tf_op jit(solution)/shard_map/ppermute | solution.py:193
  219.9 6.0 %copy-start.8 = (bf16[192,640]{1,0:T(8,128)(2,1)}, bf16[192,640]{1,0:T(8,128)(2,1)S(1)}, u32[]{:S(2)}) copy-start(bf16[192,640]{1,0:T(8,128)(2,1)S(1)} %collective-permute-done.14.refs_1_) | copy-start | bytes 737284
  219.9 16.0 %collective-permute-start.25 = (bf16[192,640]{1,0:T(8,128)(2,1)}, bf16[192,640]{1,0:T(8,128)(2,1)S(1)}, u32[]{:S(2)}, u32[]{:S(2)}) collective-permute-start(bf16[192,640]{1,0:T(8,128)(2,1)} %get-tuple-element.32), channel_id=1, source_target_pairs={{0,3},{1,2},{2,1},{3,0},{4,7},{5,6},{6,5},{7,4},{8,11},{9,10},{10,... | collective-permute-start | bytes 737288 | tf_op jit(solution)/shard_map/ppermute | solution.py:193
  221.7 4.2 %copy-start.9 = (bf16[192,640]{1,0:T(8,128)(2,1)}, bf16[192,640]{1,0:T(8,128)(2,1)S(1)}, u32[]{:S(2)}) copy-start(bf16[192,640]{1,0:T(8,128)(2,1)S(1)} %collective-permute-done.23.refs_5_) | copy-start | bytes 737284
  221.7 4.2 %copy-start.10 = (bf16[192,640]{1,0:T(8,128)(2,1)}, bf16[192,640]{1,0:T(8,128)(2,1)S(1)}, u32[]{:S(2)}) copy-start(bf16[192,640]{1,0:T(8,128)(2,1)S(1)} %collective-permute-done.17.refs_2_) | copy-start | bytes 737284
  225.9 0.7 copy-start.11
  230.5 5.5 %copy-start.6 = (bf16[192,640]{1,0:T(8,128)(2,1)}, bf16[192,640]{1,0:T(8,128)(2,1)S(1)}, u32[]{:S(2)}) copy-start(bf16[192,640]{1,0:T(8,128)(2,1)S(1)} %collective-permute-done.24.refs_1_) | copy-start | bytes 737284
  235.9 0.7 copy-start.7

commit v5 on v4

--- a/solution.py
+++ b/solution.py
@@ -88,65 +88,58 @@
         o_ref[:, at] = out.astype(jnp.bfloat16)
 
 
-def attend(reach, qn, pairs, k_diag, v_diag):
+def attend(reach, qn, pairs, k_diag, v_diag, chunk, chunks):
     rows, chans = qn.shape
-    heads = chans // HD
+    wide = chans // chunks
+    heads = wide // HD
     step = next(n for n in (5, 4, 3, 2, 1) if heads % n == 0)
     cols = step * HD
-    steps = chans // cols
-    k_spec = pl.BlockSpec((rows, cols), lambda i: (0, i))
-    v_spec = pl.BlockSpec((rows, cols), lambda i: (0, steps + i))
+    steps = wide // cols
+    k_spec = pl.BlockSpec((rows, cols), lambda i: (0, chunk * steps + i))
+    v_spec = pl.BlockSpec((rows, cols), lambda i: (0, (chunks + chunk) * steps + i))
     return pl.pallas_call(
         attend_kernel,
         grid=(steps,),
-        out_shape=jax.ShapeDtypeStruct((rows, chans), jnp.bfloat16),
+        out_shape=jax.ShapeDtypeStruct((rows, wide), jnp.bfloat16),
         in_specs=[pl.BlockSpec(memory_space=pltpu.SMEM)] + [k_spec] * 4 + [v_spec] * 3 + [k_spec] * 2,
-        out_specs=k_spec,
-        name="attend",
+        out_specs=pl.BlockSpec((rows, cols), lambda i: (0, i)),
     )(reach, qn, *pairs, *pairs, k_diag, v_diag)
 
 
-def project_kernel(share, gate_ref, *refs):
-    slots = len(refs) - 6
-    att_refs, w_refs, outs = refs[:2], refs[2 : 2 + slots], refs[2 + slots : 4 + slots]
-    w_ref, sems = refs[4 + slots :]
+def project_kernel(share, count, gate_ref, *refs):
+    slots = len(refs) - count - 3
+    att_refs, w_refs, outs = refs[:count], refs[count : count + slots], refs[-3:-1]
+    a_ref = refs[-1]
+    rows, wide = att_refs[0].shape
     depth, cols = w_refs[0].shape
+    chunks = count // 2
     place = lax.axis_index("tm")
     line = place // 4
-    copies = []
+    for i, ref in enumerate(att_refs):
+        p, j = i // chunks, i % chunks
+        a_ref[p * rows : (p + 1) * rows, j * wide : (j + 1) * wide] = ref[...]
+    acc = None
     for i, ref in enumerate(w_refs):
-        start = pl.multiple_of((line ^ i) * depth, depth) if slots > 1 else 0
-        copies.append(pltpu.make_async_copy(ref, w_ref.at[pl.ds(start, depth)], sems.at[i]))
-    for copy in copies:
-        copy.start()
-    rows = att_refs[0].shape[0]
-    acc = None
-    group = 2 if slots > 1 else 1
-    for i in range(0, slots, group):
-        for copy in copies[i : i + group]:
-            copy.wait()
-        start = pl.multiple_of((line // 2 ^ i // 2) * 2 * depth, HD) if slots > 1 else 0
-        weight = w_ref[pl.ds(start, group * depth), :]
-        both = jnp.concatenate([ref[:, pl.ds(start, group * depth)] for ref in att_refs], axis=0)
-        term = jnp.dot(both, weight, preferred_element_type=jnp.float32)
+        start = pl.multiple_of((line ^ i) * depth, HD) if slots > 1 else 0
+        term = jnp.dot(a_ref[:, pl.ds(start, depth)], ref[...], preferred_element_type=jnp.float32)
         acc = term if acc is None else acc + term
     first = ((place % 4) * 2 + (lax.axis_index("groups") ^ share)) * (cols // HD)
     for p in range(2):
         for b in range(cols // HD):
             at = slice(b * HD, (b + 1) * HD)
-            outs[p][:, at] = (gate_ref[pl.ds(first + b, 1), :] * acc[p * rows : (p + 1) * rows, at]).astype(jnp.bfloat16)
+            scaled = gate_ref[pl.ds(first + b, 1), :] * acc[p * rows : (p + 1) * rows, at]
+            outs[p][:, at] = scaled.astype(jnp.bfloat16)
 
 
 def project(gate, att, weights, share):
-    rows, chans = att[0].shape
+    rows, wide = att[0].shape
     cols = weights[0].shape[1]
-    slots = len(weights)
-    return pl.pallas_call(
-        functools.partial(project_kernel, share),
+    return pl.pallas_call(
+        functools.partial(project_kernel, share, len(att)),
         out_shape=[jax.ShapeDtypeStruct((rows, cols), jnp.bfloat16)] * 2,
-        in_specs=whole(3) + [pl.BlockSpec(memory_space=pl.ANY)] * slots,
+        in_specs=whole(1 + len(att) + len(weights)),
         out_specs=whole(2),
-        scratch_shapes=[pltpu.VMEM((chans, cols), jnp.bfloat16), pltpu.SemaphoreType.DMA((slots,))],
+        scratch_shapes=[pltpu.VMEM((2 * rows, wide * len(att) // 2), jnp.bfloat16)],
     )(gate.reshape(-1, HD), *att, *weights)
 
 
@@ -187,7 +180,9 @@
     line = place // 4
     lines = peers // 4
     _, width = out_weight.shape
+    _, chans = queries.shape
     cols = width // 8
+    chunks = 2 if chans // HD % 2 == 0 else 1
 
     def swap(x, bits):
         return lax.ppermute(x, "tm", [(i, i ^ bits) for i in range(peers)])
@@ -251,9 +246,14 @@
         slots = [lax.all_gather(block, "tm", axis_index_groups=members, axis=0, tiled=True)]
     shares = [slots, [group_swap(slot) for slot in slots]]
 
-    own = attend(reach, qn, near, k_diag, v_diag)
-    over = swap(own, 2)
-    here, there = [own, swap(own, 1)], [over, swap(over, 1)]
+    here, there = [], []
+    for i in range(chunks):
+        own = attend(reach, qn, near, k_diag, v_diag, i, chunks)
+        over = swap(own, 2)
+        here.append([own, swap(own, 1)])
+        there.append([over, swap(over, 1)])
+    here = [pair[p] for p in range(2) for pair in here]
+    there = [pair[p] for p in range(2) for pair in there]
     pieces = {}
     for j in range(2):
         made = project(out_gate, here, shares[j], j)

time: 239 us -> 241 us (level)
  the two profiles are of different devices: /device:TPU:23 before, /device:TPU:11 now
where the time goes in v5:
time: 241 us
  waiting for transfers between devices  146 us (61%)
  Pallas kernels  44.3 us (18%)
  starting transfers between devices  42.5 us (18%)
  local copies, waits for them, and re-layouts  4.73 us (2%)
  other arithmetic  2.79 us (1%)
    ppermute x15, waiting for transfers between devices, swap(): return lax.ppermute(x, 'tm', [(i, i ^ bits) for i in range(peers)])  62.5 us
    ppermute x4, waiting for transfers between devices, group_swap(): return lax.ppermute(x, 'groups', [(0, 1), (1, 0)])  47.9 us
    ppermute x5, waiting for transfers between devices, along(): lax.ppermute(x, 'tm', [(4 * a + i, 4 * b + i) for a, b in moves for i in...  35.4 us
    pallas_call x4, Pallas kernels, project(): pl.pallas_call(functools.partial(project_kernel, share, len(att)), out_sh...  21.1 us
    ppermute x15, starting transfers between devices, swap(): return lax.ppermute(x, 'tm', [(i, i ^ bits) for i in range(peers)])  16.1 us
    pallas_call x2, Pallas kernels, attend(): pl.pallas_call(attend_kernel, grid=(steps,), out_shape=jax.ShapeDtypeStru...  12.2 us
    ppermute x5, starting transfers between devices, along(): lax.ppermute(x, 'tm', [(4 * a + i, 4 * b + i) for a, b in moves for i in...  12.2 us
    ppermute x5, starting transfers between devices, send(): return lax.ppermute(x, 'tm', pairs)  12.2 us
  transfers between devices with their start and end apart: 29, of which 10 were waited for; matrix products, arithmetic and copies ran while one was open for 1% of the time, Pallas kernels for 18%

profile of v5, /device:TPU:11, one launch (start us, length us, event | category | flops | bytes accessed | tf_op | source)
XLA Modules:
  0.0 240.7 jit_solution(13600810884712626399)
XLA Ops:
  0.0 1.3 constant_dynamic-slice_fusion
  1.3 0.7 collective-permute-start.9
  2.1 3.8 %shard_map.83 = (bf16[192,5120]{1,0:T(8,128)(2,1)}, bf16[192,2560]{1,0:T(8,128)(2,1)}) custom-call(bf16[192,2560]{1,0:T(8,128)(2,1)} %k_ref.1, bf16[192,2560]{1,0:T(8,128)(2,1)} %v_ref.1, f32[20,128]{1,0:T(8,128)} %bitcast.7), custom_call_target="tpu_custom_call" | custom-call | tf_op jit(solution)/shard_map/pallas_call | solution.py:50
  5.9 3.0 %collective-permute-start = (bf16[192,5120]{1,0:T(8,128)(2,1)}, bf16[192,5120]{1,0:T(8,128)(2,1)S(1)}, u32[]{:S(2)}, u32[]{:S(2)}) collective-permute-start(bf16[192,5120]{1,0:T(8,128)(2,1)} %get-tuple-element.19.k_ref.v_ref), channel_id=1, source_target_pairs={{0,1},{1,2},{2,3},{4,5},{5,6},{6,7},{8,9},{9,10},{10,11},{12,13},{... | collective-permute-start | bytes 5898248 | tf_op jit(solution)/shard_map/ppermute | solution.py:197
  8.9 1.9 collective-permute-start.1
  10.9 1.3 collective-permute-start.3
  12.2 1.8 collective-permute-start.7
  14.0 3.2 %collective-permute-start.8 = (bf16[160,640]{1,0:T(8,128)(2,1)S(1)}, bf16[160,640]{1,0:T(8,128)(2,1)S(1)}, u32[]{:S(2)}, u32[]{:S(2)}) collective-permute-start(bf16[160,640]{1,0:T(8,128)(2,1)S(1)} %get-tuple-element.22), channel_id=1, source_target_pairs={{0,2},{1,3},{2,0},{3,1},{4,6},{5,7},{6,4},{7,5},{8,10},{9,11},{10,... | collective-permute-start | bytes 614408 | tf_op jit(solution)/shard_map/ppermute | solution.py:188
  17.3 45.5 %collective-permute-done.7 = bf16[160,640]{1,0:T(8,128)(2,1)S(1)} collective-permute-done((bf16[160,640]{1,0:T(8,128)(2,1)S(1)}, bf16[160,640]{1,0:T(8,128)(2,1)S(1)}, u32[]{:S(2)}, u32[]{:S(2)}) %collective-permute-start.7) | collective-permute-done | bytes 204832 | tf_op jit(solution)/shard_map/ppermute | solution.py:188
  62.7 0.7 collective-permute-start.2
  63.9 4.5 %collective-permute-start.12 = (bf16[640,640]{1,0:T(8,128)(2,1)S(1)}, bf16[640,640]{1,0:T(8,128)(2,1)}, u32[]{:S(2)}, u32[]{:S(2)}) collective-permute-start(bf16[640,640]{1,0:T(8,128)(2,1)S(1)} %pad_maximum_fusion.refs_4_), channel_id=1, source_target_pairs={{4,8},{5,9},{6,10},{7,11},{8,4},{9,5},{10,6},{11,7},{20,24},{21,25... | collective-permute-start | bytes 2457608 | tf_op jit(solution)/shard_map/ppermute | solution.py:194
  68.4 5.2 %collective-permute-start.4 = (bf16[192,2560]{1,0:T(8,128)(2,1)}, bf16[192,2560]{1,0:T(8,128)(2,1)}, u32[]{:S(2)}, u32[]{:S(2)}) collective-permute-start(bf16[192,2560]{1,0:T(8,128)(2,1)} %collective-permute-done.3), channel_id=1, source_target_pairs={{1,4},{5,8},{9,12},{6,3},{10,7},{14,11},{17,20},{21,24},{25,28},{2... | collective-permute-start | bytes 2949128 | tf_op jit(solution)/shard_map/ppermute | solution.py:197
  73.5 8.0 %collective-permute-done.10.refs_5_ = bf16[640,640]{1,0:T(8,128)(2,1)S(1)} collective-permute-done((bf16[640,640]{1,0:T(8,128)(2,1)S(1)}, bf16[640,640]{1,0:T(8,128)(2,1)S(1)}, u32[]{:S(2)}, u32[]{:S(2)}) %collective-permute-start.10) | collective-permute-done | bytes 819232 | tf_op jit(solution)/shard_map/ppermute | solution.py:194
  81.6 3.2 %collective-permute-start.11 = (bf16[640,640]{1,0:T(8,128)(2,1)S(1)}, bf16[640,640]{1,0:T(8,128)(2,1)}, u32[]{:S(2)}, u32[]{:S(2)}) collective-permute-start(bf16[640,640]{1,0:T(8,128)(2,1)S(1)} %collective-permute-done.10.refs_5_), channel_id=1, source_target_pairs={{4,8},{5,9},{6,10},{7,11},{8,4},{9,5},{10,6},{11,7},{20,24},{21,25... | collective-permute-start | bytes 2457608 | tf_op jit(solution)/shard_map/ppermute | solution.py:194
  84.8 2.3 collective-permute-start.13
  87.1 27.4 %collective-permute-done.11 = bf16[640,640]{1,0:T(8,128)(2,1)} collective-permute-done((bf16[640,640]{1,0:T(8,128)(2,1)S(1)}, bf16[640,640]{1,0:T(8,128)(2,1)}, u32[]{:S(2)}, u32[]{:S(2)}) %collective-permute-start.11) | collective-permute-done | bytes 819232 | tf_op jit(solution)/shard_map/ppermute | solution.py:194
  114.5 2.2 collective-permute-start.14
  116.6 2.7 %shard_map.82.q_ref = bf16[192,2560]{1,0:T(8,128)(2,1)} custom-call(bf16[192,2560]{1,0:T(8,128)(2,1)} %x_ref.1, f32[20,128]{1,0:T(8,128)} %bitcast.8), custom_call_target="tpu_custom_call" | custom-call | tf_op jit(solution)/shard_map/pallas_call | solution.py:40
  119.4 1.3 copy-done
  120.6 6.1 %shard_map.84.refs_0_ = bf16[192,1280]{1,0:T(8,128)(2,1)} custom-call(s32[1,2]{1,0:T(1,128)} %reach_ref.3, bf16[192,2560]{1,0:T(8,128)(2,1)} %shard_map.82.q_ref, bf16[192,5120]{1,0:T(8,128)(2,1)} %copy-done, bf16[192,5120]{1,0:T(8,128)(2,1)} %get-tuple-element.19.k_ref.v_ref, bf16[192,5120]{1,0:T(8,128)(2,1)} %collective-permute-done.1.ka_ref.va_ref, ...), custom_call_target="tpu_custom_call" | custom-call | tf_op jit(solution)/shard_map/pallas_call | solution.py:100
  126.9 6.1 %shard_map.85.refs_1_ = bf16[192,1280]{1,0:T(8,128)(2,1)} custom-call(s32[1,2]{1,0:T(1,128)} %reach_ref.3, bf16[192,2560]{1,0:T(8,128)(2,1)} %shard_map.82.q_ref, bf16[192,5120]{1,0:T(8,128)(2,1)} %copy-done, bf16[192,5120]{1,0:T(8,128)(2,1)} %get-tuple-element.19.k_ref.v_ref, bf16[192,5120]{1,0:T(8,128)(2,1)} %collective-permute-done.1.ka_ref.va_ref, ...), custom_call_target="tpu_custom_call" | custom-call | tf_op jit(solution)/shard_map/pallas_call | solution.py:100
  133.0 0.5 collective-permute-start.6
  133.5 1.4 collective-permute-start.17
  134.9 4.5 %collective-permute-done.16.refs_0_ = bf16[192,1280]{1,0:T(8,128)(2,1)} collective-permute-done((bf16[192,1280]{1,0:T(8,128)(2,1)}, bf16[192,1280]{1,0:T(8,128)(2,1)}, u32[]{:S(2)}, u32[]{:S(2)}) %collective-permute-start.16) | collective-permute-done | bytes 491552 | tf_op jit(solution)/shard_map/ppermute | solution.py:188
  139.4 1.2 broadcast_select_fusion.1.refs_6_
  141.0 1.2 broadcast_select_fusion.refs_7_
  142.3 1.3 collective-permute-start.23
  143.8 0.6 copy-done.7
  144.4 4.4 %collective-permute-done.17.refs_1_ = bf16[192,1280]{1,0:T(8,128)(2,1)} collective-permute-done((bf16[192,1280]{1,0:T(8,128)(2,1)}, bf16[192,1280]{1,0:T(8,128)(2,1)}, u32[]{:S(2)}, u32[]{:S(2)}) %collective-permute-start.17) | collective-permute-done | bytes 491552 | tf_op jit(solution)/shard_map/ppermute | solution.py:188
  149.1 5.3 %shard_map.86 = (bf16[192,640]{1,0:T(8,128)(2,1)}, bf16[192,640]{1,0:T(8,128)(2,1)}) custom-call(f32[40,128]{1,0:T(8,128)} %bitcast.3, bf16[192,1280]{1,0:T(8,128)(2,1)} %shard_map.84.refs_0_, bf16[192,1280]{1,0:T(8,128)(2,1)} %shard_map.85.refs_1_, bf16[192,1280]{1,0:T(8,128)(2,1)} %collective-permute-done.5.refs_2_, bf16[192,1280]{1,0:T(8,128)(2,1)} %copy-done.7, ...), custom_call_target="tpu_custom_call" | custom-call | tf_op jit(solution)/shard_map/pallas_call | solution.py:137
  154.4 0.5 collective-permute-start.15
  154.9 5.3 %shard_map.87 = (bf16[192,640]{1,0:T(8,128)(2,1)}, bf16[192,640]{1,0:T(8,128)(2,1)}) custom-call(f32[40,128]{1,0:T(8,128)} %bitcast.4, bf16[192,1280]{1,0:T(8,128)(2,1)} %collective-permute-done.16.refs_0_, bf16[192,1280]{1,0:T(8,128)(2,1)} %collective-permute-done.17.refs_1_, bf16[192,1280]{1,0:T(8,128)(2,1)} %collective-permute-done.18.refs_2_, ...), custom_call_target="tpu_custom_call" | custom-call | tf_op jit(solution)/shard_map/pallas_call | solution.py:137
  160.2 1.7 collective-permute-start.20
  161.9 15.8 %collective-permute-done.23.refs_5_ = bf16[640,640]{1,0:T(8,128)(2,1)} collective-permute-done((bf16[640,640]{1,0:T(8,128)(2,1)S(1)}, bf16[640,640]{1,0:T(8,128)(2,1)}, u32[]{:S(2)}, u32[]{:S(2)}) %collective-permute-start.23) | collective-permute-done | bytes 819232 | tf_op jit(solution)/shard_map/ppermute | solution.py:191
  177.7 3.1 %collective-permute-start.21 = (bf16[192,640]{1,0:T(8,128)(2,1)}, bf16[192,640]{1,0:T(8,128)(2,1)S(1)}, u32[]{:S(2)}, u32[]{:S(2)}) collective-permute-start(bf16[192,640]{1,0:T(8,128)(2,1)} %get-tuple-element.28), channel_id=1, source_target_pairs={{0,3},{1,2},{2,1},{3,0},{4,7},{5,6},{6,5},{7,4},{8,11},{9,10},{10,... | collective-permute-start | bytes 737288 | tf_op jit(solution)/shard_map/ppermute | solution.py:188
  180.8 14.5 %collective-permute-done.24.refs_6_ = bf16[640,640]{1,0:T(8,128)(2,1)} collective-permute-done((bf16[640,640]{1,0:T(8,128)(2,1)S(1)}, bf16[640,640]{1,0:T(8,128)(2,1)}, u32[]{:S(2)}, u32[]{:S(2)}) %collective-permute-start.24) | collective-permute-done | bytes 819232 | tf_op jit(solution)/shard_map/ppermute | solution.py:191
  195.3 17.6 %collective-permute-done.25.refs_7_ = bf16[640,640]{1,0:T(8,128)(2,1)} collective-permute-done((bf16[640,640]{1,0:T(8,128)(2,1)S(1)}, bf16[640,640]{1,0:T(8,128)(2,1)}, u32[]{:S(2)}, u32[]{:S(2)}) %collective-permute-start.25) | collective-permute-done | bytes 819232 | tf_op jit(solution)/shard_map/ppermute | solution.py:191
  212.8 5.3 %shard_map.88 = (bf16[192,640]{1,0:T(8,128)(2,1)}, bf16[192,640]{1,0:T(8,128)(2,1)}) custom-call(f32[40,128]{1,0:T(8,128)} %bitcast.5, bf16[192,1280]{1,0:T(8,128)(2,1)} %shard_map.84.refs_0_, bf16[192,1280]{1,0:T(8,128)(2,1)} %shard_map.85.refs_1_, bf16[192,1280]{1,0:T(8,128)(2,1)} %collective-permute-done.5.refs_2_, bf16[192,1280]{1,0:T(8,128)(2,1)} %copy-done.7, ...), custom_call_target="tpu_custom_call" | custom-call | tf_op jit(solution)/shard_map/pallas_call | solution.py:137
  218.1 1.4 collective-permute-start.26
  219.5 5.3 %shard_map.90 = (bf16[192,640]{1,0:T(8,128)(2,1)}, bf16[192,640]{1,0:T(8,128)(2,1)}) custom-call(f32[40,128]{1,0:T(8,128)} %bitcast.6, bf16[192,1280]{1,0:T(8,128)(2,1)} %collective-permute-done.16.refs_0_, bf16[192,1280]{1,0:T(8,128)(2,1)} %collective-permute-done.17.refs_1_, bf16[192,1280]{1,0:T(8,128)(2,1)} %collective-permute-done.18.refs_2_, ...), custom_call_target="tpu_custom_call" | custom-call | tf_op jit(solution)/shard_map/pallas_call | solution.py:137
  224.8 0.9 collective-permute-start.27
  225.6 0.8 collective-permute-start.28
  226.5 0.6 copy-done.11
  227.3 2.6 %shard_map.89.refs_0_ = bf16[192,5120]{1,0:T(8,128)(2,1)} custom-call(bf16[192,640]{1,0:T(8,128)(2,1)} %get-tuple-element.25.refs_0_, bf16[192,640]{1,0:T(8,128)(2,1)} %copy-done.10, bf16[192,640]{1,0:T(8,128)(2,1)} %copy-done.11, bf16[192,640]{1,0:T(8,128)(2,1)} %copy-done.12, bf16[192,640]{1,0:T(8,128)(2,1)} %get-tuple-element.29.refs_4_, ...), custom_call_target="tpu_custom_call" | custom-call | tf_op jit(solution)/shard_map/pallas_call | solution.py:165
  229.9 2.6 %collective-permute-done.27.refs_1_ = bf16[192,640]{1,0:T(8,128)(2,1)S(1)} collective-permute-done((bf16[192,640]{1,0:T(8,128)(2,1)}, bf16[192,640]{1,0:T(8,128)(2,1)S(1)}, u32[]{:S(2)}, u32[]{:S(2)}) %collective-permute-start.27) | collective-permute-done | bytes 245792 | tf_op jit(solution)/shard_map/ppermute | solution.py:188
  232.5 5.4 %collective-permute-done.28.refs_2_ = bf16[192,640]{1,0:T(8,128)(2,1)S(1)} collective-permute-done((bf16[192,640]{1,0:T(8,128)(2,1)}, bf16[192,640]{1,0:T(8,128)(2,1)S(1)}, u32[]{:S(2)}, u32[]{:S(2)}) %collective-permute-start.28) | collective-permute-done | bytes 245792 | tf_op jit(solution)/shard_map/ppermute | solution.py:188
  237.9 0.7 copy-done.9
  238.6 1.9 shard_map.91
  (55 shorter events, 1.6 us)
Async XLA Ops:
  1.3 12.6 %collective-permute-start.9 = (bf16[160,640]{1,0:T(8,128)(2,1)S(1)}, bf16[160,640]{1,0:T(8,128)(2,1)S(1)}, u32[]{:S(2)}, u32[]{:S(2)}) collective-permute-start(bf16[160,640]{1,0:T(8,128)(2,1)S(1)} %get-tuple-element.23), channel_id=1, source_target_pairs={{0,1},{1,0},{2,3},{3,2},{4,5},{5,4},{6,7},{7,6},{8,9},{9,8},{10,11... | collective-permute-start | bytes 614408 | tf_op jit(solution)/shard_map/ppermute | solution.py:188
  5.9 113.5 %collective-permute-start = (bf16[192,5120]{1,0:T(8,128)(2,1)}, bf16[192,5120]{1,0:T(8,128)(2,1)S(1)}, u32[]{:S(2)}, u32[]{:S(2)}) collective-permute-start(bf16[192,5120]{1,0:T(8,128)(2,1)} %get-tuple-element.19.k_ref.v_ref), channel_id=1, source_target_pairs={{0,1},{1,2},{2,3},{4,5},{5,6},{6,7},{8,9},{9,10},{10,11},{12,13},{... | collective-permute-start | bytes 5898248 | tf_op jit(solution)/shard_map/ppermute | solution.py:197
  8.9 110.4 %collective-permute-start.1 = (bf16[192,5120]{1,0:T(8,128)(2,1)}, bf16[192,5120]{1,0:T(8,128)(2,1)}, u32[]{:S(2)}, u32[]{:S(2)}) collective-permute-start(bf16[192,5120]{1,0:T(8,128)(2,1)} %get-tuple-element.19.k_ref.v_ref), channel_id=1, source_target_pairs={{1,0},{2,1},{3,2},{5,4},{6,5},{7,6},{9,8},{10,9},{11,10},{13,12},{... | collective-permute-start | bytes 5898248 | tf_op jit(solution)/shard_map/ppermute | solution.py:197
  10.9 57.5 %collective-permute-start.3 = (bf16[192,2560]{1,0:T(8,128)(2,1)}, bf16[192,2560]{1,0:T(8,128)(2,1)}, u32[]{:S(2)}, u32[]{:S(2)}) collective-permute-start(bf16[192,2560]{1,0:T(8,128)(2,1)} %v_ref.1), channel_id=1, source_target_pairs={{0,2},{3,1},{4,6},{7,5},{8,10},{11,9},{12,14},{15,13},{16,18},{19,... | collective-permute-start | bytes 2949128 | tf_op jit(solution)/shard_map/ppermute | solution.py:197
  12.2 50.6 %collective-permute-start.7 = (bf16[160,640]{1,0:T(8,128)(2,1)S(1)}, bf16[160,640]{1,0:T(8,128)(2,1)S(1)}, u32[]{:S(2)}, u32[]{:S(2)}) collective-permute-start(bf16[160,640]{1,0:T(8,128)(2,1)S(1)} %get-tuple-element.21), channel_id=1, source_target_pairs={{0,3},{1,2},{2,1},{3,0},{4,7},{5,6},{6,5},{7,4},{8,11},{9,10},{10,... | collective-permute-start | bytes 614408 | tf_op jit(solution)/shard_map/ppermute | solution.py:188
  14.0 49.5 %collective-permute-start.8 = (bf16[160,640]{1,0:T(8,128)(2,1)S(1)}, bf16[160,640]{1,0:T(8,128)(2,1)S(1)}, u32[]{:S(2)}, u32[]{:S(2)}) collective-permute-start(bf16[160,640]{1,0:T(8,128)(2,1)S(1)} %get-tuple-element.22), channel_id=1, source_target_pairs={{0,2},{1,3},{2,0},{3,1},{4,6},{5,7},{6,4},{7,5},{8,10},{9,11},{10,... | collective-permute-start | bytes 614408 | tf_op jit(solution)/shard_map/ppermute | solution.py:188
  62.7 1.1 collective-permute-start.2
  63.8 76.9 %copy-start.1 = (bf16[640,640]{1,0:T(8,128)(2,1)}, bf16[640,640]{1,0:T(8,128)(2,1)S(1)}, u32[]{:S(2)}) copy-start(bf16[640,640]{1,0:T(8,128)(2,1)S(1)} %pad_maximum_fusion.refs_4_) | copy-start | bytes 2457604
  63.8 17.8 %collective-permute-start.10 = (bf16[640,640]{1,0:T(8,128)(2,1)S(1)}, bf16[640,640]{1,0:T(8,128)(2,1)S(1)}, u32[]{:S(2)}, u32[]{:S(2)}) collective-permute-start(bf16[640,640]{1,0:T(8,128)(2,1)S(1)} %pad_maximum_fusion.refs_4_), channel_id=1, source_target_pairs={{0,4},{1,5},{2,6},{3,7},{4,0},{5,1},{6,2},{7,3},{8,12},{9,13},{10,... | collective-permute-start | bytes 2457608 | tf_op jit(solution)/shard_map/ppermute | solution.py:194
  63.9 21.0 %copy-start.4 = (bf16[192,2560]{1,0:T(8,128)(2,1)}, bf16[192,2560]{1,0:T(8,128)(2,1)S(1)}, u32[]{:S(2)}) copy-start(bf16[192,2560]{1,0:T(8,128)(2,1)S(1)} %collective-permute-done.2.kd_ref) | copy-start | bytes 2949124
  63.9 20.9 %collective-permute-start.12 = (bf16[640,640]{1,0:T(8,128)(2,1)S(1)}, bf16[640,640]{1,0:T(8,128)(2,1)}, u32[]{:S(2)}, u32[]{:S(2)}) collective-permute-start(bf16[640,640]{1,0:T(8,128)(2,1)S(1)} %pad_maximum_fusion.refs_4_), channel_id=1, source_target_pairs={{4,8},{5,9},{6,10},{7,11},{8,4},{9,5},{10,6},{11,7},{20,24},{21,25... | collective-permute-start | bytes 2457608 | tf_op jit(solution)/shard_map/ppermute | solution.py:194
  68.4 51.0 %collective-permute-start.4 = (bf16[192,2560]{1,0:T(8,128)(2,1)}, bf16[192,2560]{1,0:T(8,128)(2,1)}, u32[]{:S(2)}, u32[]{:S(2)}) collective-permute-start(bf16[192,2560]{1,0:T(8,128)(2,1)} %collective-permute-done.3), channel_id=1, source_target_pairs={{1,4},{5,8},{9,12},{6,3},{10,7},{14,11},{17,20},{21,24},{25,28},{2... | collective-permute-start | bytes 2949128 | tf_op jit(solution)/shard_map/ppermute | solution.py:197
  81.6 5.5 %copy-start.5 = (bf16[640,640]{1,0:T(8,128)(2,1)}, bf16[640,640]{1,0:T(8,128)(2,1)S(1)}, u32[]{:S(2)}) copy-start(bf16[640,640]{1,0:T(8,128)(2,1)S(1)} %collective-permute-done.10.refs_5_) | copy-start | bytes 2457604
  81.6 32.9 %collective-permute-start.11 = (bf16[640,640]{1,0:T(8,128)(2,1)S(1)}, bf16[640,640]{1,0:T(8,128)(2,1)}, u32[]{:S(2)}, u32[]{:S(2)}) collective-permute-start(bf16[640,640]{1,0:T(8,128)(2,1)S(1)} %collective-permute-done.10.refs_5_), channel_id=1, source_target_pairs={{4,8},{5,9},{6,10},{7,11},{8,4},{9,5},{10,6},{11,7},{20,24},{21,25... | collective-permute-start | bytes 2457608 | tf_op jit(solution)/shard_map/ppermute | solution.py:194
  84.8 48.7 %collective-permute-start.13 = (bf16[640,640]{1,0:T(8,128)(2,1)}, bf16[640,640]{1,0:T(8,128)(2,1)}, u32[]{:S(2)}, u32[]{:S(2)}) collective-permute-start(bf16[640,640]{1,0:T(8,128)(2,1)} %collective-permute-done.12), channel_id=1, source_target_pairs={{4,0},{5,1},{6,2},{7,3},{8,12},{9,13},{10,14},{11,15},{20,16},{21,... | collective-permute-start | bytes 2457608 | tf_op jit(solution)/shard_map/ppermute | solution.py:194
  114.5 26.2 %collective-permute-start.14 = (bf16[640,640]{1,0:T(8,128)(2,1)}, bf16[640,640]{1,0:T(8,128)(2,1)}, u32[]{:S(2)}, u32[]{:S(2)}) collective-permute-start(bf16[640,640]{1,0:T(8,128)(2,1)} %collective-permute-done.11), channel_id=1, source_target_pairs={{4,0},{5,1},{6,2},{7,3},{8,12},{9,13},{10,14},{11,15},{20,16},{21,... | collective-permute-start | bytes 2457608 | tf_op jit(solution)/shard_map/ppermute | solution.py:194
  119.4 1.3 copy-start
  126.7 12.7 %collective-permute-start.16 = (bf16[192,1280]{1,0:T(8,128)(2,1)}, bf16[192,1280]{1,0:T(8,128)(2,1)}, u32[]{:S(2)}, u32[]{:S(2)}) collective-permute-start(bf16[192,1280]{1,0:T(8,128)(2,1)} %shard_map.84.refs_0_), channel_id=1, source_target_pairs={{0,2},{1,3},{2,0},{3,1},{4,6},{5,7},{6,4},{7,5},{8,10},{9,11},{10,... | collective-permute-start | bytes 1474568 | tf_op jit(solution)/shard_map/ppermute | solution.py:188
  126.8 15.5 %collective-permute-start.5 = (bf16[192,1280]{1,0:T(8,128)(2,1)}, bf16[192,1280]{1,0:T(8,128)(2,1)}, u32[]{:S(2)}, u32[]{:S(2)}) collective-permute-start(bf16[192,1280]{1,0:T(8,128)(2,1)} %shard_map.84.refs_0_), channel_id=1, source_target_pairs={{0,1},{1,0},{2,3},{3,2},{4,5},{5,4},{6,7},{7,6},{8,9},{9,8},{10,11... | collective-permute-start | bytes 1474568 | tf_op jit(solution)/shard_map/ppermute | solution.py:188
  133.0 9.3 %copy-start.6 = (bf16[640,640]{1,0:T(8,128)(2,1)S(1)}, bf16[640,640]{1,0:T(8,128)(2,1)}, u32[]{:S(2)}) copy-start(bf16[640,640]{1,0:T(8,128)(2,1)} %copy-done.5) | copy-start | bytes 2457604
  133.0 10.6 %collective-permute-start.6 = (bf16[192,1280]{1,0:T(8,128)(2,1)}, bf16[192,1280]{1,0:T(8,128)(2,1)S(1)}, u32[]{:S(2)}, u32[]{:S(2)}) collective-permute-start(bf16[192,1280]{1,0:T(8,128)(2,1)} %shard_map.85.refs_1_), channel_id=1, source_target_pairs={{0,1},{1,0},{2,3},{3,2},{4,5},{5,4},{6,7},{7,6},{8,9},{9,8},{10,11... | collective-permute-start | bytes 1474568 | tf_op jit(solution)/shard_map/ppermute | solution.py:188
  133.5 15.3 %collective-permute-start.17 = (bf16[192,1280]{1,0:T(8,128)(2,1)}, bf16[192,1280]{1,0:T(8,128)(2,1)}, u32[]{:S(2)}, u32[]{:S(2)}) collective-permute-start(bf16[192,1280]{1,0:T(8,128)(2,1)} %shard_map.85.refs_1_), channel_id=1, source_target_pairs={{0,2},{1,3},{2,0},{3,1},{4,6},{5,7},{6,4},{7,5},{8,10},{9,11},{10,... | collective-permute-start | bytes 1474568 | tf_op jit(solution)/shard_map/ppermute | solution.py:188
  139.4 9.6 %collective-permute-start.18 = (bf16[192,1280]{1,0:T(8,128)(2,1)}, bf16[192,1280]{1,0:T(8,128)(2,1)}, u32[]{:S(2)}, u32[]{:S(2)}) collective-permute-start(bf16[192,1280]{1,0:T(8,128)(2,1)} %collective-permute-done.16.refs_0_), channel_id=1, source_target_pairs={{0,1},{1,0},{2,3},{3,2},{4,5},{5,4},{6,7},{7,6},{8,9},{9,8},{10,11... | collective-permute-start | bytes 1474568 | tf_op jit(solution)/shard_map/ppermute | solution.py:188
  140.7 8.4 %copy-start.2 = (bf16[640,640]{1,0:T(8,128)(2,1)}, bf16[640,640]{1,0:T(8,128)(2,1)S(1)}, u32[]{:S(2)}) copy-start(bf16[640,640]{1,0:T(8,128)(2,1)S(1)} %broadcast_select_fusion.1.refs_6_) | copy-start | bytes 2457604
  140.7 19.5 %collective-permute-start.22 = (bf16[640,640]{1,0:T(8,128)(2,1)S(1)}, bf16[640,640]{1,0:T(8,128)(2,1)}, u32[]{:S(2)}, u32[]{:S(2)}) collective-permute-start(bf16[640,640]{1,0:T(8,128)(2,1)S(1)} %pad_maximum_fusion.refs_4_), channel_id=1, source_target_pairs={{0,16},{16,0},{1,17},{17,1},{2,18},{18,2},{3,19},{19,3},{4,20},{20... | collective-permute-start | bytes 2457608 | tf_op jit(solution)/shard_map/ppermute | solution.py:191
  142.3 6.8 %copy-start.3 = (bf16[640,640]{1,0:T(8,128)(2,1)}, bf16[640,640]{1,0:T(8,128)(2,1)S(1)}, u32[]{:S(2)}) copy-start(bf16[640,640]{1,0:T(8,128)(2,1)S(1)} %broadcast_select_fusion.refs_7_) | copy-start | bytes 2457604
  142.3 35.4 %collective-permute-start.23 = (bf16[640,640]{1,0:T(8,128)(2,1)S(1)}, bf16[640,640]{1,0:T(8,128)(2,1)}, u32[]{:S(2)}, u32[]{:S(2)}) collective-permute-start(bf16[640,640]{1,0:T(8,128)(2,1)S(1)} %copy-done.6), channel_id=1, source_target_pairs={{0,16},{16,0},{1,17},{17,1},{2,18},{18,2},{3,19},{19,3},{4,20},{20... | collective-permute-start | bytes 2457608 | tf_op jit(solution)/shard_map/ppermute | solution.py:191
  143.6 0.8 copy-start.7
  143.6 51.7 %collective-permute-start.24 = (bf16[640,640]{1,0:T(8,128)(2,1)S(1)}, bf16[640,640]{1,0:T(8,128)(2,1)}, u32[]{:S(2)}, u32[]{:S(2)}) collective-permute-start(bf16[640,640]{1,0:T(8,128)(2,1)S(1)} %broadcast_select_fusion.1.refs_6_), channel_id=1, source_target_pairs={{0,16},{16,0},{1,17},{17,1},{2,18},{18,2},{3,19},{19,3},{4,20},{20... | collective-permute-start | bytes 2457608 | tf_op jit(solution)/shard_map/ppermute | solution.py:191
  148.8 64.0 %collective-permute-start.25 = (bf16[640,640]{1,0:T(8,128)(2,1)S(1)}, bf16[640,640]{1,0:T(8,128)(2,1)}, u32[]{:S(2)}, u32[]{:S(2)}) collective-permute-start(bf16[640,640]{1,0:T(8,128)(2,1)S(1)} %broadcast_select_fusion.refs_7_), channel_id=1, source_target_pairs={{0,16},{16,0},{1,17},{17,1},{2,18},{18,2},{3,19},{19,3},{4,20},{20... | collective-permute-start | bytes 2457608 | tf_op jit(solution)/shard_map/ppermute | solution.py:191
  149.1 5.3 %collective-permute-start.19 = (bf16[192,1280]{1,0:T(8,128)(2,1)}, bf16[192,1280]{1,0:T(8,128)(2,1)}, u32[]{:S(2)}, u32[]{:S(2)}) collective-permute-start(bf16[192,1280]{1,0:T(8,128)(2,1)} %collective-permute-done.17.refs_1_), channel_id=1, source_target_pairs={{0,1},{1,0},{2,3},{3,2},{4,5},{5,4},{6,7},{7,6},{8,9},{9,8},{10,11... | collective-permute-start | bytes 1474568 | tf_op jit(solution)/shard_map/ppermute | solution.py:188
  154.4 71.3 %collective-permute-start.15 = (bf16[192,640]{1,0:T(8,128)(2,1)}, bf16[192,640]{1,0:T(8,128)(2,1)S(1)}, u32[]{:S(2)}, u32[]{:S(2)}) collective-permute-start(bf16[192,640]{1,0:T(8,128)(2,1)} %get-tuple-element.26), channel_id=1, source_target_pairs={{0,1},{1,0},{2,3},{3,2},{4,5},{5,4},{6,7},{7,6},{8,9},{9,8},{10,11... | collective-permute-start | bytes 737288 | tf_op jit(solution)/shard_map/ppermute | solution.py:188
  160.2 66.2 %collective-permute-start.20 = (bf16[192,640]{1,0:T(8,128)(2,1)}, bf16[192,640]{1,0:T(8,128)(2,1)S(1)}, u32[]{:S(2)}, u32[]{:S(2)}) collective-permute-start(bf16[192,640]{1,0:T(8,128)(2,1)} %get-tuple-element.27), channel_id=1, source_target_pairs={{0,2},{1,3},{2,0},{3,1},{4,6},{5,7},{6,4},{7,5},{8,10},{9,11},{10,... | collective-permute-start | bytes 737288 | tf_op jit(solution)/shard_map/ppermute | solution.py:188
  177.7 48.7 %collective-permute-start.21 = (bf16[192,640]{1,0:T(8,128)(2,1)}, bf16[192,640]{1,0:T(8,128)(2,1)S(1)}, u32[]{:S(2)}, u32[]{:S(2)}) collective-permute-start(bf16[192,640]{1,0:T(8,128)(2,1)} %get-tuple-element.28), channel_id=1, source_target_pairs={{0,3},{1,2},{2,1},{3,0},{4,7},{5,6},{6,5},{7,4},{8,11},{9,10},{10,... | collective-permute-start | bytes 737288 | tf_op jit(solution)/shard_map/ppermute | solution.py:188
  218.1 8.3 %collective-permute-start.26 = (bf16[192,640]{1,0:T(8,128)(2,1)}, bf16[192,640]{1,0:T(8,128)(2,1)S(1)}, u32[]{:S(2)}, u32[]{:S(2)}) collective-permute-start(bf16[192,640]{1,0:T(8,128)(2,1)} %get-tuple-element.30), channel_id=1, source_target_pairs={{0,1},{1,0},{2,3},{3,2},{4,5},{5,4},{6,7},{7,6},{8,9},{9,8},{10,11... | collective-permute-start | bytes 737288 | tf_op jit(solution)/shard_map/ppermute | solution.py:188
  224.8 7.7 %collective-permute-start.27 = (bf16[192,640]{1,0:T(8,128)(2,1)}, bf16[192,640]{1,0:T(8,128)(2,1)S(1)}, u32[]{:S(2)}, u32[]{:S(2)}) collective-permute-start(bf16[192,640]{1,0:T(8,128)(2,1)} %get-tuple-element.31), channel_id=1, source_target_pairs={{0,2},{1,3},{2,0},{3,1},{4,6},{5,7},{6,4},{7,5},{8,10},{9,11},{10,... | collective-permute-start | bytes 737288 | tf_op jit(solution)/shard_map/ppermute | solution.py:188
  225.6 0.8 copy-start.10
  225.6 12.3 %collective-permute-start.28 = (bf16[192,640]{1,0:T(8,128)(2,1)}, bf16[192,640]{1,0:T(8,128)(2,1)S(1)}, u32[]{:S(2)}, u32[]{:S(2)}) collective-permute-start(bf16[192,640]{1,0:T(8,128)(2,1)} %get-tuple-element.32), channel_id=1, source_target_pairs={{0,3},{1,2},{2,1},{3,0},{4,7},{5,6},{6,5},{7,4},{8,11},{9,10},{10,... | collective-permute-start | bytes 737288 | tf_op jit(solution)/shard_map/ppermute | solution.py:188
  226.4 0.7 copy-start.11
  226.4 0.8 copy-start.12
  226.4 0.9 copy-start.13
  232.5 5.4 %copy-start.8 = (bf16[192,640]{1,0:T(8,128)(2,1)}, bf16[192,640]{1,0:T(8,128)(2,1)S(1)}, u32[]{:S(2)}) copy-start(bf16[192,640]{1,0:T(8,128)(2,1)S(1)} %collective-permute-done.27.refs_1_) | copy-start | bytes 737284
  237.9 0.7 copy-start.9

commit v6 on v5

--- a/solution.py
+++ b/solution.py
@@ -11,6 +11,9 @@
 HD = 128
 
 
+LIMIT = pltpu.CompilerParams(vmem_limit_bytes=16 * 1024 * 1024)
+
+
 def whole(count):
     return [pl.BlockSpec(memory_space=pltpu.VMEM)] * count
 
@@ -42,6 +45,7 @@
         out_shape=jax.ShapeDtypeStruct(x.shape, jnp.bfloat16),
         in_specs=whole(2),
         out_specs=pl.BlockSpec(memory_space=pltpu.VMEM),
+        compiler_params=LIMIT,
     )(x, gain.reshape(-1, HD))
 
 
@@ -52,6 +56,7 @@
         out_shape=[jax.ShapeDtypeStruct((rows, n * chans), jnp.bfloat16) for n in (2, 1)],
         in_specs=whole(3),
         out_specs=whole(2),
+        compiler_params=LIMIT,
     )(keys, values, gain.reshape(-1, HD))
 
 
@@ -103,6 +108,7 @@
         out_shape=jax.ShapeDtypeStruct((rows, wide), jnp.bfloat16),
         in_specs=[pl.BlockSpec(memory_space=pltpu.SMEM)] + [k_spec] * 4 + [v_spec] * 3 + [k_spec] * 2,
         out_specs=pl.BlockSpec((rows, cols), lambda i: (0, i)),
+        compiler_params=LIMIT,
     )(reach, qn, *pairs, *pairs, k_diag, v_diag)
 
 
@@ -140,6 +146,7 @@
         in_specs=whole(1 + len(att) + len(weights)),
         out_specs=whole(2),
         scratch_shapes=[pltpu.VMEM((2 * rows, wide * len(att) // 2), jnp.bfloat16)],
+        compiler_params=LIMIT,
     )(gate.reshape(-1, HD), *att, *weights)
 
 
@@ -169,6 +176,7 @@
         out_specs=anywhere,
         scratch_shapes=[pltpu.SemaphoreType.DMA((len(pieces),))],
         input_output_aliases={0: 0} if aliased else {},
+        compiler_params=LIMIT,
     )(*([] if base is None else [base]), *pieces)
 
 

time: 241 us -> 229 us (0.950)
  the two profiles are of different devices: /device:TPU:11 before, /device:TPU:15 now
where the time goes in v6:
time: 229 us
  waiting for transfers between devices  145 us (63%)
  starting transfers between devices  48.1 us (21%)
  Pallas kernels  25 us (11%)
  local copies, waits for them, and re-layouts  6.24 us (3%)
  other arithmetic  3.72 us (2%)
    ppermute x15, waiting for transfers between devices, swap(): return lax.ppermute(x, 'tm', [(i, i ^ bits) for i in range(peers)])  60.1 us
    ppermute x4, waiting for transfers between devices, group_swap(): return lax.ppermute(x, 'groups', [(0, 1), (1, 0)])  55.5 us
    ppermute x5, waiting for transfers between devices, along(): lax.ppermute(x, 'tm', [(4 * a + i, 4 * b + i) for a, b in moves for i in...  29.5 us
    ppermute x15, starting transfers between devices, swap(): return lax.ppermute(x, 'tm', [(i, i ^ bits) for i in range(peers)])  21.9 us
    ppermute x5, starting transfers between devices, send(): return lax.ppermute(x, 'tm', pairs)  13.1 us
    ppermute x5, starting transfers between devices, along(): lax.ppermute(x, 'tm', [(4 * a + i, 4 * b + i) for a, b in moves for i in...  10.9 us
    pallas_call x2, Pallas kernels, attend(): pl.pallas_call(attend_kernel, grid=(steps,), out_shape=jax.ShapeDtypeStru...  10.4 us
    pallas_call x4, Pallas kernels, project(): pl.pallas_call(functools.partial(project_kernel, share, len(att)), out_sh...  10.2 us
  transfers between devices with their start and end apart: 29, of which 12 were waited for; matrix products, arithmetic and copies ran while one was open for 2% of the time, Pallas kernels for 11%

profile of v6, /device:TPU:15, one launch (start us, length us, event | category | flops | bytes accessed | tf_op | source)
XLA Modules:
  0.0 228.6 jit_solution(6375894797333121109)
XLA Ops:
  0.0 2.1 constant_dynamic-slice_fusion
  2.1 0.7 collective-permute-start.9
  2.8 0.7 copy-done.11
  3.5 1.9 shard_map.83
  5.5 0.9 copy-done.14
  6.4 1.3 collective-permute-start
  7.7 4.3 %collective-permute-start.1 = (bf16[192,5120]{1,0:T(8,128)(2,1)S(1)}, bf16[192,5120]{1,0:T(8,128)(2,1)}, u32[]{:S(2)}, u32[]{:S(2)}) collective-permute-start(bf16[192,5120]{1,0:T(8,128)(2,1)S(1)} %get-tuple-element.19.k_ref.v_ref), channel_id=1, source_target_pairs={{1,0},{2,1},{3,2},{5,4},{6,5},{7,6},{9,8},{10,9},{11,10},{13,12},{... | collective-permute-start | bytes 5898248 | tf_op jit(solution)/shard_map/ppermute | solution.py:205
  12.0 3.2 %collective-permute-start.3 = (bf16[192,2560]{1,0:T(8,128)(2,1)}, bf16[192,2560]{1,0:T(8,128)(2,1)}, u32[]{:S(2)}, u32[]{:S(2)}) collective-permute-start(bf16[192,2560]{1,0:T(8,128)(2,1)} %v_ref.1), channel_id=1, source_target_pairs={{0,2},{3,1},{4,6},{7,5},{8,10},{11,9},{12,14},{15,13},{16,18},{19,... | collective-permute-start | bytes 2949128 | tf_op jit(solution)/shard_map/ppermute | solution.py:205
  15.2 1.3 collective-permute-start.7
  16.5 1.0 broadcast_select_fusion.5
  17.5 25.3 %collective-permute-done.7 = bf16[160,640]{1,0:T(8,128)(2,1)S(1)} collective-permute-done((bf16[160,640]{1,0:T(8,128)(2,1)}, bf16[160,640]{1,0:T(8,128)(2,1)S(1)}, u32[]{:S(2)}, u32[]{:S(2)}) %collective-permute-start.7) | collective-permute-done | bytes 204832 | tf_op jit(solution)/shard_map/ppermute | solution.py:196
  42.8 3.0 %collective-permute-start.2 = (bf16[192,2560]{1,0:T(8,128)(2,1)}, bf16[192,2560]{1,0:T(8,128)(2,1)S(1)}, u32[]{:S(2)}, u32[]{:S(2)}) collective-permute-start(bf16[192,2560]{1,0:T(8,128)(2,1)} %copy-done.14), channel_id=1, source_target_pairs={{3,4},{7,8},{11,12},{4,3},{8,7},{12,11},{19,20},{23,24},{27,28},{2... | collective-permute-start | bytes 2949128 | tf_op jit(solution)/shard_map/ppermute | solution.py:205
  45.9 15.6 %collective-permute-done.8 = bf16[160,640]{1,0:T(8,128)(2,1)S(1)} collective-permute-done((bf16[160,640]{1,0:T(8,128)(2,1)S(1)}, bf16[160,640]{1,0:T(8,128)(2,1)S(1)}, u32[]{:S(2)}, u32[]{:S(2)}) %collective-permute-start.8) | collective-permute-done | bytes 204832 | tf_op jit(solution)/shard_map/ppermute | solution.py:196
  62.1 3.1 %collective-permute-start.12 = (bf16[640,640]{1,0:T(8,128)(2,1)S(1)}, bf16[640,640]{1,0:T(8,128)(2,1)}, u32[]{:S(2)}, u32[]{:S(2)}) collective-permute-start(bf16[640,640]{1,0:T(8,128)(2,1)S(1)} %pad_maximum_fusion.refs_4_), channel_id=1, source_target_pairs={{4,8},{5,9},{6,10},{7,11},{8,4},{9,5},{10,6},{11,7},{20,24},{21,25... | collective-permute-start | bytes 2457608 | tf_op jit(solution)/shard_map/ppermute | solution.py:202
  65.1 1.3 collective-permute-start.4
  66.4 12.9 %collective-permute-done.10.refs_5_ = bf16[640,640]{1,0:T(8,128)(2,1)S(1)} collective-permute-done((bf16[640,640]{1,0:T(8,128)(2,1)S(1)}, bf16[640,640]{1,0:T(8,128)(2,1)S(1)}, u32[]{:S(2)}, u32[]{:S(2)}) %collective-permute-start.10) | collective-permute-done | bytes 819232 | tf_op jit(solution)/shard_map/ppermute | solution.py:202
  79.3 3.2 %collective-permute-start.11 = (bf16[640,640]{1,0:T(8,128)(2,1)S(1)}, bf16[640,640]{1,0:T(8,128)(2,1)}, u32[]{:S(2)}, u32[]{:S(2)}) collective-permute-start(bf16[640,640]{1,0:T(8,128)(2,1)S(1)} %collective-permute-done.10.refs_5_), channel_id=1, source_target_pairs={{4,8},{5,9},{6,10},{7,11},{8,4},{9,5},{10,6},{11,7},{20,24},{21,25... | collective-permute-start | bytes 2457608 | tf_op jit(solution)/shard_map/ppermute | solution.py:202
  82.6 2.2 collective-permute-start.13
  84.7 16.5 %collective-permute-done.11 = bf16[640,640]{1,0:T(8,128)(2,1)} collective-permute-done((bf16[640,640]{1,0:T(8,128)(2,1)S(1)}, bf16[640,640]{1,0:T(8,128)(2,1)}, u32[]{:S(2)}, u32[]{:S(2)}) %collective-permute-start.11) | collective-permute-done | bytes 819232 | tf_op jit(solution)/shard_map/ppermute | solution.py:202
  101.3 2.3 collective-permute-start.14
  103.6 0.5 shard_map.82.q_ref
  104.1 5.4 %shard_map.84.refs_0_ = bf16[192,1280]{1,0:T(8,128)(2,1)S(1)} custom-call(s32[1,2]{1,0:T(1,128)S(1)} %copy-done.13, bf16[192,2560]{1,0:T(8,128)(2,1)S(1)} %shard_map.82.q_ref, bf16[192,5120]{1,0:T(8,128)(2,1)} %collective-permute-done.kb_ref.vb_ref, bf16[192,5120]{1,0:T(8,128)(2,1)S(1)} %get-tuple-element.19.k_ref.v_ref, ...), custom_call_target="tpu_custom_call" | custom-call | tf_op jit(solution)/shard_map/pallas_call | solution.py:105
  109.5 13.9 %collective-permute-start.16 = (bf16[192,1280]{1,0:T(8,128)(2,1)S(1)}, bf16[192,1280]{1,0:T(8,128)(2,1)}, u32[]{:S(2)}, u32[]{:S(2)}) collective-permute-start(bf16[192,1280]{1,0:T(8,128)(2,1)S(1)} %shard_map.84.refs_0_), channel_id=1, source_target_pairs={{0,2},{1,3},{2,0},{3,1},{4,6},{5,7},{6,4},{7,5},{8,10},{9,11},{10,... | collective-permute-start | bytes 1474568 | tf_op jit(solution)/shard_map/ppermute | solution.py:196
  123.4 1.2 copy-done.3
  124.6 1.2 copy-done.5
  125.8 5.1 %shard_map.85.refs_1_ = bf16[192,1280]{1,0:T(8,128)(2,1)S(1)} custom-call(s32[1,2]{1,0:T(1,128)S(1)} %copy-done.13, bf16[192,2560]{1,0:T(8,128)(2,1)S(1)} %shard_map.82.q_ref, bf16[192,5120]{1,0:T(8,128)(2,1)} %collective-permute-done.kb_ref.vb_ref, bf16[192,5120]{1,0:T(8,128)(2,1)S(1)} %get-tuple-element.19.k_ref.v_ref, ...), custom_call_target="tpu_custom_call" | custom-call | tf_op jit(solution)/shard_map/pallas_call | solution.py:105
  130.9 0.6 collective-permute-start.6
  131.6 3.0 %collective-permute-done.16.refs_0_ = bf16[192,1280]{1,0:T(8,128)(2,1)} collective-permute-done((bf16[192,1280]{1,0:T(8,128)(2,1)S(1)}, bf16[192,1280]{1,0:T(8,128)(2,1)}, u32[]{:S(2)}, u32[]{:S(2)}) %collective-permute-start.16) | collective-permute-done | bytes 491552 | tf_op jit(solution)/shard_map/ppermute | solution.py:196
  134.8 1.2 broadcast_select_fusion.1.refs_6_
  136.4 1.2 broadcast_select_fusion.refs_7_
  137.7 1.3 collective-permute-start.23
  139.2 6.1 %collective-permute-done.17.refs_1_ = bf16[192,1280]{1,0:T(8,128)(2,1)S(1)} collective-permute-done((bf16[192,1280]{1,0:T(8,128)(2,1)S(1)}, bf16[192,1280]{1,0:T(8,128)(2,1)S(1)}, u32[]{:S(2)}, u32[]{:S(2)}) %collective-permute-start.17) | collective-permute-done | bytes 491552 | tf_op jit(solution)/shard_map/ppermute | solution.py:196
  145.5 0.7 collective-permute-start.19
  146.2 2.0 shard_map.86
  148.4 3.1 %shard_map.87 = (bf16[192,640]{1,0:T(8,128)(2,1)S(1)}, bf16[192,640]{1,0:T(8,128)(2,1)S(1)}) custom-call(f32[40,128]{1,0:T(8,128)S(1)} %bitcast.4, bf16[192,1280]{1,0:T(8,128)(2,1)} %collective-permute-done.16.refs_0_, bf16[192,1280]{1,0:T(8,128)(2,1)S(1)} %collective-permute-done.17.refs_1_, bf16[192,1280]{1,0:T(8,128)(2,1)S(1)} %collective-permute-done.18.refs_2_, ...), custom_call_target="tpu_custom_call" | custom-call | tf_op jit(solution)/shard_map/pallas_call | solution.py:143
  151.4 4.3 %collective-permute-done.22.refs_4_ = bf16[640,640]{1,0:T(8,128)(2,1)S(1)} collective-permute-done((bf16[640,640]{1,0:T(8,128)(2,1)S(1)}, bf16[640,640]{1,0:T(8,128)(2,1)S(1)}, u32[]{:S(2)}, u32[]{:S(2)}) %collective-permute-start.22) | collective-permute-done | bytes 819232 | tf_op jit(solution)/shard_map/ppermute | solution.py:199
  155.7 17.6 %collective-permute-done.23.refs_5_ = bf16[640,640]{1,0:T(8,128)(2,1)S(1)} collective-permute-done((bf16[640,640]{1,0:T(8,128)(2,1)S(1)}, bf16[640,640]{1,0:T(8,128)(2,1)S(1)}, u32[]{:S(2)}, u32[]{:S(2)}) %collective-permute-start.23) | collective-permute-done | bytes 819232 | tf_op jit(solution)/shard_map/ppermute | solution.py:199
  173.3 1.4 collective-permute-start.21
  174.7 16.1 %collective-permute-done.24.refs_6_ = bf16[640,640]{1,0:T(8,128)(2,1)S(1)} collective-permute-done((bf16[640,640]{1,0:T(8,128)(2,1)S(1)}, bf16[640,640]{1,0:T(8,128)(2,1)S(1)}, u32[]{:S(2)}, u32[]{:S(2)}) %collective-permute-start.24) | collective-permute-done | bytes 819232 | tf_op jit(solution)/shard_map/ppermute | solution.py:199
  190.8 17.6 %collective-permute-done.25.refs_7_ = bf16[640,640]{1,0:T(8,128)(2,1)S(1)} collective-permute-done((bf16[640,640]{1,0:T(8,128)(2,1)S(1)}, bf16[640,640]{1,0:T(8,128)(2,1)S(1)}, u32[]{:S(2)}, u32[]{:S(2)}) %collective-permute-start.25) | collective-permute-done | bytes 819232 | tf_op jit(solution)/shard_map/ppermute | solution.py:199
  208.4 2.0 shard_map.88
  210.4 1.2 collective-permute-start.26
  211.6 3.1 %shard_map.90 = (bf16[192,640]{1,0:T(8,128)(2,1)S(1)}, bf16[192,640]{1,0:T(8,128)(2,1)S(1)}) custom-call(f32[40,128]{1,0:T(8,128)S(1)} %bitcast.6, bf16[192,1280]{1,0:T(8,128)(2,1)} %collective-permute-done.16.refs_0_, bf16[192,1280]{1,0:T(8,128)(2,1)S(1)} %collective-permute-done.17.refs_1_, bf16[192,1280]{1,0:T(8,128)(2,1)S(1)} %collective-permute-done.18.refs_2_, ...), custom_call_target="tpu_custom_call" | custom-call | tf_op jit(solution)/shard_map/pallas_call | solution.py:143
  214.8 1.6 collective-permute-start.28
  216.4 1.2 shard_map.89.refs_0_
  217.6 4.7 %collective-permute-done.27.refs_1_ = bf16[192,640]{1,0:T(8,128)(2,1)S(1)} collective-permute-done((bf16[192,640]{1,0:T(8,128)(2,1)S(1)}, bf16[192,640]{1,0:T(8,128)(2,1)S(1)}, u32[]{:S(2)}, u32[]{:S(2)}) %collective-permute-start.27) | collective-permute-done | bytes 245792 | tf_op jit(solution)/shard_map/ppermute | solution.py:196
  222.2 5.5 %collective-permute-done.28.refs_2_ = bf16[192,640]{1,0:T(8,128)(2,1)S(1)} collective-permute-done((bf16[192,640]{1,0:T(8,128)(2,1)S(1)}, bf16[192,640]{1,0:T(8,128)(2,1)S(1)}, u32[]{:S(2)}, u32[]{:S(2)}) %collective-permute-start.28) | collective-permute-done | bytes 245792 | tf_op jit(solution)/shard_map/ppermute | solution.py:196
  227.7 0.8 shard_map.91
  (57 shorter events, 1.9 us)
Async XLA Ops:
  0.0 2.8 %copy-start.8 = (bf16[192,2560]{1,0:T(8,128)(2,1)S(1)}, bf16[192,2560]{1,0:T(8,128)(2,1)}, u32[]{:S(2)}) copy-start(bf16[192,2560]{1,0:T(8,128)(2,1)} %k_ref.1) | copy-start | bytes 2949124
  2.1 14.4 %collective-permute-start.9 = (bf16[160,640]{1,0:T(8,128)(2,1)}, bf16[160,640]{1,0:T(8,128)(2,1)}, u32[]{:S(2)}, u32[]{:S(2)}) collective-permute-start(bf16[160,640]{1,0:T(8,128)(2,1)} %get-tuple-element.23), channel_id=1, source_target_pairs={{0,1},{1,0},{2,3},{3,2},{4,5},{5,4},{6,7},{7,6},{8,9},{9,8},{10,11... | collective-permute-start | bytes 614408 | tf_op jit(solution)/shard_map/ppermute | solution.py:196
  2.8 0.7 copy-start.11
  5.5 0.9 copy-start.14
  6.4 97.6 %collective-permute-start = (bf16[192,5120]{1,0:T(8,128)(2,1)S(1)}, bf16[192,5120]{1,0:T(8,128)(2,1)}, u32[]{:S(2)}, u32[]{:S(2)}) collective-permute-start(bf16[192,5120]{1,0:T(8,128)(2,1)S(1)} %get-tuple-element.19.k_ref.v_ref), channel_id=1, source_target_pairs={{0,1},{1,2},{2,3},{4,5},{5,6},{6,7},{8,9},{9,10},{10,11},{12,13},{... | collective-permute-start | bytes 5898248 | tf_op jit(solution)/shard_map/ppermute | solution.py:205
  7.7 96.4 %collective-permute-start.1 = (bf16[192,5120]{1,0:T(8,128)(2,1)S(1)}, bf16[192,5120]{1,0:T(8,128)(2,1)}, u32[]{:S(2)}, u32[]{:S(2)}) collective-permute-start(bf16[192,5120]{1,0:T(8,128)(2,1)S(1)} %get-tuple-element.19.k_ref.v_ref), channel_id=1, source_target_pairs={{1,0},{2,1},{3,2},{5,4},{6,5},{7,6},{9,8},{10,9},{11,10},{13,12},{... | collective-permute-start | bytes 5898248 | tf_op jit(solution)/shard_map/ppermute | solution.py:205
  12.0 53.1 %collective-permute-start.3 = (bf16[192,2560]{1,0:T(8,128)(2,1)}, bf16[192,2560]{1,0:T(8,128)(2,1)}, u32[]{:S(2)}, u32[]{:S(2)}) collective-permute-start(bf16[192,2560]{1,0:T(8,128)(2,1)} %v_ref.1), channel_id=1, source_target_pairs={{0,2},{3,1},{4,6},{7,5},{8,10},{11,9},{12,14},{15,13},{16,18},{19,... | collective-permute-start | bytes 2949128 | tf_op jit(solution)/shard_map/ppermute | solution.py:205
  15.2 27.6 %collective-permute-start.7 = (bf16[160,640]{1,0:T(8,128)(2,1)}, bf16[160,640]{1,0:T(8,128)(2,1)S(1)}, u32[]{:S(2)}, u32[]{:S(2)}) collective-permute-start(bf16[160,640]{1,0:T(8,128)(2,1)} %get-tuple-element.21), channel_id=1, source_target_pairs={{0,3},{1,2},{2,1},{3,0},{4,7},{5,6},{6,5},{7,4},{8,11},{9,10},{10,... | collective-permute-start | bytes 614408 | tf_op jit(solution)/shard_map/ppermute | solution.py:196
  16.5 45.0 %collective-permute-start.8 = (bf16[160,640]{1,0:T(8,128)(2,1)S(1)}, bf16[160,640]{1,0:T(8,128)(2,1)S(1)}, u32[]{:S(2)}, u32[]{:S(2)}) collective-permute-start(bf16[160,640]{1,0:T(8,128)(2,1)S(1)} %get-tuple-element.22), channel_id=1, source_target_pairs={{0,2},{1,3},{2,0},{3,1},{4,6},{5,7},{6,4},{7,5},{8,10},{9,11},{10,... | collective-permute-start | bytes 614408 | tf_op jit(solution)/shard_map/ppermute | solution.py:196
  42.8 60.7 %copy-start.9 = (bf16[192,2560]{1,0:T(8,128)(2,1)S(1)}, bf16[192,2560]{1,0:T(8,128)(2,1)}, u32[]{:S(2)}) copy-start(bf16[192,2560]{1,0:T(8,128)(2,1)} %x_ref.1) | copy-start | bytes 2949124
  42.8 60.7 %copy-start.12 = (f32[2560]{0:T(1024)S(1)}, f32[2560]{0:T(1024)}, u32[]{:S(2)}) copy-start(f32[2560]{0:T(1024)} %param.11) | copy-start | bytes 30724
  42.8 19.2 %collective-permute-start.2 = (bf16[192,2560]{1,0:T(8,128)(2,1)}, bf16[192,2560]{1,0:T(8,128)(2,1)S(1)}, u32[]{:S(2)}, u32[]{:S(2)}) collective-permute-start(bf16[192,2560]{1,0:T(8,128)(2,1)} %copy-done.14), channel_id=1, source_target_pairs={{3,4},{7,8},{11,12},{4,3},{8,7},{12,11},{19,20},{23,24},{27,28},{2... | collective-permute-start | bytes 2949128 | tf_op jit(solution)/shard_map/ppermute | solution.py:205
  61.7 42.4 %copy-start.13 = (s32[1,2]{1,0:T(1,128)S(1)}, s32[1,2]{1,0:T(1,128)}, u32[]{:S(2)}) copy-start(s32[1,2]{1,0:T(1,128)} %reach_ref.3) | copy-start | bytes 28
  61.8 41.8 %copy-start = (bf16[640,640]{1,0:T(8,128)(2,1)}, bf16[640,640]{1,0:T(8,128)(2,1)S(1)}, u32[]{:S(2)}) copy-start(bf16[640,640]{1,0:T(8,128)(2,1)S(1)} %pad_maximum_fusion.refs_4_) | copy-start | bytes 2457604
  61.8 17.5 %collective-permute-start.10 = (bf16[640,640]{1,0:T(8,128)(2,1)S(1)}, bf16[640,640]{1,0:T(8,128)(2,1)S(1)}, u32[]{:S(2)}, u32[]{:S(2)}) collective-permute-start(bf16[640,640]{1,0:T(8,128)(2,1)S(1)} %pad_maximum_fusion.refs_4_), channel_id=1, source_target_pairs={{0,4},{1,5},{2,6},{3,7},{4,0},{5,1},{6,2},{7,3},{8,12},{9,13},{10,... | collective-permute-start | bytes 2457608 | tf_op jit(solution)/shard_map/ppermute | solution.py:202
  62.1 47.4 %copy-start.2 = (bf16[192,2560]{1,0:T(8,128)(2,1)}, bf16[192,2560]{1,0:T(8,128)(2,1)S(1)}, u32[]{:S(2)}) copy-start(bf16[192,2560]{1,0:T(8,128)(2,1)S(1)} %collective-permute-done.2.kd_ref) | copy-start | bytes 2949124
  62.1 20.5 %collective-permute-start.12 = (bf16[640,640]{1,0:T(8,128)(2,1)S(1)}, bf16[640,640]{1,0:T(8,128)(2,1)}, u32[]{:S(2)}, u32[]{:S(2)}) collective-permute-start(bf16[640,640]{1,0:T(8,128)(2,1)S(1)} %pad_maximum_fusion.refs_4_), channel_id=1, source_target_pairs={{4,8},{5,9},{6,10},{7,11},{8,4},{9,5},{10,6},{11,7},{20,24},{21,25... | collective-permute-start | bytes 2457608 | tf_op jit(solution)/shard_map/ppermute | solution.py:202
  65.1 38.9 %collective-permute-start.4 = (bf16[192,2560]{1,0:T(8,128)(2,1)}, bf16[192,2560]{1,0:T(8,128)(2,1)S(1)}, u32[]{:S(2)}, u32[]{:S(2)}) collective-permute-start(bf16[192,2560]{1,0:T(8,128)(2,1)} %collective-permute-done.3), channel_id=1, source_target_pairs={{1,4},{5,8},{9,12},{6,3},{10,7},{14,11},{17,20},{21,24},{25,28},{2... | collective-permute-start | bytes 2949128 | tf_op jit(solution)/shard_map/ppermute | solution.py:205
  79.3 24.2 %copy-start.6 = (bf16[640,640]{1,0:T(8,128)(2,1)}, bf16[640,640]{1,0:T(8,128)(2,1)S(1)}, u32[]{:S(2)}) copy-start(bf16[640,640]{1,0:T(8,128)(2,1)S(1)} %collective-permute-done.10.refs_5_) | copy-start | bytes 2457604
  79.3 22.0 %collective-permute-start.11 = (bf16[640,640]{1,0:T(8,128)(2,1)S(1)}, bf16[640,640]{1,0:T(8,128)(2,1)}, u32[]{:S(2)}, u32[]{:S(2)}) collective-permute-start(bf16[640,640]{1,0:T(8,128)(2,1)S(1)} %collective-permute-done.10.refs_5_), channel_id=1, source_target_pairs={{4,8},{5,9},{6,10},{7,11},{8,4},{9,5},{10,6},{11,7},{20,24},{21,25... | collective-permute-start | bytes 2457608 | tf_op jit(solution)/shard_map/ppermute | solution.py:202
  82.6 49.0 %collective-permute-start.13 = (bf16[640,640]{1,0:T(8,128)(2,1)}, bf16[640,640]{1,0:T(8,128)(2,1)}, u32[]{:S(2)}, u32[]{:S(2)}) collective-permute-start(bf16[640,640]{1,0:T(8,128)(2,1)} %collective-permute-done.12), channel_id=1, source_target_pairs={{4,0},{5,1},{6,2},{7,3},{8,12},{9,13},{10,14},{11,15},{20,16},{21,... | collective-permute-start | bytes 2457608 | tf_op jit(solution)/shard_map/ppermute | solution.py:202
  101.3 34.8 %collective-permute-start.14 = (bf16[640,640]{1,0:T(8,128)(2,1)}, bf16[640,640]{1,0:T(8,128)(2,1)}, u32[]{:S(2)}, u32[]{:S(2)}) collective-permute-start(bf16[640,640]{1,0:T(8,128)(2,1)} %collective-permute-done.11), channel_id=1, source_target_pairs={{4,0},{5,1},{6,2},{7,3},{8,12},{9,13},{10,14},{11,15},{20,16},{21,... | collective-permute-start | bytes 2457608 | tf_op jit(solution)/shard_map/ppermute | solution.py:202
  104.1 5.4 %copy-start.4 = (bf16[192,2560]{1,0:T(8,128)(2,1)}, bf16[192,2560]{1,0:T(8,128)(2,1)S(1)}, u32[]{:S(2)}) copy-start(bf16[192,2560]{1,0:T(8,128)(2,1)S(1)} %collective-permute-done.4.vd_ref) | copy-start | bytes 2949124
  109.5 25.1 %collective-permute-start.16 = (bf16[192,1280]{1,0:T(8,128)(2,1)S(1)}, bf16[192,1280]{1,0:T(8,128)(2,1)}, u32[]{:S(2)}, u32[]{:S(2)}) collective-permute-start(bf16[192,1280]{1,0:T(8,128)(2,1)S(1)} %shard_map.84.refs_0_), channel_id=1, source_target_pairs={{0,2},{1,3},{2,0},{3,1},{4,6},{5,7},{6,4},{7,5},{8,10},{9,11},{10,... | collective-permute-start | bytes 1474568 | tf_op jit(solution)/shard_map/ppermute | solution.py:196
  123.4 14.2 %collective-permute-start.5 = (bf16[192,1280]{1,0:T(8,128)(2,1)S(1)}, bf16[192,1280]{1,0:T(8,128)(2,1)S(1)}, u32[]{:S(2)}, u32[]{:S(2)}) collective-permute-start(bf16[192,1280]{1,0:T(8,128)(2,1)S(1)} %shard_map.84.refs_0_), channel_id=1, source_target_pairs={{0,1},{1,0},{2,3},{3,2},{4,5},{5,4},{6,7},{7,6},{8,9},{9,8},{10,11... | collective-permute-start | bytes 1474568 | tf_op jit(solution)/shard_map/ppermute | solution.py:196
  123.4 1.2 copy-start.3
  124.6 1.2 copy-start.5
  130.9 5.2 %copy-start.1 = (bf16[640,640]{1,0:T(8,128)(2,1)S(1)}, bf16[640,640]{1,0:T(8,128)(2,1)}, u32[]{:S(2)}) copy-start(bf16[640,640]{1,0:T(8,128)(2,1)} %copy-done) | copy-start | bytes 2457604
  130.9 6.7 %copy-start.7 = (bf16[640,640]{1,0:T(8,128)(2,1)S(1)}, bf16[640,640]{1,0:T(8,128)(2,1)}, u32[]{:S(2)}) copy-start(bf16[640,640]{1,0:T(8,128)(2,1)} %copy-done.6) | copy-start | bytes 2457604
  130.9 15.3 %copy-start.10 = (f32[5120]{0:T(1024)S(1)}, f32[5120]{0:T(1024)}, u32[]{:S(2)}) copy-start(f32[5120]{0:T(1024)} %param.14) | copy-start | bytes 61444
  130.9 8.0 %collective-permute-start.6 = (bf16[192,1280]{1,0:T(8,128)(2,1)S(1)}, bf16[192,1280]{1,0:T(8,128)(2,1)S(1)}, u32[]{:S(2)}, u32[]{:S(2)}) collective-permute-start(bf16[192,1280]{1,0:T(8,128)(2,1)S(1)} %shard_map.85.refs_1_), channel_id=1, source_target_pairs={{0,1},{1,0},{2,3},{3,2},{4,5},{5,4},{6,7},{7,6},{8,9},{9,8},{10,11... | collective-permute-start | bytes 1474568 | tf_op jit(solution)/shard_map/ppermute | solution.py:196
  131.5 13.8 %collective-permute-start.17 = (bf16[192,1280]{1,0:T(8,128)(2,1)S(1)}, bf16[192,1280]{1,0:T(8,128)(2,1)S(1)}, u32[]{:S(2)}, u32[]{:S(2)}) collective-permute-start(bf16[192,1280]{1,0:T(8,128)(2,1)S(1)} %shard_map.85.refs_1_), channel_id=1, source_target_pairs={{0,2},{1,3},{2,0},{3,1},{4,6},{5,7},{6,4},{7,5},{8,10},{9,11},{10,... | collective-permute-start | bytes 1474568 | tf_op jit(solution)/shard_map/ppermute | solution.py:196
  134.6 11.0 %collective-permute-start.18 = (bf16[192,1280]{1,0:T(8,128)(2,1)}, bf16[192,1280]{1,0:T(8,128)(2,1)S(1)}, u32[]{:S(2)}, u32[]{:S(2)}) collective-permute-start(bf16[192,1280]{1,0:T(8,128)(2,1)} %collective-permute-done.16.refs_0_), channel_id=1, source_target_pairs={{0,1},{1,0},{2,3},{3,2},{4,5},{5,4},{6,7},{7,6},{8,9},{9,8},{10,11... | collective-permute-start | bytes 1474568 | tf_op jit(solution)/shard_map/ppermute | solution.py:196
  136.1 19.6 %collective-permute-start.22 = (bf16[640,640]{1,0:T(8,128)(2,1)S(1)}, bf16[640,640]{1,0:T(8,128)(2,1)S(1)}, u32[]{:S(2)}, u32[]{:S(2)}) collective-permute-start(bf16[640,640]{1,0:T(8,128)(2,1)S(1)} %copy-done.1), channel_id=1, source_target_pairs={{0,16},{16,0},{1,17},{17,1},{2,18},{18,2},{3,19},{19,3},{4,20},{20... | collective-permute-start | bytes 2457608 | tf_op jit(solution)/shard_map/ppermute | solution.py:199
  137.7 35.6 %collective-permute-start.23 = (bf16[640,640]{1,0:T(8,128)(2,1)S(1)}, bf16[640,640]{1,0:T(8,128)(2,1)S(1)}, u32[]{:S(2)}, u32[]{:S(2)}) collective-permute-start(bf16[640,640]{1,0:T(8,128)(2,1)S(1)} %copy-done.7), channel_id=1, source_target_pairs={{0,16},{16,0},{1,17},{17,1},{2,18},{18,2},{3,19},{19,3},{4,20},{20... | collective-permute-start | bytes 2457608 | tf_op jit(solution)/shard_map/ppermute | solution.py:199
  139.0 51.9 %collective-permute-start.24 = (bf16[640,640]{1,0:T(8,128)(2,1)S(1)}, bf16[640,640]{1,0:T(8,128)(2,1)S(1)}, u32[]{:S(2)}, u32[]{:S(2)}) collective-permute-start(bf16[640,640]{1,0:T(8,128)(2,1)S(1)} %broadcast_select_fusion.1.refs_6_), channel_id=1, source_target_pairs={{0,16},{16,0},{1,17},{17,1},{2,18},{18,2},{3,19},{19,3},{4,20},{20... | collective-permute-start | bytes 2457608 | tf_op jit(solution)/shard_map/ppermute | solution.py:199
  145.3 63.1 %collective-permute-start.25 = (bf16[640,640]{1,0:T(8,128)(2,1)S(1)}, bf16[640,640]{1,0:T(8,128)(2,1)S(1)}, u32[]{:S(2)}, u32[]{:S(2)}) collective-permute-start(bf16[640,640]{1,0:T(8,128)(2,1)S(1)} %broadcast_select_fusion.refs_7_), channel_id=1, source_target_pairs={{0,16},{16,0},{1,17},{17,1},{2,18},{18,2},{3,19},{19,3},{4,20},{20... | collective-permute-start | bytes 2457608 | tf_op jit(solution)/shard_map/ppermute | solution.py:199
  145.5 2.7 %collective-permute-start.19 = (bf16[192,1280]{1,0:T(8,128)(2,1)S(1)}, bf16[192,1280]{1,0:T(8,128)(2,1)S(1)}, u32[]{:S(2)}, u32[]{:S(2)}) collective-permute-start(bf16[192,1280]{1,0:T(8,128)(2,1)S(1)} %collective-permute-done.17.refs_1_), channel_id=1, source_target_pairs={{0,1},{1,0},{2,3},{3,2},{4,5},{5,4},{6,7},{7,6},{8,9},{9,8},{10,11... | collective-permute-start | bytes 1474568 | tf_op jit(solution)/shard_map/ppermute | solution.py:196
  148.3 66.5 %collective-permute-start.15 = (bf16[192,640]{1,0:T(8,128)(2,1)S(1)}, bf16[192,640]{1,0:T(8,128)(2,1)S(1)}, u32[]{:S(2)}, u32[]{:S(2)}) collective-permute-start(bf16[192,640]{1,0:T(8,128)(2,1)S(1)} %get-tuple-element.26), channel_id=1, source_target_pairs={{0,1},{1,0},{2,3},{3,2},{4,5},{5,4},{6,7},{7,6},{8,9},{9,8},{10,11... | collective-permute-start | bytes 737288 | tf_op jit(solution)/shard_map/ppermute | solution.py:196
  155.7 60.7 %collective-permute-start.20 = (bf16[192,640]{1,0:T(8,128)(2,1)S(1)}, bf16[192,640]{1,0:T(8,128)(2,1)S(1)}, u32[]{:S(2)}, u32[]{:S(2)}) collective-permute-start(bf16[192,640]{1,0:T(8,128)(2,1)S(1)} %get-tuple-element.27), channel_id=1, source_target_pairs={{0,2},{1,3},{2,0},{3,1},{4,6},{5,7},{6,4},{7,5},{8,10},{9,11},{10,... | collective-permute-start | bytes 737288 | tf_op jit(solution)/shard_map/ppermute | solution.py:196
  173.3 43.1 %collective-permute-start.21 = (bf16[192,640]{1,0:T(8,128)(2,1)S(1)}, bf16[192,640]{1,0:T(8,128)(2,1)S(1)}, u32[]{:S(2)}, u32[]{:S(2)}) collective-permute-start(bf16[192,640]{1,0:T(8,128)(2,1)S(1)} %get-tuple-element.28), channel_id=1, source_target_pairs={{0,3},{1,2},{2,1},{3,0},{4,7},{5,6},{6,5},{7,4},{8,11},{9,10},{10,... | collective-permute-start | bytes 737288 | tf_op jit(solution)/shard_map/ppermute | solution.py:196
  210.4 6.0 %collective-permute-start.26 = (bf16[192,640]{1,0:T(8,128)(2,1)S(1)}, bf16[192,640]{1,0:T(8,128)(2,1)S(1)}, u32[]{:S(2)}, u32[]{:S(2)}) collective-permute-start(bf16[192,640]{1,0:T(8,128)(2,1)S(1)} %get-tuple-element.30), channel_id=1, source_target_pairs={{0,1},{1,0},{2,3},{3,2},{4,5},{5,4},{6,7},{7,6},{8,9},{9,8},{10,11... | collective-permute-start | bytes 737288 | tf_op jit(solution)/shard_map/ppermute | solution.py:196
  214.7 7.6 %collective-permute-start.27 = (bf16[192,640]{1,0:T(8,128)(2,1)S(1)}, bf16[192,640]{1,0:T(8,128)(2,1)S(1)}, u32[]{:S(2)}, u32[]{:S(2)}) collective-permute-start(bf16[192,640]{1,0:T(8,128)(2,1)S(1)} %get-tuple-element.31), channel_id=1, source_target_pairs={{0,2},{1,3},{2,0},{3,1},{4,6},{5,7},{6,4},{7,5},{8,10},{9,11},{10,... | collective-permute-start | bytes 737288 | tf_op jit(solution)/shard_map/ppermute | solution.py:196
  214.8 12.9 %collective-permute-start.28 = (bf16[192,640]{1,0:T(8,128)(2,1)S(1)}, bf16[192,640]{1,0:T(8,128)(2,1)S(1)}, u32[]{:S(2)}, u32[]{:S(2)}) collective-permute-start(bf16[192,640]{1,0:T(8,128)(2,1)S(1)} %get-tuple-element.32), channel_id=1, source_target_pairs={{0,3},{1,2},{2,1},{3,0},{4,7},{5,6},{6,5},{7,4},{8,11},{9,10},{10,... | collective-permute-start | bytes 737288 | tf_op jit(solution)/shard_map/ppermute | solution.py:196

commit v7 on v6

--- a/solution.py
+++ b/solution.py
@@ -31,11 +31,10 @@
         out_ref[:, i * HD : (i + 1) * HD] = piece
 
 
-def pair_kernel(k_ref, v_ref, gain_ref, out_ref, kn_ref):
+def pair_kernel(k_ref, v_ref, gain_ref, out_ref):
     chans = k_ref.shape[1]
     for i, piece in scaled_heads(k_ref, gain_ref):
         out_ref[:, i * HD : (i + 1) * HD] = piece
-        kn_ref[:, i * HD : (i + 1) * HD] = piece
     out_ref[:, chans:] = v_ref[...]
 
 
@@ -53,14 +52,14 @@
     rows, chans = keys.shape
     return pl.pallas_call(
         pair_kernel,
-        out_shape=[jax.ShapeDtypeStruct((rows, n * chans), jnp.bfloat16) for n in (2, 1)],
+        out_shape=jax.ShapeDtypeStruct((rows, 2 * chans), jnp.bfloat16),
         in_specs=whole(3),
-        out_specs=whole(2),
+        out_specs=pl.BlockSpec(memory_space=pltpu.VMEM),
         compiler_params=LIMIT,
     )(keys, values, gain.reshape(-1, HD))
 
 
-def attend_kernel(reach_ref, q_ref, kb_ref, k_ref, ka_ref, vb_ref, v_ref, va_ref, kd_ref, vd_ref, o_ref):
+def attend_kernel(reach_ref, q_ref, kb_ref, k_ref, ka_ref, kd_ref, vb_ref, v_ref, va_ref, vd_ref, o_ref):
     scale = HD ** (-0.5)
     place = lax.axis_index("tm")
     peers = lax.axis_size("tm")
@@ -93,7 +92,7 @@
         o_ref[:, at] = out.astype(jnp.bfloat16)
 
 
-def attend(reach, qn, pairs, k_diag, v_diag, chunk, chunks):
+def attend(reach, qn, pairs, chunk, chunks):
     rows, chans = qn.shape
     wide = chans // chunks
     heads = wide // HD
@@ -106,16 +105,18 @@
         attend_kernel,
         grid=(steps,),
         out_shape=jax.ShapeDtypeStruct((rows, wide), jnp.bfloat16),
-        in_specs=[pl.BlockSpec(memory_space=pltpu.SMEM)] + [k_spec] * 4 + [v_spec] * 3 + [k_spec] * 2,
+        in_specs=[pl.BlockSpec(memory_space=pltpu.SMEM)] + [k_spec] * 5 + [v_spec] * 4,
         out_specs=pl.BlockSpec((rows, cols), lambda i: (0, i)),
         compiler_params=LIMIT,
-    )(reach, qn, *pairs, *pairs, k_diag, v_diag)
-
-
-def project_kernel(share, count, gate_ref, *refs):
-    slots = len(refs) - count - 3
-    att_refs, w_refs, outs = refs[:count], refs[count : count + slots], refs[-3:-1]
-    a_ref = refs[-1]
+    )(reach, qn, *pairs, *pairs)
+
+
+def project_kernel(share, count, slots, total, final, resumed, gate_ref, *refs):
+    refs = list(refs)
+    a_ref = refs.pop()
+    base_ref = refs.pop(0) if resumed else None
+    att_refs, w_refs = refs[:count], refs[count : count + len(slots)]
+    outs = refs[count + len(slots) :]
     rows, wide = att_refs[0].shape
     depth, cols = w_refs[0].shape
     chunks = count // 2
@@ -124,11 +125,14 @@
     for i, ref in enumerate(att_refs):
         p, j = i // chunks, i % chunks
         a_ref[p * rows : (p + 1) * rows, j * wide : (j + 1) * wide] = ref[...]
-    acc = None
-    for i, ref in enumerate(w_refs):
-        start = pl.multiple_of((line ^ i) * depth, HD) if slots > 1 else 0
+    acc = base_ref[...] if resumed else None
+    for i, ref in zip(slots, w_refs):
+        start = pl.multiple_of((line ^ i) * depth, HD) if total > 1 else 0
         term = jnp.dot(a_ref[:, pl.ds(start, depth)], ref[...], preferred_element_type=jnp.float32)
         acc = term if acc is None else acc + term
+    if not final:
+        outs[0][...] = acc
+        return
     first = ((place % 4) * 2 + (lax.axis_index("groups") ^ share)) * (cols // HD)
     for p in range(2):
         for b in range(cols // HD):
@@ -137,17 +141,24 @@
             outs[p][:, at] = scaled.astype(jnp.bfloat16)
 
 
-def project(gate, att, weights, share):
+def project(gate, att, weights, share, slots, final=True, base=None):
     rows, wide = att[0].shape
     cols = weights[0].shape[1]
-    return pl.pallas_call(
-        functools.partial(project_kernel, share, len(att)),
-        out_shape=[jax.ShapeDtypeStruct((rows, cols), jnp.bfloat16)] * 2,
-        in_specs=whole(1 + len(att) + len(weights)),
-        out_specs=whole(2),
+    used = [weights[i] for i in slots]
+    resumed = [] if base is None else [base]
+    if final:
+        out = [jax.ShapeDtypeStruct((rows, cols), jnp.bfloat16)] * 2
+    else:
+        out = [jax.ShapeDtypeStruct((2 * rows, cols), jnp.float32)]
+    body = functools.partial(project_kernel, share, len(att), slots, len(weights), final, bool(resumed))
+    return pl.pallas_call(
+        body,
+        out_shape=out,
+        in_specs=whole(1 + len(resumed) + len(att) + len(used)),
+        out_specs=whole(len(out)),
         scratch_shapes=[pltpu.VMEM((2 * rows, wide * len(att) // 2), jnp.bfloat16)],
         compiler_params=LIMIT,
-    )(gate.reshape(-1, HD), *att, *weights)
+    )(gate.reshape(-1, HD), *resumed, *att, *used)
 
 
 def place_kernel(spots, aliased, *refs):
@@ -210,9 +221,6 @@
     def inside(pairs):
         return [(i, j) for i, j in pairs if i // 4 == j // 4]
 
-    def outside(pairs):
-        return [(i, j) for i, j in pairs if i // 4 != j // 4]
-
     def choose(flag, a, b):
         return jnp.where(flag, a, b)
 
@@ -231,12 +239,12 @@
     ]
     block = jnp.concatenate([choose(upper, halves[1], halves[0]), choose(upper, halves[0], halves[1])], axis=0)
 
-    kv, kn = pair(keys, values, k_gain)
+    leap = [(4 * z + 3, 4 * z + 7) for z in range(lines - 1)] + [(4 * z + 4, 4 * z) for z in range(lines - 1)]
+    turn = [(4 * z + i, 4 * z + (i ^ 3)) for z in range(lines) for i in (0, 3)]
+    k_leap, v_leap = send(keys, leap), send(values, leap)
+    kv = pair(keys, values, k_gain)
     near = [send(kv, inside(up)), kv, send(kv, inside(down))]
-    k_diag = send(kn, outside(up) + outside(down))
-    turn = [(4 * z + i, 4 * z + (i ^ 2)) for z in range(lines) for i in (0, 3)]
-    leap = [(i ^ 2, j) for i, j in outside(up) + outside(down)]
-    v_diag = send(send(values, turn), leap)
+    near.append(send(pair(k_leap, v_leap, k_gain), turn))
     qn = norm(queries, q_gain)
 
     if lines == 4:
@@ -256,17 +264,22 @@
 
     here, there = [], []
     for i in range(chunks):
-        own = attend(reach, qn, near, k_diag, v_diag, i, chunks)
+        own = attend(reach, qn, near, i, chunks)
         over = swap(own, 2)
         here.append([own, swap(own, 1)])
         there.append([over, swap(over, 1)])
     here = [pair[p] for p in range(2) for pair in here]
     there = [pair[p] for p in range(2) for pair in there]
     pieces = {}
+    every = tuple(range(len(slots)))
     for j in range(2):
-        made = project(out_gate, here, shares[j], j)
+        made = project(out_gate, here, shares[j], j, every)
         pieces[0, j], pieces[1, j] = made[0], swap(made[1], 1)
-        made = project(out_gate, there, shares[j], j)
+        base, rest = None, every
+        if j == 1 and len(every) > 1:
+            base = project(out_gate, there, shares[j], j, every[:-1], final=False)[0]
+            rest = every[-1:]
+        made = project(out_gate, there, shares[j], j, rest, base=base)
         pieces[2, j], pieces[3, j] = swap(made[0], 2), swap(made[1], 3)
     last = [(2, 1), (3, 1)]
     most = [spot for spot in pieces if spot not in last]

time: 229 us -> 198 us (0.86)
  the two profiles are of different devices: /device:TPU:15 before, /device:TPU:21 now
where the time goes in v7:
time: 198 us; the launch traced here: 197 us
  waiting for transfers between devices  114 us (58%)
  starting transfers between devices  42.7 us (22%)
  Pallas kernels  29.8 us (15%)
  local copies, waits for them, and re-layouts  5.27 us (3%)
  other arithmetic  4.7 us (2%)
    ppermute x15, waiting for transfers between devices, swap(): return lax.ppermute(x, 'tm', [(i, i ^ bits) for i in range(peers)])  54 us
    ppermute x5, waiting for transfers between devices, along(): lax.ppermute(x, 'tm', [(4 * a + i, 4 * b + i) for a, b in moves for i in...  33.8 us
    ppermute x4, waiting for transfers between devices, group_swap(): return lax.ppermute(x, 'groups', [(0, 1), (1, 0)])  26.4 us
    ppermute x15, starting transfers between devices, swap(): return lax.ppermute(x, 'tm', [(i, i ^ bits) for i in range(peers)])  19 us
    pallas_call x5, Pallas kernels, project(): pl.pallas_call(body, out_shape=out, in_specs=whole(1 + len(resumed) + len...  13 us
    ppermute x5, starting transfers between devices, send(): return lax.ppermute(x, 'tm', pairs)  11 us
    pallas_call x2, Pallas kernels, attend(): pl.pallas_call(attend_kernel, grid=(steps,), out_shape=jax.ShapeDtypeStru...  10.5 us
    ppermute x5, starting transfers between devices, along(): lax.ppermute(x, 'tm', [(4 * a + i, 4 * b + i) for a, b in moves for i in...  9.65 us
  transfers between devices with their start and end apart: 29, of which 15 were waited for; matrix products, arithmetic and copies ran while one was open for 2% of the time, Pallas kernels for 15%

profile of v7, /device:TPU:21, one launch (start us, length us, event | category | flops | bytes accessed | tf_op | source)
XLA Modules:
  0.0 197.3 jit_solution(6028732373274251655)
XLA Ops:
  0.0 2.1 %constant_dynamic-slice_fusion = (bf16[160,640]{1,0:T(8,128)(2,1)}, bf16[160,640]{1,0:T(8,128)(2,1)}, bf16[160,640]{1,0:T(8,128)(2,1)S(1)}, bf16[160,640]{1,0:T(8,128)(2,1)S(1)}) fusion(bf16[160,5120]{1,0:T(8,128)(2,1)} %param.13, s32[]{:T(128)S(6)} %select_n.78, s32[]{:T(128)S(6)} %select_n.76, s32[]{:T(128)S(6)} %select_n.75, s32[]{:T(128)S(6)} %select_n.77), kind=kLoop, calls=%fused_computation.11 | loop fusion | bytes 1638416 | tf_op jit(solution)/shard_map/dynamic_slice | solution.py:231
  2.8 3.2 %collective-permute-start.2 = (bf16[192,2560]{1,0:T(8,128)(2,1)}, bf16[192,2560]{1,0:T(8,128)(2,1)}, u32[]{:S(2)}, u32[]{:S(2)}) collective-permute-start(bf16[192,2560]{1,0:T(8,128)(2,1)} %k_ref.1), channel_id=1, source_target_pairs={{3,7},{7,11},{11,15},{4,0},{8,4},{12,8},{19,23},{23,27},{27,31},{2... | collective-permute-start | bytes 2949128 | tf_op jit(solution)/shard_map/ppermute | solution.py:216
  6.0 1.9 collective-permute-start.3
  8.0 1.2 copy-done.3
  10.5 1.3 collective-permute-start
  12.4 1.9 collective-permute-start.8
  14.3 1.0 broadcast_select_fusion.5
  15.3 4.5 %collective-permute-done.7 = bf16[160,640]{1,0:T(8,128)(2,1)S(1)} collective-permute-done((bf16[160,640]{1,0:T(8,128)(2,1)}, bf16[160,640]{1,0:T(8,128)(2,1)S(1)}, u32[]{:S(2)}, u32[]{:S(2)}) %collective-permute-start.7) | collective-permute-done | bytes 204832 | tf_op jit(solution)/shard_map/ppermute | solution.py:207
  19.8 22.8 %collective-permute-done.8 = bf16[160,640]{1,0:T(8,128)(2,1)S(1)} collective-permute-done((bf16[160,640]{1,0:T(8,128)(2,1)S(1)}, bf16[160,640]{1,0:T(8,128)(2,1)S(1)}, u32[]{:S(2)}, u32[]{:S(2)}) %collective-permute-start.8) | collective-permute-done | bytes 204832 | tf_op jit(solution)/shard_map/ppermute | solution.py:207
  42.8 1.0 pad_maximum_fusion.refs_4_
  43.8 1.3 collective-permute-start.10
  45.1 2.5 %collective-permute-start.1 = (bf16[192,5120]{1,0:T(8,128)(2,1)S(1)}, bf16[192,5120]{1,0:T(8,128)(2,1)}, u32[]{:S(2)}, u32[]{:S(2)}) collective-permute-start(bf16[192,5120]{1,0:T(8,128)(2,1)S(1)} %shard_map.83.k_ref.v_ref), channel_id=1, source_target_pairs={{1,0},{2,1},{3,2},{5,4},{6,5},{7,6},{9,8},{10,9},{11,10},{13,12},{... | collective-permute-start | bytes 5898248 | tf_op jit(solution)/shard_map/ppermute | solution.py:216
  47.7 3.4 %shard_map.84 = bf16[192,5120]{1,0:T(8,128)(2,1)} custom-call(bf16[192,2560]{1,0:T(8,128)(2,1)} %collective-permute-done.2.k_ref, bf16[192,2560]{1,0:T(8,128)(2,1)} %collective-permute-done.3.v_ref, f32[20,128]{1,0:T(8,128)S(1)} %bitcast.9), custom_call_target="tpu_custom_call" | custom-call | tf_op jit(solution)/shard_map/pallas_call | solution.py:53
  51.0 2.0 %collective-permute-start.4 = (bf16[192,5120]{1,0:T(8,128)(2,1)}, bf16[192,5120]{1,0:T(8,128)(2,1)}, u32[]{:S(2)}, u32[]{:S(2)}) collective-permute-start(bf16[192,5120]{1,0:T(8,128)(2,1)} %shard_map.84), channel_id=1, source_target_pairs={{0,3},{3,0},{4,7},{7,4},{8,11},{11,8},{12,15},{15,12},{16,19},{19,... | collective-permute-start | bytes 5898248 | tf_op jit(solution)/shard_map/ppermute | solution.py:216
  53.1 1.9 collective-permute-start.12
  55.0 8.3 %collective-permute-done.10.refs_5_ = bf16[640,640]{1,0:T(8,128)(2,1)S(1)} collective-permute-done((bf16[640,640]{1,0:T(8,128)(2,1)}, bf16[640,640]{1,0:T(8,128)(2,1)S(1)}, u32[]{:S(2)}, u32[]{:S(2)}) %collective-permute-start.10) | collective-permute-done | bytes 819232 | tf_op jit(solution)/shard_map/ppermute | solution.py:213
  63.4 2.1 %collective-permute-start.11 = (bf16[640,640]{1,0:T(8,128)(2,1)S(1)}, bf16[640,640]{1,0:T(8,128)(2,1)}, u32[]{:S(2)}, u32[]{:S(2)}) collective-permute-start(bf16[640,640]{1,0:T(8,128)(2,1)S(1)} %collective-permute-done.10.refs_5_), channel_id=1, source_target_pairs={{4,8},{5,9},{6,10},{7,11},{8,4},{9,5},{10,6},{11,7},{20,24},{21,25... | collective-permute-start | bytes 2457608 | tf_op jit(solution)/shard_map/ppermute | solution.py:213
  65.4 10.1 %collective-permute-done.12 = bf16[640,640]{1,0:T(8,128)(2,1)} collective-permute-done((bf16[640,640]{1,0:T(8,128)(2,1)}, bf16[640,640]{1,0:T(8,128)(2,1)}, u32[]{:S(2)}, u32[]{:S(2)}) %collective-permute-start.12) | collective-permute-done | bytes 819232 | tf_op jit(solution)/shard_map/ppermute | solution.py:213
  75.6 2.2 %collective-permute-start.13 = (bf16[640,640]{1,0:T(8,128)(2,1)}, bf16[640,640]{1,0:T(8,128)(2,1)}, u32[]{:S(2)}, u32[]{:S(2)}) collective-permute-start(bf16[640,640]{1,0:T(8,128)(2,1)} %collective-permute-done.12), channel_id=1, source_target_pairs={{4,0},{5,1},{6,2},{7,3},{8,12},{9,13},{10,14},{11,15},{20,16},{21,... | collective-permute-start | bytes 2457608 | tf_op jit(solution)/shard_map/ppermute | solution.py:213
  77.7 15.0 %collective-permute-done.11 = bf16[640,640]{1,0:T(8,128)(2,1)} collective-permute-done((bf16[640,640]{1,0:T(8,128)(2,1)S(1)}, bf16[640,640]{1,0:T(8,128)(2,1)}, u32[]{:S(2)}, u32[]{:S(2)}) %collective-permute-start.11) | collective-permute-done | bytes 819232 | tf_op jit(solution)/shard_map/ppermute | solution.py:213
  92.8 1.2 collective-permute-start.22
  94.0 2.2 %collective-permute-start.14 = (bf16[640,640]{1,0:T(8,128)(2,1)}, bf16[640,640]{1,0:T(8,128)(2,1)}, u32[]{:S(2)}, u32[]{:S(2)}) collective-permute-start(bf16[640,640]{1,0:T(8,128)(2,1)} %collective-permute-done.11), channel_id=1, source_target_pairs={{4,0},{5,1},{6,2},{7,3},{8,12},{9,13},{10,14},{11,15},{20,16},{21,... | collective-permute-start | bytes 2457608 | tf_op jit(solution)/shard_map/ppermute | solution.py:213
  96.2 1.2 copy-done.4
  98.2 5.2 %shard_map.85.refs_0_ = bf16[192,1280]{1,0:T(8,128)(2,1)S(1)} custom-call(s32[1,2]{1,0:T(1,128)S(1)} %copy-done.9, bf16[192,2560]{1,0:T(8,128)(2,1)S(1)} %shard_map.82.q_ref, bf16[192,5120]{1,0:T(8,128)(2,1)} %collective-permute-done.kb_ref.vb_ref, bf16[192,5120]{1,0:T(8,128)(2,1)S(1)} %shard_map.83.k_ref.v_ref, ...), custom_call_target="tpu_custom_call" | custom-call | tf_op jit(solution)/shard_map/pallas_call | solution.py:104
  103.5 1.0 collective-permute-start.5
  104.5 5.2 %shard_map.86.refs_1_ = bf16[192,1280]{1,0:T(8,128)(2,1)S(1)} custom-call(s32[1,2]{1,0:T(1,128)S(1)} %copy-done.9, bf16[192,2560]{1,0:T(8,128)(2,1)S(1)} %shard_map.82.q_ref, bf16[192,5120]{1,0:T(8,128)(2,1)} %collective-permute-done.kb_ref.vb_ref, bf16[192,5120]{1,0:T(8,128)(2,1)S(1)} %shard_map.83.k_ref.v_ref, ...), custom_call_target="tpu_custom_call" | custom-call | tf_op jit(solution)/shard_map/pallas_call | solution.py:104
  109.9 1.3 broadcast_select_fusion.1.refs_6_
  111.2 1.3 collective-permute-done.22.refs_4_
  112.8 1.2 collective-permute-start.17
  114.0 1.2 broadcast_select_fusion.refs_7_
  115.2 1.3 collective-permute-start.24
  116.8 6.4 %collective-permute-done.16.refs_0_.refs_1_ = bf16[192,1280]{1,0:T(8,128)(2,1)S(1)} collective-permute-done((bf16[192,1280]{1,0:T(8,128)(2,1)S(1)}, bf16[192,1280]{1,0:T(8,128)(2,1)S(1)}, u32[]{:S(2)}, u32[]{:S(2)}) %collective-permute-start.16) | collective-permute-done | bytes 491552 | tf_op jit(solution)/shard_map/ppermute | solution.py:207
  123.2 5.5 %collective-permute-start.18 = (bf16[192,1280]{1,0:T(8,128)(2,1)S(1)}, bf16[192,1280]{1,0:T(8,128)(2,1)S(1)}, u32[]{:S(2)}, u32[]{:S(2)}) collective-permute-start(bf16[192,1280]{1,0:T(8,128)(2,1)S(1)} %collective-permute-done.16.refs_0_.refs_1_), channel_id=1, source_target_pairs={{0,1},{1,0},{2,3},{3,2},{4,5},{5,4},{6,7},{7,6},{8,9},{9,8},{10,11... | collective-permute-start | bytes 1474568 | tf_op jit(solution)/shard_map/ppermute | solution.py:207
  128.7 5.0 %collective-permute-done.17.refs_1_.refs_2_ = bf16[192,1280]{1,0:T(8,128)(2,1)S(1)} collective-permute-done((bf16[192,1280]{1,0:T(8,128)(2,1)S(1)}, bf16[192,1280]{1,0:T(8,128)(2,1)S(1)}, u32[]{:S(2)}, u32[]{:S(2)}) %collective-permute-start.17) | collective-permute-done | bytes 491552 | tf_op jit(solution)/shard_map/ppermute | solution.py:207
  133.7 3.0 %collective-permute-start.19 = (bf16[192,1280]{1,0:T(8,128)(2,1)S(1)}, bf16[192,1280]{1,0:T(8,128)(2,1)S(1)}, u32[]{:S(2)}, u32[]{:S(2)}) collective-permute-start(bf16[192,1280]{1,0:T(8,128)(2,1)S(1)} %collective-permute-done.17.refs_1_.refs_2_), channel_id=1, source_target_pairs={{0,1},{1,0},{2,3},{3,2},{4,5},{5,4},{6,7},{7,6},{8,9},{9,8},{10,11... | collective-permute-start | bytes 1474568 | tf_op jit(solution)/shard_map/ppermute | solution.py:207
  136.7 3.2 %shard_map.87 = (bf16[192,640]{1,0:T(8,128)(2,1)S(1)}, bf16[192,640]{1,0:T(8,128)(2,1)S(1)}) custom-call(f32[40,128]{1,0:T(8,128)S(1)} %bitcast.3, bf16[192,1280]{1,0:T(8,128)(2,1)S(1)} %shard_map.85.refs_0_, bf16[192,1280]{1,0:T(8,128)(2,1)S(1)} %shard_map.86.refs_1_, bf16[192,1280]{1,0:T(8,128)(2,1)S(1)} %collective-permute-done.5.refs_2_, ...), custom_call_target="tpu_custom_call" | custom-call | tf_op jit(solution)/shard_map/pallas_call | solution.py:154
  139.9 7.6 %collective-permute-done.24.refs_6_ = bf16[640,640]{1,0:T(8,128)(2,1)S(1)} collective-permute-done((bf16[640,640]{1,0:T(8,128)(2,1)S(1)}, bf16[640,640]{1,0:T(8,128)(2,1)S(1)}, u32[]{:S(2)}, u32[]{:S(2)}) %collective-permute-start.24) | collective-permute-done | bytes 819232 | tf_op jit(solution)/shard_map/ppermute | solution.py:210
  147.5 17.6 %collective-permute-done.25.refs_7_.refs_5_ = bf16[640,640]{1,0:T(8,128)(2,1)S(1)} collective-permute-done((bf16[640,640]{1,0:T(8,128)(2,1)S(1)}, bf16[640,640]{1,0:T(8,128)(2,1)S(1)}, u32[]{:S(2)}, u32[]{:S(2)}) %collective-permute-start.25) | collective-permute-done | bytes 819232 | tf_op jit(solution)/shard_map/ppermute | solution.py:210
  165.1 3.2 %shard_map.89 = (bf16[192,640]{1,0:T(8,128)(2,1)S(1)}, bf16[192,640]{1,0:T(8,128)(2,1)S(1)}) custom-call(f32[40,128]{1,0:T(8,128)S(1)} %bitcast.4, bf16[192,1280]{1,0:T(8,128)(2,1)S(1)} %shard_map.85.refs_0_, bf16[192,1280]{1,0:T(8,128)(2,1)S(1)} %shard_map.86.refs_1_, bf16[192,1280]{1,0:T(8,128)(2,1)S(1)} %collective-permute-done.5.refs_2_, ...), custom_call_target="tpu_custom_call" | custom-call | tf_op jit(solution)/shard_map/pallas_call | solution.py:154
  168.2 1.3 collective-permute-start.26
  169.6 3.2 %shard_map.88 = (bf16[192,640]{1,0:T(8,128)(2,1)S(1)}, bf16[192,640]{1,0:T(8,128)(2,1)S(1)}) custom-call(f32[40,128]{1,0:T(8,128)S(1)} %bitcast.5, bf16[192,1280]{1,0:T(8,128)(2,1)S(1)} %collective-permute-done.16.refs_0_.refs_1_, bf16[192,1280]{1,0:T(8,128)(2,1)S(1)} %collective-permute-done.17.refs_1_.refs_2_, ...), custom_call_target="tpu_custom_call" | custom-call | tf_op jit(solution)/shard_map/pallas_call | solution.py:154
  172.8 1.6 collective-permute-start.21
  174.5 2.7 %shard_map.91.refs_0_ = f32[384,640]{1,0:T(8,128)S(1)} custom-call(f32[40,128]{1,0:T(8,128)S(1)} %bitcast.6, bf16[192,1280]{1,0:T(8,128)(2,1)S(1)} %collective-permute-done.16.refs_0_.refs_1_, bf16[192,1280]{1,0:T(8,128)(2,1)S(1)} %collective-permute-done.17.refs_1_.refs_2_, bf16[192,1280]{1,0:T(8,128)(2,1)S(1)} %collective-permute-done.18.refs_2_.refs_3_, ...), custom_call_target="tpu_custom_call" | custom-call | tf_op jit(solution)/shard_map/pallas_call | solution.py:154
  178.1 1.8 collective-permute-start.28
  180.3 6.0 %collective-permute-done.21.refs_3_ = bf16[192,640]{1,0:T(8,128)(2,1)S(1)} collective-permute-done((bf16[192,640]{1,0:T(8,128)(2,1)S(1)}, bf16[192,640]{1,0:T(8,128)(2,1)S(1)}, u32[]{:S(2)}, u32[]{:S(2)}) %collective-permute-start.21) | collective-permute-done | bytes 245792 | tf_op jit(solution)/shard_map/ppermute | solution.py:207
  186.3 1.1 shard_map.90.refs_0_
  187.4 3.4 %collective-permute-done.27.refs_1_ = bf16[192,640]{1,0:T(8,128)(2,1)S(1)} collective-permute-done((bf16[192,640]{1,0:T(8,128)(2,1)S(1)}, bf16[192,640]{1,0:T(8,128)(2,1)S(1)}, u32[]{:S(2)}, u32[]{:S(2)}) %collective-permute-start.27) | collective-permute-done | bytes 245792 | tf_op jit(solution)/shard_map/ppermute | solution.py:207
  190.8 5.5 %collective-permute-done.28.refs_2_ = bf16[192,640]{1,0:T(8,128)(2,1)S(1)} collective-permute-done((bf16[192,640]{1,0:T(8,128)(2,1)S(1)}, bf16[192,640]{1,0:T(8,128)(2,1)S(1)}, u32[]{:S(2)}, u32[]{:S(2)}) %collective-permute-start.28) | collective-permute-done | bytes 245792 | tf_op jit(solution)/shard_map/ppermute | solution.py:207
  (49 shorter events, 6.5 us)
Async XLA Ops:
  0.0 7.9 %copy-start.2 = (bf16[192,2560]{1,0:T(8,128)(2,1)S(1)}, bf16[192,2560]{1,0:T(8,128)(2,1)}, u32[]{:S(2)}) copy-start(bf16[192,2560]{1,0:T(8,128)(2,1)} %k_ref.1) | copy-start | bytes 2949124
  2.1 10.3 %collective-permute-start.9 = (bf16[160,640]{1,0:T(8,128)(2,1)}, bf16[160,640]{1,0:T(8,128)(2,1)}, u32[]{:S(2)}, u32[]{:S(2)}) collective-permute-start(bf16[160,640]{1,0:T(8,128)(2,1)} %get-tuple-element.19), channel_id=1, source_target_pairs={{0,1},{1,0},{2,3},{3,2},{4,5},{5,4},{6,7},{7,6},{8,9},{9,8},{10,11... | collective-permute-start | bytes 614408 | tf_op jit(solution)/shard_map/ppermute | solution.py:207
  2.8 44.8 %collective-permute-start.2 = (bf16[192,2560]{1,0:T(8,128)(2,1)}, bf16[192,2560]{1,0:T(8,128)(2,1)}, u32[]{:S(2)}, u32[]{:S(2)}) collective-permute-start(bf16[192,2560]{1,0:T(8,128)(2,1)} %k_ref.1), channel_id=1, source_target_pairs={{3,7},{7,11},{11,15},{4,0},{8,4},{12,8},{19,23},{23,27},{27,31},{2... | collective-permute-start | bytes 2949128 | tf_op jit(solution)/shard_map/ppermute | solution.py:216
  6.0 41.6 %collective-permute-start.3 = (bf16[192,2560]{1,0:T(8,128)(2,1)}, bf16[192,2560]{1,0:T(8,128)(2,1)}, u32[]{:S(2)}, u32[]{:S(2)}) collective-permute-start(bf16[192,2560]{1,0:T(8,128)(2,1)} %v_ref.1), channel_id=1, source_target_pairs={{3,7},{7,11},{11,15},{4,0},{8,4},{12,8},{19,23},{23,27},{27,31},{2... | collective-permute-start | bytes 2949128 | tf_op jit(solution)/shard_map/ppermute | solution.py:216
  8.0 1.2 copy-start.3
  9.2 0.7 copy-start.6
  10.5 83.5 %collective-permute-start = (bf16[192,5120]{1,0:T(8,128)(2,1)S(1)}, bf16[192,5120]{1,0:T(8,128)(2,1)}, u32[]{:S(2)}, u32[]{:S(2)}) collective-permute-start(bf16[192,5120]{1,0:T(8,128)(2,1)S(1)} %shard_map.83.k_ref.v_ref), channel_id=1, source_target_pairs={{0,1},{1,2},{2,3},{4,5},{5,6},{6,7},{8,9},{9,10},{10,11},{12,13},{... | collective-permute-start | bytes 5898248 | tf_op jit(solution)/shard_map/ppermute | solution.py:216
  11.8 8.0 %collective-permute-start.7 = (bf16[160,640]{1,0:T(8,128)(2,1)}, bf16[160,640]{1,0:T(8,128)(2,1)S(1)}, u32[]{:S(2)}, u32[]{:S(2)}) collective-permute-start(bf16[160,640]{1,0:T(8,128)(2,1)} %get-tuple-element.17), channel_id=1, source_target_pairs={{0,3},{1,2},{2,1},{3,0},{4,7},{5,6},{6,5},{7,4},{8,11},{9,10},{10,... | collective-permute-start | bytes 614408 | tf_op jit(solution)/shard_map/ppermute | solution.py:207
  12.4 30.2 %collective-permute-start.8 = (bf16[160,640]{1,0:T(8,128)(2,1)S(1)}, bf16[160,640]{1,0:T(8,128)(2,1)S(1)}, u32[]{:S(2)}, u32[]{:S(2)}) collective-permute-start(bf16[160,640]{1,0:T(8,128)(2,1)S(1)} %get-tuple-element.18), channel_id=1, source_target_pairs={{0,2},{1,3},{2,0},{3,1},{4,6},{5,7},{6,4},{7,5},{8,10},{9,11},{10,... | collective-permute-start | bytes 614408 | tf_op jit(solution)/shard_map/ppermute | solution.py:207
  15.3 32.4 %copy-start.7 = (f32[2560]{0:T(1024)S(1)}, f32[2560]{0:T(1024)}, u32[]{:S(2)}) copy-start(f32[2560]{0:T(1024)} %param.12) | copy-start | bytes 30724
  43.8 52.4 %copy-start.8 = (f32[2560]{0:T(1024)S(1)}, f32[2560]{0:T(1024)}, u32[]{:S(2)}) copy-start(f32[2560]{0:T(1024)} %param.11) | copy-start | bytes 30724
  43.8 19.5 %collective-permute-start.10 = (bf16[640,640]{1,0:T(8,128)(2,1)}, bf16[640,640]{1,0:T(8,128)(2,1)S(1)}, u32[]{:S(2)}, u32[]{:S(2)}) collective-permute-start(bf16[640,640]{1,0:T(8,128)(2,1)} %pad_maximum_fusion.refs_4_), channel_id=1, source_target_pairs={{0,4},{1,5},{2,6},{3,7},{4,0},{5,1},{6,2},{7,3},{8,12},{9,13},{10,... | collective-permute-start | bytes 2457608 | tf_op jit(solution)/shard_map/ppermute | solution.py:213
  45.1 52.8 %collective-permute-start.1 = (bf16[192,5120]{1,0:T(8,128)(2,1)S(1)}, bf16[192,5120]{1,0:T(8,128)(2,1)}, u32[]{:S(2)}, u32[]{:S(2)}) collective-permute-start(bf16[192,5120]{1,0:T(8,128)(2,1)S(1)} %shard_map.83.k_ref.v_ref), channel_id=1, source_target_pairs={{1,0},{2,1},{3,2},{5,4},{6,5},{7,6},{9,8},{10,9},{11,10},{13,12},{... | collective-permute-start | bytes 5898248 | tf_op jit(solution)/shard_map/ppermute | solution.py:216
  51.0 47.2 %copy-start.9 = (s32[1,2]{1,0:T(1,128)S(1)}, s32[1,2]{1,0:T(1,128)}, u32[]{:S(2)}) copy-start(s32[1,2]{1,0:T(1,128)} %reach_ref.3) | copy-start | bytes 28
  51.0 47.2 %collective-permute-start.4 = (bf16[192,5120]{1,0:T(8,128)(2,1)}, bf16[192,5120]{1,0:T(8,128)(2,1)}, u32[]{:S(2)}, u32[]{:S(2)}) collective-permute-start(bf16[192,5120]{1,0:T(8,128)(2,1)} %shard_map.84), channel_id=1, source_target_pairs={{0,3},{3,0},{4,7},{7,4},{8,11},{11,8},{12,15},{15,12},{16,19},{19,... | collective-permute-start | bytes 5898248 | tf_op jit(solution)/shard_map/ppermute | solution.py:216
  53.1 22.5 %collective-permute-start.12 = (bf16[640,640]{1,0:T(8,128)(2,1)}, bf16[640,640]{1,0:T(8,128)(2,1)}, u32[]{:S(2)}, u32[]{:S(2)}) collective-permute-start(bf16[640,640]{1,0:T(8,128)(2,1)} %pad_maximum_fusion.refs_4_), channel_id=1, source_target_pairs={{4,8},{5,9},{6,10},{7,11},{8,4},{9,5},{10,6},{11,7},{20,24},{21,25... | collective-permute-start | bytes 2457608 | tf_op jit(solution)/shard_map/ppermute | solution.py:213
  63.4 30.6 %copy-start = (bf16[640,640]{1,0:T(8,128)(2,1)}, bf16[640,640]{1,0:T(8,128)(2,1)S(1)}, u32[]{:S(2)}) copy-start(bf16[640,640]{1,0:T(8,128)(2,1)S(1)} %collective-permute-done.10.refs_5_) | copy-start | bytes 2457604
  63.4 29.4 %collective-permute-start.11 = (bf16[640,640]{1,0:T(8,128)(2,1)S(1)}, bf16[640,640]{1,0:T(8,128)(2,1)}, u32[]{:S(2)}, u32[]{:S(2)}) collective-permute-start(bf16[640,640]{1,0:T(8,128)(2,1)S(1)} %collective-permute-done.10.refs_5_), channel_id=1, source_target_pairs={{4,8},{5,9},{6,10},{7,11},{8,4},{9,5},{10,6},{11,7},{20,24},{21,25... | collective-permute-start | bytes 2457608 | tf_op jit(solution)/shard_map/ppermute | solution.py:213
  75.6 34.2 %collective-permute-start.13 = (bf16[640,640]{1,0:T(8,128)(2,1)}, bf16[640,640]{1,0:T(8,128)(2,1)}, u32[]{:S(2)}, u32[]{:S(2)}) collective-permute-start(bf16[640,640]{1,0:T(8,128)(2,1)} %collective-permute-done.12), channel_id=1, source_target_pairs={{4,0},{5,1},{6,2},{7,3},{8,12},{9,13},{10,14},{11,15},{20,16},{21,... | collective-permute-start | bytes 2457608 | tf_op jit(solution)/shard_map/ppermute | solution.py:213
  92.8 19.7 %collective-permute-start.22 = (bf16[640,640]{1,0:T(8,128)(2,1)}, bf16[640,640]{1,0:T(8,128)(2,1)}, u32[]{:S(2)}, u32[]{:S(2)}) collective-permute-start(bf16[640,640]{1,0:T(8,128)(2,1)} %pad_maximum_fusion.refs_4_), channel_id=1, source_target_pairs={{0,16},{16,0},{1,17},{17,1},{2,18},{18,2},{3,19},{19,3},{4,20},{20... | collective-permute-start | bytes 2457608 | tf_op jit(solution)/shard_map/ppermute | solution.py:210
  94.0 18.8 %collective-permute-start.14 = (bf16[640,640]{1,0:T(8,128)(2,1)}, bf16[640,640]{1,0:T(8,128)(2,1)}, u32[]{:S(2)}, u32[]{:S(2)}) collective-permute-start(bf16[640,640]{1,0:T(8,128)(2,1)} %collective-permute-done.11), channel_id=1, source_target_pairs={{4,0},{5,1},{6,2},{7,3},{8,12},{9,13},{10,14},{11,15},{20,16},{21,... | collective-permute-start | bytes 2457608 | tf_op jit(solution)/shard_map/ppermute | solution.py:213
  96.2 1.2 copy-start.4
  97.9 42.0 %collective-permute-start.23 = (bf16[640,640]{1,0:T(8,128)(2,1)}, bf16[640,640]{1,0:T(8,128)(2,1)S(1)}, u32[]{:S(2)}, u32[]{:S(2)}) collective-permute-start(bf16[640,640]{1,0:T(8,128)(2,1)} %copy-done), channel_id=1, source_target_pairs={{0,16},{16,0},{1,17},{17,1},{2,18},{18,2},{3,19},{19,3},{4,20},{20... | collective-permute-start | bytes 2457608 | tf_op jit(solution)/shard_map/ppermute | solution.py:210
  103.5 11.8 %collective-permute-start.5 = (bf16[192,1280]{1,0:T(8,128)(2,1)S(1)}, bf16[192,1280]{1,0:T(8,128)(2,1)S(1)}, u32[]{:S(2)}, u32[]{:S(2)}) collective-permute-start(bf16[192,1280]{1,0:T(8,128)(2,1)S(1)} %shard_map.85.refs_0_), channel_id=1, source_target_pairs={{0,1},{1,0},{2,3},{3,2},{4,5},{5,4},{6,7},{7,6},{8,9},{9,8},{10,11... | collective-permute-start | bytes 1474568 | tf_op jit(solution)/shard_map/ppermute | solution.py:207
  109.7 27.0 %copy-start.1 = (bf16[640,640]{1,0:T(8,128)(2,1)S(1)}, bf16[640,640]{1,0:T(8,128)(2,1)}, u32[]{:S(2)}) copy-start(bf16[640,640]{1,0:T(8,128)(2,1)} %copy-done) | copy-start | bytes 2457604
  109.7 27.0 %copy-start.5 = (f32[5120]{0:T(1024)S(1)}, f32[5120]{0:T(1024)}, u32[]{:S(2)}) copy-start(f32[5120]{0:T(1024)} %param.14) | copy-start | bytes 61444
  109.7 6.8 %collective-permute-start.6 = (bf16[192,1280]{1,0:T(8,128)(2,1)S(1)}, bf16[192,1280]{1,0:T(8,128)(2,1)S(1)}, u32[]{:S(2)}, u32[]{:S(2)}) collective-permute-start(bf16[192,1280]{1,0:T(8,128)(2,1)S(1)} %shard_map.86.refs_1_), channel_id=1, source_target_pairs={{0,1},{1,0},{2,3},{3,2},{4,5},{5,4},{6,7},{7,6},{8,9},{9,8},{10,11... | collective-permute-start | bytes 1474568 | tf_op jit(solution)/shard_map/ppermute | solution.py:207
  112.5 10.7 %collective-permute-start.16 = (bf16[192,1280]{1,0:T(8,128)(2,1)S(1)}, bf16[192,1280]{1,0:T(8,128)(2,1)S(1)}, u32[]{:S(2)}, u32[]{:S(2)}) collective-permute-start(bf16[192,1280]{1,0:T(8,128)(2,1)S(1)} %shard_map.85.refs_0_), channel_id=1, source_target_pairs={{0,2},{1,3},{2,0},{3,1},{4,6},{5,7},{6,4},{7,5},{8,10},{9,11},{10,... | collective-permute-start | bytes 1474568 | tf_op jit(solution)/shard_map/ppermute | solution.py:207
  112.8 20.9 %collective-permute-start.17 = (bf16[192,1280]{1,0:T(8,128)(2,1)S(1)}, bf16[192,1280]{1,0:T(8,128)(2,1)S(1)}, u32[]{:S(2)}, u32[]{:S(2)}) collective-permute-start(bf16[192,1280]{1,0:T(8,128)(2,1)S(1)} %shard_map.86.refs_1_), channel_id=1, source_target_pairs={{0,2},{1,3},{2,0},{3,1},{4,6},{5,7},{6,4},{7,5},{8,10},{9,11},{10,... | collective-permute-start | bytes 1474568 | tf_op jit(solution)/shard_map/ppermute | solution.py:207
  115.2 32.3 %collective-permute-start.24 = (bf16[640,640]{1,0:T(8,128)(2,1)S(1)}, bf16[640,640]{1,0:T(8,128)(2,1)S(1)}, u32[]{:S(2)}, u32[]{:S(2)}) collective-permute-start(bf16[640,640]{1,0:T(8,128)(2,1)S(1)} %broadcast_select_fusion.1.refs_6_), channel_id=1, source_target_pairs={{0,16},{16,0},{1,17},{17,1},{2,18},{18,2},{3,19},{19,3},{4,20},{20... | collective-permute-start | bytes 2457608 | tf_op jit(solution)/shard_map/ppermute | solution.py:210
  116.5 48.6 %collective-permute-start.25 = (bf16[640,640]{1,0:T(8,128)(2,1)S(1)}, bf16[640,640]{1,0:T(8,128)(2,1)S(1)}, u32[]{:S(2)}, u32[]{:S(2)}) collective-permute-start(bf16[640,640]{1,0:T(8,128)(2,1)S(1)} %broadcast_select_fusion.refs_7_), channel_id=1, source_target_pairs={{0,16},{16,0},{1,17},{17,1},{2,18},{18,2},{3,19},{19,3},{4,20},{20... | collective-permute-start | bytes 2457608 | tf_op jit(solution)/shard_map/ppermute | solution.py:210
  123.2 46.4 %collective-permute-start.18 = (bf16[192,1280]{1,0:T(8,128)(2,1)S(1)}, bf16[192,1280]{1,0:T(8,128)(2,1)S(1)}, u32[]{:S(2)}, u32[]{:S(2)}) collective-permute-start(bf16[192,1280]{1,0:T(8,128)(2,1)S(1)} %collective-permute-done.16.refs_0_.refs_1_), channel_id=1, source_target_pairs={{0,1},{1,0},{2,3},{3,2},{4,5},{5,4},{6,7},{7,6},{8,9},{9,8},{10,11... | collective-permute-start | bytes 1474568 | tf_op jit(solution)/shard_map/ppermute | solution.py:207
  133.7 35.9 %collective-permute-start.19 = (bf16[192,1280]{1,0:T(8,128)(2,1)S(1)}, bf16[192,1280]{1,0:T(8,128)(2,1)S(1)}, u32[]{:S(2)}, u32[]{:S(2)}) collective-permute-start(bf16[192,1280]{1,0:T(8,128)(2,1)S(1)} %collective-permute-done.17.refs_1_.refs_2_), channel_id=1, source_target_pairs={{0,1},{1,0},{2,3},{3,2},{4,5},{5,4},{6,7},{7,6},{8,9},{9,8},{10,11... | collective-permute-start | bytes 1474568 | tf_op jit(solution)/shard_map/ppermute | solution.py:207
  139.9 38.2 %collective-permute-start.15 = (bf16[192,640]{1,0:T(8,128)(2,1)S(1)}, bf16[192,640]{1,0:T(8,128)(2,1)S(1)}, u32[]{:S(2)}, u32[]{:S(2)}) collective-permute-start(bf16[192,640]{1,0:T(8,128)(2,1)S(1)} %get-tuple-element.22), channel_id=1, source_target_pairs={{0,1},{1,0},{2,3},{3,2},{4,5},{5,4},{6,7},{7,6},{8,9},{9,8},{10,11... | collective-permute-start | bytes 737288 | tf_op jit(solution)/shard_map/ppermute | solution.py:207
  168.2 11.6 %collective-permute-start.26 = (bf16[192,640]{1,0:T(8,128)(2,1)S(1)}, bf16[192,640]{1,0:T(8,128)(2,1)S(1)}, u32[]{:S(2)}, u32[]{:S(2)}) collective-permute-start(bf16[192,640]{1,0:T(8,128)(2,1)S(1)} %get-tuple-element.26), channel_id=1, source_target_pairs={{0,1},{1,0},{2,3},{3,2},{4,5},{5,4},{6,7},{7,6},{8,9},{9,8},{10,11... | collective-permute-start | bytes 737288 | tf_op jit(solution)/shard_map/ppermute | solution.py:207
  172.8 7.5 %collective-permute-start.20 = (bf16[192,640]{1,0:T(8,128)(2,1)S(1)}, bf16[192,640]{1,0:T(8,128)(2,1)S(1)}, u32[]{:S(2)}, u32[]{:S(2)}) collective-permute-start(bf16[192,640]{1,0:T(8,128)(2,1)S(1)} %get-tuple-element.23), channel_id=1, source_target_pairs={{0,2},{1,3},{2,0},{3,1},{4,6},{5,7},{6,4},{7,5},{8,10},{9,11},{10,... | collective-permute-start | bytes 737288 | tf_op jit(solution)/shard_map/ppermute | solution.py:207
  172.8 13.4 %collective-permute-start.21 = (bf16[192,640]{1,0:T(8,128)(2,1)S(1)}, bf16[192,640]{1,0:T(8,128)(2,1)S(1)}, u32[]{:S(2)}, u32[]{:S(2)}) collective-permute-start(bf16[192,640]{1,0:T(8,128)(2,1)S(1)} %get-tuple-element.24), channel_id=1, source_target_pairs={{0,3},{1,2},{2,1},{3,0},{4,7},{5,6},{6,5},{7,4},{8,11},{9,10},{10,... | collective-permute-start | bytes 737288 | tf_op jit(solution)/shard_map/ppermute | solution.py:207
  178.0 12.9 %collective-permute-start.27 = (bf16[192,640]{1,0:T(8,128)(2,1)S(1)}, bf16[192,640]{1,0:T(8,128)(2,1)S(1)}, u32[]{:S(2)}, u32[]{:S(2)}) collective-permute-start(bf16[192,640]{1,0:T(8,128)(2,1)S(1)} %get-tuple-element.27), channel_id=1, source_target_pairs={{0,2},{1,3},{2,0},{3,1},{4,6},{5,7},{6,4},{7,5},{8,10},{9,11},{10,... | collective-permute-start | bytes 737288 | tf_op jit(solution)/shard_map/ppermute | solution.py:207
  178.1 18.2 %collective-permute-start.28 = (bf16[192,640]{1,0:T(8,128)(2,1)S(1)}, bf16[192,640]{1,0:T(8,128)(2,1)S(1)}, u32[]{:S(2)}, u32[]{:S(2)}) collective-permute-start(bf16[192,640]{1,0:T(8,128)(2,1)S(1)} %get-tuple-element.28), channel_id=1, source_target_pairs={{0,3},{1,2},{2,1},{3,0},{4,7},{5,6},{6,5},{7,4},{8,11},{9,10},{10,... | collective-permute-start | bytes 737288 | tf_op jit(solution)/shard_map/ppermute | solution.py:207

commit v8 on v7

--- a/solution.py
+++ b/solution.py
@@ -31,10 +31,11 @@
         out_ref[:, i * HD : (i + 1) * HD] = piece
 
 
-def pair_kernel(k_ref, v_ref, gain_ref, out_ref):
+def pair_kernel(k_ref, v_ref, gain_ref, out_ref, kn_ref):
     chans = k_ref.shape[1]
     for i, piece in scaled_heads(k_ref, gain_ref):
         out_ref[:, i * HD : (i + 1) * HD] = piece
+        kn_ref[:, i * HD : (i + 1) * HD] = piece
     out_ref[:, chans:] = v_ref[...]
 
 
@@ -52,14 +53,14 @@
     rows, chans = keys.shape
     return pl.pallas_call(
         pair_kernel,
-        out_shape=jax.ShapeDtypeStruct((rows, 2 * chans), jnp.bfloat16),
+        out_shape=[jax.ShapeDtypeStruct((rows, n * chans), jnp.bfloat16) for n in (2, 1)],
         in_specs=whole(3),
-        out_specs=pl.BlockSpec(memory_space=pltpu.VMEM),
+        out_specs=whole(2),
         compiler_params=LIMIT,
     )(keys, values, gain.reshape(-1, HD))
 
 
-def attend_kernel(reach_ref, q_ref, kb_ref, k_ref, ka_ref, kd_ref, vb_ref, v_ref, va_ref, vd_ref, o_ref):
+def attend_kernel(reach_ref, q_ref, kb_ref, k_ref, ka_ref, vb_ref, v_ref, va_ref, kd_ref, vd_ref, o_ref):
     scale = HD ** (-0.5)
     place = lax.axis_index("tm")
     peers = lax.axis_size("tm")
@@ -92,7 +93,7 @@
         o_ref[:, at] = out.astype(jnp.bfloat16)
 
 
-def attend(reach, qn, pairs, chunk, chunks):
+def attend(reach, qn, pairs, k_diag, v_diag, chunk, chunks):
     rows, chans = qn.shape
     wide = chans // chunks
     heads = wide // HD
@@ -105,10 +106,53 @@
         attend_kernel,
         grid=(steps,),
         out_shape=jax.ShapeDtypeStruct((rows, wide), jnp.bfloat16),
-        in_specs=[pl.BlockSpec(memory_space=pltpu.SMEM)] + [k_spec] * 5 + [v_spec] * 4,
+        in_specs=[pl.BlockSpec(memory_space=pltpu.SMEM)] + [k_spec] * 4 + [v_spec] * 3 + [k_spec] * 2,
         out_specs=pl.BlockSpec((rows, cols), lambda i: (0, i)),
         compiler_params=LIMIT,
-    )(reach, qn, *pairs, *pairs)
+    )(reach, qn, *pairs, *pairs, k_diag, v_diag)
+
+
+def join_kernel(*refs):
+    pieces, out_ref = refs[:-1], refs[-1]
+    depth = pieces[0].shape[0]
+    low = lax.axis_index("tm") % 4
+    for i, ref in enumerate(pieces):
+        out_ref[pl.ds(pl.multiple_of((low ^ i) * depth, depth), depth), :] = ref[...]
+
+
+def join(pieces):
+    depth, cols = pieces[0].shape
+    return pl.pallas_call(
+        join_kernel,
+        out_shape=jax.ShapeDtypeStruct((4 * depth, cols), jnp.bfloat16),
+        in_specs=whole(4),
+        out_specs=pl.BlockSpec(memory_space=pltpu.VMEM),
+        compiler_params=LIMIT,
+        name="join",
+    )(*pieces)
+
+
+def pick_kernel(inner_ref, outer_ref, out_ref):
+    line = lax.axis_index("tm") // 4
+    inner = (line > 0) & (line < lax.axis_size("tm") // 4 - 1)
+
+    @pl.when(inner)
+    def _():
+        out_ref[...] = inner_ref[...]
+
+    @pl.when(jnp.logical_not(inner))
+    def _():
+        out_ref[...] = outer_ref[...]
+
+
+def pick(inner, outer):
+    return pl.pallas_call(
+        pick_kernel,
+        out_shape=jax.ShapeDtypeStruct(inner.shape, inner.dtype),
+        in_specs=whole(2),
+        out_specs=pl.BlockSpec(memory_space=pltpu.VMEM),
+        compiler_params=LIMIT,
+    )(inner, outer)
 
 
 def project_kernel(share, count, slots, total, final, resumed, gate_ref, *refs):
@@ -196,9 +240,8 @@
     place = lax.axis_index("tm")
     group = lax.axis_index("groups")
     low = place % 4
-    line = place // 4
     lines = peers // 4
-    _, width = out_weight.shape
+    depth, width = out_weight.shape
     _, chans = queries.shape
     cols = width // 8
     chunks = 2 if chans // HD % 2 == 0 else 1
@@ -221,6 +264,9 @@
     def inside(pairs):
         return [(i, j) for i, j in pairs if i // 4 == j // 4]
 
+    def outside(pairs):
+        return [(i, j) for i, j in pairs if i // 4 != j // 4]
+
     def choose(flag, a, b):
         return jnp.where(flag, a, b)
 
@@ -232,30 +278,32 @@
 
     cuts = lax.optimization_barrier([weight_part(low ^ i) for i in range(4)])
     parts = [cuts[0]] + [swap(cuts[i], i) for i in (1, 2, 3)]
-    odd, upper = (low % 2) == 1, low >= 2
-    halves = [
-        jnp.concatenate([choose(odd, b, a), choose(odd, a, b)], axis=0)
-        for a, b in ((parts[0], parts[1]), (parts[2], parts[3]))
-    ]
-    block = jnp.concatenate([choose(upper, halves[1], halves[0]), choose(upper, halves[0], halves[1])], axis=0)
-
-    leap = [(4 * z + 3, 4 * z + 7) for z in range(lines - 1)] + [(4 * z + 4, 4 * z) for z in range(lines - 1)]
-    turn = [(4 * z + i, 4 * z + (i ^ 3)) for z in range(lines) for i in (0, 3)]
-    k_leap, v_leap = send(keys, leap), send(values, leap)
-    kv = pair(keys, values, k_gain)
+    if depth % 16 == 0:
+        block = join(parts)
+    else:
+        odd, upper = (low % 2) == 1, low >= 2
+        halves = [
+            jnp.concatenate([choose(odd, b, a), choose(odd, a, b)], axis=0)
+            for a, b in ((parts[0], parts[1]), (parts[2], parts[3]))
+        ]
+        block = jnp.concatenate([choose(upper, halves[1], halves[0]), choose(upper, halves[0], halves[1])], axis=0)
+
+    kv, kn = pair(keys, values, k_gain)
     near = [send(kv, inside(up)), kv, send(kv, inside(down))]
-    near.append(send(pair(k_leap, v_leap, k_gain), turn))
+    k_diag = send(kn, outside(up) + outside(down))
+    turn = [(4 * z + i, 4 * z + (i ^ 2)) for z in range(lines) for i in (0, 3)]
+    leap = [(i ^ 2, j) for i, j in outside(up) + outside(down)]
+    v_diag = send(send(values, turn), leap)
     qn = norm(queries, q_gain)
 
     if lines == 4:
-        middle = (line == 1) | (line == 2)
         beside = along(block, ((0, 1), (1, 0), (2, 3), (3, 2)))
         across = along(block, ((1, 2), (2, 1)))
         across_far = along(beside, ((1, 2), (2, 1)))
         edge = along(across, ((1, 0), (2, 3)))
         edge_far = along(across_far, ((1, 0), (2, 3)))
-        second = choose(middle, across_far, edge)
-        third = choose(middle, across, edge_far)
+        second = pick(across_far, edge)
+        third = pick(across, edge_far)
         slots = [block, beside, second, third]
     else:
         members = [[z * 4 + i for z in range(lines)] for i in range(4)]
@@ -264,7 +312,7 @@
 
     here, there = [], []
     for i in range(chunks):
-        own = attend(reach, qn, near, i, chunks)
+        own = attend(reach, qn, near, k_diag, v_diag, i, chunks)
         over = swap(own, 2)
         here.append([own, swap(own, 1)])
         there.append([over, swap(over, 1)])

time: 198 us -> 203 us (1.025)
  the two profiles are of different devices: /device:TPU:21 before, /device:TPU:11 now
where the time goes in v8:
time: 203 us
  waiting for transfers between devices  138 us (68%)
  starting transfers between devices  37.9 us (19%)
  Pallas kernels  21.9 us (11%)
  local copies, waits for them, and re-layouts  4.52 us (2%)
    ppermute x15, waiting for transfers between devices, swap(): return lax.ppermute(x, 'tm', [(i, i ^ bits) for i in range(peers)])  57 us
    ppermute x4, waiting for transfers between devices, group_swap(): return lax.ppermute(x, 'groups', [(0, 1), (1, 0)])  53.5 us
    ppermute x5, waiting for transfers between devices, along(): lax.ppermute(x, 'tm', [(4 * a + i, 4 * b + i) for a, b in moves for i in...  18.2 us
    ppermute x15, starting transfers between devices, swap(): return lax.ppermute(x, 'tm', [(i, i ^ bits) for i in range(peers)])  15.5 us
    ppermute x5, starting transfers between devices, along(): lax.ppermute(x, 'tm', [(4 * a + i, 4 * b + i) for a, b in moves for i in...  12.5 us
    ppermute x5, waiting for transfers between devices, send(): return lax.ppermute(x, 'tm', pairs)  9.4 us
    pallas_call x2, Pallas kernels, attend(): pl.pallas_call(attend_kernel, grid=(steps,), out_shape=jax.ShapeDtypeStru...  9 us
    pallas_call x5, Pallas kernels, project(): pl.pallas_call(body, out_shape=out, in_specs=whole(1 + len(resumed) + len...  8.42 us
  transfers between devices with their start and end apart: 29, of which 14 were waited for; matrix products, arithmetic and copies ran while one was open for 1% of the time, Pallas kernels for 10%

profile of v8, /device:TPU:11, one launch (start us, length us, event | category | flops | bytes accessed | tf_op | source)
XLA Modules:
  0.0 203.0 jit_solution(18174346748059737682)
XLA Ops:
  0.0 1.2 copy-done
  1.2 1.2 copy-done.1
  2.4 0.7 copy-done.4
  3.1 1.7 shard_map.83
  4.8 0.8 collective-permute-start.2
  5.7 1.4 constant_dynamic-slice_fusion
  7.1 2.8 %collective-permute-start.7 = (bf16[160,640]{1,0:T(8,128)(2,1)S(1)}, bf16[160,640]{1,0:T(8,128)(2,1)S(1)}, u32[]{:S(2)}, u32[]{:S(2)}) collective-permute-start(bf16[160,640]{1,0:T(8,128)(2,1)S(1)} %get-tuple-element.22), channel_id=1, source_target_pairs={{0,1},{1,0},{2,3},{3,2},{4,5},{5,4},{6,7},{7,6},{8,9},{9,8},{10,11... | collective-permute-start | bytes 614408 | tf_op jit(solution)/shard_map/ppermute | solution.py:250
  9.9 1.6 collective-permute-start.8
  11.5 2.2 %collective-permute-start = (bf16[192,5120]{1,0:T(8,128)(2,1)S(1)}, bf16[192,5120]{1,0:T(8,128)(2,1)S(1)}, u32[]{:S(2)}, u32[]{:S(2)}) collective-permute-start(bf16[192,5120]{1,0:T(8,128)(2,1)S(1)} %get-tuple-element.19.k_ref.v_ref), channel_id=1, source_target_pairs={{0,1},{1,2},{2,3},{4,5},{5,6},{6,7},{8,9},{9,10},{10,11},{12,13},{... | collective-permute-start | bytes 5898248 | tf_op jit(solution)/shard_map/ppermute | solution.py:259
  13.7 2.2 %collective-permute-start.1 = (bf16[192,5120]{1,0:T(8,128)(2,1)S(1)}, bf16[192,5120]{1,0:T(8,128)(2,1)S(1)}, u32[]{:S(2)}, u32[]{:S(2)}) collective-permute-start(bf16[192,5120]{1,0:T(8,128)(2,1)S(1)} %get-tuple-element.19.k_ref.v_ref), channel_id=1, source_target_pairs={{1,0},{2,1},{3,2},{5,4},{6,5},{7,6},{9,8},{10,9},{11,10},{13,12},{... | collective-permute-start | bytes 5898248 | tf_op jit(solution)/shard_map/ppermute | solution.py:259
  15.9 1.3 collective-permute-start.3
  17.2 8.8 %collective-permute-done.8.refs_2_ = bf16[160,640]{1,0:T(8,128)(2,1)S(1)} collective-permute-done((bf16[160,640]{1,0:T(8,128)(2,1)S(1)}, bf16[160,640]{1,0:T(8,128)(2,1)S(1)}, u32[]{:S(2)}, u32[]{:S(2)}) %collective-permute-start.8) | collective-permute-done | bytes 204832 | tf_op jit(solution)/shard_map/ppermute | solution.py:250
  26.0 1.7 collective-permute-start.9
  27.7 34.4 %collective-permute-done.9.refs_3_ = bf16[160,640]{1,0:T(8,128)(2,1)S(1)} collective-permute-done((bf16[160,640]{1,0:T(8,128)(2,1)S(1)}, bf16[160,640]{1,0:T(8,128)(2,1)S(1)}, u32[]{:S(2)}, u32[]{:S(2)}) %collective-permute-start.9) | collective-permute-done | bytes 204832 | tf_op jit(solution)/shard_map/ppermute | solution.py:250
  62.3 4.5 %collective-permute-start.12 = (bf16[640,640]{1,0:T(8,128)(2,1)S(1)}, bf16[640,640]{1,0:T(8,128)(2,1)S(1)}, u32[]{:S(2)}, u32[]{:S(2)}) collective-permute-start(bf16[640,640]{1,0:T(8,128)(2,1)S(1)} %join.1.refs_4_), channel_id=1, source_target_pairs={{4,8},{5,9},{6,10},{7,11},{8,4},{9,5},{10,6},{11,7},{20,24},{21,25... | collective-permute-start | bytes 2457608 | tf_op jit(solution)/shard_map/ppermute | solution.py:256
  66.8 1.4 collective-permute-start.4
  68.1 5.6 %collective-permute-done.10.refs_5_ = bf16[640,640]{1,0:T(8,128)(2,1)S(1)} collective-permute-done((bf16[640,640]{1,0:T(8,128)(2,1)S(1)}, bf16[640,640]{1,0:T(8,128)(2,1)S(1)}, u32[]{:S(2)}, u32[]{:S(2)}) %collective-permute-start.10) | collective-permute-done | bytes 819232 | tf_op jit(solution)/shard_map/ppermute | solution.py:256
  73.7 5.3 %collective-permute-start.11 = (bf16[640,640]{1,0:T(8,128)(2,1)S(1)}, bf16[640,640]{1,0:T(8,128)(2,1)S(1)}, u32[]{:S(2)}, u32[]{:S(2)}) collective-permute-start(bf16[640,640]{1,0:T(8,128)(2,1)S(1)} %collective-permute-done.10.refs_5_), channel_id=1, source_target_pairs={{4,8},{5,9},{6,10},{7,11},{8,4},{9,5},{10,6},{11,7},{20,24},{21,25... | collective-permute-start | bytes 2457608 | tf_op jit(solution)/shard_map/ppermute | solution.py:256
  79.0 5.0 %collective-permute-done.12.inner_ref = bf16[640,640]{1,0:T(8,128)(2,1)S(1)} collective-permute-done((bf16[640,640]{1,0:T(8,128)(2,1)S(1)}, bf16[640,640]{1,0:T(8,128)(2,1)S(1)}, u32[]{:S(2)}, u32[]{:S(2)}) %collective-permute-start.12) | collective-permute-done | bytes 819232 | tf_op jit(solution)/shard_map/ppermute | solution.py:256
  84.1 1.3 collective-permute-start.13
  85.9 9.4 %collective-permute-done.4.vd_ref = bf16[192,2560]{1,0:T(8,128)(2,1)S(1)} collective-permute-done((bf16[192,2560]{1,0:T(8,128)(2,1)S(1)}, bf16[192,2560]{1,0:T(8,128)(2,1)S(1)}, u32[]{:S(2)}, u32[]{:S(2)}) %collective-permute-start.4) | collective-permute-done | bytes 983072 | tf_op jit(solution)/shard_map/ppermute | solution.py:259
  95.3 4.5 %shard_map.84.refs_0_ = bf16[192,1280]{1,0:T(8,128)(2,1)S(1)} custom-call(s32[1,2]{1,0:T(1,128)S(1)} %copy-done.6, bf16[192,2560]{1,0:T(8,128)(2,1)S(1)} %shard_map.82.q_ref, bf16[192,5120]{1,0:T(8,128)(2,1)S(1)} %collective-permute-done.kb_ref.vb_ref, bf16[192,5120]{1,0:T(8,128)(2,1)S(1)} %get-tuple-element.19.k_ref.v_ref, ...), custom_call_target="tpu_custom_call" | custom-call | tf_op jit(solution)/shard_map/pallas_call | solution.py:105
  99.8 1.4 collective-permute-start.16
  101.2 2.9 %collective-permute-done.11.inner_ref = bf16[640,640]{1,0:T(8,128)(2,1)S(1)} collective-permute-done((bf16[640,640]{1,0:T(8,128)(2,1)S(1)}, bf16[640,640]{1,0:T(8,128)(2,1)S(1)}, u32[]{:S(2)}, u32[]{:S(2)}) %collective-permute-start.11) | collective-permute-done | bytes 819232 | tf_op jit(solution)/shard_map/ppermute | solution.py:256
  104.1 1.3 collective-permute-start.14
  105.5 4.5 %shard_map.85.refs_1_ = bf16[192,1280]{1,0:T(8,128)(2,1)S(1)} custom-call(s32[1,2]{1,0:T(1,128)S(1)} %copy-done.6, bf16[192,2560]{1,0:T(8,128)(2,1)S(1)} %shard_map.82.q_ref, bf16[192,5120]{1,0:T(8,128)(2,1)S(1)} %collective-permute-done.kb_ref.vb_ref, bf16[192,5120]{1,0:T(8,128)(2,1)S(1)} %get-tuple-element.19.k_ref.v_ref, ...), custom_call_target="tpu_custom_call" | custom-call | tf_op jit(solution)/shard_map/pallas_call | solution.py:105
  110.6 1.6 collective-permute-start.17
  112.2 0.7 collective-permute-start.18
  113.2 4.7 %collective-permute-done.14.outer_ref = bf16[640,640]{1,0:T(8,128)(2,1)S(1)} collective-permute-done((bf16[640,640]{1,0:T(8,128)(2,1)S(1)}, bf16[640,640]{1,0:T(8,128)(2,1)S(1)}, u32[]{:S(2)}, u32[]{:S(2)}) %collective-permute-start.14) | collective-permute-done | bytes 819232 | tf_op jit(solution)/shard_map/ppermute | solution.py:256
  118.4 1.3 collective-permute-start.24
  119.7 3.7 %collective-permute-done.17.refs_1_.refs_2_ = bf16[192,1280]{1,0:T(8,128)(2,1)S(1)} collective-permute-done((bf16[192,1280]{1,0:T(8,128)(2,1)S(1)}, bf16[192,1280]{1,0:T(8,128)(2,1)S(1)}, u32[]{:S(2)}, u32[]{:S(2)}) %collective-permute-start.17) | collective-permute-done | bytes 491552 | tf_op jit(solution)/shard_map/ppermute | solution.py:250
  123.6 1.3 collective-permute-start.19
  124.9 2.0 shard_map.88
  127.0 2.0 shard_map.89
  129.0 3.6 %collective-permute-done.22.refs_4_ = bf16[640,640]{1,0:T(8,128)(2,1)S(1)} collective-permute-done((bf16[640,640]{1,0:T(8,128)(2,1)S(1)}, bf16[640,640]{1,0:T(8,128)(2,1)S(1)}, u32[]{:S(2)}, u32[]{:S(2)}) %collective-permute-start.22) | collective-permute-done | bytes 819232 | tf_op jit(solution)/shard_map/ppermute | solution.py:253
  132.6 17.6 %collective-permute-done.23.refs_5_ = bf16[640,640]{1,0:T(8,128)(2,1)S(1)} collective-permute-done((bf16[640,640]{1,0:T(8,128)(2,1)S(1)}, bf16[640,640]{1,0:T(8,128)(2,1)S(1)}, u32[]{:S(2)}, u32[]{:S(2)}) %collective-permute-start.23) | collective-permute-done | bytes 819232 | tf_op jit(solution)/shard_map/ppermute | solution.py:253
  150.2 1.2 collective-permute-start.21
  151.3 16.4 %collective-permute-done.24.refs_6_ = bf16[640,640]{1,0:T(8,128)(2,1)S(1)} collective-permute-done((bf16[640,640]{1,0:T(8,128)(2,1)S(1)}, bf16[640,640]{1,0:T(8,128)(2,1)S(1)}, u32[]{:S(2)}, u32[]{:S(2)}) %collective-permute-start.24) | collective-permute-done | bytes 819232 | tf_op jit(solution)/shard_map/ppermute | solution.py:253
  167.7 1.6 shard_map.92.refs_0_
  169.3 15.9 %collective-permute-done.25.refs_7_.refs_5_ = bf16[640,640]{1,0:T(8,128)(2,1)S(1)} collective-permute-done((bf16[640,640]{1,0:T(8,128)(2,1)S(1)}, bf16[640,640]{1,0:T(8,128)(2,1)S(1)}, u32[]{:S(2)}, u32[]{:S(2)}) %collective-permute-start.25) | collective-permute-done | bytes 819232 | tf_op jit(solution)/shard_map/ppermute | solution.py:253
  185.3 2.0 %shard_map.90 = (bf16[192,640]{1,0:T(8,128)(2,1)S(1)}, bf16[192,640]{1,0:T(8,128)(2,1)S(1)}) custom-call(f32[40,128]{1,0:T(8,128)S(1)} %bitcast.6, bf16[192,1280]{1,0:T(8,128)(2,1)S(1)} %shard_map.84.refs_0_, bf16[192,1280]{1,0:T(8,128)(2,1)S(1)} %shard_map.85.refs_1_, bf16[192,1280]{1,0:T(8,128)(2,1)S(1)} %collective-permute-done.5.refs_2_, ...), custom_call_target="tpu_custom_call" | custom-call | tf_op jit(solution)/shard_map/pallas_call | solution.py:198
  187.3 1.0 collective-permute-start.26
  188.3 0.7 shard_map.93
  189.1 1.6 collective-permute-start.28
  190.8 1.2 shard_map.91.refs_0_
  191.9 4.7 %collective-permute-done.27.refs_1_ = bf16[192,640]{1,0:T(8,128)(2,1)S(1)} collective-permute-done((bf16[192,640]{1,0:T(8,128)(2,1)S(1)}, bf16[192,640]{1,0:T(8,128)(2,1)S(1)}, u32[]{:S(2)}, u32[]{:S(2)}) %collective-permute-start.27) | collective-permute-done | bytes 245792 | tf_op jit(solution)/shard_map/ppermute | solution.py:250
  196.6 5.5 %collective-permute-done.28.refs_2_ = bf16[192,640]{1,0:T(8,128)(2,1)S(1)} collective-permute-done((bf16[192,640]{1,0:T(8,128)(2,1)S(1)}, bf16[192,640]{1,0:T(8,128)(2,1)S(1)}, u32[]{:S(2)}, u32[]{:S(2)}) %collective-permute-start.28) | collective-permute-done | bytes 245792 | tf_op jit(solution)/shard_map/ppermute | solution.py:250
  202.0 0.8 shard_map.94
  (39 shorter events, 2.5 us)
Async XLA Ops:
  0.0 1.2 copy-start
  1.2 1.2 copy-start.1
  2.4 0.7 copy-start.4
  4.8 80.6 %copy-start.5 = (f32[2560]{0:T(1024)S(1)}, f32[2560]{0:T(1024)}, u32[]{:S(2)}) copy-start(f32[2560]{0:T(1024)} %param.11) | copy-start | bytes 30724
  4.8 57.5 %collective-permute-start.2 = (bf16[192,2560]{1,0:T(8,128)(2,1)}, bf16[192,2560]{1,0:T(8,128)(2,1)S(1)}, u32[]{:S(2)}, u32[]{:S(2)}) collective-permute-start(bf16[192,2560]{1,0:T(8,128)(2,1)} %get-tuple-element.20), channel_id=1, source_target_pairs={{3,4},{7,8},{11,12},{4,3},{8,7},{12,11},{19,20},{23,24},{27,28},{2... | collective-permute-start | bytes 2949128 | tf_op jit(solution)/shard_map/ppermute | solution.py:259
  5.7 79.7 %copy-start.2 = (bf16[192,2560]{1,0:T(8,128)(2,1)S(1)}, bf16[192,2560]{1,0:T(8,128)(2,1)}, u32[]{:S(2)}) copy-start(bf16[192,2560]{1,0:T(8,128)(2,1)} %x_ref.1) | copy-start | bytes 2949124
  7.1 88.2 %copy-start.6 = (s32[1,2]{1,0:T(1,128)S(1)}, s32[1,2]{1,0:T(1,128)}, u32[]{:S(2)}) copy-start(s32[1,2]{1,0:T(1,128)} %reach_ref.3) | copy-start | bytes 28
  7.1 8.8 %collective-permute-start.7 = (bf16[160,640]{1,0:T(8,128)(2,1)S(1)}, bf16[160,640]{1,0:T(8,128)(2,1)S(1)}, u32[]{:S(2)}, u32[]{:S(2)}) collective-permute-start(bf16[160,640]{1,0:T(8,128)(2,1)S(1)} %get-tuple-element.22), channel_id=1, source_target_pairs={{0,1},{1,0},{2,3},{3,2},{4,5},{5,4},{6,7},{7,6},{8,9},{9,8},{10,11... | collective-permute-start | bytes 614408 | tf_op jit(solution)/shard_map/ppermute | solution.py:250
  9.9 16.2 %collective-permute-start.8 = (bf16[160,640]{1,0:T(8,128)(2,1)S(1)}, bf16[160,640]{1,0:T(8,128)(2,1)S(1)}, u32[]{:S(2)}, u32[]{:S(2)}) collective-permute-start(bf16[160,640]{1,0:T(8,128)(2,1)S(1)} %get-tuple-element.23), channel_id=1, source_target_pairs={{0,2},{1,3},{2,0},{3,1},{4,6},{5,7},{6,4},{7,5},{8,10},{9,11},{10,... | collective-permute-start | bytes 614408 | tf_op jit(solution)/shard_map/ppermute | solution.py:250
  11.5 74.4 %collective-permute-start = (bf16[192,5120]{1,0:T(8,128)(2,1)S(1)}, bf16[192,5120]{1,0:T(8,128)(2,1)S(1)}, u32[]{:S(2)}, u32[]{:S(2)}) collective-permute-start(bf16[192,5120]{1,0:T(8,128)(2,1)S(1)} %get-tuple-element.19.k_ref.v_ref), channel_id=1, source_target_pairs={{0,1},{1,2},{2,3},{4,5},{5,6},{6,7},{8,9},{9,10},{10,11},{12,13},{... | collective-permute-start | bytes 5898248 | tf_op jit(solution)/shard_map/ppermute | solution.py:259
  13.7 72.2 %collective-permute-start.1 = (bf16[192,5120]{1,0:T(8,128)(2,1)S(1)}, bf16[192,5120]{1,0:T(8,128)(2,1)S(1)}, u32[]{:S(2)}, u32[]{:S(2)}) collective-permute-start(bf16[192,5120]{1,0:T(8,128)(2,1)S(1)} %get-tuple-element.19.k_ref.v_ref), channel_id=1, source_target_pairs={{1,0},{2,1},{3,2},{5,4},{6,5},{7,6},{9,8},{10,9},{11,10},{13,12},{... | collective-permute-start | bytes 5898248 | tf_op jit(solution)/shard_map/ppermute | solution.py:259
  15.9 50.8 %collective-permute-start.3 = (bf16[192,2560]{1,0:T(8,128)(2,1)}, bf16[192,2560]{1,0:T(8,128)(2,1)S(1)}, u32[]{:S(2)}, u32[]{:S(2)}) collective-permute-start(bf16[192,2560]{1,0:T(8,128)(2,1)} %v_ref.1), channel_id=1, source_target_pairs={{0,2},{3,1},{4,6},{7,5},{8,10},{11,9},{12,14},{15,13},{16,18},{19,... | collective-permute-start | bytes 2949128 | tf_op jit(solution)/shard_map/ppermute | solution.py:259
  26.0 36.0 %collective-permute-start.9 = (bf16[160,640]{1,0:T(8,128)(2,1)S(1)}, bf16[160,640]{1,0:T(8,128)(2,1)S(1)}, u32[]{:S(2)}, u32[]{:S(2)}) collective-permute-start(bf16[160,640]{1,0:T(8,128)(2,1)S(1)} %get-tuple-element.24), channel_id=1, source_target_pairs={{0,3},{1,2},{2,1},{3,0},{4,7},{5,6},{6,5},{7,4},{8,11},{9,10},{10,... | collective-permute-start | bytes 614408 | tf_op jit(solution)/shard_map/ppermute | solution.py:250
  62.2 11.6 %collective-permute-start.10 = (bf16[640,640]{1,0:T(8,128)(2,1)S(1)}, bf16[640,640]{1,0:T(8,128)(2,1)S(1)}, u32[]{:S(2)}, u32[]{:S(2)}) collective-permute-start(bf16[640,640]{1,0:T(8,128)(2,1)S(1)} %join.1.refs_4_), channel_id=1, source_target_pairs={{0,4},{1,5},{2,6},{3,7},{4,0},{5,1},{6,2},{7,3},{8,12},{9,13},{10,... | collective-permute-start | bytes 2457608 | tf_op jit(solution)/shard_map/ppermute | solution.py:256
  62.3 21.8 %collective-permute-start.12 = (bf16[640,640]{1,0:T(8,128)(2,1)S(1)}, bf16[640,640]{1,0:T(8,128)(2,1)S(1)}, u32[]{:S(2)}, u32[]{:S(2)}) collective-permute-start(bf16[640,640]{1,0:T(8,128)(2,1)S(1)} %join.1.refs_4_), channel_id=1, source_target_pairs={{4,8},{5,9},{6,10},{7,11},{8,4},{9,5},{10,6},{11,7},{20,24},{21,25... | collective-permute-start | bytes 2457608 | tf_op jit(solution)/shard_map/ppermute | solution.py:256
  66.8 28.6 %collective-permute-start.4 = (bf16[192,2560]{1,0:T(8,128)(2,1)S(1)}, bf16[192,2560]{1,0:T(8,128)(2,1)S(1)}, u32[]{:S(2)}, u32[]{:S(2)}) collective-permute-start(bf16[192,2560]{1,0:T(8,128)(2,1)S(1)} %collective-permute-done.3), channel_id=1, source_target_pairs={{1,4},{5,8},{9,12},{6,3},{10,7},{14,11},{17,20},{21,24},{25,28},{2... | collective-permute-start | bytes 2949128 | tf_op jit(solution)/shard_map/ppermute | solution.py:259
  73.7 30.4 %collective-permute-start.11 = (bf16[640,640]{1,0:T(8,128)(2,1)S(1)}, bf16[640,640]{1,0:T(8,128)(2,1)S(1)}, u32[]{:S(2)}, u32[]{:S(2)}) collective-permute-start(bf16[640,640]{1,0:T(8,128)(2,1)S(1)} %collective-permute-done.10.refs_5_), channel_id=1, source_target_pairs={{4,8},{5,9},{6,10},{7,11},{8,4},{9,5},{10,6},{11,7},{20,24},{21,25... | collective-permute-start | bytes 2457608 | tf_op jit(solution)/shard_map/ppermute | solution.py:256
  84.1 26.5 %collective-permute-start.13 = (bf16[640,640]{1,0:T(8,128)(2,1)S(1)}, bf16[640,640]{1,0:T(8,128)(2,1)S(1)}, u32[]{:S(2)}, u32[]{:S(2)}) collective-permute-start(bf16[640,640]{1,0:T(8,128)(2,1)S(1)} %collective-permute-done.12.inner_ref), channel_id=1, source_target_pairs={{4,0},{5,1},{6,2},{7,3},{8,12},{9,13},{10,14},{11,15},{20,16},{21,... | collective-permute-start | bytes 2457608 | tf_op jit(solution)/shard_map/ppermute | solution.py:256
  99.8 12.4 %collective-permute-start.16 = (bf16[192,1280]{1,0:T(8,128)(2,1)S(1)}, bf16[192,1280]{1,0:T(8,128)(2,1)S(1)}, u32[]{:S(2)}, u32[]{:S(2)}) collective-permute-start(bf16[192,1280]{1,0:T(8,128)(2,1)S(1)} %shard_map.84.refs_0_), channel_id=1, source_target_pairs={{0,2},{1,3},{2,0},{3,1},{4,6},{5,7},{6,4},{7,5},{8,10},{9,11},{10,... | collective-permute-start | bytes 1474568 | tf_op jit(solution)/shard_map/ppermute | solution.py:250
  104.1 13.8 %collective-permute-start.14 = (bf16[640,640]{1,0:T(8,128)(2,1)S(1)}, bf16[640,640]{1,0:T(8,128)(2,1)S(1)}, u32[]{:S(2)}, u32[]{:S(2)}) collective-permute-start(bf16[640,640]{1,0:T(8,128)(2,1)S(1)} %collective-permute-done.11.inner_ref), channel_id=1, source_target_pairs={{4,0},{5,1},{6,2},{7,3},{8,12},{9,13},{10,14},{11,15},{20,16},{21,... | collective-permute-start | bytes 2457608 | tf_op jit(solution)/shard_map/ppermute | solution.py:256
  105.4 7.4 %collective-permute-start.5 = (bf16[192,1280]{1,0:T(8,128)(2,1)S(1)}, bf16[192,1280]{1,0:T(8,128)(2,1)S(1)}, u32[]{:S(2)}, u32[]{:S(2)}) collective-permute-start(bf16[192,1280]{1,0:T(8,128)(2,1)S(1)} %shard_map.84.refs_0_), channel_id=1, source_target_pairs={{0,1},{1,0},{2,3},{3,2},{4,5},{5,4},{6,7},{7,6},{8,9},{9,8},{10,11... | collective-permute-start | bytes 1474568 | tf_op jit(solution)/shard_map/ppermute | solution.py:250
  110.0 14.8 %copy-start.3 = (f32[5120]{0:T(1024)S(1)}, f32[5120]{0:T(1024)}, u32[]{:S(2)}) copy-start(f32[5120]{0:T(1024)} %param.14) | copy-start | bytes 61444
  110.1 8.3 %collective-permute-start.6 = (bf16[192,1280]{1,0:T(8,128)(2,1)S(1)}, bf16[192,1280]{1,0:T(8,128)(2,1)S(1)}, u32[]{:S(2)}, u32[]{:S(2)}) collective-permute-start(bf16[192,1280]{1,0:T(8,128)(2,1)S(1)} %shard_map.85.refs_1_), channel_id=1, source_target_pairs={{0,1},{1,0},{2,3},{3,2},{4,5},{5,4},{6,7},{7,6},{8,9},{9,8},{10,11... | collective-permute-start | bytes 1474568 | tf_op jit(solution)/shard_map/ppermute | solution.py:250
  110.6 12.7 %collective-permute-start.17 = (bf16[192,1280]{1,0:T(8,128)(2,1)S(1)}, bf16[192,1280]{1,0:T(8,128)(2,1)S(1)}, u32[]{:S(2)}, u32[]{:S(2)}) collective-permute-start(bf16[192,1280]{1,0:T(8,128)(2,1)S(1)} %shard_map.85.refs_1_), channel_id=1, source_target_pairs={{0,2},{1,3},{2,0},{3,1},{4,6},{5,7},{6,4},{7,5},{8,10},{9,11},{10,... | collective-permute-start | bytes 1474568 | tf_op jit(solution)/shard_map/ppermute | solution.py:250
  112.2 11.4 %collective-permute-start.18 = (bf16[192,1280]{1,0:T(8,128)(2,1)S(1)}, bf16[192,1280]{1,0:T(8,128)(2,1)S(1)}, u32[]{:S(2)}, u32[]{:S(2)}) collective-permute-start(bf16[192,1280]{1,0:T(8,128)(2,1)S(1)} %collective-permute-done.16.refs_0_.refs_1_), channel_id=1, source_target_pairs={{0,1},{1,0},{2,3},{3,2},{4,5},{5,4},{6,7},{7,6},{8,9},{9,8},{10,11... | collective-permute-start | bytes 1474568 | tf_op jit(solution)/shard_map/ppermute | solution.py:250
  112.9 19.7 %collective-permute-start.22 = (bf16[640,640]{1,0:T(8,128)(2,1)S(1)}, bf16[640,640]{1,0:T(8,128)(2,1)S(1)}, u32[]{:S(2)}, u32[]{:S(2)}) collective-permute-start(bf16[640,640]{1,0:T(8,128)(2,1)S(1)} %join.1.refs_4_), channel_id=1, source_target_pairs={{0,16},{16,0},{1,17},{17,1},{2,18},{18,2},{3,19},{19,3},{4,20},{20... | collective-permute-start | bytes 2457608 | tf_op jit(solution)/shard_map/ppermute | solution.py:253
  117.9 32.3 %collective-permute-start.23 = (bf16[640,640]{1,0:T(8,128)(2,1)S(1)}, bf16[640,640]{1,0:T(8,128)(2,1)S(1)}, u32[]{:S(2)}, u32[]{:S(2)}) collective-permute-start(bf16[640,640]{1,0:T(8,128)(2,1)S(1)} %collective-permute-done.10.refs_5_), channel_id=1, source_target_pairs={{0,16},{16,0},{1,17},{17,1},{2,18},{18,2},{3,19},{19,3},{4,20},{20... | collective-permute-start | bytes 2457608 | tf_op jit(solution)/shard_map/ppermute | solution.py:253
  118.4 49.3 %collective-permute-start.24 = (bf16[640,640]{1,0:T(8,128)(2,1)S(1)}, bf16[640,640]{1,0:T(8,128)(2,1)S(1)}, u32[]{:S(2)}, u32[]{:S(2)}) collective-permute-start(bf16[640,640]{1,0:T(8,128)(2,1)S(1)} %shard_map.86.refs_6_), channel_id=1, source_target_pairs={{0,16},{16,0},{1,17},{17,1},{2,18},{18,2},{3,19},{19,3},{4,20},{20... | collective-permute-start | bytes 2457608 | tf_op jit(solution)/shard_map/ppermute | solution.py:253
  123.3 61.9 %collective-permute-start.25 = (bf16[640,640]{1,0:T(8,128)(2,1)S(1)}, bf16[640,640]{1,0:T(8,128)(2,1)S(1)}, u32[]{:S(2)}, u32[]{:S(2)}) collective-permute-start(bf16[640,640]{1,0:T(8,128)(2,1)S(1)} %shard_map.87.refs_7_), channel_id=1, source_target_pairs={{0,16},{16,0},{1,17},{17,1},{2,18},{18,2},{3,19},{19,3},{4,20},{20... | collective-permute-start | bytes 2457608 | tf_op jit(solution)/shard_map/ppermute | solution.py:253
  123.6 3.3 %collective-permute-start.19 = (bf16[192,1280]{1,0:T(8,128)(2,1)S(1)}, bf16[192,1280]{1,0:T(8,128)(2,1)S(1)}, u32[]{:S(2)}, u32[]{:S(2)}) collective-permute-start(bf16[192,1280]{1,0:T(8,128)(2,1)S(1)} %collective-permute-done.17.refs_1_.refs_2_), channel_id=1, source_target_pairs={{0,1},{1,0},{2,3},{3,2},{4,5},{5,4},{6,7},{7,6},{8,9},{9,8},{10,11... | collective-permute-start | bytes 1474568 | tf_op jit(solution)/shard_map/ppermute | solution.py:250
  126.9 62.2 %collective-permute-start.15 = (bf16[192,640]{1,0:T(8,128)(2,1)S(1)}, bf16[192,640]{1,0:T(8,128)(2,1)S(1)}, u32[]{:S(2)}, u32[]{:S(2)}) collective-permute-start(bf16[192,640]{1,0:T(8,128)(2,1)S(1)} %get-tuple-element.26), channel_id=1, source_target_pairs={{0,1},{1,0},{2,3},{3,2},{4,5},{5,4},{6,7},{7,6},{8,9},{9,8},{10,11... | collective-permute-start | bytes 737288 | tf_op jit(solution)/shard_map/ppermute | solution.py:250
  132.6 58.2 %collective-permute-start.20 = (bf16[192,640]{1,0:T(8,128)(2,1)S(1)}, bf16[192,640]{1,0:T(8,128)(2,1)S(1)}, u32[]{:S(2)}, u32[]{:S(2)}) collective-permute-start(bf16[192,640]{1,0:T(8,128)(2,1)S(1)} %get-tuple-element.27), channel_id=1, source_target_pairs={{0,2},{1,3},{2,0},{3,1},{4,6},{5,7},{6,4},{7,5},{8,10},{9,11},{10,... | collective-permute-start | bytes 737288 | tf_op jit(solution)/shard_map/ppermute | solution.py:250
  150.2 40.6 %collective-permute-start.21 = (bf16[192,640]{1,0:T(8,128)(2,1)S(1)}, bf16[192,640]{1,0:T(8,128)(2,1)S(1)}, u32[]{:S(2)}, u32[]{:S(2)}) collective-permute-start(bf16[192,640]{1,0:T(8,128)(2,1)S(1)} %get-tuple-element.28), channel_id=1, source_target_pairs={{0,3},{1,2},{2,1},{3,0},{4,7},{5,6},{6,5},{7,4},{8,11},{9,10},{10,... | collective-permute-start | bytes 737288 | tf_op jit(solution)/shard_map/ppermute | solution.py:250
  187.3 3.4 %collective-permute-start.26 = (bf16[192,640]{1,0:T(8,128)(2,1)S(1)}, bf16[192,640]{1,0:T(8,128)(2,1)S(1)}, u32[]{:S(2)}, u32[]{:S(2)}) collective-permute-start(bf16[192,640]{1,0:T(8,128)(2,1)S(1)} %get-tuple-element.30), channel_id=1, source_target_pairs={{0,1},{1,0},{2,3},{3,2},{4,5},{5,4},{6,7},{7,6},{8,9},{9,8},{10,11... | collective-permute-start | bytes 737288 | tf_op jit(solution)/shard_map/ppermute | solution.py:250
  189.0 7.6 %collective-permute-start.27 = (bf16[192,640]{1,0:T(8,128)(2,1)S(1)}, bf16[192,640]{1,0:T(8,128)(2,1)S(1)}, u32[]{:S(2)}, u32[]{:S(2)}) collective-permute-start(bf16[192,640]{1,0:T(8,128)(2,1)S(1)} %get-tuple-element.31), channel_id=1, source_target_pairs={{0,2},{1,3},{2,0},{3,1},{4,6},{5,7},{6,4},{7,5},{8,10},{9,11},{10,... | collective-permute-start | bytes 737288 | tf_op jit(solution)/shard_map/ppermute | solution.py:250
  189.1 12.9 %collective-permute-start.28 = (bf16[192,640]{1,0:T(8,128)(2,1)S(1)}, bf16[192,640]{1,0:T(8,128)(2,1)S(1)}, u32[]{:S(2)}, u32[]{:S(2)}) collective-permute-start(bf16[192,640]{1,0:T(8,128)(2,1)S(1)} %get-tuple-element.32), channel_id=1, source_target_pairs={{0,3},{1,2},{2,1},{3,0},{4,7},{5,6},{6,5},{7,4},{8,11},{9,10},{10,... | collective-permute-start | bytes 737288 | tf_op jit(solution)/shard_map/ppermute | solution.py:250
